TPU v7x, 256 devices: a whole 4x4x8 slice. The times are simulated.
256 devices in a mesh: gx: 4 (over x), gy: 16 (over z_lo, y), gz: 4 (over z_hi, core).
Axes of the slice: x: 4, y: 4, z: 8 (z_hi: 2, z_lo: 4; z = z_hi * 4 + z_lo), core: 2. Of those that a mesh axis runs over, the one named last changes fastest.
Arguments:
- atom_embedding: bfloat16 [4, 16, 4, 64, 512], P('gx', 'gy', 'gz'), may hold values from -6 to 6
- output_adjoint: bfloat16 [4, 16, 4, 64, 512], P('gx', 'gy', 'gz'), may hold values from -6 to 6
- fractional_coords: float32 [4, 16, 4, 3, 512], P('gx', 'gy', 'gz'), may hold values from 0 to 1, as said below
- element_labels: int32 [4, 16, 4, 512], P('gx', 'gy', 'gz'), may hold values from 0 to 3
- adjacent_ghost_entries: int32 [4, 16, 4, 16, 512], P('gx', 'gy', 'gz'), may hold values from 0 to 13823, as said below
- miller_triples: int32 [3, 2048], replicated, may hold values from -8 to 8
- reciprocal_kernel: float32 [2048, 64], replicated, may hold values from 0.02 to 0.2
- channel_mixing_matrix: bfloat16 [64, 64], replicated, may hold values from -0.75 to 0.75
- element_channel_factor: float32 [4, 64], replicated, may hold values from 0.25 to 1.75
- distance_kernel: float32 [16, 64], replicated, may hold values from -1.5 to 1.5
Outputs:
- atom_grad: bfloat16 [4, 16, 4, 64, 512], P('gx', 'gy', 'gz')
- position_grad: float32 [4, 16, 4, 3, 512], P('gx', 'gy', 'gz')
- weight_grad: float32 [64, 64], replicated
- radial_grad: float32 [16, 64], replicated
- filter_grad: float32 [2048, 64], P(('gx', 'gy', 'gz'))
Inputs may be any that keep to these rules, and one draw needn't show every extreme that they name: `adjacent_ghost_entries`: the atoms of a brick form 32 blocks of 16 in order; block q < 27 is the cell of offset (q // 9 - 1, (q // 3) % 3 - 1, q % 3 - 1) of the brick, blocks 27 to 31 lie in its central cell. A ghost entry e names atom e % 512 of slot e // 512; an entry in a slot of offset o names an atom of a block whose cell offset equals -o in every dimension where o is not zero, and o is zero in every dimension where the listing atom's cell offset is zero; every slot occurs. `fractional_coords`: an atom of a block whose cell offset is -1 or 1 in a dimension lies within a quarter of the brick length of that face in that dimension. `miller_triples`: integer components; any triple may occur, the zero triple too.
All inputs are finite; a program needn't handle non-finite values.
Results may differ from a plain program's by a relative error of at most 0.0053.
Values may be sent and summed in bfloat16 or wider, within the bound.
No kernel may reach another device: no remote copies, remote signals or barrier semaphores. Data moves between devices by JAX's collectives and lax.ppermute only.
A program may use at most 128 MiB of HBM per device.

v0:
```python
import functools
import math

import jax
import jax.numpy as jnp
from jax import lax
from jax.sharding import Mesh
from jax.sharding import PartitionSpec as P

GY = ("gy_0", "gy_1")
GZ = ("gz_0", "gz_1")
GX_GY_GZ = ("gx", "gy_0", "gy_1", "gz_0", "gz_1")


circle_angle = 2.0 * math.pi
reach_sq = 0.75
block_len = 512


def from_behind(x, axis, by):
    devices = lax.axis_size(axis)
    return lax.ppermute(x, axis, [(i, (i + by) % devices) for i in range(devices)])


def shortened(x):
    return jax.tree.map(lambda a: a.astype(jnp.bfloat16) if a.dtype == jnp.float32 else a, x)


def padded(x, sides, width):
    for axis, dim in sides:
        devices, length = (lax.axis_size(axis), x.shape[dim])
        up = [(i, (i + 1) % devices) for i in range(devices)]
        down = [(j, i) for i, j in up]
        last = lax.slice_in_dim(x, length - width, length, axis=dim)
        initial = lax.slice_in_dim(x, 0, width, axis=dim)
        before = lax.ppermute(last, axis, up)
        after = lax.ppermute(initial, axis, down)
        x = jnp.concatenate([before, x, after], axis=dim)
    return x


def by_axis(x, axes):
    return functools.reduce(lax.psum, axes, x)


def phases(local_pos, anchor, reciprocal_points_rescaled):
    absolute = local_pos + anchor[:, None]
    angles = absolute[0][:, None] * reciprocal_points_rescaled[0][None, :]
    angles = angles + absolute[1][:, None] * reciprocal_points_rescaled[1][None, :]
    angles = angles + absolute[2][:, None] * reciprocal_points_rescaled[2][None, :]
    return (jnp.cos(angles).astype(jnp.bfloat16), jnp.sin(angles).astype(jnp.bfloat16))


def structure_terms(cos_part, sin_part, stacked):
    contract = (((0,), (1,)), ((), ()))
    with_cos = lax.dot_general(cos_part, stacked, contract, preferred_element_type=jnp.float32)
    with_sin = lax.dot_general(sin_part, stacked, contract, preferred_element_type=jnp.float32)
    return jnp.concatenate([with_cos, with_sin], axis=1)


def coefficients(totals, filt_rows, norm_atoms, norm_k):
    channels = filt_rows.shape[1]
    cos_struct = totals[:, 0:channels] * norm_atoms
    cos_back = totals[:, channels : 2 * channels] * norm_k
    sin_struct = totals[:, 2 * channels : 3 * channels] * norm_atoms
    sin_back = totals[:, 3 * channels : 4 * channels] * norm_k
    coeffs = jnp.concatenate(
        [
            norm_atoms * filt_rows * cos_back,
            norm_k * filt_rows * cos_struct,
            norm_atoms * filt_rows * sin_back,
            norm_k * filt_rows * sin_struct,
        ],
        axis=1,
    )
    return (coeffs.astype(jnp.bfloat16), cos_struct * cos_back + sin_struct * sin_back)


def ewald_pieces(
    running, piece_rows, start_at, cos_all, sin_all, stacked, reciprocal_points_rescaled
):
    count_rows = piece_rows.shape[0]
    channels = stacked.shape[0] // 2
    cos_part = lax.dynamic_slice_in_dim(cos_all, start_at, count_rows, 1)
    sin_part = lax.dynamic_slice_in_dim(sin_all, start_at, count_rows, 1)
    kv_part = lax.dynamic_slice_in_dim(reciprocal_points_rescaled, start_at, count_rows, 1)
    contract = (((0,), (1,)), ((), ()))
    atom_part = lax.dot_general(
        piece_rows[:, 0:channels], cos_part, contract, preferred_element_type=jnp.float32
    )
    atom_part = atom_part + lax.dot_general(
        piece_rows[:, 2 * channels : 3 * channels],
        sin_part,
        contract,
        preferred_element_type=jnp.float32,
    )
    along_u = lax.dot_general(
        stacked, piece_rows[:, 0 : 2 * channels], contract, preferred_element_type=jnp.float32
    )
    along_v = lax.dot_general(
        stacked,
        piece_rows[:, 2 * channels : 4 * channels],
        contract,
        preferred_element_type=jnp.float32,
    )
    angle_grad = along_v * cos_part.astype(jnp.float32) - along_u * sin_part.astype(jnp.float32)
    pos_part = lax.dot_general(
        kv_part, angle_grad, (((1,), (1,)), ((), ())), precision=lax.Precision.HIGHEST
    )
    return (running[0] + atom_part, running[1] + pos_part)


def species_gains(table, kinds):
    onehot = (kinds[None, :] == jnp.arange(table.shape[0], dtype=jnp.int32)[:, None]).astype(
        jnp.float32
    )
    return lax.dot_general(table, onehot, (((0,), (0,)), ((), ())), precision=lax.Precision.HIGHEST)


def offset_table():
    steps_one = jnp.arange(3, dtype=jnp.float32) - 1.0
    along_x = jnp.broadcast_to(steps_one[:, None, None], (3, 3, 3))
    along_y = jnp.broadcast_to(steps_one[None, :, None], (3, 3, 3))
    along_z = jnp.broadcast_to(steps_one[None, None, :], (3, 3, 3))
    return jnp.stack([along_x, along_y, along_z], axis=-1)


def short_range(ghost_values, ghost_places, neighbour_ids, radial_weights):
    channels = ghost_values.shape[1]
    flat_z = jnp.transpose(ghost_values, (1, 0, 2)).reshape(channels, -1)
    flat_pos = jnp.transpose(ghost_places, (1, 0, 2)).reshape(3, -1)
    near_z = flat_z[:, neighbour_ids]
    near_pos = flat_pos[:, neighbour_ids]
    relative = near_pos - ghost_places[13][:, None, :]
    dist_sq = jnp.sum(relative * relative, axis=0)
    basis_count = radial_weights.shape[0]
    spacing = reach_sq / (basis_count - 1)
    centres = jnp.arange(basis_count, dtype=jnp.float32) * spacing
    radial_basis = jnp.exp(
        -jnp.square((dist_sq[None, :, :] - centres[:, None, None]) / (2.0 * spacing))
    )
    filters = jnp.einsum(
        "bc,bja->cja", radial_weights, radial_basis, precision=lax.Precision.HIGHEST
    )
    agg = jnp.sum(filters * near_z, axis=1) * neighbour_ids.shape[0] ** (-0.5)
    return jax.nn.silu(agg)


def local_backward(ghost_z, ghost_pos, neighbour_ids, distance_kernel, upstream):

    def mapped(ghost_values, ghost_places, radial_weights):
        return short_range(ghost_values, ghost_places, neighbour_ids, radial_weights)

    _, pullback = jax.vjp(mapped, ghost_z.astype(jnp.float32), ghost_pos, distance_kernel)
    return pullback(upstream.astype(jnp.float32))


def fold_gx(grad_z, grad_p, along_axis):
    total_z = lax.index_in_dim(grad_z, 1, along_axis, False)
    total_p = lax.index_in_dim(grad_p, 1, along_axis, False)
    for step_by in (1, -1):
        moved_z, moved_p = (
            from_behind(
                lax.index_in_dim(grad_z, 1 + step_by, along_axis, False).astype(jnp.bfloat16),
                "gx",
                step_by,
            ).astype(jnp.float32),
            from_behind(
                lax.index_in_dim(grad_p, 1 + step_by, along_axis, False).astype(jnp.bfloat16),
                "gx",
                step_by,
            ).astype(jnp.float32),
        )
        total_z = total_z + moved_z
        total_p = total_p + moved_p
    return (total_z, total_p)


def fold_gy(grad_z, grad_p, along_axis):
    total_z = lax.index_in_dim(grad_z, 1, along_axis, False)
    total_p = lax.index_in_dim(grad_p, 1, along_axis, False)
    for step_by in (1, -1):
        moved_z, moved_p = from_behind(
            (
                shortened(lax.index_in_dim(grad_z, 1 + step_by, along_axis, False)),
                shortened(lax.index_in_dim(grad_p, 1 + step_by, along_axis, False)),
            ),
            GY,
            step_by,
        )
        total_z = total_z + moved_z
        total_p = total_p + moved_p
    return (total_z, total_p)


def fold_gz(grad_z, grad_p, along_axis):
    total_z = lax.index_in_dim(grad_z, 1, along_axis, False)
    total_p = lax.index_in_dim(grad_p, 1, along_axis, False)
    for step_by in (1, -1):
        moved_z, moved_p = from_behind(
            (
                lax.index_in_dim(grad_z, 1 + step_by, along_axis, False),
                lax.index_in_dim(grad_p, 1 + step_by, along_axis, False),
            ),
            GZ,
            step_by,
        )
        total_z = total_z + moved_z
        total_p = total_p + moved_p
    return (total_z, total_p)


def shards(
    atom_embedding,
    output_adjoint,
    fractional_coords,
    element_labels,
    adjacent_ghost_entries,
    miller_triples,
    reciprocal_kernel,
    channel_mixing_matrix,
    element_channel_factor,
    distance_kernel,
):
    own_features = atom_embedding[0, 0, 0]
    own_cotangent = output_adjoint[0, 0, 0]
    own_positions = fractional_coords[0, 0, 0]
    channels = own_features.shape[0]
    atom_count = own_features.shape[1]
    reciprocal_total = miller_triples.shape[1]
    device_count = lax.axis_size(GX_GY_GZ)
    norm_atoms = (atom_count * device_count) ** (-0.5)
    norm_k = reciprocal_total ** (-0.5)
    accumulated_entries = jnp.array(
        [lax.axis_size("gx"), lax.axis_size(GY), lax.axis_size(GZ)], jnp.float32
    )
    reciprocal_points_rescaled = (
        miller_triples.astype(jnp.float32) * (circle_angle / accumulated_entries)[:, None]
    )
    anchor = jnp.stack([lax.axis_index("gx"), lax.axis_index(GY), lax.axis_index(GZ)]).astype(
        jnp.float32
    )
    cos_all, sin_all = phases(own_positions, anchor, reciprocal_points_rescaled)
    stacked = jnp.concatenate([own_features, own_cotangent], axis=0)
    share_rows = reciprocal_total // device_count
    share_start = lax.axis_index(GX_GY_GZ) * share_rows
    zeros_pair = (
        jnp.zeros((channels, atom_count), jnp.float32),
        jnp.zeros((3, atom_count), jnp.float32),
    )
    totals = lax.psum(structure_terms(cos_all, sin_all, stacked), GX_GY_GZ)
    coeffs, filter_full = coefficients(totals, reciprocal_kernel, norm_atoms, norm_k)
    filter_share = lax.dynamic_slice_in_dim(filter_full, share_start, share_rows, 0)
    step_rows = min(block_len, reciprocal_total)
    running = zeros_pair
    for offset in range(0, reciprocal_total, step_rows):
        running = ewald_pieces(
            running,
            coeffs[offset : offset + step_rows],
            offset,
            cos_all,
            sin_all,
            stacked,
            reciprocal_points_rescaled,
        )
    ewald_h, ewald_pos = running
    gain_rows = species_gains(element_channel_factor, element_labels[0, 0, 0])
    projected = lax.dot_general(
        channel_mixing_matrix,
        own_features,
        (((0,), (0,)), ((), ())),
        preferred_element_type=jnp.float32,
    )
    z_local = (projected * gain_rows).astype(jnp.bfloat16)
    shifts_all = offset_table().reshape(27, 3)[:, :, None]
    ghost_z = padded(z_local[None, None, None], (("gx", 0), (GY, 1), (GZ, 2)), 1)
    ghost_p = padded(fractional_coords, (("gx", 0), (GY, 1), (GZ, 2)), 1)
    ghost_p = ghost_p.reshape(27, 3, atom_count) + shifts_all
    grad_z, grad_p, grad_radial = local_backward(
        ghost_z.reshape(27, channels, atom_count),
        ghost_p,
        adjacent_ghost_entries[0, 0, 0],
        distance_kernel,
        own_cotangent,
    )
    grad_z = grad_z.reshape(3, 3, 3, channels, atom_count)
    grad_p = grad_p.reshape(3, 3, 3, 3, atom_count)
    grad_z, grad_p = fold_gx(grad_z, grad_p, 0)
    grad_z, grad_p = fold_gy(grad_z, grad_p, 0)
    zgrad, pos_short = fold_gz(grad_z, grad_p, 0)
    zscaled = (zgrad * gain_rows).astype(jnp.bfloat16)
    atom_short = jnp.dot(channel_mixing_matrix, zscaled, preferred_element_type=jnp.float32)
    atom_grad = (own_cotangent.astype(jnp.float32) + ewald_h + atom_short).astype(jnp.bfloat16)
    weight_local = lax.dot_general(
        own_features, zscaled, (((1,), (1,)), ((), ())), preferred_element_type=jnp.float32
    )
    weight_grad, radial_grad = (by_axis(weight_local, GX_GY_GZ), by_axis(grad_radial, GX_GY_GZ))
    position_grad = ewald_pos + pos_short
    return (
        atom_grad[None, None, None],
        position_grad[None, None, None],
        weight_grad,
        radial_grad,
        filter_share,
    )


def solution(mesh):
    finer = Mesh(
        mesh.devices.reshape(mesh.shape["gx"], 4, 4, 2, 2), ("gx", "gy_0", "gy_1", "gz_0", "gz_1")
    )
    in_specs = (
        P("gx", GY, GZ, None, None),
        P("gx", GY, GZ, None, None),
        P("gx", GY, GZ, None, None),
        P("gx", GY, GZ, None),
        P("gx", GY, GZ, None, None),
        P(),
        P(),
        P(),
        P(),
        P(),
    )
    out_specs = (
        P("gx", GY, GZ, None, None),
        P("gx", GY, GZ, None, None),
        P(),
        P(),
        P(GX_GY_GZ, None),
    )
    return jax.shard_map(
        shards, mesh=finer, in_specs=in_specs, out_specs=out_specs, check_vma=False
    )
```

profile of v0, /device:TPU:1, one launch (start us, length us, event | category | flops | bytes accessed | tf_op | source)
XLA Modules:
  0.0 459.9 jit_solution(1965531941578786956)
XLA Ops:
  7.2 2.1 collective-permute-start
  16.8 15.4 %fusion.113 = f32[2048,128]{0,1:T(8,128)S(1)} fusion(bf16[64,512]{1,0:T(8,128)(2,1)} %bitcast.195, bf16[64,512]{1,0:T(8,128)(2,1)} %bitcast.205, f32[2048]{0:T(1024)S(1)} %bitcast.228, f32[512]{0:T(512)S(1)} %bitcast.237, f32[2048]{0:T(1024)S(1)} %bitcast.231, f32[512]{0:T(512)S(1)} %bitcast.240, f32[2048]{0:T(1024)S(1)} %bitcast.225, f32[512]{0:T(512)S(1)} %bitcast.234), kind=kOutput, calls=%fused_computation.203 | convolution fusion | flops 274989056 | bytes 1210368 | tf_op jit(solution)/shard_map/dot_general | solution.py:56
  32.2 14.5 %fusion.114 = f32[2048,128]{0,1:T(8,128)S(1)} fusion(bf16[64,512]{1,0:T(8,128)(2,1)S(1)} %bitcast.196, bf16[64,512]{1,0:T(8,128)(2,1)S(1)} %bitcast.206, f32[2048]{0:T(1024)S(1)} %bitcast.229, f32[512]{0:T(512)S(1)} %bitcast.238, f32[2048]{0:T(1024)S(1)} %bitcast.232, f32[512]{0:T(512)S(1)} %bitcast.241, f32[2048]{0:T(1024)S(1)} %bitcast.226, ...), kind=kOutput, calls=%fused_computation.204 | convolution fusion | flops 274989056 | bytes 1210368 | tf_op jit(solution)/shard_map/dot_general | solution.py:57
  48.3 17.0 %sine_convert_fusion = (bf16[512,2048]{1,0:T(8,128)(2,1)}, bf16[512,2048]{1,0:T(8,128)(2,1)}) fusion(f32[2048]{0:T(1024)S(1)} %bitcast.230, f32[512]{0:T(512)S(1)} %bitcast.239, f32[2048]{0:T(1024)S(1)} %bitcast.233, f32[512]{0:T(512)S(1)} %bitcast.242, f32[2048]{0:T(1024)S(1)} %bitcast.227, f32[512]{0:T(512)S(1)} %bitcast.236), kind=kLoop, calls=%fused_computation.7 | loop fusion | flops 7340032 | bytes 4225024 | tf_op jit(solution)/shard_map/convert_element_type | solution.py:51
  65.4 7.0 %collective-permute-start.3 = (f32[3,1,1,3,512]{4,2,3,1,0:T(1,128)S(1)}, f32[3,1,1,3,512]{4,2,3,1,0:T(1,128)S(1)}, u32[]{:S(2)}, u32[]{:S(2)}) collective-permute-start(f32[3,1,1,3,512]{4,2,3,1,0:T(1,128)S(1)} %constant_dynamic-update-slice_fusion), channel_id=1, source_target_pairs={{4,0},{8,4},{12,8},{16,12},{20,16},{24,20},{28,24},{32,28},{36,32}... | collective-permute-start | bytes 55304 | tf_op jit(solution)/shard_map/ppermute | solution.py:37
  73.3 5.7 %collective-permute-done.2 = f32[3,1,1,3,512]{4,2,3,1,0:T(1,128)S(1)} collective-permute-done((f32[3,1,1,3,512]{4,2,3,1,0:T(1,128)S(1)}, f32[3,1,1,3,512]{4,2,3,1,0:T(1,128)S(1)}, u32[]{:S(2)}, u32[]{:S(2)}) %collective-permute-start.2) | collective-permute-done | bytes 18464 | tf_op jit(solution)/shard_map/ppermute | solution.py:36
  79.0 3.3 collective-permute-start.5
  82.3 4.2 collective-permute-start.4
  86.6 1.8 collective-permute-start.8
  89.4 2.3 collective-permute-done.9
  91.7 4.5 collective-permute-done.8
  96.4 5.6 %collective-permute-start.10 = (bf16[3,3,1,64,512]{4,3,2,1,0:T(8,128)(2,1)S(1)}, bf16[3,3,1,64,512]{4,3,2,1,0:T(8,128)(2,1)S(1)}, u32[]{:S(2)}, u32[]{:S(2)}) collective-permute-start(bf16[3,3,1,64,512]{4,3,2,1,0:T(8,128)(2,1)S(1)} %pad_maximum_fusion.2), channel_id=1, source_target_pairs={{0,1},{1,2},{2,3},{3,0},{4,5},{5,6},{6,7},{7,4},{8,9},{9,10},{10,1... | collective-permute-start | bytes 1769480 | tf_op jit(solution)/shard_map/ppermute | solution.py:36
  102.3 4.1 copy.37
  106.5 30.7 %gather_fusion = f32[8192,3]{1,0:T(8,128)} fusion(f32[3,13824]{0,1:T(8,128)} %bitcast.194, s32[8192]{0:T(1024)S(1)} %broadcast_clamp_fusion), kind=kCustom, calls=%fused_computation | custom fusion | bytes 229376 | tf_op jit(solution)/shard_map/jvp()/gather | solution.py:133
  137.2 3.9 multiply_reduce_fusion
  142.0 4.4 copy.39
  146.5 33.4 %gather_fusion.1 = f32[8192,64]{1,0:T(8,128)} fusion(f32[64,13824]{0,1:T(8,128)} %bitcast.187, s32[8192]{0:T(1024)} %copy-done.16), kind=kCustom, calls=%fused_computation.1 | custom fusion | bytes 4227072 | tf_op jit(solution)/shard_map/jvp()/gather | solution.py:132
  179.9 2.9 copy.41
  182.8 2.1 fusion.4
  187.2 3.1 add_multiply_fusion
  190.3 2.5 reduce_sum.41
  193.5 2.8 copy.54
  196.3 47.7 %scatter_custom_fusion = f32[64,13824]{0,1:T(8,128)} fusion(s32[8192]{0:T(1024)} %bitcast.221, f32[8192,64]{1,0:T(8,128)} %bitcast.216, f32[]{:T(128)} %constant.22.clone.1), kind=kCustom, calls=%fused_computation.13 | custom fusion | flops 524288 | bytes 3539456 | tf_op jit(solution)/shard_map/transpose(jvp())/scatter-add | solution.py:132
  244.0 4.7 %copy.44 = f32[64,27,512]{2,0,1:T(8,128)S(1)} copy(f32[64,27,512]{0,2,1:T(8,128)} %bitcast.189) | data formatting | bytes 7077888 | tf_op jit(solution)/shard_map/transpose(jvp())/reshape | solution.py:130
  250.2 47.6 %scatter_custom_fusion.1 = f32[3,13824]{0,1:T(8,128)} fusion(s32[8192]{0:T(1024)} %bitcast.222, f32[8192,3]{1,0:T(8,128)} %bitcast.192, f32[]{:T(128)} %constant.22.clone.1), kind=kCustom, calls=%fused_computation.11 | custom fusion | flops 24576 | bytes 166400 | tf_op jit(solution)/shard_map/transpose(jvp())/scatter-add | solution.py:133
  297.8 7.2 %fusion.116 = (bf16[27,3,512]{1,2,0:T(8,128)(2,1)S(1)}, f32[27,3,512]{1,2,0:T(8,128)}) fusion(f32[27,3,512]{1,2,0:T(8,128)} %bitcast.188, f32[1,3,512]{1,2,0:T(8,128)} %negate_bitcast_fusion), kind=kLoop, calls=%fused_computation.206 | loop fusion | flops 82944 | bytes 420864 | tf_op jit(solution)/shard_map/convert.6
  305.0 1.6 fusion.118
  306.7 2.3 copy.46
  309.0 2.3 copy.47
  311.3 2.3 collective-permute-start.19
  313.6 2.4 fusion.119
  315.9 3.3 slice.274
  319.2 3.0 copy.45
  323.2 5.4 %collective-permute-start.21 = (bf16[3,3,512]{2,1,0:T(4,128)(2,1)S(1)}, bf16[3,3,512]{2,1,0:T(4,128)(2,1)S(1)}, u32[]{:S(2)}, u32[]{:S(2)}) collective-permute-start(bf16[3,3,512]{2,1,0:T(4,128)(2,1)S(1)} %get-tuple-element.53), channel_id=1, source_target_pairs={{0,60},{4,0},{8,4},{12,8},{16,12},{20,16},{24,20},{28,24},{32,28},... | collective-permute-start | bytes 27656 | tf_op jit(solution)/shard_map/ppermute | solution.py:22
  328.6 4.0 fusion.27
  333.8 2.7 collective-permute-start.13
  336.5 1.7 collective-permute-start.22
  338.2 2.1 multiply_convert_fusion.1
  353.6 1.7 fusion.117
  355.5 5.4 %collective-permute-start.15 = (bf16[3,64,512]{2,1,0:T(8,128)(2,1)S(1)}, bf16[3,64,512]{2,1,0:T(8,128)(2,1)S(1)}, u32[]{:S(2)}, u32[]{:S(2)}) collective-permute-start(bf16[3,64,512]{2,1,0:T(8,128)(2,1)S(1)} %get-tuple-element.49), channel_id=1, source_target_pairs={{0,60},{4,0},{8,4},{12,8},{16,12},{20,16},{24,20},{28,24},{32,28},... | collective-permute-start | bytes 589832 | tf_op jit(solution)/shard_map/ppermute | solution.py:22
  361.2 2.8 collective-permute-done.14
  364.0 7.8 %collective-permute-start.16 = (f32[64,512]{1,0:T(8,128)S(1)}, f32[64,512]{1,0:T(8,128)S(1)}, u32[]{:S(2)}, u32[]{:S(2)}) collective-permute-start(f32[64,512]{1,0:T(8,128)S(1)} %get-tuple-element.50), channel_id=1, source_target_pairs={{0,1},{1,2},{2,3},{3,0},{4,5},{5,6},{6,7},{7,4},{8,9},{9,10},{10,1... | collective-permute-start | bytes 393224 | tf_op jit(solution)/shard_map/ppermute | solution.py:22
  373.8 6.4 %collective-permute-done.17 = f32[64,512]{1,0:T(8,128)S(1)} collective-permute-done((f32[64,512]{1,0:T(8,128)S(1)}, f32[64,512]{1,0:T(8,128)S(1)}, u32[]{:S(2)}, u32[]{:S(2)}) %collective-permute-start.17) | collective-permute-done | bytes 131104 | tf_op jit(solution)/shard_map/ppermute | solution.py:22
  381.1 14.1 %all-reduce.3 = (f32[64,64]{0,1:T(8,128)S(1)}, f32[16,64]{1,0:T(8,128)S(1)}) all-reduce(f32[64,64]{0,1:T(8,128)S(1)} %convolution_bitcast_fusion.2, f32[16,64]{1,0:T(8,128)S(1)} %copy-done.20), channel_id=1, replica_groups=mesh['gx'=4,'gy_0'=4,'gy_1'=4,'gz_0'=2,'gz_1'=2] {'gx'}, use_global_device_ids=true, to_apply=%region_7.8 | all-reduce | flops 5120 | bytes 40960 | tf_op jit(solution)/shard_map/psum | solution.py:43
  395.2 12.7 %all-reduce.2 = (f32[64,64]{0,1:T(8,128)S(1)}, f32[16,64]{1,0:T(8,128)S(1)}) all-reduce(f32[64,64]{0,1:T(8,128)S(1)} %get-tuple-element.24, f32[16,64]{1,0:T(8,128)S(1)} %get-tuple-element.25), channel_id=1, replica_groups=mesh['gx'=4,'gy_0'=4,'gy_1'=4,'gz_0'=2,'gz_1'=2] {'gy_0'}, use_global_device_ids=true, to_apply=%region_8.9 | all-reduce | flops 5120 | bytes 40960 | tf_op jit(solution)/shard_map/psum | solution.py:43
  407.9 17.5 %all-reduce.1 = (f32[64,64]{0,1:T(8,128)S(1)}, f32[16,64]{1,0:T(8,128)S(1)}) all-reduce(f32[64,64]{0,1:T(8,128)S(1)} %get-tuple-element.22, f32[16,64]{1,0:T(8,128)S(1)} %get-tuple-element.23), channel_id=1, replica_groups=mesh['gx'=4,'gy_0'=4,'gy_1'=4,'gz_0'=2,'gz_1'=2] {'gy_1'}, use_global_device_ids=true, to_apply=%region_9.10 | all-reduce | flops 5120 | bytes 40960 | tf_op jit(solution)/shard_map/psum | solution.py:43
  425.4 14.1 %all-reduce.5 = (f32[64,64]{0,1:T(8,128)S(1)}, f32[16,64]{1,0:T(8,128)S(1)}) all-reduce(f32[64,64]{0,1:T(8,128)S(1)} %get-tuple-element.20, f32[16,64]{1,0:T(8,128)S(1)} %get-tuple-element.21), channel_id=1, replica_groups=mesh['gx'=4,'gy_0'=4,'gy_1'=4,'gz_0'=2,'gz_1'=2] {'gz_0'}, use_global_device_ids=true, to_apply=%region_10.11 | all-reduce | flops 5120 | bytes 40960 | tf_op jit(solution)/shard_map/psum | solution.py:43
  439.6 12.6 %all-reduce.4 = (f32[64,64]{0,1:T(8,128)S(1)}, f32[16,64]{1,0:T(8,128)}) all-reduce(f32[64,64]{0,1:T(8,128)S(1)} %get-tuple-element.28, f32[16,64]{1,0:T(8,128)S(1)} %get-tuple-element.29), channel_id=1, replica_groups=mesh['gx'=4,'gy_0'=4,'gy_1'=4,'gz_0'=2,'gz_1'=2] {'gz_1'}, use_global_device_ids=true, to_apply=%region_11.12 | all-reduce | flops 5120 | bytes 40960 | tf_op jit(solution)/shard_map/psum | solution.py:43
  (158 shorter events, 36.2 us)
Async XLA Ops:
  7.2 5.1 %copy-start = (bf16[64,64]{1,0:T(8,128)(2,1)S(1)}, bf16[64,64]{1,0:T(8,128)(2,1)}, u32[]{:S(2)}) copy-start(bf16[64,64]{1,0:T(8,128)(2,1)} %param.18) | copy-start | bytes 24580
  7.2 331.0 %all-reduce.8.cloned.1.call-start = ((), (), s32[]{:S(2)}) async-start(), calls=%async_computation | async-start | bytes 4194304 | tf_op jit(solution)/shard_map/psum | solution.py:251
  7.2 58.2 %collective-permute-start = (f32[1,1,1,3,512]{4,2,3,1,0:T(1,128)}, f32[1,1,1,3,512]{4,2,3,1,0:T(1,128)S(1)}, u32[]{:S(2)}, u32[]{:S(2)}) collective-permute-start(f32[1,1,1,3,512]{4,2,3,1,0:T(1,128)} %param.13), channel_id=1, source_target_pairs={{0,64},{64,128},{128,192},{192,0},{1,65},{65,129},{129,193},{193,1... | collective-permute-start | bytes 18440 | tf_op jit(solution)/shard_map/ppermute | solution.py:36
  9.3 56.1 %collective-permute-start.1 = (f32[1,1,1,3,512]{4,2,3,1,0:T(1,128)}, f32[1,1,1,3,512]{4,2,3,1,0:T(1,128)S(1)}, u32[]{:S(2)}, u32[]{:S(2)}) collective-permute-start(f32[1,1,1,3,512]{4,2,3,1,0:T(1,128)} %param.13), channel_id=1, source_target_pairs={{64,0},{128,64},{192,128},{0,192},{65,1},{129,65},{193,129},{1,193... | collective-permute-start | bytes 18440 | tf_op jit(solution)/shard_map/ppermute | solution.py:37
  13.3 73.2 %collective-permute-start.7 = (bf16[1,1,1,64,512]{4,3,2,1,0:T(8,128)(2,1)S(1)}, bf16[1,1,1,64,512]{4,3,2,1,0:T(8,128)(2,1)S(1)}, u32[]{:S(2)}, u32[]{:S(2)}) collective-permute-start(bf16[1,1,1,64,512]{4,3,2,1,0:T(8,128)(2,1)S(1)} %fusion.26), channel_id=1, source_target_pairs={{64,0},{128,64},{192,128},{0,192},{65,1},{129,65},{193,129},{1,193... | collective-permute-start | bytes 196616 | tf_op jit(solution)/shard_map/ppermute | solution.py:37
  14.8 71.7 %collective-permute-start.6 = (bf16[1,1,1,64,512]{4,3,2,1,0:T(8,128)(2,1)S(1)}, bf16[1,1,1,64,512]{4,3,2,1,0:T(8,128)(2,1)S(1)}, u32[]{:S(2)}, u32[]{:S(2)}) collective-permute-start(bf16[1,1,1,64,512]{4,3,2,1,0:T(8,128)(2,1)S(1)} %fusion.26), channel_id=1, source_target_pairs={{0,64},{64,128},{128,192},{192,0},{1,65},{65,129},{129,193},{193,1... | collective-permute-start | bytes 196616 | tf_op jit(solution)/shard_map/ppermute | solution.py:36
  15.9 16.3 %copy-start.5 = (bf16[1,1,1,64,512]{4,3,2,1,0:T(8,128)(2,1)S(1)}, bf16[1,1,1,64,512]{4,3,2,1,0:T(8,128)(2,1)}, u32[]{:S(2)}) copy-start(bf16[1,1,1,64,512]{4,3,2,1,0:T(8,128)(2,1)} %param.12) | copy-start | bytes 196612
  15.9 16.4 %copy-start.8 = (bf16[1,1,1,64,512]{4,3,2,1,0:T(8,128)(2,1)S(1)}, bf16[1,1,1,64,512]{4,3,2,1,0:T(8,128)(2,1)}, u32[]{:S(2)}) copy-start(bf16[1,1,1,64,512]{4,3,2,1,0:T(8,128)(2,1)} %param.11) | copy-start | bytes 196612
  16.8 29.9 %copy-start.17 = (f32[3,2048]{1,0:T(4,128)}, f32[3,2048]{1,0:T(4,128)S(1)}, u32[]{:S(2)}) copy-start(f32[3,2048]{1,0:T(4,128)S(1)} %convert_multiply_fusion.2) | copy-start | bytes 73732
  48.2 17.1 %copy-start.21 = (s32[1,1,1,16,512]{4,3,2,1,0:T(8,128)S(1)}, s32[1,1,1,16,512]{4,3,2,1,0:T(8,128)}, u32[]{:S(2)}) copy-start(s32[1,1,1,16,512]{4,3,2,1,0:T(8,128)} %param.15) | copy-start | bytes 98308
  48.2 17.2 %copy-start.22 = (f32[1,1,1,3,512]{4,2,3,1,0:T(1,128)S(1)}, f32[1,1,1,3,512]{4,2,3,1,0:T(1,128)}, u32[]{:S(2)}) copy-start(f32[1,1,1,3,512]{4,2,3,1,0:T(1,128)} %param.13) | copy-start | bytes 18436
  65.3 21.2 %copy-start.19 = (s32[2,4,8,128]{3,1,2,0:T(4,128)}, s32[2,4,8,128]{3,1,2,0:T(4,128)S(1)}, u32[]{:S(2)}) copy-start(s32[2,4,8,128]{3,1,2,0:T(4,128)S(1)} %copy.57) | copy-start | bytes 98308
  65.4 41.1 %copy-start.16 = (s32[8192]{0:T(1024)}, s32[8192]{0:T(1024)S(1)}, u32[]{:S(2)}) copy-start(s32[8192]{0:T(1024)S(1)} %broadcast_clamp_fusion) | copy-start | bytes 98308
  65.4 7.9 %collective-permute-start.3 = (f32[3,1,1,3,512]{4,2,3,1,0:T(1,128)S(1)}, f32[3,1,1,3,512]{4,2,3,1,0:T(1,128)S(1)}, u32[]{:S(2)}, u32[]{:S(2)}) collective-permute-start(f32[3,1,1,3,512]{4,2,3,1,0:T(1,128)S(1)} %constant_dynamic-update-slice_fusion), channel_id=1, source_target_pairs={{4,0},{8,4},{12,8},{16,12},{20,16},{24,20},{28,24},{32,28},{36,32}... | collective-permute-start | bytes 55304 | tf_op jit(solution)/shard_map/ppermute | solution.py:37
  72.4 6.5 %collective-permute-start.2 = (f32[3,1,1,3,512]{4,2,3,1,0:T(1,128)S(1)}, f32[3,1,1,3,512]{4,2,3,1,0:T(1,128)S(1)}, u32[]{:S(2)}, u32[]{:S(2)}) collective-permute-start(f32[3,1,1,3,512]{4,2,3,1,0:T(1,128)S(1)} %constant_dynamic-update-slice_fusion), channel_id=1, source_target_pairs={{0,4},{4,8},{8,12},{12,16},{16,20},{20,24},{24,28},{28,32},{32,36}... | collective-permute-start | bytes 55304 | tf_op jit(solution)/shard_map/ppermute | solution.py:36
  79.0 10.1 %collective-permute-start.5 = (f32[3,3,1,3,512]{4,2,3,1,0:T(1,128)S(1)}, f32[3,3,1,3,512]{4,2,3,1,0:T(1,128)S(1)}, u32[]{:S(2)}, u32[]{:S(2)}) collective-permute-start(f32[3,3,1,3,512]{4,2,3,1,0:T(1,128)S(1)} %pad_maximum_fusion.10), channel_id=1, source_target_pairs={{1,0},{2,1},{3,2},{0,3},{5,4},{6,5},{7,6},{4,7},{9,8},{10,9},{11,1... | collective-permute-start | bytes 165896 | tf_op jit(solution)/shard_map/ppermute | solution.py:37
  82.3 6.8 %collective-permute-start.4 = (f32[3,3,1,3,512]{4,2,3,1,0:T(1,128)S(1)}, f32[3,3,1,3,512]{4,2,3,1,0:T(1,128)S(1)}, u32[]{:S(2)}, u32[]{:S(2)}) collective-permute-start(f32[3,3,1,3,512]{4,2,3,1,0:T(1,128)S(1)} %pad_maximum_fusion.10), channel_id=1, source_target_pairs={{0,1},{1,2},{2,3},{3,0},{4,5},{5,6},{6,7},{7,4},{8,9},{9,10},{10,1... | collective-permute-start | bytes 165896 | tf_op jit(solution)/shard_map/ppermute | solution.py:36
  86.5 5.2 %collective-permute-start.9 = (bf16[3,1,1,64,512]{4,3,2,1,0:T(8,128)(2,1)S(1)}, bf16[3,1,1,64,512]{4,3,2,1,0:T(8,128)(2,1)S(1)}, u32[]{:S(2)}, u32[]{:S(2)}) collective-permute-start(bf16[3,1,1,64,512]{4,3,2,1,0:T(8,128)(2,1)S(1)} %pad_maximum_fusion.4), channel_id=1, source_target_pairs={{4,0},{8,4},{12,8},{16,12},{20,16},{24,20},{28,24},{32,28},{36,32}... | collective-permute-start | bytes 589832 | tf_op jit(solution)/shard_map/ppermute | solution.py:37
  86.6 9.6 %collective-permute-start.8 = (bf16[3,1,1,64,512]{4,3,2,1,0:T(8,128)(2,1)S(1)}, bf16[3,1,1,64,512]{4,3,2,1,0:T(8,128)(2,1)S(1)}, u32[]{:S(2)}, u32[]{:S(2)}) collective-permute-start(bf16[3,1,1,64,512]{4,3,2,1,0:T(8,128)(2,1)S(1)} %pad_maximum_fusion.4), channel_id=1, source_target_pairs={{0,4},{4,8},{8,12},{12,16},{16,20},{20,24},{24,28},{28,32},{32,36}... | collective-permute-start | bytes 589832 | tf_op jit(solution)/shard_map/ppermute | solution.py:36
  96.3 44.9 %collective-permute-start.11 = (bf16[3,3,1,64,512]{4,3,2,1,0:T(8,128)(2,1)S(1)}, bf16[3,3,1,64,512]{4,3,2,1,0:T(8,128)(2,1)S(1)}, u32[]{:S(2)}, u32[]{:S(2)}) collective-permute-start(bf16[3,3,1,64,512]{4,3,2,1,0:T(8,128)(2,1)S(1)} %pad_maximum_fusion.2), channel_id=1, source_target_pairs={{1,0},{2,1},{3,2},{0,3},{5,4},{6,5},{7,6},{4,7},{9,8},{10,9},{11,1... | collective-permute-start | bytes 1769480 | tf_op jit(solution)/shard_map/ppermute | solution.py:37
  96.4 44.8 %collective-permute-start.10 = (bf16[3,3,1,64,512]{4,3,2,1,0:T(8,128)(2,1)S(1)}, bf16[3,3,1,64,512]{4,3,2,1,0:T(8,128)(2,1)S(1)}, u32[]{:S(2)}, u32[]{:S(2)}) collective-permute-start(bf16[3,3,1,64,512]{4,3,2,1,0:T(8,128)(2,1)S(1)} %pad_maximum_fusion.2), channel_id=1, source_target_pairs={{0,1},{1,2},{2,3},{3,0},{4,5},{5,6},{6,7},{7,4},{8,9},{9,10},{10,1... | collective-permute-start | bytes 1769480 | tf_op jit(solution)/shard_map/ppermute | solution.py:36
  102.2 35.0 %copy-start.10 = (f32[1,3,512]{1,2,0:T(8,128)}, f32[1,3,512]{1,2,0:T(8,128)S(1)}, u32[]{:S(2)}) copy-start(f32[1,3,512]{1,2,0:T(8,128)S(1)} %copy.51) | copy-start | bytes 18436
  179.9 2.9 copy-start.15
  179.9 2.9 copy-start.23
  179.9 2.9 copy-start.24
  182.8 3.6 copy-start.2
  182.8 2.1 copy-start.6
  184.9 2.2 copy-start.4
  184.9 2.3 copy-start.11
  185.0 1.4 copy-start.12
  311.3 10.9 %collective-permute-start.19 = (bf16[3,3,3,512]{3,2,1,0:T(4,128)(2,1)}, bf16[3,3,3,512]{3,2,1,0:T(4,128)(2,1)}, u32[]{:S(2)}, u32[]{:S(2)}) collective-permute-start(bf16[3,3,3,512]{3,2,1,0:T(4,128)(2,1)} %bitcast.224), channel_id=1, source_target_pairs={{0,192},{64,0},{128,64},{192,128},{1,193},{65,1},{129,65},{193,129... | collective-permute-start | bytes 82952 | tf_op jit(solution)/shard_map/ppermute | solution.py:22
  313.6 8.6 %collective-permute-start.18 = (bf16[3,3,3,512]{3,2,1,0:T(4,128)(2,1)}, bf16[3,3,3,512]{3,2,1,0:T(4,128)(2,1)}, u32[]{:S(2)}, u32[]{:S(2)}) collective-permute-start(bf16[3,3,3,512]{3,2,1,0:T(4,128)(2,1)} %bitcast.223), channel_id=1, source_target_pairs={{0,64},{64,128},{128,192},{192,0},{1,65},{65,129},{129,193},{193,1... | collective-permute-start | bytes 82952 | tf_op jit(solution)/shard_map/ppermute | solution.py:22
  323.1 13.3 %collective-permute-start.20 = (bf16[3,3,512]{2,1,0:T(4,128)(2,1)S(1)}, bf16[3,3,512]{2,1,0:T(4,128)(2,1)S(1)}, u32[]{:S(2)}, u32[]{:S(2)}) collective-permute-start(bf16[3,3,512]{2,1,0:T(4,128)(2,1)S(1)} %get-tuple-element.52), channel_id=1, source_target_pairs={{0,4},{4,8},{8,12},{12,16},{16,20},{20,24},{24,28},{28,32},{32,36}... | collective-permute-start | bytes 27656 | tf_op jit(solution)/shard_map/ppermute | solution.py:22
  323.2 13.2 %collective-permute-start.21 = (bf16[3,3,512]{2,1,0:T(4,128)(2,1)S(1)}, bf16[3,3,512]{2,1,0:T(4,128)(2,1)S(1)}, u32[]{:S(2)}, u32[]{:S(2)}) collective-permute-start(bf16[3,3,512]{2,1,0:T(4,128)(2,1)S(1)} %get-tuple-element.53), channel_id=1, source_target_pairs={{0,60},{4,0},{8,4},{12,8},{16,12},{20,16},{24,20},{28,24},{32,28},... | collective-permute-start | bytes 27656 | tf_op jit(solution)/shard_map/ppermute | solution.py:22
  333.8 6.6 %copy-start.1 = (bf16[512,2048]{1,0:T(8,128)(2,1)S(1)}, bf16[512,2048]{1,0:T(8,128)(2,1)}, u32[]{:S(2)}) copy-start(bf16[512,2048]{1,0:T(8,128)(2,1)} %get-tuple-element.58) | copy-start | bytes 6291460
  333.8 19.8 %collective-permute-start.13 = (bf16[3,3,64,512]{3,2,1,0:T(8,128)(2,1)}, bf16[3,3,64,512]{3,2,1,0:T(8,128)(2,1)S(1)}, u32[]{:S(2)}, u32[]{:S(2)}) collective-permute-start(bf16[3,3,64,512]{3,2,1,0:T(8,128)(2,1)} %bitcast.33), channel_id=1, source_target_pairs={{0,192},{64,0},{128,64},{192,128},{1,193},{65,1},{129,65},{193,129... | collective-permute-start | bytes 1769480 | tf_op jit(solution)/shard_map/ppermute | solution.py:22
  336.4 17.2 %collective-permute-start.12 = (bf16[3,3,64,512]{3,2,1,0:T(8,128)(2,1)}, bf16[3,3,64,512]{3,2,1,0:T(8,128)(2,1)}, u32[]{:S(2)}, u32[]{:S(2)}) collective-permute-start(bf16[3,3,64,512]{3,2,1,0:T(8,128)(2,1)} %bitcast.32), channel_id=1, source_target_pairs={{0,64},{64,128},{128,192},{192,0},{1,65},{65,129},{129,193},{193,1... | collective-permute-start | bytes 1769480 | tf_op jit(solution)/shard_map/ppermute | solution.py:22
  336.5 13.0 %collective-permute-start.22 = (f32[3,512]{1,0:T(4,128)S(1)}, f32[3,512]{1,0:T(4,128)S(1)}, u32[]{:S(2)}, u32[]{:S(2)}) collective-permute-start(f32[3,512]{1,0:T(4,128)S(1)} %get-tuple-element.59), channel_id=1, source_target_pairs={{0,1},{1,2},{2,3},{3,0},{4,5},{5,6},{6,7},{7,4},{8,9},{9,10},{10,1... | collective-permute-start | bytes 18440 | tf_op jit(solution)/shard_map/ppermute | solution.py:22
  338.2 2.8 copy-start.7
  338.2 2.8 copy-start.9
  338.2 11.3 %collective-permute-start.23 = (f32[3,512]{1,0:T(4,128)S(1)}, f32[3,512]{1,0:T(4,128)S(1)}, u32[]{:S(2)}, u32[]{:S(2)}) collective-permute-start(f32[3,512]{1,0:T(4,128)S(1)} %get-tuple-element.60), channel_id=1, source_target_pairs={{0,3},{1,0},{2,1},{3,2},{4,7},{5,4},{6,5},{7,6},{8,11},{9,8},{10,9... | collective-permute-start | bytes 18440 | tf_op jit(solution)/shard_map/ppermute | solution.py:22
  338.2 2.8 copy-start.3
  353.6 26.5 %copy-start.14 = (f32[64,512]{1,0:T(8,128)S(1)}, f32[64,512]{1,0:T(8,128)}, u32[]{:S(2)}) copy-start(f32[64,512]{1,0:T(8,128)} %copy-done.13) | copy-start | bytes 393220
  355.4 25.7 %copy-start.20 = (f32[16,64]{1,0:T(8,128)S(1)}, f32[16,64]{1,0:T(8,128)}, u32[]{:S(2)}) copy-start(f32[16,64]{1,0:T(8,128)} %fusion.27) | copy-start | bytes 12292
  355.4 8.5 %collective-permute-start.14 = (bf16[3,64,512]{2,1,0:T(8,128)(2,1)S(1)}, bf16[3,64,512]{2,1,0:T(8,128)(2,1)S(1)}, u32[]{:S(2)}, u32[]{:S(2)}) collective-permute-start(bf16[3,64,512]{2,1,0:T(8,128)(2,1)S(1)} %get-tuple-element.48), channel_id=1, source_target_pairs={{0,4},{4,8},{8,12},{12,16},{16,20},{20,24},{24,28},{28,32},{32,36}... | collective-permute-start | bytes 589832 | tf_op jit(solution)/shard_map/ppermute | solution.py:22
  355.5 8.4 %collective-permute-start.15 = (bf16[3,64,512]{2,1,0:T(8,128)(2,1)S(1)}, bf16[3,64,512]{2,1,0:T(8,128)(2,1)S(1)}, u32[]{:S(2)}, u32[]{:S(2)}) collective-permute-start(bf16[3,64,512]{2,1,0:T(8,128)(2,1)S(1)} %get-tuple-element.49), channel_id=1, source_target_pairs={{0,60},{4,0},{8,4},{12,8},{16,12},{20,16},{24,20},{28,24},{32,28},... | collective-permute-start | bytes 589832 | tf_op jit(solution)/shard_map/ppermute | solution.py:22
  364.0 9.7 %collective-permute-start.16 = (f32[64,512]{1,0:T(8,128)S(1)}, f32[64,512]{1,0:T(8,128)S(1)}, u32[]{:S(2)}, u32[]{:S(2)}) collective-permute-start(f32[64,512]{1,0:T(8,128)S(1)} %get-tuple-element.50), channel_id=1, source_target_pairs={{0,1},{1,2},{2,3},{3,0},{4,5},{5,6},{6,7},{7,4},{8,9},{9,10},{10,1... | collective-permute-start | bytes 393224 | tf_op jit(solution)/shard_map/ppermute | solution.py:22
  371.8 8.3 %collective-permute-start.17 = (f32[64,512]{1,0:T(8,128)S(1)}, f32[64,512]{1,0:T(8,128)S(1)}, u32[]{:S(2)}, u32[]{:S(2)}) collective-permute-start(f32[64,512]{1,0:T(8,128)S(1)} %get-tuple-element.51), channel_id=1, source_target_pairs={{0,3},{1,0},{2,1},{3,2},{4,7},{5,4},{6,5},{7,6},{8,11},{9,8},{10,9... | collective-permute-start | bytes 393224 | tf_op jit(solution)/shard_map/ppermute | solution.py:22
  (2 other events, 1.4 us)
Sparse Core Ops, SparseCore 0:
  48.4 283.5 all-reduce.7
where the time goes:
time: 464 us; the launch traced here: 460 us
  other arithmetic  142 us (31%)
  local copies, waits for them, and re-layouts  103 us (22%)
  blocking collectives  71 us (15%)
  matrix products  53.5 us (12%)
  starting transfers between devices  52.6 us (11%)
  waiting for transfers between devices  23 us (5%)
  between operations  15 us (3%)
    psum x5, blocking collectives, by_axis(): return functools.reduce(lax.psum, axes, x)  71 us
    scatter-add x1, other arithmetic, short_range(): near_z = flat_z[:, neighbour_ids]  47.7 us
    scatter-add x1, other arithmetic, short_range(): near_pos = flat_pos[:, neighbour_ids]  47.6 us
    gather x2, local copies, waits for them, and re-layouts, short_range(): near_z = flat_z[:, neighbour_ids]  36.3 us
    gather x1, local copies, waits for them, and re-layouts, short_range(): near_pos = flat_pos[:, neighbour_ids]  30.7 us
    ppermute x12, starting transfers between devices, from_behind(): lax.ppermute(x, axis, [(i, (i + by) % devices) for i in range(devices)])  25.3 us
    convert_element_type x1, other arithmetic, phases(): jnp.sin(angles).astype(jnp.bfloat16)  17 us
    dot_general x1, matrix products, structure_terms(): lax.dot_general(cos_part, stacked, contract, preferred_element_type=jnp.f...  15.4 us
  transfers between devices with their start and end apart: 25, of which 7 were waited for; matrix products, arithmetic and copies ran while one was open for 64% of the time, Pallas kernels for 0%

commit v1 on v0

v1 whole, which is shorter than its diff:
```python
import functools
import math

import jax
import jax.numpy as jnp
from jax import lax
from jax.experimental import pallas as pl
from jax.experimental.pallas import tpu as pltpu
from jax.sharding import Mesh
from jax.sharding import PartitionSpec as P

GY = ("gy_0", "gy_1")
GZ = ("gz_0", "gz_1")
GX_GY_GZ = ("gx", "gy_0", "gy_1", "gz_0", "gz_1")

circle_angle = 2.0 * math.pi
CHUNK = 256
SIN_TERMS = (6.28316404, -41.33714227, 81.34076528, -70.99339569)
COS_TERMS = (0.99999995, -19.73917143, 64.93459054, -85.24032775, 56.2423573)
WHOLE = pl.BlockSpec(memory_space=pltpu.VMEM)

reach_sq = 0.75
GROUPS = 4
ROWS = 72
BLOCKS = 132
HIGH = BLOCKS // GROUPS * 16


def split_two(x):
    high = x.astype(jnp.bfloat16)
    return high, (x - high.astype(jnp.float32)).astype(jnp.bfloat16)


def row_pick(first, second, third, shape):
    row = lax.broadcasted_iota(jnp.int32, shape, 0) % 4
    spread = lambda v: jnp.broadcast_to(v, shape)
    return jnp.where(
        row == 0,
        spread(first),
        jnp.where(row == 1, spread(second), jnp.where(row == 2, spread(third), 0.0)),
    )


def short_kernel(
    table_ref,
    ids_ref,
    pos_ref,
    dy_ref,
    radial_ref,
    zgrad_ref,
    own_ref,
    rgrad_ref,
    lhs_ref,
    high_ref,
    low_ref,
    near_ref,
    rel_ref,
    basis_ref,
    filt_ref,
    acc_ref,
):
    channels, atoms = dy_ref.shape
    listed = ids_ref.shape[0]
    count = radial_ref.shape[0]
    f32, bf16 = jnp.float32, jnp.bfloat16
    spacing = reach_sq / (count - 1)
    width = 2.0 * spacing
    share = listed ** (-0.5)
    for g in range(GROUPS):
        part = table_ref[g * HIGH : (g + 1) * HIGH, :].astype(f32)
        lhs_ref[g * ROWS : (g + 1) * ROWS, :] = jnp.transpose(part)[0:ROWS, :].astype(bf16)
    ids = ids_ref[...]
    slot = lax.shift_right_logical(ids, 9)
    atom = jnp.bitwise_and(ids, 511)
    block = lax.shift_right_logical(atom, 4)
    ox = slot // 9
    oy = (slot // 3) % 3
    oz = slot % 3
    qx = block // 9
    qy = (block // 3) % 3
    qz = block % 3
    grid = ((3 * ox + qx - 2) * 5 + 3 * oy + qy - 2) * 5 + 3 * oz + qz - 2
    grid = jnp.where(block >= 27, block + (125 - 27), grid)
    low = grid // (BLOCKS // GROUPS)
    high = (grid - low * (BLOCKS // GROUPS)) * 16 + jnp.bitwise_and(atom, 15)
    high_ref[...] = high
    low_ref[...] = low
    offs = [(o - 1).astype(f32) for o in (ox, oy, oz)]
    own = pos_ref[...]
    own8 = row_pick(own[0:1], own[1:2], own[2:3], (8, atoms))
    w_hi, w_lo = split_two(radial_ref[...])
    w_stack = jnp.concatenate([w_hi, w_hi, w_lo], axis=0)
    centre = lax.broadcasted_iota(jnp.int32, (count, 1), 0).astype(f32) * spacing
    iota = lax.broadcasted_iota(jnp.int32, (HIGH, atoms), 0)

    def hot(j):
        return (high_ref[pl.ds(j, 1), :] == iota).astype(f32).astype(bf16)

    agg = jnp.zeros((channels, atoms), f32)
    for j in range(listed):
        found = jnp.dot(lhs_ref[...], hot(j), preferred_element_type=f32)
        low_j = low_ref[j : j + 1, :]
        near = found[0:ROWS]
        for g in range(1, GROUPS):
            near = jnp.where(low_j == g, found[g * ROWS : (g + 1) * ROWS], near)
        near_z = near[0:channels]
        near_ref[j] = near_z.astype(bf16)
        halves = near[channels : channels + 8]
        off8 = row_pick(offs[0][j : j + 1], offs[1][j : j + 1], offs[2][j : j + 1], (8, atoms))
        rel = halves + pltpu.roll(halves, 4, 0) + off8 - own8
        rel_ref[j] = rel
        dist = 0.5 * jnp.sum(rel * rel, axis=0, keepdims=True)
        scaled = (dist - centre) / width
        basis = jnp.exp(-(scaled * scaled))
        basis_ref[j] = basis
        b_hi, b_lo = split_two(basis)
        filt = lax.dot_general(
            w_stack,
            jnp.concatenate([b_hi, b_lo, b_hi], axis=0),
            (((0,), (0,)), ((), ())),
            preferred_element_type=f32,
        )
        filt_ref[j] = filt
        agg = agg + filt * near_z
    agg = agg * share
    gate = 1.0 / (1.0 + jnp.exp(-agg))
    g_all = dy_ref[...].astype(f32) * (gate * (1.0 + agg * (1.0 - gate))) * share
    acc_ref[...] = jnp.zeros_like(acc_ref)
    own_grad = jnp.zeros((8, atoms), f32)
    radial = jnp.zeros((2 * count, 2 * channels), f32)
    w_wide = jnp.concatenate([w_hi, w_hi, w_lo], axis=1)
    for j in range(listed):
        near_z = near_ref[j].astype(f32)
        dz = filt_ref[j] * g_all
        df = near_z * g_all
        f_hi, f_lo = split_two(df)
        basis = basis_ref[j]
        b_hi, b_lo = split_two(basis)
        radial = radial + lax.dot_general(
            jnp.concatenate([b_hi, b_lo], axis=0),
            jnp.concatenate([f_hi, f_lo], axis=0),
            (((1,), (1,)), ((), ())),
            preferred_element_type=f32,
        )
        dbasis = jnp.dot(
            w_wide, jnp.concatenate([f_hi, f_lo, f_hi], axis=0), preferred_element_type=f32
        )
        rel = rel_ref[j]
        dist = 0.5 * jnp.sum(rel * rel, axis=0, keepdims=True)
        slope = dbasis * basis * (dist - centre)
        ddist = jnp.sum(slope, axis=0, keepdims=True) * (-2.0 / (width * width))
        gpos = rel * (2.0 * ddist)
        own_grad = own_grad - gpos
        p_hi = gpos.astype(bf16).astype(f32)
        row8 = lax.broadcasted_iota(jnp.int32, (8, atoms), 0)
        tail = jnp.where(row8 < 4, p_hi, gpos - p_hi)
        full = jnp.concatenate([dz, tail], axis=0)
        low_j = low_ref[j : j + 1, :]
        spread = jnp.concatenate(
            [jnp.where(low_j == g, full, 0.0) for g in range(GROUPS)], axis=0
        ).astype(bf16)
        acc_ref[...] += lax.dot_general(
            spread, hot(j), (((1,), (1,)), ((), ())), preferred_element_type=f32
        )
    own_ref[...] = own_grad
    rgrad_ref[...] = (
        radial[0:count, 0:channels]
        + radial[count:, 0:channels]
        + radial[0:count, channels:]
        + radial[count:, channels:]
    )
    for g in range(GROUPS):
        part = jnp.transpose(acc_ref[g * ROWS : (g + 1) * ROWS, :])
        zgrad_ref[g * HIGH : (g + 1) * HIGH, :] = jnp.concatenate(
            [part, jnp.zeros((HIGH, 128 - ROWS), f32)], axis=1
        )


def short_range(table, ids, pos, dy, radial, interpret=False):
    channels, atoms = dy.shape
    listed = ids.shape[0]
    count = radial.shape[0]
    vmem = lambda s, d: pltpu.VMEM(s, d)
    spec = pl.BlockSpec(memory_space=pltpu.VMEM)
    return pl.pallas_call(
        short_kernel,
        out_shape=(
            jax.ShapeDtypeStruct((GROUPS * HIGH, 128), jnp.float32),
            jax.ShapeDtypeStruct((8, atoms), jnp.float32),
            jax.ShapeDtypeStruct((count, channels), jnp.float32),
        ),
        in_specs=[spec] * 5,
        out_specs=(spec,) * 3,
        scratch_shapes=[
            vmem((GROUPS * ROWS, HIGH), jnp.bfloat16),
            vmem((listed, atoms), jnp.int32),
            vmem((listed, atoms), jnp.int32),
            vmem((listed, channels, atoms), jnp.bfloat16),
            vmem((listed, 8, atoms), jnp.float32),
            vmem((listed, count, atoms), jnp.float32),
            vmem((listed, channels, atoms), jnp.float32),
            vmem((GROUPS * ROWS, HIGH), jnp.float32),
        ],
        interpret=interpret,
        name="short_range",
    )(table, ids, pos, dy, radial)


def from_behind(x, axis, by):
    devices = lax.axis_size(axis)
    return lax.ppermute(x, axis, [(i, (i + by) % devices) for i in range(devices)])


def project_kernel(h_ref, mix_ref, gain_ref, kind_ref, pos_ref, table_ref, gains_ref):
    f32, bf16 = jnp.float32, jnp.bfloat16
    channels, atoms = h_ref.shape
    kinds = gain_ref.shape[0]
    columns = jnp.transpose(gain_ref[...])
    label = kind_ref[...]
    gains = jnp.zeros((channels, atoms), f32)
    for kind in range(kinds):
        gains = jnp.where(label == kind, columns[:, kind : kind + 1], gains)
    gains_ref[...] = gains
    projected = lax.dot_general(
        mix_ref[...], h_ref[...], (((0,), (0,)), ((), ())), preferred_element_type=f32
    )
    z = (projected * gains).astype(bf16).astype(f32)
    pos = pos_ref[...]
    p_hi, p_lo = split_two(pos)
    none = jnp.zeros((1, atoms), f32)
    rows = jnp.concatenate(
        [z, p_hi.astype(f32), none, p_lo.astype(f32), none, jnp.zeros((128 - ROWS, atoms), f32)],
        axis=0,
    )
    table_ref[...] = jnp.transpose(rows).astype(bf16)


def project(h, mix, table, kinds, pos):
    channels, atoms = h.shape
    return pl.pallas_call(
        project_kernel,
        out_shape=(
            jax.ShapeDtypeStruct((atoms, 128), jnp.bfloat16),
            jax.ShapeDtypeStruct((channels, atoms), jnp.float32),
        ),
        in_specs=[WHOLE] * 5,
        out_specs=(WHOLE,) * 2,
        name="project",
    )(h, mix, table, kinds, pos)


def phase_kernel(turns_ref, miller_ref, stacked_ref, cos_ref, sin_ref, part_ref, flip_ref, t_ref):
    f32, bf16 = jnp.float32, jnp.bfloat16
    width = stacked_ref.shape[0]

    @pl.when(pl.program_id(0) == 0)
    def _():
        flip_ref[...] = jnp.transpose(stacked_ref[...])

    whole = turns_ref[...]
    t_hi, t_rest = whole.astype(bf16), whole - whole.astype(bf16).astype(f32)
    t_mid = t_rest.astype(bf16)
    t_lo = (t_rest - t_mid.astype(f32)).astype(bf16)
    rhs = jnp.concatenate([t_hi, t_mid, t_lo], axis=0)
    m = miller_ref[...].astype(f32).astype(bf16)
    lhs = jnp.concatenate([m, m, m], axis=0)
    t_ref[...] = lax.dot_general(lhs, rhs, (((0,), (0,)), ((), ())), preferred_element_type=f32)
    rows, lanes = 16, 256
    for top in range(0, t_ref.shape[0], rows):
        for left in range(0, t_ref.shape[1], lanes):
            at = (slice(top, top + rows), slice(left, left + lanes))
            t = t_ref[at]
            r = t - jnp.round(t)
            u = jnp.abs(r) - 0.25
            q = u * u
            s = SIN_TERMS[3]
            for term in SIN_TERMS[2::-1]:
                s = s * q + term
            c = COS_TERMS[4]
            for term in COS_TERMS[3::-1]:
                c = c * q + term
            cos_ref[at] = -(s * u).astype(bf16)
            sin_ref[at] = jnp.where(r < 0.0, -c, c).astype(bf16)
    part_ref[:, 0:width] = jnp.dot(
        cos_ref[...], flip_ref[...], preferred_element_type=f32
    ).astype(part_ref.dtype)
    part_ref[:, width:] = jnp.dot(
        sin_ref[...], flip_ref[...], preferred_element_type=f32
    ).astype(part_ref.dtype)


def phase_sums(turns, miller, stacked):
    points = miller.shape[1]
    width, atoms = stacked.shape
    step = min(CHUNK, points)
    return pl.pallas_call(
        phase_kernel,
        grid=(points // step,),
        out_shape=(
            jax.ShapeDtypeStruct((points, atoms), jnp.bfloat16),
            jax.ShapeDtypeStruct((points, atoms), jnp.bfloat16),
            jax.ShapeDtypeStruct((points, 2 * width), jnp.bfloat16),
        ),
        in_specs=[
            pl.BlockSpec(turns.shape, lambda i: (0, 0)),
            pl.BlockSpec((miller.shape[0], step), lambda i: (0, i)),
            pl.BlockSpec(stacked.shape, lambda i: (0, 0)),
        ],
        out_specs=(
            pl.BlockSpec((step, atoms), lambda i: (i, 0)),
            pl.BlockSpec((step, atoms), lambda i: (i, 0)),
            pl.BlockSpec((step, 2 * width), lambda i: (i, 0)),
        ),
        scratch_shapes=[
            pltpu.VMEM((atoms, width), jnp.bfloat16),
            pltpu.VMEM((step, atoms), jnp.float32),
        ],
        name="phase_sums",
    )(turns, miller, stacked)


def ewald_kernel(coeff_ref, cos_ref, sin_ref, miller_ref, stacked_ref, h_ref, pos_ref):
    f32, bf16 = jnp.float32, jnp.bfloat16
    width = stacked_ref.shape[0]
    channels = width // 2

    @pl.when(pl.program_id(0) == 0)
    def _():
        h_ref[...] = jnp.zeros_like(h_ref)
        pos_ref[...] = jnp.zeros_like(pos_ref)

    coeffs = coeff_ref[...]
    cos_part, sin_part = cos_ref[...], sin_ref[...]
    over_rows = (((0,), (0,)), ((), ()))
    h_ref[...] += lax.dot_general(
        coeffs[:, 0:channels], cos_part, over_rows, preferred_element_type=f32
    ) + lax.dot_general(
        coeffs[:, width : width + channels], sin_part, over_rows, preferred_element_type=f32
    )
    along_u = jnp.dot(coeffs[:, 0:width], stacked_ref[...], preferred_element_type=f32)
    along_v = jnp.dot(coeffs[:, width:], stacked_ref[...], preferred_element_type=f32)
    angle = along_v * cos_part.astype(f32) - along_u * sin_part.astype(f32)
    a_hi, a_lo = split_two(angle)
    m = miller_ref[...].astype(f32).astype(bf16)
    pos_ref[...] += jnp.dot(m, a_hi, preferred_element_type=f32) + jnp.dot(
        m, a_lo, preferred_element_type=f32
    )


def ewald(coeffs, cos_all, sin_all, miller, stacked):
    points, atoms = cos_all.shape
    width = stacked.shape[0]
    step = min(CHUNK, points)
    return pl.pallas_call(
        ewald_kernel,
        grid=(points // step,),
        out_shape=(
            jax.ShapeDtypeStruct((width // 2, atoms), jnp.float32),
            jax.ShapeDtypeStruct((miller.shape[0], atoms), jnp.float32),
        ),
        in_specs=[
            pl.BlockSpec((step, coeffs.shape[1]), lambda i: (i, 0)),
            pl.BlockSpec((step, atoms), lambda i: (i, 0)),
            pl.BlockSpec((step, atoms), lambda i: (i, 0)),
            pl.BlockSpec((miller.shape[0], step), lambda i: (0, i)),
            pl.BlockSpec(stacked.shape, lambda i: (0, 0)),
        ],
        out_specs=(
            pl.BlockSpec((width // 2, atoms), lambda i: (0, 0)),
            pl.BlockSpec((miller.shape[0], atoms), lambda i: (0, 0)),
        ),
        name="ewald",
    )(coeffs, cos_all, sin_all, miller, stacked)


def finish_kernel(rows_ref, gains_ref, mix_ref, h_ref, own_ref, short_ref, weight_ref, pos_ref):
    f32, bf16 = jnp.float32, jnp.bfloat16
    channels = h_ref.shape[0]
    flat = jnp.transpose(rows_ref[...])
    zscaled = (flat[0:channels] * gains_ref[...]).astype(bf16)
    short_ref[...] = jnp.dot(mix_ref[...], zscaled, preferred_element_type=f32)
    weight_ref[...] = lax.dot_general(
        h_ref[...], zscaled, (((1,), (1,)), ((), ())), preferred_element_type=f32
    )
    halves = flat[channels : channels + 8]
    pos_ref[...] = halves + pltpu.roll(halves, 4, 0) + own_ref[...]


def finish(rows, gains, mix, h, own):
    channels, atoms = h.shape
    return pl.pallas_call(
        finish_kernel,
        out_shape=(
            jax.ShapeDtypeStruct((channels, atoms), jnp.float32),
            jax.ShapeDtypeStruct((channels, channels), jnp.float32),
            jax.ShapeDtypeStruct((8, atoms), jnp.float32),
        ),
        in_specs=[WHOLE] * 5,
        out_specs=(WHOLE,) * 3,
        name="finish",
    )(rows, gains, mix, h, own)


def coefficients(totals, filt_rows, norm_atoms, norm_k):
    channels = filt_rows.shape[1]
    cos_struct = totals[:, 0:channels] * norm_atoms
    cos_back = totals[:, channels : 2 * channels] * norm_k
    sin_struct = totals[:, 2 * channels : 3 * channels] * norm_atoms
    sin_back = totals[:, 3 * channels : 4 * channels] * norm_k
    coeffs = jnp.concatenate(
        [
            norm_atoms * filt_rows * cos_back,
            norm_k * filt_rows * cos_struct,
            norm_atoms * filt_rows * sin_back,
            norm_k * filt_rows * sin_struct,
        ],
        axis=1,
    )
    return (coeffs.astype(jnp.bfloat16), cos_struct * cos_back + sin_struct * sin_back)


def widened(x, sides):
    for axis, dim in sides:
        length = x.shape[dim]
        before = from_behind(lax.slice_in_dim(x, length - 1, length, axis=dim), axis, 1)
        after = from_behind(lax.slice_in_dim(x, 0, 1, axis=dim), axis, -1)
        x = jnp.concatenate([before, x, after], axis=dim)
    return x


def folded(x, sides):
    for axis, dim in sides:
        length = x.shape[dim]
        first = lax.slice_in_dim(x, 0, 1, axis=dim).astype(jnp.bfloat16)
        last = lax.slice_in_dim(x, length - 1, length, axis=dim).astype(jnp.bfloat16)
        to_last = from_behind(first, axis, -1).astype(jnp.float32)
        to_first = from_behind(last, axis, 1).astype(jnp.float32)
        inner = lax.slice_in_dim(x, 1, length - 1, axis=dim)
        low = lax.slice_in_dim(inner, 0, 1, axis=dim) + to_first
        middle = lax.slice_in_dim(inner, 1, length - 3, axis=dim)
        high = lax.slice_in_dim(inner, length - 3, length - 2, axis=dim) + to_last
        x = jnp.concatenate([low, middle, high], axis=dim)
    return x


def shards(
    atom_embedding,
    output_adjoint,
    fractional_coords,
    element_labels,
    adjacent_ghost_entries,
    miller_triples,
    reciprocal_kernel,
    channel_mixing_matrix,
    element_channel_factor,
    distance_kernel,
):
    h = atom_embedding[0, 0, 0]
    dy = output_adjoint[0, 0, 0]
    pos = fractional_coords[0, 0, 0]
    channels, atoms = h.shape
    points = miller_triples.shape[1]
    devices = lax.axis_size(GX_GY_GZ)
    norm_atoms = (atoms * devices) ** (-0.5)
    norm_k = points ** (-0.5)
    lengths = jnp.array([lax.axis_size("gx"), lax.axis_size(GY), lax.axis_size(GZ)], jnp.float32)
    anchor = jnp.stack([lax.axis_index("gx"), lax.axis_index(GY), lax.axis_index(GZ)]).astype(
        jnp.float32
    )
    share_rows = points // devices
    share_start = lax.axis_index(GX_GY_GZ) * share_rows

    own_table, gains = project(
        h, channel_mixing_matrix, element_channel_factor, element_labels[0, 0], pos
    )
    sides = ((GZ, 2), (GY, 1), ("gx", 0))
    cells = own_table[0:432].reshape(3, 3, 3, 16, 128)
    wide = widened(cells, sides)

    turns = (pos + anchor[:, None]) / lengths[:, None]
    stacked = jnp.concatenate([h, dy], axis=0)
    cos_all, sin_all, part = phase_sums(turns, miller_triples, stacked)
    pieces = lax.all_to_all(part.reshape(devices, share_rows, 4 * channels), GX_GY_GZ, 0, 0)
    totals = jnp.sum(pieces.astype(jnp.float32), axis=0)
    filt_rows = lax.dynamic_slice_in_dim(reciprocal_kernel, share_start, share_rows, 0)
    own_coeffs, filter_share = coefficients(totals, filt_rows, norm_atoms, norm_k)
    spread = jnp.broadcast_to(own_coeffs[None], (devices, share_rows, 4 * channels))
    coeffs = lax.all_to_all(spread, GX_GY_GZ, 0, 0).reshape(points, 4 * channels)

    table = jnp.concatenate(
        [
            wide.reshape(2000, 128),
            own_table[432:512],
            jnp.zeros((GROUPS * HIGH - 2080, 128), jnp.bfloat16),
        ],
        axis=0,
    )
    ghost_grad, own_grad, grad_radial = short_range(
        table, adjacent_ghost_entries[0, 0, 0], pos, dy, distance_kernel
    )
    grid = ghost_grad[0:2000].reshape(5, 5, 5, 16, 128)
    inner = folded(grid, sides[::-1])
    rows = jnp.concatenate([inner.reshape(432, 128), ghost_grad[2000:2080]], axis=0)
    atom_short, weight_local, pos_short = finish(rows, gains, channel_mixing_matrix, h, own_grad)
    summed = lax.psum(jnp.concatenate([weight_local, grad_radial], axis=0), GX_GY_GZ)
    weight_grad, radial_grad = summed[0:channels], summed[channels:]

    ewald_h, ewald_pos = ewald(coeffs, cos_all, sin_all, miller_triples, stacked)
    atom_grad = (dy.astype(jnp.float32) + ewald_h + atom_short).astype(jnp.bfloat16)
    position_grad = ewald_pos * (circle_angle / lengths)[:, None] + pos_short[0:3]
    return (
        atom_grad[None, None, None],
        position_grad[None, None, None],
        weight_grad,
        radial_grad,
        filter_share,
    )


def solution(mesh):
    finer = Mesh(
        mesh.devices.reshape(mesh.shape["gx"], 4, 4, 2, 2), ("gx", "gy_0", "gy_1", "gz_0", "gz_1")
    )
    in_specs = (
        P("gx", GY, GZ, None, None),
        P("gx", GY, GZ, None, None),
        P("gx", GY, GZ, None, None),
        P("gx", GY, GZ, None),
        P("gx", GY, GZ, None, None),
        P(),
        P(),
        P(),
        P(),
        P(),
    )
    out_specs = (
        P("gx", GY, GZ, None, None),
        P("gx", GY, GZ, None, None),
        P(),
        P(),
        P(GX_GY_GZ, None),
    )
    return jax.shard_map(
        shards, mesh=finer, in_specs=in_specs, out_specs=out_specs, check_vma=False
    )
```

time: 464 us -> 238 us (0.51)
  other arithmetic: 142 us -> 10.8 us
  local copies, waits for them, and re-layouts: 103 us -> 6.72 us
  matrix products: 53.5 us -> 0 us
  Pallas kernels: 0 us -> 37.3 us
  waiting for transfers between devices: 23 us -> 51.1 us
  between operations: 15 us -> 0.83 us
    scatter-add x2 -> x0, other arithmetic: 95.4 us -> none  [the longest x1 47.7 us: short_range(): near_z = flat_z[:, neighbour_ids]]
    gather x3 -> x0, local copies, waits for them, and re-layouts: 67 us -> none  [the longest x2 36.3 us: short_range(): near_z = flat_z[:, neighbour_ids]]
    dot_general x29 -> x0, matrix products: 53.5 us -> none  [the longest x1 15.4 us: structure_terms(): lax.dot_general(cos_part, stacked, contract, preferred_element_type=jnp.f...]
    ppermute x12, waiting for transfers between devices: 9.77 us -> 51.1 us  [from_behind(): lax.ppermute(x, axis, [(i, (i + by) % devices) for i in range(devices)])]
    pallas_call x0 -> x5, Pallas kernels: none -> 37.3 us  [the longest x1 16.7 us: short_range(): pl.pallas_call(short_kernel, out_shape=(jax.ShapeDtypeStruct((GROUPS * HI...]
    all_to_all x0 -> x2, starting transfers between devices: none -> 27.3 us  [the longest x1 15.6 us: shards(): lax.all_to_all(part.reshape(devices, share_rows, 4 * channels), GX_GY_GZ,...]
    ppermute x12 -> x0, starting transfers between devices: 27.3 us -> none  [the longest x6 14 us: padded(): before = lax.ppermute(last, axis, up)]
    convert_element_type x2 -> x0, other arithmetic: 17.1 us -> none  [the longest x1 17 us: phases(): jnp.sin(angles).astype(jnp.bfloat16)]
  transfers between devices with their start and end apart: 25 -> 14, of which waited for: 7 -> 7; matrix products, arithmetic and copies ran while one was open for 64% -> 4% of each run, Pallas kernels for 0% -> 9%
where the time goes in v1:
time: 238 us
  blocking collectives  74.3 us (31%)
  starting transfers between devices  56.5 us (24%)
  waiting for transfers between devices  51.1 us (21%)
  Pallas kernels  37.3 us (16%)
  other arithmetic  10.8 us (5%)
  local copies, waits for them, and re-layouts  6.72 us (3%)
    psum x1, blocking collectives, shards(): lax.psum(jnp.concatenate([weight_local, grad_radial], axis=0), GX_GY_GZ)  74.3 us
    ppermute x12, waiting for transfers between devices, from_behind(): lax.ppermute(x, axis, [(i, (i + by) % devices) for i in range(devices)])  51.1 us
    ppermute x12, starting transfers between devices, from_behind(): lax.ppermute(x, axis, [(i, (i + by) % devices) for i in range(devices)])  29.2 us
    pallas_call x1, Pallas kernels, short_range(): pl.pallas_call(short_kernel, out_shape=(jax.ShapeDtypeStruct((GROUPS * HI...  16.7 us
    all_to_all x1, starting transfers between devices, shards(): lax.all_to_all(part.reshape(devices, share_rows, 4 * channels), GX_GY_GZ,...  15.6 us
    all_to_all x1, starting transfers between devices, shards(): lax.all_to_all(spread, GX_GY_GZ, 0, 0).reshape(points, 4 * channels)  11.7 us
    pallas_call x1, Pallas kernels, phase_sums(): pl.pallas_call(phase_kernel, grid=(points // step,), out_shape=(jax.Shape...  8.46 us
    pallas_call x1, Pallas kernels, ewald(): pl.pallas_call(ewald_kernel, grid=(points // step,), out_shape=(jax.Shape...  8.29 us
  transfers between devices with their start and end apart: 14, of which 7 were waited for; matrix products, arithmetic and copies ran while one was open for 4% of the time, Pallas kernels for 9%

profile of v1, /device:TPU:1, one launch (start us, length us, event | category | flops | bytes accessed | tf_op | source)
XLA Modules:
  0.0 237.6 jit_solution(18090156751509250148)
XLA Ops:
  0.7 1.6 pad_maximum_fusion.5.stacked_ref
  2.3 1.4 add_multiply_fusion.turns_ref
  3.7 8.5 %phase_sums.1 = (bf16[2048,512]{1,0:T(8,128)(2,1)}, bf16[2048,512]{1,0:T(8,128)(2,1)}, bf16[2048,256]{1,0:T(8,128)(2,1)}) custom-call(f32[3,512]{1,0:T(4,128)} %add_multiply_fusion.turns_ref, s32[3,2048]{1,0:T(4,128)} %miller_ref.3, bf16[128,512]{1,0:T(8,128)(2,1)} %pad_maximum_fusion.5.stacked_ref), custom_call_target="tpu_custom_call" | custom-call | tf_op jit(solution)/shard_map/phase_sums/pallas_call | solution.py:296
  12.2 15.6 %all-to-all-start = ((bf16[256,8,256]{2,1,0:T(8,128)(2,1)}), bf16[256,8,256]{2,1,0:T(8,128)(2,1)S(1)}, u32[]{:S(2)}, u32[]{:S(2)}) async-start(bf16[256,8,256]{2,1,0:T(8,128)(2,1)} %bitcast.35), calls=%async_computation | async-start | bytes 2097152 | tf_op jit(solution)/shard_map/all_to_all | solution.py:483
  27.8 0.6 copy.23
  28.4 1.8 project.1
  30.2 0.9 slice.131
  31.2 6.5 %collective-permute-start = (bf16[3,3,1,16,128]{4,3,2,1,0:T(8,128)(2,1)S(1)}, bf16[3,3,1,16,128]{4,3,2,1,0:T(8,128)(2,1)S(1)}, u32[]{:S(2)}, u32[]{:S(2)}) collective-permute-start(bf16[3,3,1,16,128]{4,3,2,1,0:T(8,128)(2,1)S(1)} %get-tuple-element.55), channel_id=1, source_target_pairs={{0,1},{1,2},{2,3},{3,0},{4,5},{5,6},{6,7},{7,4},{8,9},{9,10},{10,1... | collective-permute-start | bytes 110600 | tf_op jit(solution)/shard_map/ppermute | solution.py:211
  37.7 4.4 %collective-permute-done = bf16[3,3,1,16,128]{4,3,2,1,0:T(8,128)(2,1)S(1)} collective-permute-done((bf16[3,3,1,16,128]{4,3,2,1,0:T(8,128)(2,1)S(1)}, bf16[3,3,1,16,128]{4,3,2,1,0:T(8,128)(2,1)S(1)}, u32[]{:S(2)}, u32[]{:S(2)}) %collective-permute-start) | collective-permute-done | bytes 36896 | tf_op jit(solution)/shard_map/ppermute | solution.py:211
  42.1 15.3 %collective-permute-done.1 = bf16[3,3,1,16,128]{4,3,2,1,0:T(8,128)(2,1)S(1)} collective-permute-done((bf16[3,3,1,16,128]{4,3,2,1,0:T(8,128)(2,1)S(1)}, bf16[3,3,1,16,128]{4,3,2,1,0:T(8,128)(2,1)S(1)}, u32[]{:S(2)}, u32[]{:S(2)}) %collective-permute-start.1) | collective-permute-done | bytes 36896 | tf_op jit(solution)/shard_map/ppermute | solution.py:211
  57.5 1.3 collective-permute-start.2
  58.8 4.2 %collective-permute-start.3 = (bf16[3,1,5,16,128]{4,3,2,1,0:T(8,128)(2,1)S(1)}, bf16[3,1,5,16,128]{4,3,2,1,0:T(8,128)(2,1)S(1)}, u32[]{:S(2)}, u32[]{:S(2)}) collective-permute-start(bf16[3,1,5,16,128]{4,3,2,1,0:T(8,128)(2,1)S(1)} %get-tuple-element.54), channel_id=1, source_target_pairs={{0,60},{4,0},{8,4},{12,8},{16,12},{20,16},{24,20},{28,24},{32,28},... | collective-permute-start | bytes 184328 | tf_op jit(solution)/shard_map/ppermute | solution.py:211
  62.9 0.7 slice.138
  63.7 1.3 collective-permute-done.2
  65.0 1.3 collective-permute-start.4
  66.3 1.5 collective-permute-start.5
  67.8 0.1 constant_dynamic-slice_fusion
  67.9 0.1 pad.15.clone
  68.0 1.7 collective-permute-done.4
  69.8 0.1 pad_maximum_fusion.1
  69.9 1.2 maximum_maximum_fusion.table_ref
  71.1 16.7 %short_range.1 = (f32[2112,128]{1,0:T(8,128)}, f32[8,512]{1,0:T(8,128)}, f32[16,64]{1,0:T(8,128)}) custom-call(bf16[2112,128]{1,0:T(8,128)(2,1)} %maximum_maximum_fusion.table_ref, s32[16,512]{1,0:T(8,128)} %bitcast.48, f32[3,512]{1,0:T(4,128)} %bitcast.47, bf16[64,512]{1,0:T(8,128)(2,1)} %bitcast.43, f32[16,64]{1,0:T(8,128)} %radial_ref.1), custom_call_target="tpu_custom_call" | custom-call | tf_op jit(solution)/shard_map/short_range/pallas_call | solution.py:185
  87.8 1.4 convert.28
  89.2 0.2 copy-done.2
  89.4 1.8 collective-permute-start.6
  91.2 1.3 collective-permute-start.7
  92.5 0.3 convert_reduce_fusion
  92.8 0.7 multiply_convert_fusion.3
  93.5 0.1 pad_maximum_fusion.15
  93.6 1.1 broadcast_in_dim.8
  94.7 11.7 %all-to-all-start.1 = ((bf16[256,8,256]{2,1,0:T(8,128)(2,1)}), bf16[256,8,256]{2,1,0:T(8,128)(2,1)S(1)}, u32[]{:S(2)}, u32[]{:S(2)}) async-start(bf16[256,8,256]{2,1,0:T(8,128)(2,1)} %broadcast_in_dim.8), calls=%async_computation.1 | async-start | bytes 2097152 | tf_op jit(solution)/shard_map/all_to_all | solution.py:488
  106.5 1.4 collective-permute-start.8
  108.0 4.9 %collective-permute-start.9 = (bf16[3,1,5,16,128]{4,3,2,1,0:T(8,128)(2,1)S(1)}, bf16[3,1,5,16,128]{4,3,2,1,0:T(8,128)(2,1)S(1)}, u32[]{:S(2)}, u32[]{:S(2)}) collective-permute-start(bf16[3,1,5,16,128]{4,3,2,1,0:T(8,128)(2,1)S(1)} %get-tuple-element.48), channel_id=1, source_target_pairs={{0,60},{4,0},{8,4},{12,8},{16,12},{20,16},{24,20},{28,24},{32,28},... | collective-permute-start | bytes 184328 | tf_op jit(solution)/shard_map/ppermute | solution.py:211
  112.9 21.1 %collective-permute-done.8 = bf16[3,1,5,16,128]{4,3,2,1,0:T(8,128)(2,1)S(1)} collective-permute-done((bf16[3,1,5,16,128]{4,3,2,1,0:T(8,128)(2,1)S(1)}, bf16[3,1,5,16,128]{4,3,2,1,0:T(8,128)(2,1)S(1)}, u32[]{:S(2)}, u32[]{:S(2)}) %collective-permute-start.8) | collective-permute-done | bytes 61472 | tf_op jit(solution)/shard_map/ppermute | solution.py:211
  134.0 5.0 %collective-permute-start.10 = (bf16[3,3,1,16,128]{4,3,2,1,0:T(8,128)(2,1)S(1)}, bf16[3,3,1,16,128]{4,3,2,1,0:T(8,128)(2,1)S(1)}, u32[]{:S(2)}, u32[]{:S(2)}) collective-permute-start(bf16[3,3,1,16,128]{4,3,2,1,0:T(8,128)(2,1)S(1)} %get-tuple-element.51), channel_id=1, source_target_pairs={{0,1},{1,2},{2,3},{3,0},{4,5},{5,6},{6,7},{7,4},{8,9},{9,10},{10,1... | collective-permute-start | bytes 110600 | tf_op jit(solution)/shard_map/ppermute | solution.py:211
  139.0 1.0 collective-permute-done.10
  140.1 6.2 %collective-permute-done.11 = bf16[3,3,1,16,128]{4,3,2,1,0:T(8,128)(2,1)S(1)} collective-permute-done((bf16[3,3,1,16,128]{4,3,2,1,0:T(8,128)(2,1)S(1)}, bf16[3,3,1,16,128]{4,3,2,1,0:T(8,128)(2,1)S(1)}, u32[]{:S(2)}, u32[]{:S(2)}) %collective-permute-start.11) | collective-permute-done | bytes 36896 | tf_op jit(solution)/shard_map/ppermute | solution.py:211
  146.3 0.7 pad_maximum_fusion.3.rows_ref
  147.1 2.0 finish.1
  149.1 0.8 pad_maximum_fusion.14
  149.8 74.3 %psum.7 = f32[80,64]{1,0:T(8,128)S(1)} all-reduce(f32[80,64]{1,0:T(8,128)S(1)} %pad_maximum_fusion.14), channel_id=1, replica_groups=mesh['gx'=4,'gy_0'=4,'gy_1'=4,'gz_0'=2,'gz_1'=2] {'gx','gy_0','gy_1','gz..., use_global_device_ids=true, to_apply=%region_1.0 | all-reduce | flops 5120 | bytes 40960 | tf_op jit(solution)/shard_map/psum | solution.py:505
  224.1 0.6 slice.179
  224.7 0.6 slice.180
  225.4 1.0 copy-done.1
  226.4 8.3 %ewald.1 = (f32[64,512]{1,0:T(8,128)}, f32[3,512]{1,0:T(4,128)}) custom-call(bf16[2048,256]{1,0:T(8,128)(2,1)} %bitcast.27, bf16[2048,512]{1,0:T(8,128)(2,1)} %get-tuple-element.19.cos_ref, bf16[2048,512]{1,0:T(8,128)(2,1)} %get-tuple-element.20.sin_ref, s32[3,2048]{1,0:T(4,128)} %miller_ref.3, bf16[128,512]{1,0:T(8,128)(2,1)} %pad_maximum_fusion.5.stacked_ref), custom_call_target="tpu_custom_call" | custom-call | tf_op jit(solution)/shard_map/ewald/pallas_call | solution.py:354
  234.7 0.8 add_bitcast_fusion
  235.5 0.6 copy.17
  236.1 1.6 fusion
  (45 shorter events, 0.6 us)
Async XLA Ops:
  0.6 67.2 %copy-start = (f32[2048,64]{0,1:T(8,128)S(1)}, f32[2048,64]{0,1:T(8,128)}, u32[]{:S(2)}) copy-start(f32[2048,64]{0,1:T(8,128)} %param.17) | copy-start | bytes 1572868
  12.2 15.7 %copy-start.5 = (f32[1,1,1,3,512]{4,2,3,1,0:T(1,128)S(1)}, f32[1,1,1,3,512]{4,2,3,1,0:T(1,128)}, u32[]{:S(2)}) copy-start(f32[1,1,1,3,512]{4,2,3,1,0:T(1,128)} %param.13) | copy-start | bytes 18436
  12.2 80.4 %all-to-all-start = ((bf16[256,8,256]{2,1,0:T(8,128)(2,1)}), bf16[256,8,256]{2,1,0:T(8,128)(2,1)S(1)}, u32[]{:S(2)}, u32[]{:S(2)}) async-start(bf16[256,8,256]{2,1,0:T(8,128)(2,1)} %bitcast.35), calls=%async_computation | async-start | bytes 2097152 | tf_op jit(solution)/shard_map/all_to_all | solution.py:483
  31.2 11.0 %collective-permute-start = (bf16[3,3,1,16,128]{4,3,2,1,0:T(8,128)(2,1)S(1)}, bf16[3,3,1,16,128]{4,3,2,1,0:T(8,128)(2,1)S(1)}, u32[]{:S(2)}, u32[]{:S(2)}) collective-permute-start(bf16[3,3,1,16,128]{4,3,2,1,0:T(8,128)(2,1)S(1)} %get-tuple-element.55), channel_id=1, source_target_pairs={{0,1},{1,2},{2,3},{3,0},{4,5},{5,6},{6,7},{7,4},{8,9},{9,10},{10,1... | collective-permute-start | bytes 110600 | tf_op jit(solution)/shard_map/ppermute | solution.py:211
  37.7 19.8 %collective-permute-start.1 = (bf16[3,3,1,16,128]{4,3,2,1,0:T(8,128)(2,1)S(1)}, bf16[3,3,1,16,128]{4,3,2,1,0:T(8,128)(2,1)S(1)}, u32[]{:S(2)}, u32[]{:S(2)}) collective-permute-start(bf16[3,3,1,16,128]{4,3,2,1,0:T(8,128)(2,1)S(1)} %get-tuple-element.56), channel_id=1, source_target_pairs={{0,3},{1,0},{2,1},{3,2},{4,7},{5,4},{6,5},{7,6},{8,11},{9,8},{10,9... | collective-permute-start | bytes 110600 | tf_op jit(solution)/shard_map/ppermute | solution.py:211
  57.5 7.4 %collective-permute-start.2 = (bf16[3,1,5,16,128]{4,3,2,1,0:T(8,128)(2,1)S(1)}, bf16[3,1,5,16,128]{4,3,2,1,0:T(8,128)(2,1)S(1)}, u32[]{:S(2)}, u32[]{:S(2)}) collective-permute-start(bf16[3,1,5,16,128]{4,3,2,1,0:T(8,128)(2,1)S(1)} %get-tuple-element.53), channel_id=1, source_target_pairs={{0,4},{4,8},{8,12},{12,16},{16,20},{20,24},{24,28},{28,32},{32,36}... | collective-permute-start | bytes 184328 | tf_op jit(solution)/shard_map/ppermute | solution.py:211
  58.8 6.2 %collective-permute-start.3 = (bf16[3,1,5,16,128]{4,3,2,1,0:T(8,128)(2,1)S(1)}, bf16[3,1,5,16,128]{4,3,2,1,0:T(8,128)(2,1)S(1)}, u32[]{:S(2)}, u32[]{:S(2)}) collective-permute-start(bf16[3,1,5,16,128]{4,3,2,1,0:T(8,128)(2,1)S(1)} %get-tuple-element.54), channel_id=1, source_target_pairs={{0,60},{4,0},{8,4},{12,8},{16,12},{20,16},{24,20},{28,24},{32,28},... | collective-permute-start | bytes 184328 | tf_op jit(solution)/shard_map/ppermute | solution.py:211
  65.0 4.8 %collective-permute-start.4 = (bf16[1,5,5,16,128]{4,3,2,1,0:T(8,128)(2,1)S(1)}, bf16[1,5,5,16,128]{4,3,2,1,0:T(8,128)(2,1)S(1)}, u32[]{:S(2)}, u32[]{:S(2)}) collective-permute-start(bf16[1,5,5,16,128]{4,3,2,1,0:T(8,128)(2,1)S(1)} %get-tuple-element.49), channel_id=1, source_target_pairs={{0,64},{64,128},{128,192},{192,0},{1,65},{65,129},{129,193},{193,1... | collective-permute-start | bytes 307208 | tf_op jit(solution)/shard_map/ppermute | solution.py:211
  66.3 3.5 %collective-permute-start.5 = (bf16[1,5,5,16,128]{4,3,2,1,0:T(8,128)(2,1)S(1)}, bf16[1,5,5,16,128]{4,3,2,1,0:T(8,128)(2,1)S(1)}, u32[]{:S(2)}, u32[]{:S(2)}) collective-permute-start(bf16[1,5,5,16,128]{4,3,2,1,0:T(8,128)(2,1)S(1)} %get-tuple-element.50), channel_id=1, source_target_pairs={{0,192},{64,0},{128,64},{192,128},{1,193},{65,1},{129,65},{193,129... | collective-permute-start | bytes 307208 | tf_op jit(solution)/shard_map/ppermute | solution.py:211
  87.8 1.6 copy-start.2
  89.4 17.0 %collective-permute-start.6 = (bf16[1,5,5,16,128]{4,3,2,1,0:T(8,128)(2,1)S(1)}, bf16[1,5,5,16,128]{4,3,2,1,0:T(8,128)(2,1)S(1)}, u32[]{:S(2)}, u32[]{:S(2)}) collective-permute-start(bf16[1,5,5,16,128]{4,3,2,1,0:T(8,128)(2,1)S(1)} %bitcast.45), channel_id=1, source_target_pairs={{0,64},{64,128},{128,192},{192,0},{1,65},{65,129},{129,193},{193,1... | collective-permute-start | bytes 307208 | tf_op jit(solution)/shard_map/ppermute | solution.py:211
  91.2 15.2 %collective-permute-start.7 = (bf16[1,5,5,16,128]{4,3,2,1,0:T(8,128)(2,1)S(1)}, bf16[1,5,5,16,128]{4,3,2,1,0:T(8,128)(2,1)S(1)}, u32[]{:S(2)}, u32[]{:S(2)}) collective-permute-start(bf16[1,5,5,16,128]{4,3,2,1,0:T(8,128)(2,1)S(1)} %bitcast.44), channel_id=1, source_target_pairs={{0,192},{64,0},{128,64},{192,128},{1,193},{65,1},{129,65},{193,129... | collective-permute-start | bytes 307208 | tf_op jit(solution)/shard_map/ppermute | solution.py:211
  94.7 130.7 %all-to-all-start.1 = ((bf16[256,8,256]{2,1,0:T(8,128)(2,1)}), bf16[256,8,256]{2,1,0:T(8,128)(2,1)S(1)}, u32[]{:S(2)}, u32[]{:S(2)}) async-start(bf16[256,8,256]{2,1,0:T(8,128)(2,1)} %broadcast_in_dim.8), calls=%async_computation.1 | async-start | bytes 2097152 | tf_op jit(solution)/shard_map/all_to_all | solution.py:488
  106.5 27.4 %collective-permute-start.8 = (bf16[3,1,5,16,128]{4,3,2,1,0:T(8,128)(2,1)S(1)}, bf16[3,1,5,16,128]{4,3,2,1,0:T(8,128)(2,1)S(1)}, u32[]{:S(2)}, u32[]{:S(2)}) collective-permute-start(bf16[3,1,5,16,128]{4,3,2,1,0:T(8,128)(2,1)S(1)} %get-tuple-element.47), channel_id=1, source_target_pairs={{0,4},{4,8},{8,12},{12,16},{16,20},{20,24},{24,28},{28,32},{32,36}... | collective-permute-start | bytes 184328 | tf_op jit(solution)/shard_map/ppermute | solution.py:211
  108.0 26.0 %collective-permute-start.9 = (bf16[3,1,5,16,128]{4,3,2,1,0:T(8,128)(2,1)S(1)}, bf16[3,1,5,16,128]{4,3,2,1,0:T(8,128)(2,1)S(1)}, u32[]{:S(2)}, u32[]{:S(2)}) collective-permute-start(bf16[3,1,5,16,128]{4,3,2,1,0:T(8,128)(2,1)S(1)} %get-tuple-element.48), channel_id=1, source_target_pairs={{0,60},{4,0},{8,4},{12,8},{16,12},{20,16},{24,20},{28,24},{32,28},... | collective-permute-start | bytes 184328 | tf_op jit(solution)/shard_map/ppermute | solution.py:211
  134.0 6.0 %collective-permute-start.10 = (bf16[3,3,1,16,128]{4,3,2,1,0:T(8,128)(2,1)S(1)}, bf16[3,3,1,16,128]{4,3,2,1,0:T(8,128)(2,1)S(1)}, u32[]{:S(2)}, u32[]{:S(2)}) collective-permute-start(bf16[3,3,1,16,128]{4,3,2,1,0:T(8,128)(2,1)S(1)} %get-tuple-element.51), channel_id=1, source_target_pairs={{0,1},{1,2},{2,3},{3,0},{4,5},{5,6},{6,7},{7,4},{8,9},{9,10},{10,1... | collective-permute-start | bytes 110600 | tf_op jit(solution)/shard_map/ppermute | solution.py:211
  139.0 7.3 %collective-permute-start.11 = (bf16[3,3,1,16,128]{4,3,2,1,0:T(8,128)(2,1)S(1)}, bf16[3,3,1,16,128]{4,3,2,1,0:T(8,128)(2,1)S(1)}, u32[]{:S(2)}, u32[]{:S(2)}) collective-permute-start(bf16[3,3,1,16,128]{4,3,2,1,0:T(8,128)(2,1)S(1)} %get-tuple-element.52), channel_id=1, source_target_pairs={{0,3},{1,0},{2,1},{3,2},{4,7},{5,4},{6,5},{7,6},{8,11},{9,8},{10,9... | collective-permute-start | bytes 110600 | tf_op jit(solution)/shard_map/ppermute | solution.py:211
  139.0 10.0 %copy-start.6 = (f32[16,64]{1,0:T(8,128)S(1)}, f32[16,64]{1,0:T(8,128)}, u32[]{:S(2)}) copy-start(f32[16,64]{1,0:T(8,128)} %get-tuple-element.30) | copy-start | bytes 12292
  225.3 1.0 copy-start.1
  226.4 8.3 %copy-start.7 = (f32[8,512]{1,0:T(8,128)S(1)}, f32[8,512]{1,0:T(8,128)}, u32[]{:S(2)}) copy-start(f32[8,512]{1,0:T(8,128)} %get-tuple-element.28) | copy-start | bytes 49156
  226.4 8.3 %copy-start.8 = (f32[3]{0:T(128)S(1)}, f32[3]{0:T(128)}, u32[]{:S(2)}) copy-start(f32[3]{0:T(128)} %constant.53) | copy-start | bytes 40
  226.4 9.7 %copy-start.3 = (bf16[1,1,1,64,512]{4,3,2,1,0:T(8,128)(2,1)S(1)}, bf16[1,1,1,64,512]{4,3,2,1,0:T(8,128)(2,1)}, u32[]{:S(2)}) copy-start(bf16[1,1,1,64,512]{4,3,2,1,0:T(8,128)(2,1)} %param.12) | copy-start | bytes 196612
  226.4 9.7 %copy-start.4 = (f32[64,512]{1,0:T(8,128)S(1)}, f32[64,512]{1,0:T(8,128)}, u32[]{:S(2)}) copy-start(f32[64,512]{1,0:T(8,128)} %get-tuple-element.26) | copy-start | bytes 393220

commit v2 on v1

--- a/solution.py
+++ b/solution.py
@@ -11,6 +11,8 @@
 
 GY = ("gy_0", "gy_1")
 GZ = ("gz_0", "gz_1")
+CHIPS = ("gx", "gy_0", "gy_1", "gz_0")
+PAIR = "gz_1"
 GX_GY_GZ = ("gx", "gy_0", "gy_1", "gz_0", "gz_1")
 
 circle_angle = 2.0 * math.pi
@@ -41,16 +43,28 @@
     )
 
 
+def gains_of(gain_rows, labels, shape):
+    columns = jnp.transpose(gain_rows)
+    gains = jnp.zeros(shape, jnp.float32)
+    for kind in range(gain_rows.shape[0]):
+        gains = jnp.where(labels == kind, columns[:, kind : kind + 1], gains)
+    return gains
+
+
 def short_kernel(
     table_ref,
     ids_ref,
     pos_ref,
     dy_ref,
     radial_ref,
+    mix_ref,
+    gain_ref,
     zgrad_ref,
     own_ref,
-    rgrad_ref,
+    sums_ref,
     lhs_ref,
+    feat_ref,
+    gains_ref,
     high_ref,
     low_ref,
     near_ref,
@@ -67,8 +81,17 @@
     width = 2.0 * spacing
     share = listed ** (-0.5)
     for g in range(GROUPS):
-        part = table_ref[g * HIGH : (g + 1) * HIGH, :].astype(f32)
-        lhs_ref[g * ROWS : (g + 1) * ROWS, :] = jnp.transpose(part)[0:ROWS, :].astype(bf16)
+        part = jnp.transpose(table_ref[g * HIGH : (g + 1) * HIGH, :].astype(f32))
+        feat = part[0:channels].astype(bf16)
+        gains = gains_of(gain_ref[...], part[ROWS : ROWS + 1], (channels, HIGH))
+        feat_ref[g] = feat
+        gains_ref[g] = gains
+        z = lax.dot_general(
+            mix_ref[...], feat, (((0,), (0,)), ((), ())), preferred_element_type=f32
+        )
+        lhs_ref[g * ROWS : (g + 1) * ROWS, :] = jnp.concatenate(
+            [z * gains, part[channels:ROWS]], axis=0
+        ).astype(bf16)
     ids = ids_ref[...]
     slot = lax.shift_right_logical(ids, 9)
     atom = jnp.bitwise_and(ids, 511)
@@ -163,20 +186,28 @@
             spread, hot(j), (((1,), (1,)), ((), ())), preferred_element_type=f32
         )
     own_ref[...] = own_grad
-    rgrad_ref[...] = (
+    sums_ref[...] = jnp.zeros_like(sums_ref)
+    sums_ref[channels : channels + count, 0:channels] = (
         radial[0:count, 0:channels]
         + radial[count:, 0:channels]
         + radial[0:count, channels:]
         + radial[count:, channels:]
     )
+    weight = jnp.zeros((channels, channels), f32)
     for g in range(GROUPS):
+        z_hi, z_lo = split_two(acc_ref[g * ROWS : g * ROWS + channels, :] * gains_ref[g])
+        for piece in (z_hi, z_lo):
+            weight = weight + lax.dot_general(
+                feat_ref[g], piece, (((1,), (1,)), ((), ())), preferred_element_type=f32
+            )
         part = jnp.transpose(acc_ref[g * ROWS : (g + 1) * ROWS, :])
         zgrad_ref[g * HIGH : (g + 1) * HIGH, :] = jnp.concatenate(
             [part, jnp.zeros((HIGH, 128 - ROWS), f32)], axis=1
         )
-
-
-def short_range(table, ids, pos, dy, radial, interpret=False):
+    sums_ref[0:channels, 0:channels] = weight
+
+
+def short_range(table, ids, pos, dy, radial, mix, gain, interpret=False):
     channels, atoms = dy.shape
     listed = ids.shape[0]
     count = radial.shape[0]
@@ -187,12 +218,14 @@
         out_shape=(
             jax.ShapeDtypeStruct((GROUPS * HIGH, 128), jnp.float32),
             jax.ShapeDtypeStruct((8, atoms), jnp.float32),
-            jax.ShapeDtypeStruct((count, channels), jnp.float32),
+            jax.ShapeDtypeStruct((128, 128), jnp.float32),
         ),
-        in_specs=[spec] * 5,
+        in_specs=[spec] * 7,
         out_specs=(spec,) * 3,
         scratch_shapes=[
             vmem((GROUPS * ROWS, HIGH), jnp.bfloat16),
+            vmem((GROUPS, channels, HIGH), jnp.bfloat16),
+            vmem((GROUPS, channels, HIGH), jnp.float32),
             vmem((listed, atoms), jnp.int32),
             vmem((listed, atoms), jnp.int32),
             vmem((listed, channels, atoms), jnp.bfloat16),
@@ -203,7 +236,7 @@
         ],
         interpret=interpret,
         name="short_range",
-    )(table, ids, pos, dy, radial)
+    )(table, ids, pos, dy, radial, mix, gain)
 
 
 def from_behind(x, axis, by):
@@ -211,56 +244,52 @@
     return lax.ppermute(x, axis, [(i, (i + by) % devices) for i in range(devices)])
 
 
-def project_kernel(h_ref, mix_ref, gain_ref, kind_ref, pos_ref, table_ref, gains_ref):
-    f32, bf16 = jnp.float32, jnp.bfloat16
+def pack_kernel(h_ref, kind_ref, pos_ref, table_ref):
+    f32 = jnp.float32
     channels, atoms = h_ref.shape
-    kinds = gain_ref.shape[0]
-    columns = jnp.transpose(gain_ref[...])
-    label = kind_ref[...]
-    gains = jnp.zeros((channels, atoms), f32)
-    for kind in range(kinds):
-        gains = jnp.where(label == kind, columns[:, kind : kind + 1], gains)
-    gains_ref[...] = gains
-    projected = lax.dot_general(
-        mix_ref[...], h_ref[...], (((0,), (0,)), ((), ())), preferred_element_type=f32
-    )
-    z = (projected * gains).astype(bf16).astype(f32)
-    pos = pos_ref[...]
-    p_hi, p_lo = split_two(pos)
+    p_hi, p_lo = split_two(pos_ref[...])
     none = jnp.zeros((1, atoms), f32)
     rows = jnp.concatenate(
-        [z, p_hi.astype(f32), none, p_lo.astype(f32), none, jnp.zeros((128 - ROWS, atoms), f32)],
+        [
+            h_ref[...].astype(f32),
+            p_hi.astype(f32),
+            none,
+            p_lo.astype(f32),
+            none,
+            kind_ref[...].astype(f32),
+            jnp.zeros((127 - ROWS, atoms), f32),
+        ],
         axis=0,
     )
-    table_ref[...] = jnp.transpose(rows).astype(bf16)
-
-
-def project(h, mix, table, kinds, pos):
-    channels, atoms = h.shape
+    table_ref[...] = jnp.transpose(rows).astype(jnp.bfloat16)
+
+
+def pack(h, kinds, pos):
     return pl.pallas_call(
-        project_kernel,
-        out_shape=(
-            jax.ShapeDtypeStruct((atoms, 128), jnp.bfloat16),
-            jax.ShapeDtypeStruct((channels, atoms), jnp.float32),
-        ),
-        in_specs=[WHOLE] * 5,
-        out_specs=(WHOLE,) * 2,
-        name="project",
-    )(h, mix, table, kinds, pos)
-
-
-def phase_kernel(turns_ref, miller_ref, stacked_ref, cos_ref, sin_ref, part_ref, flip_ref, t_ref):
+        pack_kernel,
+        out_shape=jax.ShapeDtypeStruct((h.shape[1], 128), jnp.bfloat16),
+        in_specs=[WHOLE] * 3,
+        out_specs=WHOLE,
+        name="pack",
+    )(h, kinds, pos)
+
+
+def phase_kernel(
+    where_ref, pos_ref, miller_ref, h_ref, dy_ref, cos_ref, sin_ref, part_ref, flip_ref, t_ref
+):
     f32, bf16 = jnp.float32, jnp.bfloat16
-    width = stacked_ref.shape[0]
+    width = 2 * h_ref.shape[0]
 
     @pl.when(pl.program_id(0) == 0)
     def _():
-        flip_ref[...] = jnp.transpose(stacked_ref[...])
-
-    whole = turns_ref[...]
-    t_hi, t_rest = whole.astype(bf16), whole - whole.astype(bf16).astype(f32)
-    t_mid = t_rest.astype(bf16)
-    t_lo = (t_rest - t_mid.astype(f32)).astype(bf16)
+        flip_ref[...] = jnp.transpose(jnp.concatenate([h_ref[...], dy_ref[...]], axis=0))
+
+    pos = pos_ref[...]
+    turns = jnp.concatenate(
+        [(pos[d : d + 1] + where_ref[0, d]) / where_ref[1, d] for d in range(3)], axis=0
+    )
+    t_hi, t_rest = split_two(turns)[0], turns - split_two(turns)[0].astype(f32)
+    t_mid, t_lo = split_two(t_rest)
     rhs = jnp.concatenate([t_hi, t_mid, t_lo], axis=0)
     m = miller_ref[...].astype(f32).astype(bf16)
     lhs = jnp.concatenate([m, m, m], axis=0)
@@ -289,22 +318,26 @@
     ).astype(part_ref.dtype)
 
 
-def phase_sums(turns, miller, stacked):
+def phase_sums(place, pos, miller, h, dy):
     points = miller.shape[1]
-    width, atoms = stacked.shape
+    channels, atoms = h.shape
+    width = 2 * channels
     step = min(CHUNK, points)
+    still = lambda i: (0, 0)
     return pl.pallas_call(
         phase_kernel,
         grid=(points // step,),
         out_shape=(
             jax.ShapeDtypeStruct((points, atoms), jnp.bfloat16),
             jax.ShapeDtypeStruct((points, atoms), jnp.bfloat16),
-            jax.ShapeDtypeStruct((points, 2 * width), jnp.bfloat16),
+            jax.ShapeDtypeStruct((points, 2 * width), jnp.float32),
         ),
         in_specs=[
-            pl.BlockSpec(turns.shape, lambda i: (0, 0)),
+            pl.BlockSpec(memory_space=pltpu.SMEM),
+            pl.BlockSpec(pos.shape, still),
             pl.BlockSpec((miller.shape[0], step), lambda i: (0, i)),
-            pl.BlockSpec(stacked.shape, lambda i: (0, 0)),
+            pl.BlockSpec(h.shape, still),
+            pl.BlockSpec(dy.shape, still),
         ],
         out_specs=(
             pl.BlockSpec((step, atoms), lambda i: (i, 0)),
@@ -315,90 +348,116 @@
             pltpu.VMEM((atoms, width), jnp.bfloat16),
             pltpu.VMEM((step, atoms), jnp.float32),
         ],
+        cost_estimate=pl.CostEstimate(
+            flops=6 * points * atoms * width, transcendentals=0, bytes_accessed=4 * points * atoms
+        ),
         name="phase_sums",
-    )(turns, miller, stacked)
-
-
-def ewald_kernel(coeff_ref, cos_ref, sin_ref, miller_ref, stacked_ref, h_ref, pos_ref):
+    )(place, pos, miller, h, dy)
+
+
+def ewald_kernel(last, where_ref, coeff_ref, cos_ref, sin_ref, miller_ref, h_ref, dy_ref, *rest):
     f32, bf16 = jnp.float32, jnp.bfloat16
-    width = stacked_ref.shape[0]
-    channels = width // 2
-
-    @pl.when(pl.program_id(0) == 0)
+    channels = h_ref.shape[0]
+    width = 2 * channels
+    step = pl.program_id(0)
+    if last:
+        from_sums, from_turn, short_ref, near_ref, atom_ref, pos_ref, both_ref, sums_ref, turn_ref = rest
+    else:
+        sums_ref, turn_ref, both_ref = rest
+
+    @pl.when(step == 0)
     def _():
-        h_ref[...] = jnp.zeros_like(h_ref)
-        pos_ref[...] = jnp.zeros_like(pos_ref)
+        both_ref[...] = jnp.concatenate([h_ref[...], dy_ref[...]], axis=0)
+        sums_ref[...] = from_sums[...] if last else jnp.zeros_like(sums_ref)
+        turn_ref[...] = from_turn[...] if last else jnp.zeros_like(turn_ref)
 
     coeffs = coeff_ref[...]
     cos_part, sin_part = cos_ref[...], sin_ref[...]
     over_rows = (((0,), (0,)), ((), ()))
-    h_ref[...] += lax.dot_general(
+    sums_ref[...] += lax.dot_general(
         coeffs[:, 0:channels], cos_part, over_rows, preferred_element_type=f32
     ) + lax.dot_general(
         coeffs[:, width : width + channels], sin_part, over_rows, preferred_element_type=f32
     )
-    along_u = jnp.dot(coeffs[:, 0:width], stacked_ref[...], preferred_element_type=f32)
-    along_v = jnp.dot(coeffs[:, width:], stacked_ref[...], preferred_element_type=f32)
+    along_u = jnp.dot(coeffs[:, 0:width], both_ref[...], preferred_element_type=f32)
+    along_v = jnp.dot(coeffs[:, width : 2 * width], both_ref[...], preferred_element_type=f32)
     angle = along_v * cos_part.astype(f32) - along_u * sin_part.astype(f32)
     a_hi, a_lo = split_two(angle)
     m = miller_ref[...].astype(f32).astype(bf16)
-    pos_ref[...] += jnp.dot(m, a_hi, preferred_element_type=f32) + jnp.dot(
+    turn_ref[...] += jnp.dot(m, a_hi, preferred_element_type=f32) + jnp.dot(
         m, a_lo, preferred_element_type=f32
     )
-
-
-def ewald(coeffs, cos_all, sin_all, miller, stacked):
+    if last:
+
+        @pl.when(step == pl.num_programs(0) - 1)
+        def _():
+            atom_ref[...] = (dy_ref[...].astype(f32) + sums_ref[...] + short_ref[...]).astype(bf16)
+            for d in range(3):
+                pos_ref[d : d + 1, :] = (
+                    turn_ref[d : d + 1, :] * (circle_angle / where_ref[1, d])
+                    + near_ref[d : d + 1, :]
+                )
+
+
+def ewald(place, coeffs, cos_all, sin_all, miller, h, dy, more=()):
     points, atoms = cos_all.shape
-    width = stacked.shape[0]
+    channels = h.shape[0]
+    dims = miller.shape[0]
     step = min(CHUNK, points)
+    last = len(more) > 0
+    still = lambda i: (0, 0)
+    sums = jax.ShapeDtypeStruct((channels, atoms), jnp.float32)
+    turn = jax.ShapeDtypeStruct((dims, atoms), jnp.float32)
+    scratch = [pltpu.VMEM((2 * channels, atoms), jnp.bfloat16)]
+    if last:
+        scratch += [pltpu.VMEM(sums.shape, jnp.float32), pltpu.VMEM(turn.shape, jnp.float32)]
+        sums = jax.ShapeDtypeStruct(sums.shape, jnp.bfloat16)
     return pl.pallas_call(
-        ewald_kernel,
+        functools.partial(ewald_kernel, last),
         grid=(points // step,),
-        out_shape=(
-            jax.ShapeDtypeStruct((width // 2, atoms), jnp.float32),
-            jax.ShapeDtypeStruct((miller.shape[0], atoms), jnp.float32),
-        ),
+        out_shape=(sums, turn),
         in_specs=[
+            pl.BlockSpec(memory_space=pltpu.SMEM),
             pl.BlockSpec((step, coeffs.shape[1]), lambda i: (i, 0)),
             pl.BlockSpec((step, atoms), lambda i: (i, 0)),
             pl.BlockSpec((step, atoms), lambda i: (i, 0)),
-            pl.BlockSpec((miller.shape[0], step), lambda i: (0, i)),
-            pl.BlockSpec(stacked.shape, lambda i: (0, 0)),
-        ],
-        out_specs=(
-            pl.BlockSpec((width // 2, atoms), lambda i: (0, 0)),
-            pl.BlockSpec((miller.shape[0], atoms), lambda i: (0, 0)),
+            pl.BlockSpec((dims, step), lambda i: (0, i)),
+            pl.BlockSpec(h.shape, still),
+            pl.BlockSpec(dy.shape, still),
+        ]
+        + [pl.BlockSpec(x.shape, still) for x in more],
+        out_specs=(pl.BlockSpec(sums.shape, still), pl.BlockSpec(turn.shape, still)),
+        scratch_shapes=scratch,
+        cost_estimate=pl.CostEstimate(
+            flops=8 * points * atoms * channels, transcendentals=0, bytes_accessed=4 * points * atoms
         ),
         name="ewald",
-    )(coeffs, cos_all, sin_all, miller, stacked)
-
-
-def finish_kernel(rows_ref, gains_ref, mix_ref, h_ref, own_ref, short_ref, weight_ref, pos_ref):
+    )(place, coeffs, cos_all, sin_all, miller, h, dy, *more)
+
+
+def finish_kernel(rows_ref, kind_ref, gain_ref, mix_ref, own_ref, short_ref, pos_ref):
     f32, bf16 = jnp.float32, jnp.bfloat16
-    channels = h_ref.shape[0]
+    channels, atoms = short_ref.shape
     flat = jnp.transpose(rows_ref[...])
-    zscaled = (flat[0:channels] * gains_ref[...]).astype(bf16)
+    gains = gains_of(gain_ref[...], kind_ref[...], (channels, atoms))
+    zscaled = (flat[0:channels] * gains).astype(bf16)
     short_ref[...] = jnp.dot(mix_ref[...], zscaled, preferred_element_type=f32)
-    weight_ref[...] = lax.dot_general(
-        h_ref[...], zscaled, (((1,), (1,)), ((), ())), preferred_element_type=f32
-    )
     halves = flat[channels : channels + 8]
     pos_ref[...] = halves + pltpu.roll(halves, 4, 0) + own_ref[...]
 
 
-def finish(rows, gains, mix, h, own):
-    channels, atoms = h.shape
+def finish(rows, kinds, gain, mix, own):
+    channels, atoms = mix.shape[0], rows.shape[0]
     return pl.pallas_call(
         finish_kernel,
         out_shape=(
             jax.ShapeDtypeStruct((channels, atoms), jnp.float32),
-            jax.ShapeDtypeStruct((channels, channels), jnp.float32),
             jax.ShapeDtypeStruct((8, atoms), jnp.float32),
         ),
         in_specs=[WHOLE] * 5,
-        out_specs=(WHOLE,) * 3,
+        out_specs=(WHOLE,) * 2,
         name="finish",
-    )(rows, gains, mix, h, own)
+    )(rows, kinds, gain, mix, own)
 
 
 def coefficients(totals, filt_rows, norm_atoms, norm_k):
@@ -458,6 +517,7 @@
     h = atom_embedding[0, 0, 0]
     dy = output_adjoint[0, 0, 0]
     pos = fractional_coords[0, 0, 0]
+    kinds = element_labels[0, 0]
     channels, atoms = h.shape
     points = miller_triples.shape[1]
     devices = lax.axis_size(GX_GY_GZ)
@@ -467,26 +527,17 @@
     anchor = jnp.stack([lax.axis_index("gx"), lax.axis_index(GY), lax.axis_index(GZ)]).astype(
         jnp.float32
     )
+    place = jnp.stack([anchor, lengths])
     share_rows = points // devices
     share_start = lax.axis_index(GX_GY_GZ) * share_rows
-
-    own_table, gains = project(
-        h, channel_mixing_matrix, element_channel_factor, element_labels[0, 0], pos
-    )
+    core = lax.axis_index(PAIR)
+    groups = lax.axis_size(CHIPS)
+    half = points // 2
+
+    own_table = pack(h, kinds, pos)
     sides = ((GZ, 2), (GY, 1), ("gx", 0))
     cells = own_table[0:432].reshape(3, 3, 3, 16, 128)
     wide = widened(cells, sides)
-
-    turns = (pos + anchor[:, None]) / lengths[:, None]
-    stacked = jnp.concatenate([h, dy], axis=0)
-    cos_all, sin_all, part = phase_sums(turns, miller_triples, stacked)
-    pieces = lax.all_to_all(part.reshape(devices, share_rows, 4 * channels), GX_GY_GZ, 0, 0)
-    totals = jnp.sum(pieces.astype(jnp.float32), axis=0)
-    filt_rows = lax.dynamic_slice_in_dim(reciprocal_kernel, share_start, share_rows, 0)
-    own_coeffs, filter_share = coefficients(totals, filt_rows, norm_atoms, norm_k)
-    spread = jnp.broadcast_to(own_coeffs[None], (devices, share_rows, 4 * channels))
-    coeffs = lax.all_to_all(spread, GX_GY_GZ, 0, 0).reshape(points, 4 * channels)
-
     table = jnp.concatenate(
         [
             wide.reshape(2000, 128),
@@ -495,19 +546,55 @@
         ],
         axis=0,
     )
-    ghost_grad, own_grad, grad_radial = short_range(
-        table, adjacent_ghost_entries[0, 0, 0], pos, dy, distance_kernel
-    )
+
+    split = miller_triples.reshape(3, groups, 2, share_rows)
+    even, odd = split[:, :, 0].reshape(3, half), split[:, :, 1].reshape(3, half)
+    miller_mine = jnp.where(core == 0, even, odd)
+    miller_next = jnp.where(core == 0, odd, even)
+    cos_next, sin_next, part_next = phase_sums(place, pos, miller_next, h, dy)
+    received = from_behind(part_next, PAIR, 1)
+    cos_mine, sin_mine, part_mine = phase_sums(place, pos, miller_mine, h, dy)
+    paired = (part_mine + received).astype(jnp.bfloat16)
+    paired, table = lax.optimization_barrier((paired, table))
+    pieces = lax.all_to_all(paired.reshape(groups, share_rows, 4 * channels), CHIPS, 0, 0)
+
+    ghost_grad, own_grad, sums = short_range(
+        table,
+        adjacent_ghost_entries[0, 0, 0],
+        pos,
+        dy,
+        distance_kernel,
+        channel_mixing_matrix,
+        element_channel_factor,
+    )
+    sums = sums + from_behind(sums, PAIR, 1)
+    tiles = sums.astype(jnp.bfloat16).reshape(1, 16, 1, 8, 128)
+    tiles = jnp.broadcast_to(tiles, (groups // 32, 16, 2, 8, 128)).reshape(groups, 8, 128)
+
+    totals = jnp.sum(pieces.astype(jnp.float32), axis=0)
+    filt_rows = lax.dynamic_slice_in_dim(reciprocal_kernel, share_start, share_rows, 0)
+    own_coeffs, filter_share = coefficients(totals, filt_rows, norm_atoms, norm_k)
+    spread = jnp.broadcast_to(own_coeffs[None], (groups, share_rows, 4 * channels))
+    got = lax.all_to_all(jnp.concatenate([spread, tiles], axis=2), CHIPS, 0, 0)
+    tile_sum = jnp.sum(got[:, :, 4 * channels :].astype(jnp.float32), axis=0)
+    coeffs_mine = got.reshape(half, 4 * channels + 128)
+    coeffs_next = from_behind(coeffs_mine, PAIR, 1)
+
     grid = ghost_grad[0:2000].reshape(5, 5, 5, 16, 128)
     inner = folded(grid, sides[::-1])
     rows = jnp.concatenate([inner.reshape(432, 128), ghost_grad[2000:2080]], axis=0)
-    atom_short, weight_local, pos_short = finish(rows, gains, channel_mixing_matrix, h, own_grad)
-    summed = lax.psum(jnp.concatenate([weight_local, grad_radial], axis=0), GX_GY_GZ)
-    weight_grad, radial_grad = summed[0:channels], summed[channels:]
-
-    ewald_h, ewald_pos = ewald(coeffs, cos_all, sin_all, miller_triples, stacked)
-    atom_grad = (dy.astype(jnp.float32) + ewald_h + atom_short).astype(jnp.bfloat16)
-    position_grad = ewald_pos * (circle_angle / lengths)[:, None] + pos_short[0:3]
+    atom_short, pos_short = finish(
+        rows, kinds, element_channel_factor, channel_mixing_matrix, own_grad
+    )
+    every = lax.all_to_all(jnp.broadcast_to(tile_sum[None], (16, 8, 128)), GY, 0, 0)
+    every = every.reshape(128, 128)
+    weight_grad = every[0:channels, 0:channels]
+    radial_grad = every[channels : channels + distance_kernel.shape[0], 0:channels]
+
+    first = ewald(place, coeffs_mine, cos_mine, sin_mine, miller_mine, h, dy)
+    atom_grad, position_grad = ewald(
+        place, coeffs_next, cos_next, sin_next, miller_next, h, dy, (*first, atom_short, pos_short)
+    )
     return (
         atom_grad[None, None, None],
         position_grad[None, None, None],

time: 238 us -> 146 us (0.61)
  blocking collectives: 74.3 us -> 0 us
  waiting for transfers between devices: 51.1 us -> 22.5 us
  starting transfers between devices: 56.5 us -> 62.6 us
  Pallas kernels: 37.3 us -> 41.3 us
  local copies, waits for them, and re-layouts: 6.72 us -> 9.54 us
  other arithmetic: 10.8 us -> 8.37 us
    psum x1 -> x0, blocking collectives: 74.3 us -> none  [shards(): lax.psum(jnp.concatenate([weight_local, grad_radial], axis=0), GX_GY_GZ)]
    ppermute x12 -> x15, waiting for transfers between devices: 51.1 us -> 19.4 us  [from_behind(): lax.ppermute(x, axis, [(i, (i + by) % devices) for i in range(devices)])]
    ppermute x12 -> x15, starting transfers between devices: 29.2 us -> 34 us  [from_behind(): lax.ppermute(x, axis, [(i, (i + by) % devices) for i in range(devices)])]
    all_to_all x2 -> x3, waiting for transfers between devices: 0.01 us -> 3.13 us  [the longest x1 3.12 us: shards(): got = lax.all_to_all(jnp.concatenate([spread, tiles], axis=2), CHIPS, 0, 0)]
    pallas_call x1 -> x2, Pallas kernels: 8.46 us -> 10.2 us  [phase_sums(): pl.pallas_call(phase_kernel, grid=(points // step,), out_shape=(jax.Shape...]
    pallas_call x2 -> x3, Pallas kernels: 10.1 us -> 11.5 us  [the longest x2 9.87 us: ewald(): pl.pallas_call(functools.partial(ewald_kernel, last), grid=(points // ste...]
    all_to_all x2 -> x3, starting transfers between devices: 27.3 us -> 28.6 us  [the longest x1 13.4 us: shards(): got = lax.all_to_all(jnp.concatenate([spread, tiles], axis=2), CHIPS, 0, 0)]
  transfers between devices with their start and end apart: 14 -> 18, of which waited for: 7 -> 6; matrix products, arithmetic and copies ran while one was open for 4% -> 7% of each run, Pallas kernels for 9% -> 24%
where the time goes in v2:
time: 146 us; the launch traced here: 145 us
  starting transfers between devices  62.6 us (43%)
  Pallas kernels  41.3 us (28%)
  waiting for transfers between devices  22.5 us (15%)
  local copies, waits for them, and re-layouts  9.54 us (7%)
  other arithmetic  8.37 us (6%)
    ppermute x15, starting transfers between devices, from_behind(): lax.ppermute(x, axis, [(i, (i + by) % devices) for i in range(devices)])  34 us
    ppermute x15, waiting for transfers between devices, from_behind(): lax.ppermute(x, axis, [(i, (i + by) % devices) for i in range(devices)])  19.4 us
    pallas_call x1, Pallas kernels, short_range(): pl.pallas_call(short_kernel, out_shape=(jax.ShapeDtypeStruct((GROUPS * HI...  17.5 us
    all_to_all x1, starting transfers between devices, shards(): got = lax.all_to_all(jnp.concatenate([spread, tiles], axis=2), CHIPS, 0, 0)  13.4 us
    all_to_all x1, starting transfers between devices, shards(): lax.all_to_all(paired.reshape(groups, share_rows, 4 * channels), CHIPS, 0...  11.7 us
    pallas_call x2, Pallas kernels, phase_sums(): pl.pallas_call(phase_kernel, grid=(points // step,), out_shape=(jax.Shape...  10.2 us
    pallas_call x2, Pallas kernels, ewald(): pl.pallas_call(functools.partial(ewald_kernel, last), grid=(points // ste...  9.87 us
    unnamed x17, local copies, waits for them, and re-layouts  3.63 us
  transfers between devices with their start and end apart: 18, of which 6 were waited for; matrix products, arithmetic and copies ran while one was open for 7% of the time, Pallas kernels for 24%

profile of v2, /device:TPU:1, one launch (start us, length us, event | category | flops | bytes accessed | tf_op | source)
XLA Modules:
  0.0 145.2 jit_solution(10391634997969431737)
XLA Ops:
  0.6 1.3 copy.25
  2.0 1.6 %pack.1 = bf16[512,128]{1,0:T(8,128)(2,1)} custom-call(bf16[64,512]{1,0:T(8,128)(2,1)} %bitcast.39, s32[1,512]{1,0:T(1,128)} %bitcast.58, f32[3,512]{1,0:T(4,128)} %bitcast.53), custom_call_target="tpu_custom_call" | custom-call | tf_op jit(solution)/shard_map/pack/pallas_call | solution.py:268
  3.6 0.9 slice.171
  4.6 3.3 %collective-permute-start.2 = (bf16[3,3,1,16,128]{4,3,2,1,0:T(8,128)(2,1)S(1)}, bf16[3,3,1,16,128]{4,3,2,1,0:T(8,128)(2,1)S(1)}, u32[]{:S(2)}, u32[]{:S(2)}) collective-permute-start(bf16[3,3,1,16,128]{4,3,2,1,0:T(8,128)(2,1)S(1)} %get-tuple-element.71), channel_id=1, source_target_pairs={{0,3},{1,0},{2,1},{3,2},{4,7},{5,4},{6,5},{7,6},{8,11},{9,8},{10,9... | collective-permute-start | bytes 110600 | tf_op jit(solution)/shard_map/ppermute | solution.py:244
  7.8 5.2 %collective-permute-start.1 = (bf16[3,3,1,16,128]{4,3,2,1,0:T(8,128)(2,1)S(1)}, bf16[3,3,1,16,128]{4,3,2,1,0:T(8,128)(2,1)S(1)}, u32[]{:S(2)}, u32[]{:S(2)}) collective-permute-start(bf16[3,3,1,16,128]{4,3,2,1,0:T(8,128)(2,1)S(1)} %get-tuple-element.70), channel_id=1, source_target_pairs={{0,1},{1,2},{2,3},{3,0},{4,5},{5,6},{6,7},{7,4},{8,9},{9,10},{10,1... | collective-permute-start | bytes 110600 | tf_op jit(solution)/shard_map/ppermute | solution.py:244
  13.0 1.4 reshape.148
  14.4 1.2 fusion.1
  15.7 5.0 %collective-permute-start.4 = (bf16[3,1,5,16,128]{4,3,2,1,0:T(8,128)(2,1)S(1)}, bf16[3,1,5,16,128]{4,3,2,1,0:T(8,128)(2,1)S(1)}, u32[]{:S(2)}, u32[]{:S(2)}) collective-permute-start(bf16[3,1,5,16,128]{4,3,2,1,0:T(8,128)(2,1)S(1)} %get-tuple-element.69), channel_id=1, source_target_pairs={{0,60},{4,0},{8,4},{12,8},{16,12},{20,16},{24,20},{28,24},{32,28},... | collective-permute-start | bytes 184328 | tf_op jit(solution)/shard_map/ppermute | solution.py:244
  20.7 0.6 pad_maximum_fusion.15.where_ref
  21.2 0.7 select_n.24.miller_ref
  22.0 5.1 %phase_sums.3 = (bf16[1024,512]{1,0:T(8,128)(2,1)}, bf16[1024,512]{1,0:T(8,128)(2,1)}, f32[1024,256]{1,0:T(8,128)}) custom-call(f32[2,3]{1,0:T(2,128)} %pad_maximum_fusion.15.where_ref, f32[3,512]{1,0:T(4,128)} %bitcast.54, s32[3,1024]{1,0:T(4,128)} %select_n.24.miller_ref, bf16[64,512]{1,0:T(8,128)(2,1)} %bitcast.40, bf16[64,512]{1,0:T(8,128)(2,1)} %bitcast.44), custom_call_target="tpu_custom_call" | custom-call | flops 402653184 | bytes 2097152 | tf_op jit(solution)/shard_map/phase_sums/pallas_call | solution.py:327
  27.1 3.9 %collective-permute-start = (f32[1024,256]{1,0:T(8,128)}, f32[1024,256]{1,0:T(8,128)S(1)}, u32[]{:S(2)}, u32[]{:S(2)}) collective-permute-start(f32[1024,256]{1,0:T(8,128)} %get-tuple-element.23), channel_id=1, source_target_pairs={{0,1},{1,0},{2,3},{3,2},{4,5},{5,4},{6,7},{7,6},{8,9},{9,8},{10,11... | collective-permute-start | bytes 3145736 | tf_op jit(solution)/shard_map/ppermute | solution.py:244
  31.0 2.6 %collective-permute-start.6 = (bf16[1,5,5,16,128]{4,3,2,1,0:T(8,128)(2,1)S(1)}, bf16[1,5,5,16,128]{4,3,2,1,0:T(8,128)(2,1)S(1)}, u32[]{:S(2)}, u32[]{:S(2)}) collective-permute-start(bf16[1,5,5,16,128]{4,3,2,1,0:T(8,128)(2,1)S(1)} %get-tuple-element.65), channel_id=1, source_target_pairs={{0,192},{64,0},{128,64},{192,128},{1,193},{65,1},{129,65},{193,129... | collective-permute-start | bytes 307208 | tf_op jit(solution)/shard_map/ppermute | solution.py:244
  33.6 0.7 select_n.22.miller_ref
  34.4 5.1 %phase_sums.2 = (bf16[1024,512]{1,0:T(8,128)(2,1)}, bf16[1024,512]{1,0:T(8,128)(2,1)}, f32[1024,256]{1,0:T(8,128)}) custom-call(f32[2,3]{1,0:T(2,128)} %pad_maximum_fusion.15.where_ref, f32[3,512]{1,0:T(4,128)} %bitcast.55, s32[3,1024]{1,0:T(4,128)} %select_n.22.miller_ref, bf16[64,512]{1,0:T(8,128)(2,1)} %bitcast.41, bf16[64,512]{1,0:T(8,128)(2,1)} %bitcast.45), custom_call_target="tpu_custom_call" | custom-call | flops 402653184 | bytes 2097152 | tf_op jit(solution)/shard_map/phase_sums/pallas_call | solution.py:327
  39.5 0.1 pad_maximum_fusion.2
  39.6 1.2 maximum_maximum_fusion.table_ref
  40.8 0.9 add_convert_fusion
  41.7 11.7 %all-to-all-start = ((bf16[128,8,256]{2,1,0:T(8,128)(2,1)}), bf16[128,8,256]{2,1,0:T(8,128)(2,1)S(1)}, u32[]{:S(2)}, u32[]{:S(2)}) async-start(bf16[128,8,256]{2,1,0:T(8,128)(2,1)} %bitcast.8), calls=%async_computation | async-start | bytes 1048576 | tf_op jit(solution)/shard_map/all_to_all | solution.py:559
  53.5 17.5 %short_range.1 = (f32[2112,128]{1,0:T(8,128)}, f32[8,512]{1,0:T(8,128)}, f32[128,128]{1,0:T(8,128)}) custom-call(bf16[2112,128]{1,0:T(8,128)(2,1)} %maximum_maximum_fusion.table_ref, s32[16,512]{1,0:T(8,128)} %bitcast.57, f32[3,512]{1,0:T(4,128)} %bitcast.56, bf16[64,512]{1,0:T(8,128)(2,1)} %bitcast.46, f32[16,64]{1,0:T(8,128)} %radial_ref.1, ...), custom_call_target="tpu_custom_call" | custom-call | tf_op jit(solution)/shard_map/short_range/pallas_call | solution.py:216
  70.9 0.9 collective-permute-start.7
  71.9 1.3 convert.28
  73.3 0.1 convert_reduce_fusion
  73.4 0.7 multiply_convert_fusion.3
  74.2 1.0 pad_maximum_fusion
  75.2 13.4 %all-to-all-start.1 = ((bf16[128,8,384]{2,1,0:T(8,128)(2,1)}), bf16[128,8,384]{2,1,0:T(8,128)(2,1)S(1)}, u32[]{:S(2)}, u32[]{:S(2)}) async-start(bf16[128,8,384]{2,1,0:T(8,128)(2,1)} %pad_maximum_fusion), calls=%async_computation.1 | async-start | bytes 1572864 | tf_op jit(solution)/shard_map/all_to_all | solution.py:578
  88.6 2.4 %collective-permute-start.10 = (bf16[1,5,5,16,128]{4,3,2,1,0:T(8,128)(2,1)S(1)}, bf16[1,5,5,16,128]{4,3,2,1,0:T(8,128)(2,1)S(1)}, u32[]{:S(2)}, u32[]{:S(2)}) collective-permute-start(bf16[1,5,5,16,128]{4,3,2,1,0:T(8,128)(2,1)S(1)} %bitcast.52), channel_id=1, source_target_pairs={{0,192},{64,0},{128,64},{192,128},{1,193},{65,1},{129,65},{193,129... | collective-permute-start | bytes 307208 | tf_op jit(solution)/shard_map/ppermute | solution.py:244
  91.2 2.9 %collective-permute-done.10 = bf16[1,5,5,16,128]{4,3,2,1,0:T(8,128)(2,1)S(1)} collective-permute-done((bf16[1,5,5,16,128]{4,3,2,1,0:T(8,128)(2,1)S(1)}, bf16[1,5,5,16,128]{4,3,2,1,0:T(8,128)(2,1)S(1)}, u32[]{:S(2)}, u32[]{:S(2)}) %collective-permute-start.10) | collective-permute-done | bytes 102432 | tf_op jit(solution)/shard_map/ppermute | solution.py:244
  94.2 3.4 %collective-permute-done.9 = bf16[1,5,5,16,128]{4,3,2,1,0:T(8,128)(2,1)S(1)} collective-permute-done((bf16[1,5,5,16,128]{4,3,2,1,0:T(8,128)(2,1)S(1)}, bf16[1,5,5,16,128]{4,3,2,1,0:T(8,128)(2,1)S(1)}, u32[]{:S(2)}, u32[]{:S(2)}) %collective-permute-start.9) | collective-permute-done | bytes 102432 | tf_op jit(solution)/shard_map/ppermute | solution.py:244
  97.7 1.4 collective-permute-start.11
  99.1 4.2 %collective-permute-start.12 = (bf16[3,1,5,16,128]{4,3,2,1,0:T(8,128)(2,1)S(1)}, bf16[3,1,5,16,128]{4,3,2,1,0:T(8,128)(2,1)S(1)}, u32[]{:S(2)}, u32[]{:S(2)}) collective-permute-start(bf16[3,1,5,16,128]{4,3,2,1,0:T(8,128)(2,1)S(1)} %get-tuple-element.63), channel_id=1, source_target_pairs={{0,60},{4,0},{8,4},{12,8},{16,12},{20,16},{24,20},{28,24},{32,28},... | collective-permute-start | bytes 184328 | tf_op jit(solution)/shard_map/ppermute | solution.py:244
  103.3 5.8 %collective-permute-done.11 = bf16[3,1,5,16,128]{4,3,2,1,0:T(8,128)(2,1)S(1)} collective-permute-done((bf16[3,1,5,16,128]{4,3,2,1,0:T(8,128)(2,1)S(1)}, bf16[3,1,5,16,128]{4,3,2,1,0:T(8,128)(2,1)S(1)}, u32[]{:S(2)}, u32[]{:S(2)}) %collective-permute-start.11) | collective-permute-done | bytes 61472 | tf_op jit(solution)/shard_map/ppermute | solution.py:244
  109.2 3.1 %all-to-all-done.1 = bf16[128,8,384]{2,1,0:T(8,128)(2,1)S(1)} async-done(((bf16[128,8,384]{2,1,0:T(8,128)(2,1)}), bf16[128,8,384]{2,1,0:T(8,128)(2,1)S(1)}, u32[]{:S(2)}, u32[]{:S(2)}) %all-to-all-start.1) | async-done | bytes 786464 | tf_op jit(solution)/shard_map/all_to_all | solution.py:578
  112.3 1.6 %collective-permute-start.8 = (bf16[1024,384]{1,0:T(8,128)(2,1)S(1)}, bf16[1024,384]{1,0:T(8,128)(2,1)S(1)}, u32[]{:S(2)}, u32[]{:S(2)}) collective-permute-start(bf16[1024,384]{1,0:T(8,128)(2,1)S(1)} %bitcast.26), channel_id=1, source_target_pairs={{0,1},{1,0},{2,3},{3,2},{4,5},{5,4},{6,7},{7,6},{8,9},{9,8},{10,11... | collective-permute-start | bytes 2359304 | tf_op jit(solution)/shard_map/ppermute | solution.py:244
  113.9 3.6 %collective-permute-start.13 = (bf16[3,3,1,16,128]{4,3,2,1,0:T(8,128)(2,1)S(1)}, bf16[3,3,1,16,128]{4,3,2,1,0:T(8,128)(2,1)S(1)}, u32[]{:S(2)}, u32[]{:S(2)}) collective-permute-start(bf16[3,3,1,16,128]{4,3,2,1,0:T(8,128)(2,1)S(1)} %get-tuple-element.66), channel_id=1, source_target_pairs={{0,1},{1,2},{2,3},{3,0},{4,5},{5,6},{6,7},{7,4},{8,9},{9,10},{10,1... | collective-permute-start | bytes 110600 | tf_op jit(solution)/shard_map/ppermute | solution.py:244
  117.5 1.0 collective-permute-done.13
  118.6 6.2 %collective-permute-done.14 = bf16[3,3,1,16,128]{4,3,2,1,0:T(8,128)(2,1)S(1)} collective-permute-done((bf16[3,3,1,16,128]{4,3,2,1,0:T(8,128)(2,1)S(1)}, bf16[3,3,1,16,128]{4,3,2,1,0:T(8,128)(2,1)S(1)}, u32[]{:S(2)}, u32[]{:S(2)}) %collective-permute-start.14) | collective-permute-done | bytes 36896 | tf_op jit(solution)/shard_map/ppermute | solution.py:244
  124.8 0.1 convert_reduce_fusion.1
  125.0 0.6 broadcast_in_dim.34
  125.6 3.5 %all-to-all-start.2 = ((f32[16,8,128]{2,1,0:T(8,128)}), f32[16,8,128]{2,1,0:T(8,128)S(1)}, u32[]{:S(2)}, u32[]{:S(2)}) async-start(f32[16,8,128]{2,1,0:T(8,128)} %broadcast_in_dim.34), calls=%async_computation.2 | async-start | bytes 131072 | tf_op jit(solution)/shard_map/all_to_all | solution.py:589
  129.1 0.7 pad_maximum_fusion.4.rows_ref
  129.9 2.0 %finish.1 = (f32[64,512]{1,0:T(8,128)}, f32[8,512]{1,0:T(8,128)}) custom-call(f32[512,128]{1,0:T(8,128)} %pad_maximum_fusion.4.rows_ref, s32[1,512]{1,0:T(1,128)} %bitcast.59, f32[4,64]{1,0:T(4,128)} %gain_ref.3, bf16[64,64]{1,0:T(8,128)(2,1)} %mix_ref.3, f32[8,512]{1,0:T(8,128)} %get-tuple-element.34.own_ref), custom_call_target="tpu_custom_call" | custom-call | tf_op jit(solution)/shard_map/finish/pallas_call | solution.py:451
  131.9 4.8 %ewald.2 = (f32[64,512]{1,0:T(8,128)}, f32[3,512]{1,0:T(4,128)}) custom-call(f32[2,3]{1,0:T(2,128)} %pad_maximum_fusion.15.where_ref, bf16[1024,384]{1,0:T(8,128)(2,1)} %bitcast.27, bf16[1024,512]{1,0:T(8,128)(2,1)} %get-tuple-element.29.cos_ref, bf16[1024,512]{1,0:T(8,128)(2,1)} %get-tuple-element.30.sin_ref, s32[3,1024]{1,0:T(4,128)} %select_n.22.miller_ref, ...), custom_call_target="tpu_custom_call" | custom-call | flops 268435456 | bytes 2097152 | tf_op jit(solution)/shard_map/ewald/pallas_call | solution.py:415
  136.7 0.6 slice.192
  137.3 0.6 slice.193
  138.0 0.9 copy-done.4
  138.8 5.1 %ewald.3 = (bf16[64,512]{1,0:T(8,128)(2,1)}, f32[3,512]{1,0:T(4,128)}) custom-call(f32[2,3]{1,0:T(2,128)} %pad_maximum_fusion.15.where_ref, bf16[1024,384]{1,0:T(8,128)(2,1)} %copy-done.4, bf16[1024,512]{1,0:T(8,128)(2,1)} %get-tuple-element.27.cos_ref, bf16[1024,512]{1,0:T(8,128)(2,1)} %get-tuple-element.28.sin_ref, s32[3,1024]{1,0:T(4,128)} %select_n.24.miller_ref, ...), custom_call_target="tpu_custom_call" | custom-call | flops 268435456 | bytes 2097152 | tf_op jit(solution)/shard_map/ewald/pallas_call | solution.py:415
  143.9 1.3 copy.21
  (57 shorter events, 1.0 us)
Async XLA Ops:
  0.6 71.1 %copy-start = (f32[2048,64]{0,1:T(8,128)S(1)}, f32[2048,64]{0,1:T(8,128)}, u32[]{:S(2)}) copy-start(f32[2048,64]{0,1:T(8,128)} %param.17) | copy-start | bytes 1572868
  2.0 18.7 %copy-start.6 = (f32[1,3]{1,0:T(1,128)S(1)}, f32[1,3]{1,0:T(1,128)}, u32[]{:S(2)}) copy-start(f32[1,3]{1,0:T(1,128)} %constant.49) | copy-start | bytes 40
  4.6 11.1 %collective-permute-start.2 = (bf16[3,3,1,16,128]{4,3,2,1,0:T(8,128)(2,1)S(1)}, bf16[3,3,1,16,128]{4,3,2,1,0:T(8,128)(2,1)S(1)}, u32[]{:S(2)}, u32[]{:S(2)}) collective-permute-start(bf16[3,3,1,16,128]{4,3,2,1,0:T(8,128)(2,1)S(1)} %get-tuple-element.71), channel_id=1, source_target_pairs={{0,3},{1,0},{2,1},{3,2},{4,7},{5,4},{6,5},{7,6},{8,11},{9,8},{10,9... | collective-permute-start | bytes 110600 | tf_op jit(solution)/shard_map/ppermute | solution.py:244
  7.8 7.8 %collective-permute-start.1 = (bf16[3,3,1,16,128]{4,3,2,1,0:T(8,128)(2,1)S(1)}, bf16[3,3,1,16,128]{4,3,2,1,0:T(8,128)(2,1)S(1)}, u32[]{:S(2)}, u32[]{:S(2)}) collective-permute-start(bf16[3,3,1,16,128]{4,3,2,1,0:T(8,128)(2,1)S(1)} %get-tuple-element.70), channel_id=1, source_target_pairs={{0,1},{1,2},{2,3},{3,0},{4,5},{5,6},{6,7},{7,4},{8,9},{9,10},{10,1... | collective-permute-start | bytes 110600 | tf_op jit(solution)/shard_map/ppermute | solution.py:244
  15.7 15.3 %collective-permute-start.4 = (bf16[3,1,5,16,128]{4,3,2,1,0:T(8,128)(2,1)S(1)}, bf16[3,1,5,16,128]{4,3,2,1,0:T(8,128)(2,1)S(1)}, u32[]{:S(2)}, u32[]{:S(2)}) collective-permute-start(bf16[3,1,5,16,128]{4,3,2,1,0:T(8,128)(2,1)S(1)} %get-tuple-element.69), channel_id=1, source_target_pairs={{0,60},{4,0},{8,4},{12,8},{16,12},{20,16},{24,20},{28,24},{32,28},... | collective-permute-start | bytes 184328 | tf_op jit(solution)/shard_map/ppermute | solution.py:244
  20.6 10.3 %collective-permute-start.3 = (bf16[3,1,5,16,128]{4,3,2,1,0:T(8,128)(2,1)S(1)}, bf16[3,1,5,16,128]{4,3,2,1,0:T(8,128)(2,1)S(1)}, u32[]{:S(2)}, u32[]{:S(2)}) collective-permute-start(bf16[3,1,5,16,128]{4,3,2,1,0:T(8,128)(2,1)S(1)} %get-tuple-element.68), channel_id=1, source_target_pairs={{0,4},{4,8},{8,12},{12,16},{16,20},{20,24},{24,28},{28,32},{32,36}... | collective-permute-start | bytes 184328 | tf_op jit(solution)/shard_map/ppermute | solution.py:244
  27.1 13.7 %collective-permute-start = (f32[1024,256]{1,0:T(8,128)}, f32[1024,256]{1,0:T(8,128)S(1)}, u32[]{:S(2)}, u32[]{:S(2)}) collective-permute-start(f32[1024,256]{1,0:T(8,128)} %get-tuple-element.23), channel_id=1, source_target_pairs={{0,1},{1,0},{2,3},{3,2},{4,5},{5,4},{6,7},{7,6},{8,9},{9,8},{10,11... | collective-permute-start | bytes 3145736 | tf_op jit(solution)/shard_map/ppermute | solution.py:244
  31.0 8.5 %collective-permute-start.6 = (bf16[1,5,5,16,128]{4,3,2,1,0:T(8,128)(2,1)S(1)}, bf16[1,5,5,16,128]{4,3,2,1,0:T(8,128)(2,1)S(1)}, u32[]{:S(2)}, u32[]{:S(2)}) collective-permute-start(bf16[1,5,5,16,128]{4,3,2,1,0:T(8,128)(2,1)S(1)} %get-tuple-element.65), channel_id=1, source_target_pairs={{0,192},{64,0},{128,64},{192,128},{1,193},{65,1},{129,65},{193,129... | collective-permute-start | bytes 307208 | tf_op jit(solution)/shard_map/ppermute | solution.py:244
  33.6 5.9 %collective-permute-start.5 = (bf16[1,5,5,16,128]{4,3,2,1,0:T(8,128)(2,1)S(1)}, bf16[1,5,5,16,128]{4,3,2,1,0:T(8,128)(2,1)S(1)}, u32[]{:S(2)}, u32[]{:S(2)}) collective-permute-start(bf16[1,5,5,16,128]{4,3,2,1,0:T(8,128)(2,1)S(1)} %get-tuple-element.64), channel_id=1, source_target_pairs={{0,64},{64,128},{128,192},{192,0},{1,65},{65,129},{129,193},{193,1... | collective-permute-start | bytes 307208 | tf_op jit(solution)/shard_map/ppermute | solution.py:244
  34.4 5.2 %slice-start = ((bf16[512,128]{1,0:T(8,128)(2,1)}), bf16[80,128]{1,0:T(8,128)(2,1)S(1)}, s32[]{:S(2)}) async-start(bf16[512,128]{1,0:T(8,128)(2,1)} %pack.1), calls=%async_computation.3 | async-start | bytes 40960 | tf_op jit(solution)/shard_map/slice | solution.py:544
  39.5 1.3 copy-start.3
  41.7 31.6 %all-to-all-start = ((bf16[128,8,256]{2,1,0:T(8,128)(2,1)}), bf16[128,8,256]{2,1,0:T(8,128)(2,1)S(1)}, u32[]{:S(2)}, u32[]{:S(2)}) async-start(bf16[128,8,256]{2,1,0:T(8,128)(2,1)} %bitcast.8), calls=%async_computation | async-start | bytes 1048576 | tf_op jit(solution)/shard_map/all_to_all | solution.py:559
  70.9 2.3 %copy-start.5 = (f32[128,128]{1,0:T(8,128)S(1)}, f32[128,128]{1,0:T(8,128)}, u32[]{:S(2)}) copy-start(f32[128,128]{1,0:T(8,128)} %get-tuple-element.26) | copy-start | bytes 196612
  70.9 2.3 %collective-permute-start.7 = (f32[128,128]{1,0:T(8,128)}, f32[128,128]{1,0:T(8,128)S(1)}, u32[]{:S(2)}, u32[]{:S(2)}) collective-permute-start(f32[128,128]{1,0:T(8,128)} %get-tuple-element.26), channel_id=1, source_target_pairs={{0,1},{1,0},{2,3},{3,2},{4,5},{5,4},{6,7},{7,6},{8,9},{9,8},{10,11... | collective-permute-start | bytes 196616 | tf_op jit(solution)/shard_map/ppermute | solution.py:244
  75.2 15.8 %copy-start.2 = (f32[2112,128]{1,0:T(8,128)S(1)}, f32[2112,128]{1,0:T(8,128)}, u32[]{:S(2)}) copy-start(f32[2112,128]{1,0:T(8,128)} %get-tuple-element.33) | copy-start | bytes 3244036
  75.2 37.1 %all-to-all-start.1 = ((bf16[128,8,384]{2,1,0:T(8,128)(2,1)}), bf16[128,8,384]{2,1,0:T(8,128)(2,1)S(1)}, u32[]{:S(2)}, u32[]{:S(2)}) async-start(bf16[128,8,384]{2,1,0:T(8,128)(2,1)} %pad_maximum_fusion), calls=%async_computation.1 | async-start | bytes 1572864 | tf_op jit(solution)/shard_map/all_to_all | solution.py:578
  88.6 5.5 %collective-permute-start.10 = (bf16[1,5,5,16,128]{4,3,2,1,0:T(8,128)(2,1)S(1)}, bf16[1,5,5,16,128]{4,3,2,1,0:T(8,128)(2,1)S(1)}, u32[]{:S(2)}, u32[]{:S(2)}) collective-permute-start(bf16[1,5,5,16,128]{4,3,2,1,0:T(8,128)(2,1)S(1)} %bitcast.52), channel_id=1, source_target_pairs={{0,192},{64,0},{128,64},{192,128},{1,193},{65,1},{129,65},{193,129... | collective-permute-start | bytes 307208 | tf_op jit(solution)/shard_map/ppermute | solution.py:244
  91.1 6.5 %collective-permute-start.9 = (bf16[1,5,5,16,128]{4,3,2,1,0:T(8,128)(2,1)S(1)}, bf16[1,5,5,16,128]{4,3,2,1,0:T(8,128)(2,1)S(1)}, u32[]{:S(2)}, u32[]{:S(2)}) collective-permute-start(bf16[1,5,5,16,128]{4,3,2,1,0:T(8,128)(2,1)S(1)} %bitcast.51), channel_id=1, source_target_pairs={{0,64},{64,128},{128,192},{192,0},{1,65},{65,129},{129,193},{193,1... | collective-permute-start | bytes 307208 | tf_op jit(solution)/shard_map/ppermute | solution.py:244
  97.7 11.4 %collective-permute-start.11 = (bf16[3,1,5,16,128]{4,3,2,1,0:T(8,128)(2,1)S(1)}, bf16[3,1,5,16,128]{4,3,2,1,0:T(8,128)(2,1)S(1)}, u32[]{:S(2)}, u32[]{:S(2)}) collective-permute-start(bf16[3,1,5,16,128]{4,3,2,1,0:T(8,128)(2,1)S(1)} %get-tuple-element.62), channel_id=1, source_target_pairs={{0,4},{4,8},{8,12},{12,16},{16,20},{20,24},{24,28},{28,32},{32,36}... | collective-permute-start | bytes 184328 | tf_op jit(solution)/shard_map/ppermute | solution.py:244
  99.1 10.0 %collective-permute-start.12 = (bf16[3,1,5,16,128]{4,3,2,1,0:T(8,128)(2,1)S(1)}, bf16[3,1,5,16,128]{4,3,2,1,0:T(8,128)(2,1)S(1)}, u32[]{:S(2)}, u32[]{:S(2)}) collective-permute-start(bf16[3,1,5,16,128]{4,3,2,1,0:T(8,128)(2,1)S(1)} %get-tuple-element.63), channel_id=1, source_target_pairs={{0,60},{4,0},{8,4},{12,8},{16,12},{20,16},{24,20},{28,24},{32,28},... | collective-permute-start | bytes 184328 | tf_op jit(solution)/shard_map/ppermute | solution.py:244
  112.3 13.3 %copy-start.1 = (bf16[128,8,384]{2,1,0:T(8,128)(2,1)}, bf16[128,8,384]{2,1,0:T(8,128)(2,1)S(1)}, u32[]{:S(2)}) copy-start(bf16[128,8,384]{2,1,0:T(8,128)(2,1)S(1)} %all-to-all-done.1) | copy-start | bytes 2359300
  112.3 25.6 %collective-permute-start.8 = (bf16[1024,384]{1,0:T(8,128)(2,1)S(1)}, bf16[1024,384]{1,0:T(8,128)(2,1)S(1)}, u32[]{:S(2)}, u32[]{:S(2)}) collective-permute-start(bf16[1024,384]{1,0:T(8,128)(2,1)S(1)} %bitcast.26), channel_id=1, source_target_pairs={{0,1},{1,0},{2,3},{3,2},{4,5},{5,4},{6,7},{7,6},{8,9},{9,8},{10,11... | collective-permute-start | bytes 2359304 | tf_op jit(solution)/shard_map/ppermute | solution.py:244
  113.9 4.7 %collective-permute-start.13 = (bf16[3,3,1,16,128]{4,3,2,1,0:T(8,128)(2,1)S(1)}, bf16[3,3,1,16,128]{4,3,2,1,0:T(8,128)(2,1)S(1)}, u32[]{:S(2)}, u32[]{:S(2)}) collective-permute-start(bf16[3,3,1,16,128]{4,3,2,1,0:T(8,128)(2,1)S(1)} %get-tuple-element.66), channel_id=1, source_target_pairs={{0,1},{1,2},{2,3},{3,0},{4,5},{5,6},{6,7},{7,4},{8,9},{9,10},{10,1... | collective-permute-start | bytes 110600 | tf_op jit(solution)/shard_map/ppermute | solution.py:244
  117.5 7.3 %collective-permute-start.14 = (bf16[3,3,1,16,128]{4,3,2,1,0:T(8,128)(2,1)S(1)}, bf16[3,3,1,16,128]{4,3,2,1,0:T(8,128)(2,1)S(1)}, u32[]{:S(2)}, u32[]{:S(2)}) collective-permute-start(bf16[3,3,1,16,128]{4,3,2,1,0:T(8,128)(2,1)S(1)} %get-tuple-element.67), channel_id=1, source_target_pairs={{0,3},{1,0},{2,1},{3,2},{4,7},{5,4},{6,5},{7,6},{8,11},{9,8},{10,9... | collective-permute-start | bytes 110600 | tf_op jit(solution)/shard_map/ppermute | solution.py:244
  125.6 11.1 %all-to-all-start.2 = ((f32[16,8,128]{2,1,0:T(8,128)}), f32[16,8,128]{2,1,0:T(8,128)S(1)}, u32[]{:S(2)}, u32[]{:S(2)}) async-start(f32[16,8,128]{2,1,0:T(8,128)} %broadcast_in_dim.34), calls=%async_computation.2 | async-start | bytes 131072 | tf_op jit(solution)/shard_map/all_to_all | solution.py:589
  138.0 0.9 copy-start.4

commit v3 on v2

v3 whole, which is shorter than its diff:
```python
import functools
import math

import jax
import jax.numpy as jnp
from jax import lax
from jax.experimental import pallas as pl
from jax.experimental.pallas import tpu as pltpu
from jax.sharding import Mesh
from jax.sharding import PartitionSpec as P

GY = ("gy_0", "gy_1")
GZ = ("gz_0", "gz_1")
CHIPS = ("gx", "gy_0", "gy_1", "gz_0")
PAIR = "gz_1"
GX_GY_GZ = ("gx", "gy_0", "gy_1", "gz_0", "gz_1")

circle_angle = 2.0 * math.pi
CHUNK = 256
SHARE = 8
SIN_TERMS = (6.28316404, -41.33714227, 81.34076528, -70.99339569)
COS_TERMS = (0.99999995, -19.73917143, 64.93459054, -85.24032775, 56.2423573)
WHOLE = pl.BlockSpec(memory_space=pltpu.VMEM)

reach_sq = 0.75
GROUPS = 9
ROWS = 72
BLOCKS = 135
HIGH = BLOCKS // GROUPS * 16


def split_two(x):
    high = x.astype(jnp.bfloat16)
    return high, (x - high.astype(jnp.float32)).astype(jnp.bfloat16)


def row_pick(first, second, third, shape):
    row = lax.broadcasted_iota(jnp.int32, shape, 0) % 4
    spread = lambda v: jnp.broadcast_to(v, shape)
    return jnp.where(
        row == 0,
        spread(first),
        jnp.where(row == 1, spread(second), jnp.where(row == 2, spread(third), 0.0)),
    )


def gains_of(gain_rows, labels, shape):
    columns = jnp.transpose(gain_rows)
    gains = jnp.zeros(shape, jnp.float32)
    for kind in range(gain_rows.shape[0]):
        gains = jnp.where(labels == kind, columns[:, kind : kind + 1], gains)
    return gains


def short_kernel(
    table_ref,
    ids_ref,
    pos_ref,
    dy_ref,
    radial_ref,
    mix_ref,
    gain_ref,
    zgrad_ref,
    thin_ref,
    own_ref,
    sums_ref,
    lhs_ref,
    feat_ref,
    gains_ref,
    high_ref,
    low_ref,
    near_ref,
    rel_ref,
    basis_ref,
    filt_ref,
    acc_ref,
):
    channels, atoms = dy_ref.shape
    listed = ids_ref.shape[0]
    count = radial_ref.shape[0]
    f32, bf16 = jnp.float32, jnp.bfloat16
    spacing = reach_sq / (count - 1)
    width = 2.0 * spacing
    share = listed ** (-0.5)
    for g in range(GROUPS):
        part = jnp.transpose(table_ref[g * HIGH : (g + 1) * HIGH, :].astype(f32))
        feat = part[0:channels].astype(bf16)
        gains = gains_of(gain_ref[...], part[ROWS : ROWS + 1], (channels, HIGH))
        feat_ref[g] = feat
        gains_ref[g] = gains
        z = lax.dot_general(
            mix_ref[...], feat, (((0,), (0,)), ((), ())), preferred_element_type=f32
        )
        lhs_ref[g * ROWS : (g + 1) * ROWS, :] = jnp.concatenate(
            [z * gains, part[channels:ROWS]], axis=0
        ).astype(bf16)
    ids = ids_ref[...]
    slot = lax.shift_right_logical(ids, 9)
    atom = jnp.bitwise_and(ids, 511)
    block = lax.shift_right_logical(atom, 4)
    ox = slot // 9
    oy = (slot // 3) % 3
    oz = slot % 3
    qx = block // 9
    qy = (block // 3) % 3
    qz = block % 3
    grid = ((3 * ox + qx - 2) * 5 + 3 * oy + qy - 2) * 5 + 3 * oz + qz - 2
    grid = jnp.where(block >= 27, block + (125 - 27), grid)
    low = grid // (BLOCKS // GROUPS)
    high = (grid - low * (BLOCKS // GROUPS)) * 16 + jnp.bitwise_and(atom, 15)
    high_ref[...] = high
    low_ref[...] = low
    offs = [(o - 1).astype(f32) for o in (ox, oy, oz)]
    own8 = row_pick(pos_ref[0], pos_ref[1], pos_ref[2], (8, atoms))
    w_hi, w_lo = split_two(radial_ref[...])
    w_stack = jnp.concatenate([w_hi, w_hi, w_lo], axis=0)
    centre = lax.broadcasted_iota(jnp.int32, (count, 1), 0).astype(f32) * spacing
    iota = lax.broadcasted_iota(jnp.int32, (HIGH, atoms), 0)

    def hot(j):
        return (high_ref[pl.ds(j, 1), :] == iota).astype(f32).astype(bf16)

    agg = jnp.zeros((channels, atoms), f32)
    for j in range(listed):
        found = jnp.dot(lhs_ref[...], hot(j), preferred_element_type=f32)
        low_j = low_ref[j : j + 1, :]
        near = found[0:ROWS]
        for g in range(1, GROUPS):
            near = jnp.where(low_j == g, found[g * ROWS : (g + 1) * ROWS], near)
        near_z = near[0:channels]
        near_ref[j] = near_z.astype(bf16)
        halves = near[channels : channels + 8]
        off8 = row_pick(offs[0][j : j + 1], offs[1][j : j + 1], offs[2][j : j + 1], (8, atoms))
        rel = halves + pltpu.roll(halves, 4, 0) + off8 - own8
        rel_ref[j] = rel
        dist = 0.5 * jnp.sum(rel * rel, axis=0, keepdims=True)
        scaled = (dist - centre) / width
        basis = jnp.exp(-(scaled * scaled))
        basis_ref[j] = basis
        b_hi, b_lo = split_two(basis)
        filt = lax.dot_general(
            w_stack,
            jnp.concatenate([b_hi, b_lo, b_hi], axis=0),
            (((0,), (0,)), ((), ())),
            preferred_element_type=f32,
        )
        filt_ref[j] = filt
        agg = agg + filt * near_z
    agg = agg * share
    gate = 1.0 / (1.0 + jnp.exp(-agg))
    g_all = dy_ref[...].astype(f32) * (gate * (1.0 + agg * (1.0 - gate))) * share
    acc_ref[...] = jnp.zeros_like(acc_ref)
    own_grad = jnp.zeros((8, atoms), f32)
    radial = jnp.zeros((2 * count, 2 * channels), f32)
    w_wide = jnp.concatenate([w_hi, w_hi, w_lo], axis=1)
    for j in range(listed):
        near_z = near_ref[j].astype(f32)
        dz = filt_ref[j] * g_all
        df = near_z * g_all
        f_hi, f_lo = split_two(df)
        basis = basis_ref[j]
        b_hi, b_lo = split_two(basis)
        radial = radial + lax.dot_general(
            jnp.concatenate([b_hi, b_lo], axis=0),
            jnp.concatenate([f_hi, f_lo], axis=0),
            (((1,), (1,)), ((), ())),
            preferred_element_type=f32,
        )
        dbasis = jnp.dot(
            w_wide, jnp.concatenate([f_hi, f_lo, f_hi], axis=0), preferred_element_type=f32
        )
        rel = rel_ref[j]
        dist = 0.5 * jnp.sum(rel * rel, axis=0, keepdims=True)
        slope = dbasis * basis * (dist - centre)
        ddist = jnp.sum(slope, axis=0, keepdims=True) * (-2.0 / (width * width))
        gpos = rel * (2.0 * ddist)
        own_grad = own_grad - gpos
        p_hi = gpos.astype(bf16).astype(f32)
        row8 = lax.broadcasted_iota(jnp.int32, (8, atoms), 0)
        tail = jnp.where(row8 < 4, p_hi, gpos - p_hi)
        full = jnp.concatenate([dz, tail], axis=0)
        low_j = low_ref[j : j + 1, :]
        spread = jnp.concatenate(
            [jnp.where(low_j == g, full, 0.0) for g in range(GROUPS)], axis=0
        ).astype(bf16)
        acc_ref[...] += lax.dot_general(
            spread, hot(j), (((1,), (1,)), ((), ())), preferred_element_type=f32
        )
    own_ref[...] = own_grad
    sums_ref[...] = jnp.zeros_like(sums_ref)
    sums_ref[channels : channels + count, 0:channels] = (
        radial[0:count, 0:channels]
        + radial[count:, 0:channels]
        + radial[0:count, channels:]
        + radial[count:, channels:]
    )
    weight = jnp.zeros((channels, channels), f32)
    for g in range(GROUPS):
        z_hi, z_lo = split_two(acc_ref[g * ROWS : g * ROWS + channels, :] * gains_ref[g])
        for piece in (z_hi, z_lo):
            weight = weight + lax.dot_general(
                feat_ref[g], piece, (((1,), (1,)), ((), ())), preferred_element_type=f32
            )
        part = jnp.transpose(acc_ref[g * ROWS : (g + 1) * ROWS, :])
        part = jnp.concatenate([part, jnp.zeros((HIGH, 128 - ROWS), f32)], axis=1)
        zgrad_ref[g * HIGH : (g + 1) * HIGH, :] = part
        thin_ref[g * HIGH : (g + 1) * HIGH, :] = part.astype(bf16)
    sums_ref[0:channels, 0:channels] = weight


def short_range(table, ids, pos, dy, radial, mix, gain, interpret=False):
    channels, atoms = dy.shape
    listed = ids.shape[0]
    count = radial.shape[0]
    vmem = lambda s, d: pltpu.VMEM(s, d)
    spec = pl.BlockSpec(memory_space=pltpu.VMEM)
    return pl.pallas_call(
        short_kernel,
        out_shape=(
            jax.ShapeDtypeStruct((GROUPS * HIGH, 128), jnp.float32),
            jax.ShapeDtypeStruct((GROUPS * HIGH, 128), jnp.bfloat16),
            jax.ShapeDtypeStruct((8, atoms), jnp.float32),
            jax.ShapeDtypeStruct((128, 128), jnp.float32),
        ),
        in_specs=[spec] * 7,
        out_specs=(spec,) * 4,
        scratch_shapes=[
            vmem((GROUPS * ROWS, HIGH), jnp.bfloat16),
            vmem((GROUPS, channels, HIGH), jnp.bfloat16),
            vmem((GROUPS, channels, HIGH), jnp.float32),
            vmem((listed, atoms), jnp.int32),
            vmem((listed, atoms), jnp.int32),
            vmem((listed, channels, atoms), jnp.bfloat16),
            vmem((listed, 8, atoms), jnp.float32),
            vmem((listed, count, atoms), jnp.float32),
            vmem((listed, channels, atoms), jnp.float32),
            vmem((GROUPS * ROWS, HIGH), jnp.float32),
        ],
        interpret=interpret,
        name="short_range",
    )(table, ids, pos, dy, radial, mix, gain)


def from_behind(x, axis, by):
    devices = lax.axis_size(axis)
    return lax.ppermute(x, axis, [(i, (i + by) % devices) for i in range(devices)])


def chosen(parity):
    column = lax.broadcasted_iota(jnp.int32, (2 * CHUNK, CHUNK), 1)
    row = lax.broadcasted_iota(jnp.int32, (2 * CHUNK, CHUNK), 0)
    picked = (column // SHARE) * (2 * SHARE) + column % SHARE + parity * SHARE
    return (row == picked).astype(jnp.float32).astype(jnp.bfloat16)


def pack_kernel(h_ref, kind_ref, pos_ref, miller_ref, table_ref, mine_ref, next_ref):
    f32, bf16 = jnp.float32, jnp.bfloat16
    channels, atoms = h_ref.shape
    none = jnp.zeros((1, atoms), f32)
    halves = [split_two(pos_ref[d]) for d in range(3)]
    rows = jnp.concatenate(
        [h_ref[...].astype(f32)]
        + [half[0].astype(f32) for half in halves]
        + [none]
        + [half[1].astype(f32) for half in halves]
        + [none, kind_ref[...].astype(f32), jnp.zeros((127 - ROWS, atoms), f32)],
        axis=0,
    )
    table_ref[...] = jnp.transpose(rows).astype(bf16)
    m = miller_ref[...].astype(f32)
    tall = jnp.concatenate([m, m, m, jnp.zeros((7, m.shape[1]), f32)], axis=0).astype(bf16)
    runs = m.shape[1] // (2 * CHUNK)
    stack = jnp.concatenate(
        [tall[:, j * 2 * CHUNK : (j + 1) * 2 * CHUNK] for j in range(runs)], axis=0
    )
    core = lax.axis_index(PAIR)
    for parity, out_ref in ((core, mine_ref), (1 - core, next_ref)):
        got = jnp.dot(stack, chosen(parity), preferred_element_type=f32).astype(bf16)
        for j in range(runs):
            out_ref[:, j * CHUNK : (j + 1) * CHUNK] = got[j * 16 : (j + 1) * 16]


def pack(h, kinds, pos, miller):
    half = jax.ShapeDtypeStruct((16, miller.shape[1] // 2), jnp.bfloat16)
    return pl.pallas_call(
        pack_kernel,
        out_shape=(jax.ShapeDtypeStruct((h.shape[1], 128), jnp.bfloat16), half, half),
        in_specs=[WHOLE] * 4,
        out_specs=(WHOLE,) * 3,
        name="pack",
    )(h, kinds, pos, miller)


def phase_kernel(
    pos_ref,
    miller_ref,
    h_ref,
    dy_ref,
    cos_out,
    sin_out,
    part_out,
    cos_ref,
    sin_ref,
    part_ref,
    flip_ref,
    rhs_ref,
    t_ref,
    sems,
):
    f32, bf16 = jnp.float32, jnp.bfloat16
    width = 2 * h_ref.shape[0]
    flip_ref[...] = jnp.transpose(jnp.concatenate([h_ref[...], dy_ref[...]], axis=0))
    axes = ("gx", GY, GZ)
    turns = jnp.concatenate(
        [
            (pos_ref[d] + lax.axis_index(axes[d]).astype(f32)) / float(lax.axis_size(axes[d]))
            for d in range(3)
        ],
        axis=0,
    )
    t_hi = turns.astype(bf16)
    t_mid, t_lo = split_two(turns - t_hi.astype(f32))
    rhs_ref[...] = jnp.concatenate(
        [t_hi, t_mid, t_lo, jnp.zeros((7, turns.shape[1]), bf16)], axis=0
    )
    steps = miller_ref.shape[1] // CHUNK
    rows, lanes = 16, 256

    def copies(i):
        at = pl.ds(pl.multiple_of(i * CHUNK, CHUNK), CHUNK)
        return [
            pltpu.make_async_copy(src.at[at], dst.at[at], sems.at[n, i])
            for n, (src, dst) in enumerate(
                ((cos_ref, cos_out), (sin_ref, sin_out), (part_ref, part_out))
            )
        ]

    def one(i, carry):
        base = pl.multiple_of(i * CHUNK, CHUNK)
        t_ref[...] = lax.dot_general(
            miller_ref[:, pl.ds(base, CHUNK)],
            rhs_ref[...],
            (((0,), (0,)), ((), ())),
            preferred_element_type=f32,
        )
        for top in range(0, CHUNK, rows):
            for left in range(0, t_ref.shape[1], lanes):
                t = t_ref[top : top + rows, left : left + lanes]
                r = t - jnp.round(t)
                u = jnp.abs(r) - 0.25
                q = u * u
                s = SIN_TERMS[3]
                for term in SIN_TERMS[2::-1]:
                    s = s * q + term
                c = COS_TERMS[4]
                for term in COS_TERMS[3::-1]:
                    c = c * q + term
                at = (pl.ds(base + top, rows), pl.ds(left, lanes))
                cos_ref[at] = -(s * u).astype(bf16)
                sin_ref[at] = jnp.where(r < 0.0, -c, c).astype(bf16)
        here = pl.ds(base, CHUNK)
        part_ref[here, 0:width] = jnp.dot(
            cos_ref[here, :], flip_ref[...], preferred_element_type=f32
        )
        part_ref[here, width:] = jnp.dot(
            sin_ref[here, :], flip_ref[...], preferred_element_type=f32
        )
        for copy in copies(i):
            copy.start()
        return carry

    lax.fori_loop(0, steps, one, 0)
    for i in range(steps):
        for copy in copies(i):
            copy.wait()


def phase_sums(pos, miller, h, dy):
    points = miller.shape[1]
    channels, atoms = h.shape
    width = 2 * channels
    wave = jax.ShapeDtypeStruct((points, atoms), jnp.bfloat16)
    sums = jax.ShapeDtypeStruct((points, 2 * width), jnp.float32)
    return pl.pallas_call(
        phase_kernel,
        out_shape=(wave, wave, sums),
        in_specs=[WHOLE] * 4,
        out_specs=(pl.BlockSpec(memory_space=pl.ANY),) * 3,
        scratch_shapes=[
            pltpu.VMEM(wave.shape, wave.dtype),
            pltpu.VMEM(wave.shape, wave.dtype),
            pltpu.VMEM(sums.shape, sums.dtype),
            pltpu.VMEM((atoms, width), jnp.bfloat16),
            pltpu.VMEM((16, atoms), jnp.bfloat16),
            pltpu.VMEM((CHUNK, atoms), jnp.float32),
            pltpu.SemaphoreType.DMA((3, points // CHUNK)),
        ],
        cost_estimate=pl.CostEstimate(
            flops=6 * points * atoms * width, transcendentals=0, bytes_accessed=4 * points * atoms
        ),
        name="phase_sums",
    )(pos, miller, h, dy)


def ewald_kernel(last, coeff_in, cos_in, sin_in, miller_ref, h_ref, dy_ref, *rest):
    f32, bf16 = jnp.float32, jnp.bfloat16
    channels = h_ref.shape[0]
    width = 2 * channels
    coeff_ref, cos_ref, sin_ref, both_ref, sems = rest[-5:]
    steps = miller_ref.shape[1] // CHUNK

    def copies(i):
        at = pl.ds(pl.multiple_of(i * CHUNK, CHUNK), CHUNK)
        wide = pl.ds(0, 2 * width)
        return [
            pltpu.make_async_copy(coeff_in.at[at, wide], coeff_ref.at[at], sems.at[0, i]),
            pltpu.make_async_copy(cos_in.at[at], cos_ref.at[at], sems.at[1, i]),
            pltpu.make_async_copy(sin_in.at[at], sin_ref.at[at], sems.at[2, i]),
        ]

    for i in range(steps):
        for copy in copies(i):
            copy.start()
    both_ref[...] = jnp.concatenate([h_ref[...], dy_ref[...]], axis=0)
    if last:
        sums_ref, turn_ref = rest[-7:-5]
        sums_ref[...] = rest[0][...]
        turn_ref[...] = rest[1][...]
    else:
        sums_ref, turn_ref = rest[0:2]
        sums_ref[...] = jnp.zeros_like(sums_ref)
        turn_ref[...] = jnp.zeros_like(turn_ref)
    over_rows = (((0,), (0,)), ((), ()))

    def one(i, carry):
        for copy in copies(i):
            copy.wait()
        at = pl.ds(pl.multiple_of(i * CHUNK, CHUNK), CHUNK)
        coeffs = coeff_ref[at, :]
        cos_part, sin_part = cos_ref[at, :], sin_ref[at, :]
        sums_ref[...] += lax.dot_general(
            coeffs[:, 0:channels], cos_part, over_rows, preferred_element_type=f32
        ) + lax.dot_general(
            coeffs[:, width : width + channels], sin_part, over_rows, preferred_element_type=f32
        )
        along_u = jnp.dot(coeffs[:, 0:width], both_ref[...], preferred_element_type=f32)
        along_v = jnp.dot(coeffs[:, width : 2 * width], both_ref[...], preferred_element_type=f32)
        angle = along_v * cos_part.astype(f32) - along_u * sin_part.astype(f32)
        a_hi, a_lo = split_two(angle)
        m = miller_ref[:, at]
        turn_ref[...] += jnp.dot(m, a_hi, preferred_element_type=f32) + jnp.dot(
            m, a_lo, preferred_element_type=f32
        )
        return carry

    lax.fori_loop(0, steps, one, 0)
    if last:
        short_ref, near_ref, all_ref, atom_ref, pos_ref, weight_ref, radial_ref = rest[2:9]
        atom_ref[...] = (dy_ref[...].astype(f32) + sums_ref[...] + short_ref[...]).astype(bf16)
        axes = ("gx", GY, GZ)
        for d in range(3):
            pos_ref[d] = (
                turn_ref[d : d + 1, :] * (circle_angle / lax.axis_size(axes[d]))
                + near_ref[d : d + 1, :]
            )
        weight_ref[...] = all_ref[0:channels, 0:channels]
        radial_ref[...] = all_ref[channels : channels + radial_ref.shape[0], 0:channels]


def ewald(coeffs, cos_all, sin_all, miller, h, dy, more=(), basis=0):
    points, atoms = cos_all.shape
    channels = h.shape[0]
    last = len(more) > 0
    sums = jax.ShapeDtypeStruct((channels, atoms), jnp.float32)
    turn = jax.ShapeDtypeStruct((16, atoms), jnp.float32)
    scratch = [
        pltpu.VMEM((points, 4 * channels), jnp.bfloat16),
        pltpu.VMEM(cos_all.shape, jnp.bfloat16),
        pltpu.VMEM(cos_all.shape, jnp.bfloat16),
        pltpu.VMEM((2 * channels, atoms), jnp.bfloat16),
        pltpu.SemaphoreType.DMA((3, points // CHUNK)),
    ]
    outs = (sums, turn)
    if last:
        scratch = [pltpu.VMEM(sums.shape, sums.dtype), pltpu.VMEM(turn.shape, turn.dtype)] + scratch
        outs = (
            jax.ShapeDtypeStruct(sums.shape, jnp.bfloat16),
            jax.ShapeDtypeStruct((3, 1, atoms), jnp.float32),
            jax.ShapeDtypeStruct((channels, channels), jnp.float32),
            jax.ShapeDtypeStruct((basis, channels), jnp.float32),
        )
    return pl.pallas_call(
        functools.partial(ewald_kernel, last),
        out_shape=outs,
        in_specs=[pl.BlockSpec(memory_space=pl.ANY)] * 3 + [WHOLE] * (3 + len(more)),
        out_specs=(WHOLE,) * len(outs),
        scratch_shapes=scratch,
        cost_estimate=pl.CostEstimate(
            flops=8 * points * atoms * channels,
            transcendentals=0,
            bytes_accessed=4 * points * atoms,
        ),
        name="ewald",
    )(coeffs, cos_all, sin_all, miller, h, dy, *more)


def finish_kernel(rows_ref, kind_ref, gain_ref, mix_ref, own_ref, short_ref, pos_ref):
    f32, bf16 = jnp.float32, jnp.bfloat16
    channels, atoms = short_ref.shape
    flat = jnp.transpose(rows_ref[...])
    gains = gains_of(gain_ref[...], kind_ref[...], (channels, atoms))
    zscaled = (flat[0:channels] * gains).astype(bf16)
    short_ref[...] = jnp.dot(mix_ref[...], zscaled, preferred_element_type=f32)
    halves = flat[channels : channels + 8]
    pos_ref[...] = halves + pltpu.roll(halves, 4, 0) + own_ref[...]


def finish(rows, kinds, gain, mix, own):
    channels, atoms = mix.shape[0], rows.shape[0]
    return pl.pallas_call(
        finish_kernel,
        out_shape=(
            jax.ShapeDtypeStruct((channels, atoms), jnp.float32),
            jax.ShapeDtypeStruct((8, atoms), jnp.float32),
        ),
        in_specs=[WHOLE] * 5,
        out_specs=(WHOLE,) * 2,
        name="finish",
    )(rows, kinds, gain, mix, own)


def coefficients(totals, filt_rows, norm_atoms, norm_k):
    channels = filt_rows.shape[1]
    cos_struct = totals[:, 0:channels] * norm_atoms
    cos_back = totals[:, channels : 2 * channels] * norm_k
    sin_struct = totals[:, 2 * channels : 3 * channels] * norm_atoms
    sin_back = totals[:, 3 * channels : 4 * channels] * norm_k
    coeffs = jnp.concatenate(
        [
            norm_atoms * filt_rows * cos_back,
            norm_k * filt_rows * cos_struct,
            norm_atoms * filt_rows * sin_back,
            norm_k * filt_rows * sin_struct,
        ],
        axis=1,
    )
    return (coeffs.astype(jnp.bfloat16), cos_struct * cos_back + sin_struct * sin_back)


def sent_out(x, axis, dim):
    length = x.shape[dim]
    before = from_behind(lax.slice_in_dim(x, length - 1, length, axis=dim), axis, 1)
    after = from_behind(lax.slice_in_dim(x, 0, 1, axis=dim), axis, -1)
    return before, after


def sent_back(x, axis, dim):
    length = x.shape[dim]
    first = lax.slice_in_dim(x, 0, 1, axis=dim).astype(jnp.bfloat16)
    last = lax.slice_in_dim(x, length - 1, length, axis=dim).astype(jnp.bfloat16)
    return from_behind(first, axis, -1), from_behind(last, axis, 1)


def folded(x, pieces, dim):
    to_last, to_first = [piece.astype(jnp.float32) for piece in pieces]
    low = lax.slice_in_dim(x, 1, 2, axis=dim) + to_first
    middle = lax.slice_in_dim(x, 2, 3, axis=dim)
    high = lax.slice_in_dim(x, 3, 4, axis=dim) + to_last
    return jnp.concatenate([low, middle, high], axis=dim)


def shards(
    atom_embedding,
    output_adjoint,
    fractional_coords,
    element_labels,
    adjacent_ghost_entries,
    miller_triples,
    reciprocal_kernel,
    channel_mixing_matrix,
    element_channel_factor,
    distance_kernel,
):
    h = atom_embedding[0, 0, 0]
    dy = output_adjoint[0, 0, 0]
    pos = fractional_coords[0, 0, 0][:, None, :]
    kinds = element_labels[0, 0]
    channels, atoms = h.shape
    points = miller_triples.shape[1]
    devices = lax.axis_size(GX_GY_GZ)
    norm_atoms = (atoms * devices) ** (-0.5)
    norm_k = points ** (-0.5)
    share_rows = points // devices
    share_start = lax.axis_index(GX_GY_GZ) * share_rows
    groups = lax.axis_size(CHIPS)
    half = points // 2

    own_table, miller_mine, miller_next = pack(h, kinds, pos, miller_triples)
    cells = own_table[0:432].reshape(3, 3, 3, 16, 128)
    below, above = sent_out(cells, GZ, 2)
    cos_next, sin_next, part_next = phase_sums(pos, miller_next, h, dy)
    received = from_behind(part_next, PAIR, 1)
    below, above, part_next = lax.optimization_barrier((below, above, part_next))
    cells = jnp.concatenate([below, cells, above], axis=2)
    below, above = sent_out(cells, GY, 1)
    cos_mine, sin_mine, part_mine = phase_sums(pos, miller_mine, h, dy)
    below, above, part_mine = lax.optimization_barrier((below, above, part_mine))
    cells = jnp.concatenate([below, cells, above], axis=1)
    below, above = sent_out(cells, "gx", 0)
    paired = (part_mine + received).astype(jnp.bfloat16)
    paired, below, above = lax.optimization_barrier((paired, below, above))
    pieces = lax.all_to_all(paired.reshape(groups, share_rows, 4 * channels), CHIPS, 0, 0)

    table = jnp.concatenate(
        [
            below.reshape(400, 128),
            cells.reshape(1200, 128),
            above.reshape(400, 128),
            own_table[432:512],
            jnp.zeros((GROUPS * HIGH - 2080, 128), jnp.bfloat16),
        ],
        axis=0,
    )
    ghost_grad, ghost_thin, own_grad, sums = short_range(
        table,
        adjacent_ghost_entries[0, 0, 0],
        pos,
        dy,
        distance_kernel,
        channel_mixing_matrix,
        element_channel_factor,
    )
    sums = sums + from_behind(sums, PAIR, 1)
    tiles = sums.astype(jnp.bfloat16).reshape(1, 16, 1, 8, 128)
    tiles = jnp.broadcast_to(tiles, (groups // 32, 16, 2, 8, 128)).reshape(groups, 8, 128)

    totals = jnp.sum(pieces.astype(jnp.float32), axis=0)
    filt_rows = lax.dynamic_slice_in_dim(reciprocal_kernel, share_start, share_rows, 0)
    own_coeffs, filter_share = coefficients(totals, filt_rows, norm_atoms, norm_k)
    spread = jnp.broadcast_to(own_coeffs[None], (groups, share_rows, 4 * channels))
    got = lax.all_to_all(jnp.concatenate([spread, tiles], axis=2), CHIPS, 0, 0)

    to_side = sent_back(ghost_thin[0:2000].reshape(5, 5, 5, 16, 128), "gx", 0)
    grid = folded(ghost_grad[0:2000].reshape(5, 5, 5, 16, 128), to_side, 0)
    grid = folded(grid, sent_back(grid, GY, 1), 1)

    tile_sum = jnp.sum(got[:, :, 4 * channels :].astype(jnp.float32), axis=0)
    coeffs_mine = got.reshape(half, 4 * channels + 128)
    coeffs_next = from_behind(coeffs_mine, PAIR, 1)
    every = lax.all_to_all(jnp.broadcast_to(tile_sum[None], (16, 8, 128)), GY, 0, 0)
    every = every.reshape(128, 128)
    to_side = sent_back(grid, GZ, 2)
    first = ewald(coeffs_mine, cos_mine, sin_mine, miller_mine, h, dy)
    to_side, first = lax.optimization_barrier((to_side, first))
    grid = folded(grid, to_side, 2)
    rows = jnp.concatenate([grid.reshape(432, 128), ghost_grad[2000:2080]], axis=0)
    atom_short, pos_short = finish(
        rows, kinds, element_channel_factor, channel_mixing_matrix, own_grad
    )
    atom_grad, position_grad, weight_grad, radial_grad = ewald(
        coeffs_next,
        cos_next,
        sin_next,
        miller_next,
        h,
        dy,
        (*first, atom_short, pos_short, every),
        distance_kernel.shape[0],
    )
    position_grad = position_grad[:, 0, :]
    return (
        atom_grad[None, None, None],
        position_grad[None, None, None],
        weight_grad,
        radial_grad,
        filter_share,
    )


def solution(mesh):
    finer = Mesh(
        mesh.devices.reshape(mesh.shape["gx"], 4, 4, 2, 2), ("gx", "gy_0", "gy_1", "gz_0", "gz_1")
    )
    in_specs = (
        P("gx", GY, GZ, None, None),
        P("gx", GY, GZ, None, None),
        P("gx", GY, GZ, None, None),
        P("gx", GY, GZ, None),
        P("gx", GY, GZ, None, None),
        P(),
        P(),
        P(),
        P(),
        P(),
    )
    out_specs = (
        P("gx", GY, GZ, None, None),
        P("gx", GY, GZ, None, None),
        P(),
        P(),
        P(GX_GY_GZ, None),
    )
    return jax.shard_map(
        shards, mesh=finer, in_specs=in_specs, out_specs=out_specs, check_vma=False
    )
```

time: 146 us -> 137 us (0.938)
  the two profiles are of different devices: /device:TPU:1 before, /device:TPU:8 now
where the time goes in v3:
time: 137 us; the launch traced here: 136 us
  starting transfers between devices  54.9 us (40%)
  Pallas kernels  39.8 us (29%)
  waiting for transfers between devices  30.4 us (22%)
  other arithmetic  6.06 us (4%)
  local copies, waits for them, and re-layouts  3.71 us (3%)
    ppermute x15, waiting for transfers between devices, from_behind(): lax.ppermute(x, axis, [(i, (i + by) % devices) for i in range(devices)])  23.7 us
    ppermute x15, starting transfers between devices, from_behind(): lax.ppermute(x, axis, [(i, (i + by) % devices) for i in range(devices)])  23.6 us
    pallas_call x1, Pallas kernels, short_range(): pl.pallas_call(short_kernel, out_shape=(jax.ShapeDtypeStruct((GROUPS * HI...  14.8 us
    all_to_all x1, starting transfers between devices, shards(): got = lax.all_to_all(jnp.concatenate([spread, tiles], axis=2), CHIPS, 0, 0)  14.1 us
    all_to_all x1, starting transfers between devices, shards(): lax.all_to_all(paired.reshape(groups, share_rows, 4 * channels), CHIPS, 0...  11.3 us
    pallas_call x2, Pallas kernels, phase_sums(): pl.pallas_call(phase_kernel, out_shape=(wave, wave, sums), in_specs=[WHOL...  10.7 us
    pallas_call x2, Pallas kernels, ewald(): pl.pallas_call(functools.partial(ewald_kernel, last), out_shape=outs, in_...  10.5 us
    all_to_all x1, waiting for transfers between devices, shards(): got = lax.all_to_all(jnp.concatenate([spread, tiles], axis=2), CHIPS, 0, 0)  6.67 us
  transfers between devices with their start and end apart: 18, of which 10 were waited for; matrix products, arithmetic and copies ran while one was open for 5% of the time, Pallas kernels for 20%

profile of v3, /device:TPU:8, one launch (start us, length us, event | category | flops | bytes accessed | tf_op | source)
XLA Modules:
  0.0 136.0 jit_solution(14331596041424981860)
XLA Ops:
  0.6 1.8 %pack.1 = (bf16[512,128]{1,0:T(8,128)(2,1)}, bf16[16,1024]{1,0:T(8,128)(2,1)}, bf16[16,1024]{1,0:T(8,128)(2,1)}) custom-call(bf16[64,512]{1,0:T(8,128)(2,1)} %bitcast.37, s32[1,512]{1,0:T(1,128)} %bitcast.57, f32[3,1,512]{2,1,0:T(1,128)} %bitcast.53, s32[3,2048]{1,0:T(4,128)} %miller_ref.1), custom_call_target="tpu_custom_call" | custom-call | tf_op jit(solution)/shard_map/pack/pallas_call | solution.py:285
  2.5 5.3 %phase_sums.2 = (bf16[1024,512]{1,0:T(8,128)(2,1)}, bf16[1024,512]{1,0:T(8,128)(2,1)}, f32[1024,256]{1,0:T(8,128)}) custom-call(f32[3,1,512]{2,1,0:T(1,128)} %bitcast.54, bf16[16,1024]{1,0:T(8,128)(2,1)} %get-tuple-element.39.miller_ref, bf16[64,512]{1,0:T(8,128)(2,1)} %bitcast.38, bf16[64,512]{1,0:T(8,128)(2,1)} %bitcast.42), custom_call_target="tpu_custom_call" | custom-call | flops 402653184 | bytes 2097152 | tf_op jit(solution)/shard_map/phase_sums/pallas_call | solution.py:384
  7.8 0.1 collective-permute-start.4
  8.0 7.4 %collective-permute-start.1 = (bf16[3,3,1,16,128]{4,3,2,1,0:T(8,128)(2,1)S(1)}, bf16[3,3,1,16,128]{4,3,2,1,0:T(8,128)(2,1)S(1)}, u32[]{:S(2)}, u32[]{:S(2)}) collective-permute-start(bf16[3,3,1,16,128]{4,3,2,1,0:T(8,128)(2,1)S(1)} %get-tuple-element.95), channel_id=1, source_target_pairs={{0,3},{1,0},{2,1},{3,2},{4,7},{5,4},{6,5},{7,6},{8,11},{9,8},{10,9... | collective-permute-start | bytes 110600 | tf_op jit(solution)/shard_map/ppermute | solution.py:246
  15.3 1.6 %collective-permute-done.1 = bf16[3,3,1,16,128]{4,3,2,1,0:T(8,128)(2,1)S(1)} collective-permute-done((bf16[3,3,1,16,128]{4,3,2,1,0:T(8,128)(2,1)S(1)}, bf16[3,3,1,16,128]{4,3,2,1,0:T(8,128)(2,1)S(1)}, u32[]{:S(2)}, u32[]{:S(2)}) %collective-permute-start.1) | collective-permute-done | bytes 36896 | tf_op jit(solution)/shard_map/ppermute | solution.py:246
  16.9 5.7 %collective-permute-done = bf16[3,3,1,16,128]{4,3,2,1,0:T(8,128)(2,1)S(1)} collective-permute-done((bf16[3,3,1,16,128]{4,3,2,1,0:T(8,128)(2,1)S(1)}, bf16[3,3,1,16,128]{4,3,2,1,0:T(8,128)(2,1)S(1)}, u32[]{:S(2)}, u32[]{:S(2)}) %collective-permute-start) | collective-permute-done | bytes 36896 | tf_op jit(solution)/shard_map/ppermute | solution.py:246
  22.6 0.5 collective-permute-start.3
  23.2 1.6 %collective-permute-start.2 = (bf16[3,1,5,16,128]{4,3,2,1,0:T(8,128)(2,1)S(1)}, bf16[3,1,5,16,128]{4,3,2,1,0:T(8,128)(2,1)S(1)}, u32[]{:S(2)}, u32[]{:S(2)}) collective-permute-start(bf16[3,1,5,16,128]{4,3,2,1,0:T(8,128)(2,1)S(1)} %get-tuple-element.94), channel_id=1, source_target_pairs={{0,4},{4,8},{8,12},{12,16},{16,20},{20,24},{24,28},{28,32},{32,36}... | collective-permute-start | bytes 184328 | tf_op jit(solution)/shard_map/ppermute | solution.py:246
  24.7 5.3 %phase_sums.3 = (bf16[1024,512]{1,0:T(8,128)(2,1)}, bf16[1024,512]{1,0:T(8,128)(2,1)}, f32[1024,256]{1,0:T(8,128)}) custom-call(f32[3,1,512]{2,1,0:T(1,128)} %bitcast.55, bf16[16,1024]{1,0:T(8,128)(2,1)} %get-tuple-element.43.miller_ref, bf16[64,512]{1,0:T(8,128)(2,1)} %bitcast.39, bf16[64,512]{1,0:T(8,128)(2,1)} %bitcast.43), custom_call_target="tpu_custom_call" | custom-call | flops 402653184 | bytes 2097152 | tf_op jit(solution)/shard_map/phase_sums/pallas_call | solution.py:384
  30.1 0.1 pad_maximum_fusion.3
  30.2 2.8 %collective-permute-start.6 = (bf16[1,5,5,16,128]{4,3,2,1,0:T(8,128)(2,1)S(1)}, bf16[1,5,5,16,128]{4,3,2,1,0:T(8,128)(2,1)S(1)}, u32[]{:S(2)}, u32[]{:S(2)}) collective-permute-start(bf16[1,5,5,16,128]{4,3,2,1,0:T(8,128)(2,1)S(1)} %get-tuple-element.89), channel_id=1, source_target_pairs={{0,192},{64,0},{128,64},{192,128},{1,193},{65,1},{129,65},{193,129... | collective-permute-start | bytes 307208 | tf_op jit(solution)/shard_map/ppermute | solution.py:246
  33.0 2.2 %add_convert_fusion = bf16[1024,256]{1,0:T(8,128)(2,1)} fusion(f32[1024,256]{1,0:T(8,128)} %get-tuple-element.45, f32[1024,256]{1,0:T(8,128)S(1)} %collective-permute-done.4), kind=kLoop, calls=%fused_computation.1 | loop fusion | flops 524288 | bytes 2621440 | tf_op jit(solution)/shard_map/convert_element_type | solution.py:610
  35.2 0.1 collective-permute-done.6
  35.3 3.6 %collective-permute-done.5 = bf16[1,5,5,16,128]{4,3,2,1,0:T(8,128)(2,1)S(1)} collective-permute-done((bf16[1,5,5,16,128]{4,3,2,1,0:T(8,128)(2,1)S(1)}, bf16[1,5,5,16,128]{4,3,2,1,0:T(8,128)(2,1)S(1)}, u32[]{:S(2)}, u32[]{:S(2)}) %collective-permute-start.5) | collective-permute-done | bytes 102432 | tf_op jit(solution)/shard_map/ppermute | solution.py:246
  38.9 11.3 %all-to-all-start = ((bf16[128,8,256]{2,1,0:T(8,128)(2,1)}), bf16[128,8,256]{2,1,0:T(8,128)(2,1)S(1)}, u32[]{:S(2)}, u32[]{:S(2)}) async-start(bf16[128,8,256]{2,1,0:T(8,128)(2,1)} %bitcast.5), calls=%async_computation | async-start | bytes 1048576 | tf_op jit(solution)/shard_map/all_to_all | solution.py:612
  50.4 0.8 copy-done.3
  51.2 14.8 %short_range.1 = (f32[2160,128]{1,0:T(8,128)}, bf16[2160,128]{1,0:T(8,128)(2,1)}, f32[8,512]{1,0:T(8,128)}, f32[128,128]{1,0:T(8,128)}) custom-call(bf16[2160,128]{1,0:T(8,128)(2,1)} %copy-done.3, s32[16,512]{1,0:T(8,128)} %bitcast.52, f32[3,1,512]{2,1,0:T(1,128)} %bitcast.56, bf16[64,512]{1,0:T(8,128)(2,1)} %bitcast.44, f32[16,64]{1,0:T(8,128)} %radial_ref.1, ...), custom_call_target="tpu_custom_call" | custom-call | tf_op jit(solution)/shard_map/short_range/pallas_call | solution.py:217
  66.0 0.1 constant_dynamic-slice_fusion
  66.1 0.1 copy.17
  66.1 1.3 collective-permute-done.7
  67.5 0.8 fusion
  68.3 0.1 convert_reduce_fusion
  68.5 0.7 multiply_convert_fusion.3
  69.1 0.1 pad_maximum_fusion.9
  69.3 1.0 pad_maximum_fusion
  70.3 14.1 %all-to-all-start.1 = ((bf16[128,8,384]{2,1,0:T(8,128)(2,1)}), bf16[128,8,384]{2,1,0:T(8,128)(2,1)S(1)}, u32[]{:S(2)}, u32[]{:S(2)}) async-start(bf16[128,8,384]{2,1,0:T(8,128)(2,1)} %pad_maximum_fusion), calls=%async_computation.1 | async-start | bytes 1572864 | tf_op jit(solution)/shard_map/all_to_all | solution.py:641
  84.4 1.0 fusion.4
  85.3 3.3 %collective-permute-start.10 = (bf16[1,5,5,16,128]{4,3,2,1,0:T(8,128)(2,1)S(1)}, bf16[1,5,5,16,128]{4,3,2,1,0:T(8,128)(2,1)S(1)}, u32[]{:S(2)}, u32[]{:S(2)}) collective-permute-start(bf16[1,5,5,16,128]{4,3,2,1,0:T(8,128)(2,1)S(1)} %bitcast.51), channel_id=1, source_target_pairs={{0,192},{64,0},{128,64},{192,128},{1,193},{65,1},{129,65},{193,129... | collective-permute-start | bytes 307208 | tf_op jit(solution)/shard_map/ppermute | solution.py:246
  88.7 0.1 collective-permute-start.9
  88.8 3.2 %collective-permute-done.10 = bf16[1,5,5,16,128]{4,3,2,1,0:T(8,128)(2,1)S(1)} collective-permute-done((bf16[1,5,5,16,128]{4,3,2,1,0:T(8,128)(2,1)S(1)}, bf16[1,5,5,16,128]{4,3,2,1,0:T(8,128)(2,1)S(1)}, u32[]{:S(2)}, u32[]{:S(2)}) %collective-permute-start.10) | collective-permute-done | bytes 102432 | tf_op jit(solution)/shard_map/ppermute | solution.py:246
  92.0 4.2 %collective-permute-done.9 = bf16[1,5,5,16,128]{4,3,2,1,0:T(8,128)(2,1)S(1)} collective-permute-done((bf16[1,5,5,16,128]{4,3,2,1,0:T(8,128)(2,1)S(1)}, bf16[1,5,5,16,128]{4,3,2,1,0:T(8,128)(2,1)S(1)}, u32[]{:S(2)}, u32[]{:S(2)}) %collective-permute-start.9) | collective-permute-done | bytes 102432 | tf_op jit(solution)/shard_map/ppermute | solution.py:246
  96.2 0.1 fusion.2
  96.3 1.6 %collective-permute-start.11 = (bf16[3,1,5,16,128]{4,3,2,1,0:T(8,128)(2,1)S(1)}, bf16[3,1,5,16,128]{4,3,2,1,0:T(8,128)(2,1)S(1)}, u32[]{:S(2)}, u32[]{:S(2)}) collective-permute-start(bf16[3,1,5,16,128]{4,3,2,1,0:T(8,128)(2,1)S(1)} %get-tuple-element.87), channel_id=1, source_target_pairs={{0,4},{4,8},{8,12},{12,16},{16,20},{20,24},{24,28},{28,32},{32,36}... | collective-permute-start | bytes 184328 | tf_op jit(solution)/shard_map/ppermute | solution.py:246
  97.9 0.5 collective-permute-start.12
  98.4 2.7 %collective-permute-done.11 = bf16[3,1,5,16,128]{4,3,2,1,0:T(8,128)(2,1)S(1)} collective-permute-done((bf16[3,1,5,16,128]{4,3,2,1,0:T(8,128)(2,1)S(1)}, bf16[3,1,5,16,128]{4,3,2,1,0:T(8,128)(2,1)S(1)}, u32[]{:S(2)}, u32[]{:S(2)}) %collective-permute-start.11) | collective-permute-done | bytes 61472 | tf_op jit(solution)/shard_map/ppermute | solution.py:246
  101.2 1.2 collective-permute-done.12
  102.5 6.7 %all-to-all-done.1 = bf16[128,8,384]{2,1,0:T(8,128)(2,1)S(1)} async-done(((bf16[128,8,384]{2,1,0:T(8,128)(2,1)}), bf16[128,8,384]{2,1,0:T(8,128)(2,1)S(1)}, u32[]{:S(2)}, u32[]{:S(2)}) %all-to-all-start.1) | async-done | bytes 786464 | tf_op jit(solution)/shard_map/all_to_all | solution.py:641
  109.2 0.5 collective-permute-start.14
  109.7 5.2 %collective-permute-start.13 = (bf16[3,3,1,16,128]{4,3,2,1,0:T(8,128)(2,1)S(1)}, bf16[3,3,1,16,128]{4,3,2,1,0:T(8,128)(2,1)S(1)}, u32[]{:S(2)}, u32[]{:S(2)}) collective-permute-start(bf16[3,3,1,16,128]{4,3,2,1,0:T(8,128)(2,1)S(1)} %get-tuple-element.92), channel_id=1, source_target_pairs={{0,3},{1,0},{2,1},{3,2},{4,7},{5,4},{6,5},{7,6},{8,11},{9,8},{10,9... | collective-permute-start | bytes 110600 | tf_op jit(solution)/shard_map/ppermute | solution.py:246
  114.9 0.1 convert_reduce_fusion.1
  115.1 0.6 broadcast_in_dim.29
  115.7 5.8 %all-to-all-start.2 = ((f32[16,8,128]{2,1,0:T(8,128)}), f32[16,8,128]{2,1,0:T(8,128)S(1)}, u32[]{:S(2)}, u32[]{:S(2)}) async-start(f32[16,8,128]{2,1,0:T(8,128)} %broadcast_in_dim.29), calls=%async_computation.2 | async-start | bytes 131072 | tf_op jit(solution)/shard_map/all_to_all | solution.py:650
  121.6 5.1 %ewald.2 = (f32[64,512]{1,0:T(8,128)}, f32[16,512]{1,0:T(8,128)}) custom-call(bf16[1024,384]{1,0:T(8,128)(2,1)} %bitcast.26, bf16[1024,512]{1,0:T(8,128)(2,1)} %get-tuple-element.56.cos_in, bf16[1024,512]{1,0:T(8,128)(2,1)} %get-tuple-element.57.sin_in, bf16[16,1024]{1,0:T(8,128)(2,1)} %get-tuple-element.43.miller_ref, bf16[64,512]{1,0:T(8,128)(2,1)} %bitcast.40, ...), custom_call_target="tpu_custom_call" | custom-call | flops 268435456 | bytes 2097152 | tf_op jit(solution)/shard_map/ewald/pallas_call | solution.py:492
  126.8 0.7 pad_maximum_fusion.4.rows_ref
  127.5 2.0 %finish.1 = (f32[64,512]{1,0:T(8,128)}, f32[8,512]{1,0:T(8,128)}) custom-call(f32[512,128]{1,0:T(8,128)} %pad_maximum_fusion.4.rows_ref, s32[1,512]{1,0:T(1,128)} %bitcast.58, f32[4,64]{1,0:T(4,128)} %gain_ref.3, bf16[64,64]{1,0:T(8,128)(2,1)} %mix_ref.3, f32[8,512]{1,0:T(8,128)} %get-tuple-element.64.own_ref), custom_call_target="tpu_custom_call" | custom-call | tf_op jit(solution)/shard_map/finish/pallas_call | solution.py:520
  129.5 0.6 copy-done.5
  130.1 0.3 copy-done.2
  130.4 5.4 %ewald.3 = (bf16[64,512]{1,0:T(8,128)(2,1)}, f32[3,1,512]{2,1,0:T(1,128)}, f32[64,64]{1,0:T(8,128)}, f32[16,64]{1,0:T(8,128)}) custom-call(bf16[1024,384]{1,0:T(8,128)(2,1)} %copy-done.2, bf16[1024,512]{1,0:T(8,128)(2,1)} %get-tuple-element.52.cos_in, bf16[1024,512]{1,0:T(8,128)(2,1)} %get-tuple-element.53.sin_in, ...), custom_call_target="tpu_custom_call" | custom-call | flops 268435456 | bytes 2097152 | tf_op jit(solution)/shard_map/ewald/pallas_call | solution.py:492
  (46 shorter events, 0.6 us)
Async XLA Ops:
  0.6 65.4 %copy-start = (f32[2048,64]{0,1:T(8,128)S(1)}, f32[2048,64]{0,1:T(8,128)}, u32[]{:S(2)}) copy-start(f32[2048,64]{0,1:T(8,128)} %param.16) | copy-start | bytes 1572868
  2.5 5.5 %copy-start.6 = (bf16[512,128]{1,0:T(8,128)(2,1)S(1)}, bf16[512,128]{1,0:T(8,128)(2,1)}, u32[]{:S(2)}) copy-start(bf16[512,128]{1,0:T(8,128)(2,1)} %get-tuple-element.38) | copy-start | bytes 393220
  7.8 25.2 %collective-permute-start.4 = (f32[1024,256]{1,0:T(8,128)}, f32[1024,256]{1,0:T(8,128)S(1)}, u32[]{:S(2)}, u32[]{:S(2)}) collective-permute-start(f32[1024,256]{1,0:T(8,128)} %get-tuple-element.40), channel_id=1, source_target_pairs={{0,1},{1,0},{2,3},{3,2},{4,5},{5,4},{6,7},{7,6},{8,9},{9,8},{10,11... | collective-permute-start | bytes 3145736 | tf_op jit(solution)/shard_map/ppermute | solution.py:246
  8.0 9.0 %collective-permute-start.1 = (bf16[3,3,1,16,128]{4,3,2,1,0:T(8,128)(2,1)S(1)}, bf16[3,3,1,16,128]{4,3,2,1,0:T(8,128)(2,1)S(1)}, u32[]{:S(2)}, u32[]{:S(2)}) collective-permute-start(bf16[3,3,1,16,128]{4,3,2,1,0:T(8,128)(2,1)S(1)} %get-tuple-element.95), channel_id=1, source_target_pairs={{0,3},{1,0},{2,1},{3,2},{4,7},{5,4},{6,5},{7,6},{8,11},{9,8},{10,9... | collective-permute-start | bytes 110600 | tf_op jit(solution)/shard_map/ppermute | solution.py:246
  15.3 7.3 %collective-permute-start = (bf16[3,3,1,16,128]{4,3,2,1,0:T(8,128)(2,1)S(1)}, bf16[3,3,1,16,128]{4,3,2,1,0:T(8,128)(2,1)S(1)}, u32[]{:S(2)}, u32[]{:S(2)}) collective-permute-start(bf16[3,3,1,16,128]{4,3,2,1,0:T(8,128)(2,1)S(1)} %get-tuple-element.96), channel_id=1, source_target_pairs={{0,1},{1,2},{2,3},{3,0},{4,5},{5,6},{6,7},{7,4},{8,9},{9,10},{10,1... | collective-permute-start | bytes 110600 | tf_op jit(solution)/shard_map/ppermute | solution.py:246
  22.6 7.4 %collective-permute-start.3 = (bf16[3,1,5,16,128]{4,3,2,1,0:T(8,128)(2,1)S(1)}, bf16[3,1,5,16,128]{4,3,2,1,0:T(8,128)(2,1)S(1)}, u32[]{:S(2)}, u32[]{:S(2)}) collective-permute-start(bf16[3,1,5,16,128]{4,3,2,1,0:T(8,128)(2,1)S(1)} %get-tuple-element.93), channel_id=1, source_target_pairs={{0,60},{4,0},{8,4},{12,8},{16,12},{20,16},{24,20},{28,24},{32,28},... | collective-permute-start | bytes 184328 | tf_op jit(solution)/shard_map/ppermute | solution.py:246
  23.2 6.9 %collective-permute-start.2 = (bf16[3,1,5,16,128]{4,3,2,1,0:T(8,128)(2,1)S(1)}, bf16[3,1,5,16,128]{4,3,2,1,0:T(8,128)(2,1)S(1)}, u32[]{:S(2)}, u32[]{:S(2)}) collective-permute-start(bf16[3,1,5,16,128]{4,3,2,1,0:T(8,128)(2,1)S(1)} %get-tuple-element.94), channel_id=1, source_target_pairs={{0,4},{4,8},{8,12},{12,16},{16,20},{20,24},{24,28},{28,32},{32,36}... | collective-permute-start | bytes 184328 | tf_op jit(solution)/shard_map/ppermute | solution.py:246
  30.2 5.1 %collective-permute-start.6 = (bf16[1,5,5,16,128]{4,3,2,1,0:T(8,128)(2,1)S(1)}, bf16[1,5,5,16,128]{4,3,2,1,0:T(8,128)(2,1)S(1)}, u32[]{:S(2)}, u32[]{:S(2)}) collective-permute-start(bf16[1,5,5,16,128]{4,3,2,1,0:T(8,128)(2,1)S(1)} %get-tuple-element.89), channel_id=1, source_target_pairs={{0,192},{64,0},{128,64},{192,128},{1,193},{65,1},{129,65},{193,129... | collective-permute-start | bytes 307208 | tf_op jit(solution)/shard_map/ppermute | solution.py:246
  33.0 5.9 %collective-permute-start.5 = (bf16[1,5,5,16,128]{4,3,2,1,0:T(8,128)(2,1)S(1)}, bf16[1,5,5,16,128]{4,3,2,1,0:T(8,128)(2,1)S(1)}, u32[]{:S(2)}, u32[]{:S(2)}) collective-permute-start(bf16[1,5,5,16,128]{4,3,2,1,0:T(8,128)(2,1)S(1)} %get-tuple-element.90), channel_id=1, source_target_pairs={{0,64},{64,128},{128,192},{192,0},{1,65},{65,129},{129,193},{193,1... | collective-permute-start | bytes 307208 | tf_op jit(solution)/shard_map/ppermute | solution.py:246
  38.9 29.4 %all-to-all-start = ((bf16[128,8,256]{2,1,0:T(8,128)(2,1)}), bf16[128,8,256]{2,1,0:T(8,128)(2,1)S(1)}, u32[]{:S(2)}, u32[]{:S(2)}) async-start(bf16[128,8,256]{2,1,0:T(8,128)(2,1)} %bitcast.5), calls=%async_computation | async-start | bytes 1048576 | tf_op jit(solution)/shard_map/all_to_all | solution.py:612
  50.3 0.8 copy-start.3
  66.0 1.5 %collective-permute-start.7 = (f32[128,128]{1,0:T(8,128)}, f32[128,128]{1,0:T(8,128)S(1)}, u32[]{:S(2)}, u32[]{:S(2)}) collective-permute-start(f32[128,128]{1,0:T(8,128)} %get-tuple-element.51), channel_id=1, source_target_pairs={{0,1},{1,0},{2,3},{3,2},{4,5},{5,4},{6,7},{7,6},{8,9},{9,8},{10,11... | collective-permute-start | bytes 196616 | tf_op jit(solution)/shard_map/ppermute | solution.py:246
  70.3 18.4 %copy-start.4 = (f32[2160,128]{1,0:T(8,128)S(1)}, f32[2160,128]{1,0:T(8,128)}, u32[]{:S(2)}) copy-start(f32[2160,128]{1,0:T(8,128)} %get-tuple-element.54) | copy-start | bytes 3317764
  70.3 38.9 %all-to-all-start.1 = ((bf16[128,8,384]{2,1,0:T(8,128)(2,1)}), bf16[128,8,384]{2,1,0:T(8,128)(2,1)S(1)}, u32[]{:S(2)}, u32[]{:S(2)}) async-start(bf16[128,8,384]{2,1,0:T(8,128)(2,1)} %pad_maximum_fusion), calls=%async_computation.1 | async-start | bytes 1572864 | tf_op jit(solution)/shard_map/all_to_all | solution.py:641
  85.3 6.6 %collective-permute-start.10 = (bf16[1,5,5,16,128]{4,3,2,1,0:T(8,128)(2,1)S(1)}, bf16[1,5,5,16,128]{4,3,2,1,0:T(8,128)(2,1)S(1)}, u32[]{:S(2)}, u32[]{:S(2)}) collective-permute-start(bf16[1,5,5,16,128]{4,3,2,1,0:T(8,128)(2,1)S(1)} %bitcast.51), channel_id=1, source_target_pairs={{0,192},{64,0},{128,64},{192,128},{1,193},{65,1},{129,65},{193,129... | collective-permute-start | bytes 307208 | tf_op jit(solution)/shard_map/ppermute | solution.py:246
  88.7 7.5 %collective-permute-start.9 = (bf16[1,5,5,16,128]{4,3,2,1,0:T(8,128)(2,1)S(1)}, bf16[1,5,5,16,128]{4,3,2,1,0:T(8,128)(2,1)S(1)}, u32[]{:S(2)}, u32[]{:S(2)}) collective-permute-start(bf16[1,5,5,16,128]{4,3,2,1,0:T(8,128)(2,1)S(1)} %bitcast.49), channel_id=1, source_target_pairs={{0,64},{64,128},{128,192},{192,0},{1,65},{65,129},{129,193},{193,1... | collective-permute-start | bytes 307208 | tf_op jit(solution)/shard_map/ppermute | solution.py:246
  96.3 4.9 %collective-permute-start.11 = (bf16[3,1,5,16,128]{4,3,2,1,0:T(8,128)(2,1)S(1)}, bf16[3,1,5,16,128]{4,3,2,1,0:T(8,128)(2,1)S(1)}, u32[]{:S(2)}, u32[]{:S(2)}) collective-permute-start(bf16[3,1,5,16,128]{4,3,2,1,0:T(8,128)(2,1)S(1)} %get-tuple-element.87), channel_id=1, source_target_pairs={{0,4},{4,8},{8,12},{12,16},{16,20},{20,24},{24,28},{28,32},{32,36}... | collective-permute-start | bytes 184328 | tf_op jit(solution)/shard_map/ppermute | solution.py:246
  97.9 4.5 %collective-permute-start.12 = (bf16[3,1,5,16,128]{4,3,2,1,0:T(8,128)(2,1)S(1)}, bf16[3,1,5,16,128]{4,3,2,1,0:T(8,128)(2,1)S(1)}, u32[]{:S(2)}, u32[]{:S(2)}) collective-permute-start(bf16[3,1,5,16,128]{4,3,2,1,0:T(8,128)(2,1)S(1)} %get-tuple-element.88), channel_id=1, source_target_pairs={{0,60},{4,0},{8,4},{12,8},{16,12},{20,16},{24,20},{28,24},{32,28},... | collective-permute-start | bytes 184328 | tf_op jit(solution)/shard_map/ppermute | solution.py:246
  109.2 12.4 %copy-start.1 = (bf16[128,8,384]{2,1,0:T(8,128)(2,1)}, bf16[128,8,384]{2,1,0:T(8,128)(2,1)S(1)}, u32[]{:S(2)}) copy-start(bf16[128,8,384]{2,1,0:T(8,128)(2,1)S(1)} %all-to-all-done.1) | copy-start | bytes 2359300
  109.2 20.4 %collective-permute-start.8 = (bf16[1024,384]{1,0:T(8,128)(2,1)S(1)}, bf16[1024,384]{1,0:T(8,128)(2,1)S(1)}, u32[]{:S(2)}, u32[]{:S(2)}) collective-permute-start(bf16[1024,384]{1,0:T(8,128)(2,1)S(1)} %bitcast.25), channel_id=1, source_target_pairs={{0,1},{1,0},{2,3},{3,2},{4,5},{5,4},{6,7},{7,6},{8,9},{9,8},{10,11... | collective-permute-start | bytes 2359304 | tf_op jit(solution)/shard_map/ppermute | solution.py:246
  109.2 17.5 %collective-permute-start.14 = (bf16[3,3,1,16,128]{4,3,2,1,0:T(8,128)(2,1)S(1)}, bf16[3,3,1,16,128]{4,3,2,1,0:T(8,128)(2,1)S(1)}, u32[]{:S(2)}, u32[]{:S(2)}) collective-permute-start(bf16[3,3,1,16,128]{4,3,2,1,0:T(8,128)(2,1)S(1)} %get-tuple-element.91), channel_id=1, source_target_pairs={{0,1},{1,2},{2,3},{3,0},{4,5},{5,6},{6,7},{7,4},{8,9},{9,10},{10,1... | collective-permute-start | bytes 110600 | tf_op jit(solution)/shard_map/ppermute | solution.py:246
  109.7 17.0 %collective-permute-start.13 = (bf16[3,3,1,16,128]{4,3,2,1,0:T(8,128)(2,1)S(1)}, bf16[3,3,1,16,128]{4,3,2,1,0:T(8,128)(2,1)S(1)}, u32[]{:S(2)}, u32[]{:S(2)}) collective-permute-start(bf16[3,3,1,16,128]{4,3,2,1,0:T(8,128)(2,1)S(1)} %get-tuple-element.92), channel_id=1, source_target_pairs={{0,3},{1,0},{2,1},{3,2},{4,7},{5,4},{6,5},{7,6},{8,11},{9,8},{10,9... | collective-permute-start | bytes 110600 | tf_op jit(solution)/shard_map/ppermute | solution.py:246
  115.7 13.8 %all-to-all-start.2 = ((f32[16,8,128]{2,1,0:T(8,128)}), f32[16,8,128]{2,1,0:T(8,128)S(1)}, u32[]{:S(2)}, u32[]{:S(2)}) async-start(f32[16,8,128]{2,1,0:T(8,128)} %broadcast_in_dim.29), calls=%async_computation.2 | async-start | bytes 131072 | tf_op jit(solution)/shard_map/all_to_all | solution.py:650
  129.5 0.6 copy-start.5
  129.5 0.9 copy-start.2

commit v4 on v3

--- a/solution.py
+++ b/solution.py
@@ -9,9 +9,11 @@
 from jax.sharding import Mesh
 from jax.sharding import PartitionSpec as P
 
+
 GY = ("gy_0", "gy_1")
 GZ = ("gz_0", "gz_1")
 CHIPS = ("gx", "gy_0", "gy_1", "gz_0")
+PLANE = ("gy_0", "gy_1", "gz_0")
 PAIR = "gz_1"
 GX_GY_GZ = ("gx", "gy_0", "gy_1", "gz_0", "gz_1")
 
@@ -255,7 +257,7 @@
 
 def pack_kernel(h_ref, kind_ref, pos_ref, miller_ref, table_ref, mine_ref, next_ref):
     f32, bf16 = jnp.float32, jnp.bfloat16
-    channels, atoms = h_ref.shape
+    _, atoms = h_ref.shape
     none = jnp.zeros((1, atoms), f32)
     halves = [split_two(pos_ref[d]) for d in range(3)]
     rows = jnp.concatenate(
@@ -298,10 +300,9 @@
     dy_ref,
     cos_out,
     sin_out,
-    part_out,
+    part_ref,
     cos_ref,
     sin_ref,
-    part_ref,
     flip_ref,
     rhs_ref,
     t_ref,
@@ -331,7 +332,7 @@
         return [
             pltpu.make_async_copy(src.at[at], dst.at[at], sems.at[n, i])
             for n, (src, dst) in enumerate(
-                ((cos_ref, cos_out), (sin_ref, sin_out), (part_ref, part_out))
+                ((cos_ref, cos_out), (sin_ref, sin_out))
             )
         ]
 
@@ -385,15 +386,14 @@
         phase_kernel,
         out_shape=(wave, wave, sums),
         in_specs=[WHOLE] * 4,
-        out_specs=(pl.BlockSpec(memory_space=pl.ANY),) * 3,
+        out_specs=(pl.BlockSpec(memory_space=pl.ANY),) * 2 + (WHOLE,),
         scratch_shapes=[
             pltpu.VMEM(wave.shape, wave.dtype),
             pltpu.VMEM(wave.shape, wave.dtype),
-            pltpu.VMEM(sums.shape, sums.dtype),
             pltpu.VMEM((atoms, width), jnp.bfloat16),
             pltpu.VMEM((16, atoms), jnp.bfloat16),
             pltpu.VMEM((CHUNK, atoms), jnp.float32),
-            pltpu.SemaphoreType.DMA((3, points // CHUNK)),
+            pltpu.SemaphoreType.DMA((2, points // CHUNK)),
         ],
         cost_estimate=pl.CostEstimate(
             flops=6 * points * atoms * width, transcendentals=0, bytes_accessed=4 * points * atoms
@@ -411,9 +411,8 @@
 
     def copies(i):
         at = pl.ds(pl.multiple_of(i * CHUNK, CHUNK), CHUNK)
-        wide = pl.ds(0, 2 * width)
         return [
-            pltpu.make_async_copy(coeff_in.at[at, wide], coeff_ref.at[at], sems.at[0, i]),
+            pltpu.make_async_copy(coeff_in.at[i, pl.ds(0, CHUNK)], coeff_ref.at[at], sems.at[0, i]),
             pltpu.make_async_copy(cos_in.at[at], cos_ref.at[at], sems.at[1, i]),
             pltpu.make_async_copy(sin_in.at[at], sin_ref.at[at], sems.at[2, i]),
         ]
@@ -424,8 +423,23 @@
     both_ref[...] = jnp.concatenate([h_ref[...], dy_ref[...]], axis=0)
     if last:
         sums_ref, turn_ref = rest[-7:-5]
-        sums_ref[...] = rest[0][...]
-        turn_ref[...] = rest[1][...]
+        first_ref, angle_ref, grid_ref, upper_ref, lower_ref = rest[0:5]
+        core_ref, own_ref, all_ref, kind_ref, gain_ref, mix_ref = rest[5:11]
+        inner = [
+            grid_ref[:, :, 1] + lower_ref[:, :, 0].astype(f32),
+            grid_ref[:, :, 2],
+            grid_ref[:, :, 3] + upper_ref[:, :, 0].astype(f32),
+        ]
+        cells = jnp.stack(inner, axis=2).reshape(432, 128)
+        flat = jnp.transpose(jnp.concatenate([cells, core_ref[...]], axis=0))
+        gains = gains_of(gain_ref[...], kind_ref[...], (channels, flat.shape[1]))
+        zscaled = (flat[0:channels] * gains).astype(bf16)
+        halves = flat[channels : channels + 8]
+        near = halves + pltpu.roll(halves, 4, 0) + own_ref[...]
+        sums_ref[...] = first_ref[...] + jnp.dot(
+            mix_ref[...], zscaled, preferred_element_type=f32
+        )
+        turn_ref[...] = angle_ref[...]
     else:
         sums_ref, turn_ref = rest[0:2]
         sums_ref[...] = jnp.zeros_like(sums_ref)
@@ -455,13 +469,13 @@
 
     lax.fori_loop(0, steps, one, 0)
     if last:
-        short_ref, near_ref, all_ref, atom_ref, pos_ref, weight_ref, radial_ref = rest[2:9]
-        atom_ref[...] = (dy_ref[...].astype(f32) + sums_ref[...] + short_ref[...]).astype(bf16)
+        atom_ref, pos_ref, weight_ref, radial_ref = rest[11:15]
+        atom_ref[...] = (dy_ref[...].astype(f32) + sums_ref[...]).astype(bf16)
         axes = ("gx", GY, GZ)
         for d in range(3):
             pos_ref[d] = (
                 turn_ref[d : d + 1, :] * (circle_angle / lax.axis_size(axes[d]))
-                + near_ref[d : d + 1, :]
+                + near[d : d + 1, :]
             )
         weight_ref[...] = all_ref[0:channels, 0:channels]
         radial_ref[...] = all_ref[channels : channels + radial_ref.shape[0], 0:channels]
@@ -504,31 +518,6 @@
     )(coeffs, cos_all, sin_all, miller, h, dy, *more)
 
 
-def finish_kernel(rows_ref, kind_ref, gain_ref, mix_ref, own_ref, short_ref, pos_ref):
-    f32, bf16 = jnp.float32, jnp.bfloat16
-    channels, atoms = short_ref.shape
-    flat = jnp.transpose(rows_ref[...])
-    gains = gains_of(gain_ref[...], kind_ref[...], (channels, atoms))
-    zscaled = (flat[0:channels] * gains).astype(bf16)
-    short_ref[...] = jnp.dot(mix_ref[...], zscaled, preferred_element_type=f32)
-    halves = flat[channels : channels + 8]
-    pos_ref[...] = halves + pltpu.roll(halves, 4, 0) + own_ref[...]
-
-
-def finish(rows, kinds, gain, mix, own):
-    channels, atoms = mix.shape[0], rows.shape[0]
-    return pl.pallas_call(
-        finish_kernel,
-        out_shape=(
-            jax.ShapeDtypeStruct((channels, atoms), jnp.float32),
-            jax.ShapeDtypeStruct((8, atoms), jnp.float32),
-        ),
-        in_specs=[WHOLE] * 5,
-        out_specs=(WHOLE,) * 2,
-        name="finish",
-    )(rows, kinds, gain, mix, own)
-
-
 def coefficients(totals, filt_rows, norm_atoms, norm_k):
     channels = filt_rows.shape[1]
     cos_struct = totals[:, 0:channels] * norm_atoms
@@ -569,7 +558,7 @@
     return jnp.concatenate([low, middle, high], axis=dim)
 
 
-def shards(
+def whole(
     atom_embedding,
     output_adjoint,
     fractional_coords,
@@ -593,22 +582,18 @@
     share_rows = points // devices
     share_start = lax.axis_index(GX_GY_GZ) * share_rows
     groups = lax.axis_size(CHIPS)
-    half = points // 2
 
     own_table, miller_mine, miller_next = pack(h, kinds, pos, miller_triples)
     cells = own_table[0:432].reshape(3, 3, 3, 16, 128)
     below, above = sent_out(cells, GZ, 2)
     cos_next, sin_next, part_next = phase_sums(pos, miller_next, h, dy)
     received = from_behind(part_next, PAIR, 1)
-    below, above, part_next = lax.optimization_barrier((below, above, part_next))
     cells = jnp.concatenate([below, cells, above], axis=2)
     below, above = sent_out(cells, GY, 1)
     cos_mine, sin_mine, part_mine = phase_sums(pos, miller_mine, h, dy)
-    below, above, part_mine = lax.optimization_barrier((below, above, part_mine))
     cells = jnp.concatenate([below, cells, above], axis=1)
     below, above = sent_out(cells, "gx", 0)
     paired = (part_mine + received).astype(jnp.bfloat16)
-    paired, below, above = lax.optimization_barrier((paired, below, above))
     pieces = lax.all_to_all(paired.reshape(groups, share_rows, 4 * channels), CHIPS, 0, 0)
 
     table = jnp.concatenate(
@@ -631,40 +616,57 @@
         element_channel_factor,
     )
     sums = sums + from_behind(sums, PAIR, 1)
-    tiles = sums.astype(jnp.bfloat16).reshape(1, 16, 1, 8, 128)
-    tiles = jnp.broadcast_to(tiles, (groups // 32, 16, 2, 8, 128)).reshape(groups, 8, 128)
+    tiles = sums.astype(jnp.bfloat16).reshape(16, 1, 8, 128)
+    tiles = jnp.broadcast_to(tiles, (16, 2, 8, 128)).reshape(32, 8, 128)
 
     totals = jnp.sum(pieces.astype(jnp.float32), axis=0)
     filt_rows = lax.dynamic_slice_in_dim(reciprocal_kernel, share_start, share_rows, 0)
     own_coeffs, filter_share = coefficients(totals, filt_rows, norm_atoms, norm_k)
-    spread = jnp.broadcast_to(own_coeffs[None], (groups, share_rows, 4 * channels))
-    got = lax.all_to_all(jnp.concatenate([spread, tiles], axis=2), CHIPS, 0, 0)
-
+    spread = jnp.broadcast_to(own_coeffs[None], (32, share_rows, 4 * channels))
+    got = lax.all_to_all(jnp.concatenate([spread, tiles], axis=2), PLANE, 0, 0)
+
+    grid = ghost_grad[0:2000].reshape(5, 5, 5, 16, 128)
     to_side = sent_back(ghost_thin[0:2000].reshape(5, 5, 5, 16, 128), "gx", 0)
-    grid = folded(ghost_grad[0:2000].reshape(5, 5, 5, 16, 128), to_side, 0)
-    grid = folded(grid, sent_back(grid, GY, 1), 1)
-
-    tile_sum = jnp.sum(got[:, :, 4 * channels :].astype(jnp.float32), axis=0)
-    coeffs_mine = got.reshape(half, 4 * channels + 128)
-    coeffs_next = from_behind(coeffs_mine, PAIR, 1)
+    grid = folded(grid, to_side, 0)
+    to_side = sent_back(grid, GY, 1)
+
+    tile_part = jnp.sum(got[:, :, 4 * channels :].astype(jnp.float32), axis=0)
+    lines = lax.axis_size("gx")
+    strip = jnp.concatenate(
+        [
+            got[:, :, 0 : 4 * channels].reshape(32 * share_rows, 4 * channels),
+            jnp.concatenate(
+                [tile_part.astype(jnp.bfloat16), jnp.zeros((8, 128), jnp.bfloat16)], axis=1
+            ),
+        ],
+        axis=0,
+    )
+    got = lax.all_to_all(jnp.broadcast_to(strip[None], (lines,) + strip.shape), "gx", 0, 0)
+    grid = folded(grid, to_side, 1)
+    to_side = sent_back(grid, GZ, 2)
+    tile_sum = jnp.sum(got[:, 32 * share_rows :, 0:128].astype(jnp.float32), axis=0)
+    got_next = from_behind(got, PAIR, 1)
     every = lax.all_to_all(jnp.broadcast_to(tile_sum[None], (16, 8, 128)), GY, 0, 0)
     every = every.reshape(128, 128)
-    to_side = sent_back(grid, GZ, 2)
-    first = ewald(coeffs_mine, cos_mine, sin_mine, miller_mine, h, dy)
-    to_side, first = lax.optimization_barrier((to_side, first))
-    grid = folded(grid, to_side, 2)
-    rows = jnp.concatenate([grid.reshape(432, 128), ghost_grad[2000:2080]], axis=0)
-    atom_short, pos_short = finish(
-        rows, kinds, element_channel_factor, channel_mixing_matrix, own_grad
-    )
+    first = ewald(got, cos_mine, sin_mine, miller_mine, h, dy)
     atom_grad, position_grad, weight_grad, radial_grad = ewald(
-        coeffs_next,
+        got_next,
         cos_next,
         sin_next,
         miller_next,
         h,
         dy,
-        (*first, atom_short, pos_short, every),
+        (
+            *first,
+            grid,
+            *to_side,
+            ghost_grad[2000:2080],
+            own_grad,
+            every,
+            kinds,
+            element_channel_factor,
+            channel_mixing_matrix,
+        ),
         distance_kernel.shape[0],
     )
     position_grad = position_grad[:, 0, :]
@@ -700,6 +702,4 @@
         P(),
         P(GX_GY_GZ, None),
     )
-    return jax.shard_map(
-        shards, mesh=finer, in_specs=in_specs, out_specs=out_specs, check_vma=False
-    )
+    return jax.shard_map(whole, mesh=finer, in_specs=in_specs, out_specs=out_specs, check_vma=False)

time: 137 us -> 143 us (1.044)
  the two profiles are of different devices: /device:TPU:8 before, /device:TPU:2 now
where the time goes in v4:
time: 143 us; the launch traced here: 142 us
  starting transfers between devices  66 us (46%)
  Pallas kernels  39.5 us (28%)
  waiting for transfers between devices  22.4 us (16%)
  local copies, waits for them, and re-layouts  8.59 us (6%)
  other arithmetic  4.84 us (3%)
    ppermute x15, starting transfers between devices, from_behind(): lax.ppermute(x, axis, [(i, (i + by) % devices) for i in range(devices)])  29.5 us
    pallas_call x1, Pallas kernels, short_range(): pl.pallas_call(short_kernel, out_shape=(jax.ShapeDtypeStruct((GROUPS * HI...  14.8 us
    all_to_all x1, starting transfers between devices, whole(): lax.all_to_all(paired.reshape(groups, share_rows, 4 * channels), CHIPS, 0...  13.6 us
    pallas_call x2, Pallas kernels, phase_sums(): pl.pallas_call(phase_kernel, out_shape=(wave, wave, sums), in_specs=[WHOL...  12.3 us
    all_to_all x1, waiting for transfers between devices, whole(): got = lax.all_to_all(jnp.concatenate([spread, tiles], axis=2), PLANE, 0, 0)  11.2 us
    pallas_call x2, Pallas kernels, ewald(): pl.pallas_call(functools.partial(ewald_kernel, last), out_shape=outs, in_...  10.6 us
    all_to_all x1, starting transfers between devices, whole(): got = lax.all_to_all(jnp.concatenate([spread, tiles], axis=2), PLANE, 0, 0)  9.46 us
    ppermute x15, waiting for transfers between devices, from_behind(): lax.ppermute(x, axis, [(i, (i + by) % devices) for i in range(devices)])  8.77 us
  transfers between devices with their start and end apart: 19, of which 5 were waited for; matrix products, arithmetic and copies ran while one was open for 6% of the time, Pallas kernels for 23%

profile of v4, /device:TPU:2, one launch (start us, length us, event | category | flops | bytes accessed | tf_op | source)
XLA Modules:
  0.0 142.4 jit_solution(11131629743907990276)
XLA Ops:
  0.6 1.8 %pack.1 = (bf16[512,128]{1,0:T(8,128)(2,1)}, bf16[16,1024]{1,0:T(8,128)(2,1)}, bf16[16,1024]{1,0:T(8,128)(2,1)}) custom-call(bf16[64,512]{1,0:T(8,128)(2,1)} %bitcast.34, s32[1,512]{1,0:T(1,128)} %bitcast.55, f32[3,1,512]{2,1,0:T(1,128)} %bitcast.51, s32[3,2048]{1,0:T(4,128)} %miller_ref.1), custom_call_target="tpu_custom_call" | custom-call | tf_op jit(solution)/shard_map/pack/pallas_call | solution.py:287
  2.5 0.9 slice.114
  3.4 0.1 collective-permute-start.1
  3.5 6.7 %collective-permute-start.2 = (bf16[3,3,1,16,128]{4,3,2,1,0:T(8,128)(2,1)S(1)}, bf16[3,3,1,16,128]{4,3,2,1,0:T(8,128)(2,1)S(1)}, u32[]{:S(2)}, u32[]{:S(2)}) collective-permute-start(bf16[3,3,1,16,128]{4,3,2,1,0:T(8,128)(2,1)S(1)} %get-tuple-element.65), channel_id=1, source_target_pairs={{0,3},{1,0},{2,1},{3,2},{4,7},{5,4},{6,5},{7,6},{8,11},{9,8},{10,9... | collective-permute-start | bytes 110600 | tf_op jit(solution)/shard_map/ppermute | solution.py:248
  10.2 6.1 %phase_sums.3 = (bf16[1024,512]{1,0:T(8,128)(2,1)}, bf16[1024,512]{1,0:T(8,128)(2,1)}, f32[1024,256]{1,0:T(8,128)}) custom-call(f32[3,1,512]{2,1,0:T(1,128)} %bitcast.52, bf16[16,1024]{1,0:T(8,128)(2,1)} %get-tuple-element.26.miller_ref, bf16[64,512]{1,0:T(8,128)(2,1)} %bitcast.35, bf16[64,512]{1,0:T(8,128)(2,1)} %bitcast.39), custom_call_target="tpu_custom_call" | custom-call | flops 402653184 | bytes 2097152 | tf_op jit(solution)/shard_map/phase_sums/pallas_call | solution.py:385
  16.3 0.7 collective-permute-start
  17.0 1.7 %collective-permute-start.3 = (bf16[3,1,5,16,128]{4,3,2,1,0:T(8,128)(2,1)S(1)}, bf16[3,1,5,16,128]{4,3,2,1,0:T(8,128)(2,1)S(1)}, u32[]{:S(2)}, u32[]{:S(2)}) collective-permute-start(bf16[3,1,5,16,128]{4,3,2,1,0:T(8,128)(2,1)S(1)} %get-tuple-element.62), channel_id=1, source_target_pairs={{0,4},{4,8},{8,12},{12,16},{16,20},{20,24},{24,28},{28,32},{32,36}... | collective-permute-start | bytes 184328 | tf_op jit(solution)/shard_map/ppermute | solution.py:248
  18.7 4.4 %collective-permute-start.4 = (bf16[3,1,5,16,128]{4,3,2,1,0:T(8,128)(2,1)S(1)}, bf16[3,1,5,16,128]{4,3,2,1,0:T(8,128)(2,1)S(1)}, u32[]{:S(2)}, u32[]{:S(2)}) collective-permute-start(bf16[3,1,5,16,128]{4,3,2,1,0:T(8,128)(2,1)S(1)} %get-tuple-element.63), channel_id=1, source_target_pairs={{0,60},{4,0},{8,4},{12,8},{16,12},{20,16},{24,20},{28,24},{32,28},... | collective-permute-start | bytes 184328 | tf_op jit(solution)/shard_map/ppermute | solution.py:248
  23.0 2.5 %collective-permute-done.3 = bf16[3,1,5,16,128]{4,3,2,1,0:T(8,128)(2,1)S(1)} collective-permute-done((bf16[3,1,5,16,128]{4,3,2,1,0:T(8,128)(2,1)S(1)}, bf16[3,1,5,16,128]{4,3,2,1,0:T(8,128)(2,1)S(1)}, u32[]{:S(2)}, u32[]{:S(2)}) %collective-permute-start.3) | collective-permute-done | bytes 61472 | tf_op jit(solution)/shard_map/ppermute | solution.py:248
  25.6 1.6 %collective-permute-start.5 = (bf16[1,5,5,16,128]{4,3,2,1,0:T(8,128)(2,1)S(1)}, bf16[1,5,5,16,128]{4,3,2,1,0:T(8,128)(2,1)S(1)}, u32[]{:S(2)}, u32[]{:S(2)}) collective-permute-start(bf16[1,5,5,16,128]{4,3,2,1,0:T(8,128)(2,1)S(1)} %get-tuple-element.59), channel_id=1, source_target_pairs={{0,64},{64,128},{128,192},{192,0},{1,65},{65,129},{129,193},{193,1... | collective-permute-start | bytes 307208 | tf_op jit(solution)/shard_map/ppermute | solution.py:248
  27.2 0.1 constant_dynamic-slice_fusion
  27.3 0.1 copy.17
  27.3 6.1 %phase_sums.2 = (bf16[1024,512]{1,0:T(8,128)(2,1)}, bf16[1024,512]{1,0:T(8,128)(2,1)}, f32[1024,256]{1,0:T(8,128)}) custom-call(f32[3,1,512]{2,1,0:T(1,128)} %bitcast.53, bf16[16,1024]{1,0:T(8,128)(2,1)} %get-tuple-element.24.miller_ref, bf16[64,512]{1,0:T(8,128)(2,1)} %bitcast.36, bf16[64,512]{1,0:T(8,128)(2,1)} %bitcast.40), custom_call_target="tpu_custom_call" | custom-call | flops 402653184 | bytes 2097152 | tf_op jit(solution)/shard_map/phase_sums/pallas_call | solution.py:385
  33.5 0.6 collective-permute-start.6
  34.2 4.1 %collective-permute-done.6 = bf16[1,5,5,16,128]{4,3,2,1,0:T(8,128)(2,1)S(1)} collective-permute-done((bf16[1,5,5,16,128]{4,3,2,1,0:T(8,128)(2,1)S(1)}, bf16[1,5,5,16,128]{4,3,2,1,0:T(8,128)(2,1)S(1)}, u32[]{:S(2)}, u32[]{:S(2)}) %collective-permute-start.6) | collective-permute-done | bytes 102432 | tf_op jit(solution)/shard_map/ppermute | solution.py:248
  38.2 2.1 %fusion = bf16[128,8,256]{2,1,0:T(8,128)(2,1)} fusion(f32[1024,256]{1,0:T(8,128)} %get-tuple-element.25, f32[1024,256]{1,0:T(8,128)S(1)} %collective-permute-done), kind=kLoop, calls=%fused_computation.3 | loop fusion | flops 524288 | bytes 2621440 | tf_op jit(solution)/shard_map/reshape | solution.py:597
  40.4 13.6 %all-to-all-start = ((bf16[128,8,256]{2,1,0:T(8,128)(2,1)}), bf16[128,8,256]{2,1,0:T(8,128)(2,1)S(1)}, u32[]{:S(2)}, u32[]{:S(2)}) async-start(bf16[128,8,256]{2,1,0:T(8,128)(2,1)} %fusion), calls=%async_computation | async-start | bytes 1048576 | tf_op jit(solution)/shard_map/all_to_all | solution.py:597
  53.9 0.7 slice_dynamic-update-slice_fusion
  54.7 0.8 copy-done.2
  55.5 14.8 %short_range.1 = (f32[2160,128]{1,0:T(8,128)}, bf16[2160,128]{1,0:T(8,128)(2,1)}, f32[8,512]{1,0:T(8,128)}, f32[128,128]{1,0:T(8,128)}) custom-call(bf16[2160,128]{1,0:T(8,128)(2,1)} %copy-done.2, s32[16,512]{1,0:T(8,128)} %bitcast.50, f32[3,1,512]{2,1,0:T(1,128)} %bitcast.54, bf16[64,512]{1,0:T(8,128)(2,1)} %bitcast.41, f32[16,64]{1,0:T(8,128)} %radial_ref.1, ...), custom_call_target="tpu_custom_call" | custom-call | tf_op jit(solution)/shard_map/short_range/pallas_call | solution.py:219
  70.3 1.2 fusion.6
  71.5 1.0 fusion.7
  72.5 1.4 slice.141.rest_5_
  73.9 1.0 collective-permute-start.10
  74.8 1.1 collective-permute-start.9
  75.9 0.1 convert_reduce_fusion
  76.1 0.7 multiply_convert_fusion.3
  76.7 0.1 pad_maximum_fusion.7
  76.9 0.7 pad_maximum_fusion.3
  77.6 9.5 %all-to-all-start.1 = ((bf16[32,8,384]{2,1,0:T(8,128)(2,1)}), bf16[32,8,384]{2,1,0:T(8,128)(2,1)S(1)}, u32[]{:S(2)}, u32[]{:S(2)}) async-start(bf16[32,8,384]{2,1,0:T(8,128)(2,1)} %pad_maximum_fusion.3), calls=%async_computation.1 | async-start | bytes 393216 | tf_op jit(solution)/shard_map/all_to_all | solution.py:626
  87.1 0.1 fusion.5
  87.2 11.2 %all-to-all-done.1 = bf16[32,8,384]{2,1,0:T(8,128)(2,1)S(1)} async-done(((bf16[32,8,384]{2,1,0:T(8,128)(2,1)}), bf16[32,8,384]{2,1,0:T(8,128)(2,1)S(1)}, u32[]{:S(2)}, u32[]{:S(2)}) %all-to-all-start.1) | async-done | bytes 196640 | tf_op jit(solution)/shard_map/all_to_all | solution.py:626
  98.4 0.8 broadcast_in_dim.36
  99.3 6.2 %all-to-all-start.2 = ((bf16[4,264,256]{2,1,0:T(8,128)(2,1)}), bf16[4,264,256]{2,1,0:T(8,128)(2,1)S(1)}, u32[]{:S(2)}, u32[]{:S(2)}) async-start(bf16[4,264,256]{2,1,0:T(8,128)(2,1)} %broadcast_in_dim.36), calls=%async_computation.2 | async-start | bytes 1081344 | tf_op jit(solution)/shard_map/all_to_all | solution.py:644
  105.4 0.1 collective-permute-start.11
  105.5 5.9 %collective-permute-start.12 = (bf16[3,1,5,16,128]{4,3,2,1,0:T(8,128)(2,1)S(1)}, bf16[3,1,5,16,128]{4,3,2,1,0:T(8,128)(2,1)S(1)}, u32[]{:S(2)}, u32[]{:S(2)}) collective-permute-start(bf16[3,1,5,16,128]{4,3,2,1,0:T(8,128)(2,1)S(1)} %get-tuple-element.57), channel_id=1, source_target_pairs={{0,60},{4,0},{8,4},{12,8},{16,12},{20,16},{24,20},{28,24},{32,28},... | collective-permute-start | bytes 184328 | tf_op jit(solution)/shard_map/ppermute | solution.py:248
  111.5 2.2 %collective-permute-done.11 = bf16[3,1,5,16,128]{4,3,2,1,0:T(8,128)(2,1)S(1)} collective-permute-done((bf16[3,1,5,16,128]{4,3,2,1,0:T(8,128)(2,1)S(1)}, bf16[3,1,5,16,128]{4,3,2,1,0:T(8,128)(2,1)S(1)}, u32[]{:S(2)}, u32[]{:S(2)}) %collective-permute-start.11) | collective-permute-done | bytes 61472 | tf_op jit(solution)/shard_map/ppermute | solution.py:248
  113.7 0.1 collective-permute-start.8
  113.9 0.6 collective-permute-start.14
  114.4 5.2 %collective-permute-start.13 = (bf16[3,3,1,16,128]{4,3,2,1,0:T(8,128)(2,1)S(1)}, bf16[3,3,1,16,128]{4,3,2,1,0:T(8,128)(2,1)S(1)}, u32[]{:S(2)}, u32[]{:S(2)}) collective-permute-start(bf16[3,3,1,16,128]{4,3,2,1,0:T(8,128)(2,1)S(1)} %get-tuple-element.61), channel_id=1, source_target_pairs={{0,3},{1,0},{2,1},{3,2},{4,7},{5,4},{6,5},{7,6},{8,11},{9,8},{10,9... | collective-permute-start | bytes 110600 | tf_op jit(solution)/shard_map/ppermute | solution.py:248
  119.6 0.6 broadcast_in_dim.37
  120.2 7.3 %all-to-all-start.3 = ((f32[16,8,128]{2,1,0:T(8,128)}), f32[16,8,128]{2,1,0:T(8,128)S(1)}, u32[]{:S(2)}, u32[]{:S(2)}) async-start(f32[16,8,128]{2,1,0:T(8,128)} %broadcast_in_dim.37), calls=%async_computation.3 | async-start | bytes 131072 | tf_op jit(solution)/shard_map/all_to_all | solution.py:649
  127.6 0.8 pad_maximum_fusion.1.rest_2_
  128.3 5.1 %ewald.2 = (f32[64,512]{1,0:T(8,128)}, f32[16,512]{1,0:T(8,128)}) custom-call(bf16[4,264,256]{2,1,0:T(8,128)(2,1)} %copy-done.1, bf16[1024,512]{1,0:T(8,128)(2,1)} %get-tuple-element.32.cos_in, bf16[1024,512]{1,0:T(8,128)(2,1)} %get-tuple-element.33.sin_in, bf16[16,1024]{1,0:T(8,128)(2,1)} %get-tuple-element.24.miller_ref, bf16[64,512]{1,0:T(8,128)(2,1)} %bitcast.37, ...), custom_call_target="tpu_custom_call" | custom-call | flops 268435456 | bytes 2097152 | tf_op jit(solution)/shard_map/ewald/pallas_call | solution.py:506
  133.5 2.4 %all-to-all-done.3 = f32[16,8,128]{2,1,0:T(8,128)S(1)} async-done(((f32[16,8,128]{2,1,0:T(8,128)}), f32[16,8,128]{2,1,0:T(8,128)S(1)}, u32[]{:S(2)}, u32[]{:S(2)}) %all-to-all-start.3) | async-done | bytes 65568 | tf_op jit(solution)/shard_map/all_to_all | solution.py:649
  136.0 0.6 copy-done.4
  136.6 0.2 copy-done.3
  136.8 5.5 %ewald.3 = (bf16[64,512]{1,0:T(8,128)(2,1)}, f32[3,1,512]{2,1,0:T(1,128)}, f32[64,64]{1,0:T(8,128)}, f32[16,64]{1,0:T(8,128)}) custom-call(bf16[4,264,256]{2,1,0:T(8,128)(2,1)} %copy-done.3, bf16[1024,512]{1,0:T(8,128)(2,1)} %get-tuple-element.30.cos_in, bf16[1024,512]{1,0:T(8,128)(2,1)} %get-tuple-element.31.sin_in, ...), custom_call_target="tpu_custom_call" | custom-call | flops 268435456 | bytes 2097152 | tf_op jit(solution)/shard_map/ewald/pallas_call | solution.py:506
  (50 shorter events, 0.5 us)
Async XLA Ops:
  0.6 26.6 %copy-start = (f32[2048,64]{0,1:T(8,128)S(1)}, f32[2048,64]{0,1:T(8,128)}, u32[]{:S(2)}) copy-start(f32[2048,64]{0,1:T(8,128)} %param.16) | copy-start | bytes 1572868
  3.4 13.6 %collective-permute-start.1 = (bf16[3,3,1,16,128]{4,3,2,1,0:T(8,128)(2,1)S(1)}, bf16[3,3,1,16,128]{4,3,2,1,0:T(8,128)(2,1)S(1)}, u32[]{:S(2)}, u32[]{:S(2)}) collective-permute-start(bf16[3,3,1,16,128]{4,3,2,1,0:T(8,128)(2,1)S(1)} %get-tuple-element.64), channel_id=1, source_target_pairs={{0,1},{1,2},{2,3},{3,0},{4,5},{5,6},{6,7},{7,4},{8,9},{9,10},{10,1... | collective-permute-start | bytes 110600 | tf_op jit(solution)/shard_map/ppermute | solution.py:248
  3.5 13.5 %collective-permute-start.2 = (bf16[3,3,1,16,128]{4,3,2,1,0:T(8,128)(2,1)S(1)}, bf16[3,3,1,16,128]{4,3,2,1,0:T(8,128)(2,1)S(1)}, u32[]{:S(2)}, u32[]{:S(2)}) collective-permute-start(bf16[3,3,1,16,128]{4,3,2,1,0:T(8,128)(2,1)S(1)} %get-tuple-element.65), channel_id=1, source_target_pairs={{0,3},{1,0},{2,1},{3,2},{4,7},{5,4},{6,5},{7,6},{8,11},{9,8},{10,9... | collective-permute-start | bytes 110600 | tf_op jit(solution)/shard_map/ppermute | solution.py:248
  16.3 21.9 %collective-permute-start = (f32[1024,256]{1,0:T(8,128)}, f32[1024,256]{1,0:T(8,128)S(1)}, u32[]{:S(2)}, u32[]{:S(2)}) collective-permute-start(f32[1024,256]{1,0:T(8,128)} %get-tuple-element.27), channel_id=1, source_target_pairs={{0,1},{1,0},{2,3},{3,2},{4,5},{5,4},{6,7},{7,6},{8,9},{9,8},{10,11... | collective-permute-start | bytes 3145736 | tf_op jit(solution)/shard_map/ppermute | solution.py:248
  17.0 8.5 %collective-permute-start.3 = (bf16[3,1,5,16,128]{4,3,2,1,0:T(8,128)(2,1)S(1)}, bf16[3,1,5,16,128]{4,3,2,1,0:T(8,128)(2,1)S(1)}, u32[]{:S(2)}, u32[]{:S(2)}) collective-permute-start(bf16[3,1,5,16,128]{4,3,2,1,0:T(8,128)(2,1)S(1)} %get-tuple-element.62), channel_id=1, source_target_pairs={{0,4},{4,8},{8,12},{12,16},{16,20},{20,24},{24,28},{28,32},{32,36}... | collective-permute-start | bytes 184328 | tf_op jit(solution)/shard_map/ppermute | solution.py:248
  18.7 6.9 %collective-permute-start.4 = (bf16[3,1,5,16,128]{4,3,2,1,0:T(8,128)(2,1)S(1)}, bf16[3,1,5,16,128]{4,3,2,1,0:T(8,128)(2,1)S(1)}, u32[]{:S(2)}, u32[]{:S(2)}) collective-permute-start(bf16[3,1,5,16,128]{4,3,2,1,0:T(8,128)(2,1)S(1)} %get-tuple-element.63), channel_id=1, source_target_pairs={{0,60},{4,0},{8,4},{12,8},{16,12},{20,16},{24,20},{28,24},{32,28},... | collective-permute-start | bytes 184328 | tf_op jit(solution)/shard_map/ppermute | solution.py:248
  25.6 8.5 %collective-permute-start.5 = (bf16[1,5,5,16,128]{4,3,2,1,0:T(8,128)(2,1)S(1)}, bf16[1,5,5,16,128]{4,3,2,1,0:T(8,128)(2,1)S(1)}, u32[]{:S(2)}, u32[]{:S(2)}) collective-permute-start(bf16[1,5,5,16,128]{4,3,2,1,0:T(8,128)(2,1)S(1)} %get-tuple-element.59), channel_id=1, source_target_pairs={{0,64},{64,128},{128,192},{192,0},{1,65},{65,129},{129,193},{193,1... | collective-permute-start | bytes 307208 | tf_op jit(solution)/shard_map/ppermute | solution.py:248
  33.5 4.7 %collective-permute-start.6 = (bf16[1,5,5,16,128]{4,3,2,1,0:T(8,128)(2,1)S(1)}, bf16[1,5,5,16,128]{4,3,2,1,0:T(8,128)(2,1)S(1)}, u32[]{:S(2)}, u32[]{:S(2)}) collective-permute-start(bf16[1,5,5,16,128]{4,3,2,1,0:T(8,128)(2,1)S(1)} %get-tuple-element.58), channel_id=1, source_target_pairs={{0,192},{64,0},{128,64},{192,128},{1,193},{65,1},{129,65},{193,129... | collective-permute-start | bytes 307208 | tf_op jit(solution)/shard_map/ppermute | solution.py:248
  40.4 35.6 %all-to-all-start = ((bf16[128,8,256]{2,1,0:T(8,128)(2,1)}), bf16[128,8,256]{2,1,0:T(8,128)(2,1)S(1)}, u32[]{:S(2)}, u32[]{:S(2)}) async-start(bf16[128,8,256]{2,1,0:T(8,128)(2,1)} %fusion), calls=%async_computation | async-start | bytes 1048576 | tf_op jit(solution)/shard_map/all_to_all | solution.py:597
  54.7 0.8 copy-start.2
  70.3 5.6 %copy-start.5 = (f32[128,128]{1,0:T(8,128)S(1)}, f32[128,128]{1,0:T(8,128)}, u32[]{:S(2)}) copy-start(f32[128,128]{1,0:T(8,128)} %get-tuple-element.29) | copy-start | bytes 196612
  70.3 5.6 %collective-permute-start.7 = (f32[128,128]{1,0:T(8,128)}, f32[128,128]{1,0:T(8,128)S(1)}, u32[]{:S(2)}, u32[]{:S(2)}) collective-permute-start(f32[128,128]{1,0:T(8,128)} %get-tuple-element.29), channel_id=1, source_target_pairs={{0,1},{1,0},{2,3},{3,2},{4,5},{5,4},{6,7},{7,6},{8,9},{9,8},{10,11... | collective-permute-start | bytes 196616 | tf_op jit(solution)/shard_map/ppermute | solution.py:248
  73.9 13.2 %collective-permute-start.10 = (bf16[1,5,5,16,128]{4,3,2,1,0:T(8,128)(2,1)S(1)}, bf16[1,5,5,16,128]{4,3,2,1,0:T(8,128)(2,1)S(1)}, u32[]{:S(2)}, u32[]{:S(2)}) collective-permute-start(bf16[1,5,5,16,128]{4,3,2,1,0:T(8,128)(2,1)S(1)} %bitcast.47), channel_id=1, source_target_pairs={{0,192},{64,0},{128,64},{192,128},{1,193},{65,1},{129,65},{193,129... | collective-permute-start | bytes 307208 | tf_op jit(solution)/shard_map/ppermute | solution.py:248
  74.8 12.2 %collective-permute-start.9 = (bf16[1,5,5,16,128]{4,3,2,1,0:T(8,128)(2,1)S(1)}, bf16[1,5,5,16,128]{4,3,2,1,0:T(8,128)(2,1)S(1)}, u32[]{:S(2)}, u32[]{:S(2)}) collective-permute-start(bf16[1,5,5,16,128]{4,3,2,1,0:T(8,128)(2,1)S(1)} %bitcast.46), channel_id=1, source_target_pairs={{0,64},{64,128},{128,192},{192,0},{1,65},{65,129},{129,193},{193,1... | collective-permute-start | bytes 307208 | tf_op jit(solution)/shard_map/ppermute | solution.py:248
  77.6 20.8 %all-to-all-start.1 = ((bf16[32,8,384]{2,1,0:T(8,128)(2,1)}), bf16[32,8,384]{2,1,0:T(8,128)(2,1)S(1)}, u32[]{:S(2)}, u32[]{:S(2)}) async-start(bf16[32,8,384]{2,1,0:T(8,128)(2,1)} %pad_maximum_fusion.3), calls=%async_computation.1 | async-start | bytes 393216 | tf_op jit(solution)/shard_map/all_to_all | solution.py:626
  99.3 14.4 %all-to-all-start.2 = ((bf16[4,264,256]{2,1,0:T(8,128)(2,1)}), bf16[4,264,256]{2,1,0:T(8,128)(2,1)S(1)}, u32[]{:S(2)}, u32[]{:S(2)}) async-start(bf16[4,264,256]{2,1,0:T(8,128)(2,1)} %broadcast_in_dim.36), calls=%async_computation.2 | async-start | bytes 1081344 | tf_op jit(solution)/shard_map/all_to_all | solution.py:644
  105.4 8.2 %collective-permute-start.11 = (bf16[3,1,5,16,128]{4,3,2,1,0:T(8,128)(2,1)S(1)}, bf16[3,1,5,16,128]{4,3,2,1,0:T(8,128)(2,1)S(1)}, u32[]{:S(2)}, u32[]{:S(2)}) collective-permute-start(bf16[3,1,5,16,128]{4,3,2,1,0:T(8,128)(2,1)S(1)} %get-tuple-element.56), channel_id=1, source_target_pairs={{0,4},{4,8},{8,12},{12,16},{16,20},{20,24},{24,28},{28,32},{32,36}... | collective-permute-start | bytes 184328 | tf_op jit(solution)/shard_map/ppermute | solution.py:248
  105.5 8.1 %collective-permute-start.12 = (bf16[3,1,5,16,128]{4,3,2,1,0:T(8,128)(2,1)S(1)}, bf16[3,1,5,16,128]{4,3,2,1,0:T(8,128)(2,1)S(1)}, u32[]{:S(2)}, u32[]{:S(2)}) collective-permute-start(bf16[3,1,5,16,128]{4,3,2,1,0:T(8,128)(2,1)S(1)} %get-tuple-element.57), channel_id=1, source_target_pairs={{0,60},{4,0},{8,4},{12,8},{16,12},{20,16},{24,20},{28,24},{32,28},... | collective-permute-start | bytes 184328 | tf_op jit(solution)/shard_map/ppermute | solution.py:248
  113.7 14.6 %copy-start.1 = (bf16[4,264,256]{2,1,0:T(8,128)(2,1)}, bf16[4,264,256]{2,1,0:T(8,128)(2,1)S(1)}, u32[]{:S(2)}) copy-start(bf16[4,264,256]{2,1,0:T(8,128)(2,1)S(1)} %all-to-all-done.2.coeff_in) | copy-start | bytes 1622020
  113.7 22.2 %collective-permute-start.8 = (bf16[4,264,256]{2,1,0:T(8,128)(2,1)S(1)}, bf16[4,264,256]{2,1,0:T(8,128)(2,1)S(1)}, u32[]{:S(2)}, u32[]{:S(2)}) collective-permute-start(bf16[4,264,256]{2,1,0:T(8,128)(2,1)S(1)} %all-to-all-done.2.coeff_in), channel_id=1, source_target_pairs={{0,1},{1,0},{2,3},{3,2},{4,5},{5,4},{6,7},{7,6},{8,9},{9,8},{10,11... | collective-permute-start | bytes 1622024 | tf_op jit(solution)/shard_map/ppermute | solution.py:248
  113.9 19.6 %collective-permute-start.14 = (bf16[3,3,1,16,128]{4,3,2,1,0:T(8,128)(2,1)S(1)}, bf16[3,3,1,16,128]{4,3,2,1,0:T(8,128)(2,1)S(1)}, u32[]{:S(2)}, u32[]{:S(2)}) collective-permute-start(bf16[3,3,1,16,128]{4,3,2,1,0:T(8,128)(2,1)S(1)} %get-tuple-element.60), channel_id=1, source_target_pairs={{0,1},{1,2},{2,3},{3,0},{4,5},{5,6},{6,7},{7,4},{8,9},{9,10},{10,1... | collective-permute-start | bytes 110600 | tf_op jit(solution)/shard_map/ppermute | solution.py:248
  114.4 19.1 %collective-permute-start.13 = (bf16[3,3,1,16,128]{4,3,2,1,0:T(8,128)(2,1)S(1)}, bf16[3,3,1,16,128]{4,3,2,1,0:T(8,128)(2,1)S(1)}, u32[]{:S(2)}, u32[]{:S(2)}) collective-permute-start(bf16[3,3,1,16,128]{4,3,2,1,0:T(8,128)(2,1)S(1)} %get-tuple-element.61), channel_id=1, source_target_pairs={{0,3},{1,0},{2,1},{3,2},{4,7},{5,4},{6,5},{7,6},{8,11},{9,8},{10,9... | collective-permute-start | bytes 110600 | tf_op jit(solution)/shard_map/ppermute | solution.py:248
  120.2 15.7 %all-to-all-start.3 = ((f32[16,8,128]{2,1,0:T(8,128)}), f32[16,8,128]{2,1,0:T(8,128)S(1)}, u32[]{:S(2)}, u32[]{:S(2)}) async-start(f32[16,8,128]{2,1,0:T(8,128)} %broadcast_in_dim.37), calls=%async_computation.3 | async-start | bytes 131072 | tf_op jit(solution)/shard_map/all_to_all | solution.py:649
  133.5 2.5 %copy-start.6 = (bf16[3,3,1,16,128]{4,3,2,1,0:T(8,128)(2,1)}, bf16[3,3,1,16,128]{4,3,2,1,0:T(8,128)(2,1)S(1)}, u32[]{:S(2)}) copy-start(bf16[3,3,1,16,128]{4,3,2,1,0:T(8,128)(2,1)S(1)} %collective-permute-done.14.rest_4_) | copy-start | bytes 110596
  133.5 2.5 %copy-start.7 = (bf16[3,3,1,16,128]{4,3,2,1,0:T(8,128)(2,1)}, bf16[3,3,1,16,128]{4,3,2,1,0:T(8,128)(2,1)S(1)}, u32[]{:S(2)}) copy-start(bf16[3,3,1,16,128]{4,3,2,1,0:T(8,128)(2,1)S(1)} %collective-permute-done.13.rest_3_) | copy-start | bytes 110596
  136.0 0.6 copy-start.4
  136.0 0.8 copy-start.3

commit v5 on v4

--- a/solution.py
+++ b/solution.py
@@ -12,8 +12,9 @@
 
 GY = ("gy_0", "gy_1")
 GZ = ("gz_0", "gz_1")
-CHIPS = ("gx", "gy_0", "gy_1", "gz_0")
-PLANE = ("gy_0", "gy_1", "gz_0")
+
+SHEET = ("gx", "gy_1")
+TOWER = ("gy_0", "gz_0")
 PAIR = "gz_1"
 GX_GY_GZ = ("gx", "gy_0", "gy_1", "gz_0", "gz_1")
 
@@ -55,15 +56,20 @@
 
 
 def short_kernel(
-    table_ref,
+    below_ref,
+    cells_ref,
+    above_ref,
+    core_ref,
     ids_ref,
     pos_ref,
     dy_ref,
     radial_ref,
     mix_ref,
     gain_ref,
-    zgrad_ref,
-    thin_ref,
+    low_out,
+    mid_out,
+    high_out,
+    core_out,
     own_ref,
     sums_ref,
     lhs_ref,
@@ -76,8 +82,15 @@
     basis_ref,
     filt_ref,
     acc_ref,
+    table_ref,
+    zgrad_ref,
 ):
     channels, atoms = dy_ref.shape
+    side, inner, rest = below_ref.shape[0], cells_ref.shape[0], core_ref.shape[0]
+    bounds = (0, side, side + inner, 2 * side + inner, 2 * side + inner + rest)
+    for n, ref in enumerate((below_ref, cells_ref, above_ref, core_ref)):
+        table_ref[bounds[n] : bounds[n + 1], :] = ref[...]
+    table_ref[bounds[4] :, :] = jnp.zeros((GROUPS * HIGH - bounds[4], 128), jnp.bfloat16)
     listed = ids_ref.shape[0]
     count = radial_ref.shape[0]
     f32, bf16 = jnp.float32, jnp.bfloat16
@@ -190,7 +203,7 @@
         )
     own_ref[...] = own_grad
     sums_ref[...] = jnp.zeros_like(sums_ref)
-    sums_ref[channels : channels + count, 0:channels] = (
+    radial = (
         radial[0:count, 0:channels]
         + radial[count:, 0:channels]
         + radial[0:count, channels:]
@@ -206,11 +219,16 @@
         part = jnp.transpose(acc_ref[g * ROWS : (g + 1) * ROWS, :])
         part = jnp.concatenate([part, jnp.zeros((HIGH, 128 - ROWS), f32)], axis=1)
         zgrad_ref[g * HIGH : (g + 1) * HIGH, :] = part
-        thin_ref[g * HIGH : (g + 1) * HIGH, :] = part.astype(bf16)
-    sums_ref[0:channels, 0:channels] = weight
-
-
-def short_range(table, ids, pos, dy, radial, mix, gain, interpret=False):
+    for n, (ref, kind) in enumerate(
+        ((low_out, bf16), (mid_out, f32), (high_out, bf16), (core_out, f32))
+    ):
+        ref[...] = zgrad_ref[bounds[n] : bounds[n + 1], :].astype(kind)
+    tall = jnp.concatenate([weight, radial], axis=0)
+    cut = (channels + count) // 2
+    sums_ref[0:cut, :] = jnp.concatenate([tall[0:cut], tall[cut:]], axis=1)
+
+
+def short_range(pieces, ids, pos, dy, radial, mix, gain, interpret=False):
     channels, atoms = dy.shape
     listed = ids.shape[0]
     count = radial.shape[0]
@@ -219,13 +237,15 @@
     return pl.pallas_call(
         short_kernel,
         out_shape=(
-            jax.ShapeDtypeStruct((GROUPS * HIGH, 128), jnp.float32),
-            jax.ShapeDtypeStruct((GROUPS * HIGH, 128), jnp.bfloat16),
+            jax.ShapeDtypeStruct(pieces[0].shape, jnp.bfloat16),
+            jax.ShapeDtypeStruct(pieces[1].shape, jnp.float32),
+            jax.ShapeDtypeStruct(pieces[2].shape, jnp.bfloat16),
+            jax.ShapeDtypeStruct(pieces[3].shape, jnp.float32),
             jax.ShapeDtypeStruct((8, atoms), jnp.float32),
-            jax.ShapeDtypeStruct((128, 128), jnp.float32),
+            jax.ShapeDtypeStruct((64, 128), jnp.float32),
         ),
-        in_specs=[spec] * 7,
-        out_specs=(spec,) * 4,
+        in_specs=[spec] * 10,
+        out_specs=(spec,) * 6,
         scratch_shapes=[
             vmem((GROUPS * ROWS, HIGH), jnp.bfloat16),
             vmem((GROUPS, channels, HIGH), jnp.bfloat16),
@@ -237,10 +257,12 @@
             vmem((listed, count, atoms), jnp.float32),
             vmem((listed, channels, atoms), jnp.float32),
             vmem((GROUPS * ROWS, HIGH), jnp.float32),
+            vmem((GROUPS * HIGH, 128), jnp.bfloat16),
+            vmem((GROUPS * HIGH, 128), jnp.float32),
         ],
         interpret=interpret,
         name="short_range",
-    )(table, ids, pos, dy, radial, mix, gain)
+    )(*pieces, ids, pos, dy, radial, mix, gain)
 
 
 def from_behind(x, axis, by):
@@ -251,11 +273,14 @@
 def chosen(parity):
     column = lax.broadcasted_iota(jnp.int32, (2 * CHUNK, CHUNK), 1)
     row = lax.broadcasted_iota(jnp.int32, (2 * CHUNK, CHUNK), 0)
-    picked = (column // SHARE) * (2 * SHARE) + column % SHARE + parity * SHARE
+    n = column // SHARE
+    outer, inner, least = [lax.axis_size(axis) for axis in ("gy_0", "gy_1", "gz_0")]
+    group = ((n // least) % outer * inner + n // (least * outer)) * least + n % least
+    picked = group * (2 * SHARE) + column % SHARE + parity * SHARE
     return (row == picked).astype(jnp.float32).astype(jnp.bfloat16)
 
 
-def pack_kernel(h_ref, kind_ref, pos_ref, miller_ref, table_ref, mine_ref, next_ref):
+def pack_kernel(h_ref, kind_ref, pos_ref, miller_ref, cells_ref, core_ref, mine_ref, next_ref):
     f32, bf16 = jnp.float32, jnp.bfloat16
     _, atoms = h_ref.shape
     none = jnp.zeros((1, atoms), f32)
@@ -268,7 +293,9 @@
         + [none, kind_ref[...].astype(f32), jnp.zeros((127 - ROWS, atoms), f32)],
         axis=0,
     )
-    table_ref[...] = jnp.transpose(rows).astype(bf16)
+    flat = jnp.transpose(rows).astype(bf16)
+    cells_ref[...] = flat[0 : cells_ref.shape[0]]
+    core_ref[...] = flat[cells_ref.shape[0] :]
     m = miller_ref[...].astype(f32)
     tall = jnp.concatenate([m, m, m, jnp.zeros((7, m.shape[1]), f32)], axis=0).astype(bf16)
     runs = m.shape[1] // (2 * CHUNK)
@@ -286,9 +313,14 @@
     half = jax.ShapeDtypeStruct((16, miller.shape[1] // 2), jnp.bfloat16)
     return pl.pallas_call(
         pack_kernel,
-        out_shape=(jax.ShapeDtypeStruct((h.shape[1], 128), jnp.bfloat16), half, half),
+        out_shape=(
+            jax.ShapeDtypeStruct((432, 128), jnp.bfloat16),
+            jax.ShapeDtypeStruct((h.shape[1] - 432, 128), jnp.bfloat16),
+            half,
+            half,
+        ),
         in_specs=[WHOLE] * 4,
-        out_specs=(WHOLE,) * 3,
+        out_specs=(WHOLE,) * 4,
         name="pack",
     )(h, kinds, pos, miller)
 
@@ -408,11 +440,17 @@
     width = 2 * channels
     coeff_ref, cos_ref, sin_ref, both_ref, sems = rest[-5:]
     steps = miller_ref.shape[1] // CHUNK
+    run = coeff_ref.shape[1]
+    few = CHUNK // run
 
     def copies(i):
         at = pl.ds(pl.multiple_of(i * CHUNK, CHUNK), CHUNK)
         return [
-            pltpu.make_async_copy(coeff_in.at[i, pl.ds(0, CHUNK)], coeff_ref.at[at], sems.at[0, i]),
+            pltpu.make_async_copy(
+                coeff_in.at[pl.ds(i * few, few), pl.ds(0, run)],
+                coeff_ref.at[pl.ds(i * few, few)],
+                sems.at[0, i],
+            ),
             pltpu.make_async_copy(cos_in.at[at], cos_ref.at[at], sems.at[1, i]),
             pltpu.make_async_copy(sin_in.at[at], sin_ref.at[at], sems.at[2, i]),
         ]
@@ -423,14 +461,22 @@
     both_ref[...] = jnp.concatenate([h_ref[...], dy_ref[...]], axis=0)
     if last:
         sums_ref, turn_ref = rest[-7:-5]
-        first_ref, angle_ref, grid_ref, upper_ref, lower_ref = rest[0:5]
-        core_ref, own_ref, all_ref, kind_ref, gain_ref, mix_ref = rest[5:11]
-        inner = [
-            grid_ref[:, :, 1] + lower_ref[:, :, 0].astype(f32),
-            grid_ref[:, :, 2],
-            grid_ref[:, :, 3] + upper_ref[:, :, 0].astype(f32),
-        ]
-        cells = jnp.stack(inner, axis=2).reshape(432, 128)
+        first_ref, angle_ref, *planes, upper_ref, lower_ref = rest[0:7]
+        core_ref, own_ref, all_ref, kind_ref, gain_ref, mix_ref = rest[7:13]
+        cells = jnp.stack(
+            [
+                jnp.stack(
+                    [
+                        plane[:, 0, 1] + lower_ref[:, n, 0].astype(f32),
+                        plane[:, 0, 2],
+                        plane[:, 0, 3] + upper_ref[:, n, 0].astype(f32),
+                    ],
+                    axis=1,
+                )
+                for n, plane in enumerate(planes)
+            ],
+            axis=1,
+        ).reshape(432, 128)
         flat = jnp.transpose(jnp.concatenate([cells, core_ref[...]], axis=0))
         gains = gains_of(gain_ref[...], kind_ref[...], (channels, flat.shape[1]))
         zscaled = (flat[0:channels] * gains).astype(bf16)
@@ -450,7 +496,7 @@
         for copy in copies(i):
             copy.wait()
         at = pl.ds(pl.multiple_of(i * CHUNK, CHUNK), CHUNK)
-        coeffs = coeff_ref[at, :]
+        coeffs = coeff_ref[pl.ds(i * few, few)].reshape(CHUNK, 2 * width)
         cos_part, sin_part = cos_ref[at, :], sin_ref[at, :]
         sums_ref[...] += lax.dot_general(
             coeffs[:, 0:channels], cos_part, over_rows, preferred_element_type=f32
@@ -469,7 +515,7 @@
 
     lax.fori_loop(0, steps, one, 0)
     if last:
-        atom_ref, pos_ref, weight_ref, radial_ref = rest[11:15]
+        atom_ref, pos_ref, weight_ref, radial_ref = rest[13:17]
         atom_ref[...] = (dy_ref[...].astype(f32) + sums_ref[...]).astype(bf16)
         axes = ("gx", GY, GZ)
         for d in range(3):
@@ -477,18 +523,22 @@
                 turn_ref[d : d + 1, :] * (circle_angle / lax.axis_size(axes[d]))
                 + near[d : d + 1, :]
             )
-        weight_ref[...] = all_ref[0:channels, 0:channels]
-        radial_ref[...] = all_ref[channels : channels + radial_ref.shape[0], 0:channels]
+        full = jnp.sum(all_ref[...], axis=1).reshape(64, 128)
+        cut = (channels + radial_ref.shape[0]) // 2
+        tall = jnp.concatenate([full[0:cut, 0:channels], full[0:cut, channels:]], axis=0)
+        weight_ref[...] = tall[0:channels]
+        radial_ref[...] = tall[channels:]
 
 
 def ewald(coeffs, cos_all, sin_all, miller, h, dy, more=(), basis=0):
     points, atoms = cos_all.shape
     channels = h.shape[0]
     last = len(more) > 0
+    lines = coeffs.shape[0]
     sums = jax.ShapeDtypeStruct((channels, atoms), jnp.float32)
     turn = jax.ShapeDtypeStruct((16, atoms), jnp.float32)
     scratch = [
-        pltpu.VMEM((points, 4 * channels), jnp.bfloat16),
+        pltpu.VMEM((lines, points // lines, 4 * channels), jnp.bfloat16),
         pltpu.VMEM(cos_all.shape, jnp.bfloat16),
         pltpu.VMEM(cos_all.shape, jnp.bfloat16),
         pltpu.VMEM((2 * channels, atoms), jnp.bfloat16),
@@ -548,14 +598,6 @@
     first = lax.slice_in_dim(x, 0, 1, axis=dim).astype(jnp.bfloat16)
     last = lax.slice_in_dim(x, length - 1, length, axis=dim).astype(jnp.bfloat16)
     return from_behind(first, axis, -1), from_behind(last, axis, 1)
-
-
-def folded(x, pieces, dim):
-    to_last, to_first = [piece.astype(jnp.float32) for piece in pieces]
-    low = lax.slice_in_dim(x, 1, 2, axis=dim) + to_first
-    middle = lax.slice_in_dim(x, 2, 3, axis=dim)
-    high = lax.slice_in_dim(x, 3, 4, axis=dim) + to_last
-    return jnp.concatenate([low, middle, high], axis=dim)
 
 
 def whole(
@@ -581,10 +623,10 @@
     norm_k = points ** (-0.5)
     share_rows = points // devices
     share_start = lax.axis_index(GX_GY_GZ) * share_rows
-    groups = lax.axis_size(CHIPS)
-
-    own_table, miller_mine, miller_next = pack(h, kinds, pos, miller_triples)
-    cells = own_table[0:432].reshape(3, 3, 3, 16, 128)
+    half = points // 2
+
+    cells, core, miller_mine, miller_next = pack(h, kinds, pos, miller_triples)
+    cells = cells.reshape(3, 3, 3, 16, 128)
     below, above = sent_out(cells, GZ, 2)
     cos_next, sin_next, part_next = phase_sums(pos, miller_next, h, dy)
     received = from_behind(part_next, PAIR, 1)
@@ -593,21 +635,13 @@
     cos_mine, sin_mine, part_mine = phase_sums(pos, miller_mine, h, dy)
     cells = jnp.concatenate([below, cells, above], axis=1)
     below, above = sent_out(cells, "gx", 0)
+    sheet, tower = lax.axis_size(SHEET), lax.axis_size(TOWER)
+    width = 4 * channels
     paired = (part_mine + received).astype(jnp.bfloat16)
-    pieces = lax.all_to_all(paired.reshape(groups, share_rows, 4 * channels), CHIPS, 0, 0)
-
-    table = jnp.concatenate(
-        [
-            below.reshape(400, 128),
-            cells.reshape(1200, 128),
-            above.reshape(400, 128),
-            own_table[432:512],
-            jnp.zeros((GROUPS * HIGH - 2080, 128), jnp.bfloat16),
-        ],
-        axis=0,
-    )
-    ghost_grad, ghost_thin, own_grad, sums = short_range(
-        table,
+    pieces = lax.all_to_all(paired.reshape(sheet, half // sheet, width), SHEET, 0, 0)
+
+    low, mid, high, core_grad, own_grad, sums = short_range(
+        (below.reshape(400, 128), cells.reshape(1200, 128), above.reshape(400, 128), core),
         adjacent_ghost_entries[0, 0, 0],
         pos,
         dy,
@@ -615,39 +649,64 @@
         channel_mixing_matrix,
         element_channel_factor,
     )
-    sums = sums + from_behind(sums, PAIR, 1)
-    tiles = sums.astype(jnp.bfloat16).reshape(16, 1, 8, 128)
-    tiles = jnp.broadcast_to(tiles, (16, 2, 8, 128)).reshape(32, 8, 128)
-
+    sums_hi = lax.reduce_precision(sums, 8, 7)
+    tiles = jnp.concatenate([sums_hi, sums - sums_hi], axis=1).astype(jnp.bfloat16)
+    tiles = tiles.reshape(tower, 8, 256)
+
+    partial = jnp.sum(pieces.astype(jnp.float32), axis=0).astype(jnp.bfloat16)
+    pieces = lax.all_to_all(partial.reshape(tower, share_rows, width), TOWER, 0, 0)
     totals = jnp.sum(pieces.astype(jnp.float32), axis=0)
     filt_rows = lax.dynamic_slice_in_dim(reciprocal_kernel, share_start, share_rows, 0)
     own_coeffs, filter_share = coefficients(totals, filt_rows, norm_atoms, norm_k)
-    spread = jnp.broadcast_to(own_coeffs[None], (32, share_rows, 4 * channels))
-    got = lax.all_to_all(jnp.concatenate([spread, tiles], axis=2), PLANE, 0, 0)
-
-    grid = ghost_grad[0:2000].reshape(5, 5, 5, 16, 128)
-    to_side = sent_back(ghost_thin[0:2000].reshape(5, 5, 5, 16, 128), "gx", 0)
-    grid = folded(grid, to_side, 0)
+    spread = jnp.broadcast_to(own_coeffs[None], (tower, share_rows, width))
+    got = lax.all_to_all(jnp.concatenate([spread, tiles], axis=2), TOWER, 0, 0)
+
+    grid = mid.reshape(3, 5, 5, 16, 128)
+    to_side = (
+        from_behind(low.reshape(1, 5, 5, 16, 128), "gx", -1),
+        from_behind(high.reshape(1, 5, 5, 16, 128), "gx", 1),
+    )
+    grid = jnp.concatenate(
+        [
+            grid[0:1] + to_side[1].astype(jnp.float32),
+            grid[1:2],
+            grid[2:3] + to_side[0].astype(jnp.float32),
+        ],
+        axis=0,
+    )
     to_side = sent_back(grid, GY, 1)
 
-    tile_part = jnp.sum(got[:, :, 4 * channels :].astype(jnp.float32), axis=0)
-    lines = lax.axis_size("gx")
+    tile_part = jnp.sum(got[:, :, width:].astype(jnp.float32), axis=0)
+    tile_part = tile_part[:, 0:128] + tile_part[:, 128:256]
+    part_hi = lax.reduce_precision(tile_part, 8, 7)
     strip = jnp.concatenate(
         [
-            got[:, :, 0 : 4 * channels].reshape(32 * share_rows, 4 * channels),
-            jnp.concatenate(
-                [tile_part.astype(jnp.bfloat16), jnp.zeros((8, 128), jnp.bfloat16)], axis=1
-            ),
+            got[:, :, 0:width].reshape(tower * share_rows, width),
+            jnp.concatenate([part_hi, tile_part - part_hi], axis=1).astype(jnp.bfloat16),
         ],
         axis=0,
     )
-    got = lax.all_to_all(jnp.broadcast_to(strip[None], (lines,) + strip.shape), "gx", 0, 0)
-    grid = folded(grid, to_side, 1)
-    to_side = sent_back(grid, GZ, 2)
-    tile_sum = jnp.sum(got[:, 32 * share_rows :, 0:128].astype(jnp.float32), axis=0)
+    got = lax.all_to_all(jnp.broadcast_to(strip[None], (sheet,) + strip.shape), SHEET, 0, 0)
+    planes = (
+        grid[:, 1:2] + to_side[1].astype(jnp.float32),
+        grid[:, 2:3],
+        grid[:, 3:4] + to_side[0].astype(jnp.float32),
+    )
+    to_side = tuple(
+        from_behind(
+            jnp.concatenate([p[:, :, at : at + 1].astype(jnp.bfloat16) for p in planes], axis=1),
+            GZ,
+            by,
+        )
+        for at, by in ((0, -1), (4, 1))
+    )
+    tile_sum = jnp.sum(got[:, tower * share_rows :].astype(jnp.float32), axis=0)
+    tile_sum = tile_sum[:, 0:128] + tile_sum[:, 128:256]
     got_next = from_behind(got, PAIR, 1)
-    every = lax.all_to_all(jnp.broadcast_to(tile_sum[None], (16, 8, 128)), GY, 0, 0)
-    every = every.reshape(128, 128)
+    every = lax.all_to_all(
+        jnp.broadcast_to(tile_sum[None], (2 * tower, 8, 128)), TOWER + (PAIR,), 0, 0
+    )
+    every = every.reshape(tower, 2, 8, 128)
     first = ewald(got, cos_mine, sin_mine, miller_mine, h, dy)
     atom_grad, position_grad, weight_grad, radial_grad = ewald(
         got_next,
@@ -658,9 +717,9 @@
         dy,
         (
             *first,
-            grid,
+            *planes,
             *to_side,
-            ghost_grad[2000:2080],
+            core_grad,
             own_grad,
             every,
             kinds,

time: 143 us -> 143 us (level)
  the two profiles are of different devices: /device:TPU:2 before, /device:TPU:1 now
where the time goes in v5:
time: 143 us; the launch traced here: 142 us
  starting transfers between devices  59.3 us (41%)
  Pallas kernels  39.3 us (27%)
  waiting for transfers between devices  30.2 us (21%)
  local copies, waits for them, and re-layouts  6.9 us (5%)
  other arithmetic  4.8 us (3%)
    ppermute x14, starting transfers between devices, from_behind(): lax.ppermute(x, axis, [(i, (i + by) % devices) for i in range(devices)])  32.8 us
    pallas_call x1, Pallas kernels, short_range(): pl.pallas_call(short_kernel, out_shape=(jax.ShapeDtypeStruct(pieces[0].sh...  14.6 us
    pallas_call x2, Pallas kernels, phase_sums(): pl.pallas_call(phase_kernel, out_shape=(wave, wave, sums), in_specs=[WHOL...  12.2 us
    pallas_call x2, Pallas kernels, ewald(): pl.pallas_call(functools.partial(ewald_kernel, last), out_shape=outs, in_...  10.6 us
    all_to_all x1, waiting for transfers between devices, whole(): lax.all_to_all(jnp.broadcast_to(strip[None], (sheet,) + strip.shape), SHE...  8.43 us
    all_to_all x1, waiting for transfers between devices, whole(): lax.all_to_all(paired.reshape(sheet, half // sheet, width), SHEET, 0, 0)  8.16 us
    all_to_all x1, waiting for transfers between devices, whole(): got = lax.all_to_all(jnp.concatenate([spread, tiles], axis=2), TOWER, 0, 0)  6.62 us
    all_to_all x1, starting transfers between devices, whole(): lax.all_to_all(partial.reshape(tower, share_rows, width), TOWER, 0, 0)  6.35 us
  transfers between devices with their start and end apart: 19, of which 7 were waited for; matrix products, arithmetic and copies ran while one was open for 6% of the time, Pallas kernels for 23%

profile of v5, /device:TPU:1, one launch (start us, length us, event | category | flops | bytes accessed | tf_op | source)
XLA Modules:
  0.0 141.7 jit_solution(7565028091947790501)
XLA Ops:
  0.6 1.9 %pack.1 = (bf16[432,128]{1,0:T(8,128)(2,1)}, bf16[80,128]{1,0:T(8,128)(2,1)}, bf16[16,1024]{1,0:T(8,128)(2,1)}, bf16[16,1024]{1,0:T(8,128)(2,1)}) custom-call(bf16[64,512]{1,0:T(8,128)(2,1)} %bitcast.35, s32[1,512]{1,0:T(1,128)} %bitcast.53, f32[3,1,512]{2,1,0:T(1,128)} %bitcast.49, s32[3,2048]{1,0:T(4,128)} %miller_ref.1), custom_call_target="tpu_custom_call" | custom-call | tf_op jit(solution)/shard_map/pack/pallas_call | solution.py:314
  2.5 0.8 fusion.11
  3.3 8.3 %collective-permute-start.1 = (bf16[3,3,1,16,128]{4,3,2,1,0:T(8,128)(2,1)S(1)}, bf16[3,3,1,16,128]{4,3,2,1,0:T(8,128)(2,1)S(1)}, u32[]{:S(2)}, u32[]{:S(2)}) collective-permute-start(bf16[3,3,1,16,128]{4,3,2,1,0:T(8,128)(2,1)S(1)} %get-tuple-element.77), channel_id=1, source_target_pairs={{0,1},{1,2},{2,3},{3,0},{4,5},{5,6},{6,7},{7,4},{8,9},{9,10},{10,1... | collective-permute-start | bytes 110600 | tf_op jit(solution)/shard_map/ppermute | solution.py:270
  11.6 6.1 %phase_sums.3 = (bf16[1024,512]{1,0:T(8,128)(2,1)}, bf16[1024,512]{1,0:T(8,128)(2,1)}, f32[1024,256]{1,0:T(8,128)}) custom-call(f32[3,1,512]{2,1,0:T(1,128)} %bitcast.50, bf16[16,1024]{1,0:T(8,128)(2,1)} %get-tuple-element.29.miller_ref, bf16[64,512]{1,0:T(8,128)(2,1)} %bitcast.36, bf16[64,512]{1,0:T(8,128)(2,1)} %bitcast.40), custom_call_target="tpu_custom_call" | custom-call | flops 402653184 | bytes 2097152 | tf_op jit(solution)/shard_map/phase_sums/pallas_call | solution.py:417
  17.7 0.6 collective-permute-start
  18.4 0.5 collective-permute-done.2
  18.9 1.6 %collective-permute-start.3 = (bf16[3,1,5,16,128]{4,3,2,1,0:T(8,128)(2,1)S(1)}, bf16[3,1,5,16,128]{4,3,2,1,0:T(8,128)(2,1)S(1)}, u32[]{:S(2)}, u32[]{:S(2)}) collective-permute-start(bf16[3,1,5,16,128]{4,3,2,1,0:T(8,128)(2,1)S(1)} %get-tuple-element.75), channel_id=1, source_target_pairs={{0,4},{4,8},{8,12},{12,16},{16,20},{20,24},{24,28},{28,32},{32,36}... | collective-permute-start | bytes 184328 | tf_op jit(solution)/shard_map/ppermute | solution.py:270
  20.5 3.8 %collective-permute-start.4 = (bf16[3,1,5,16,128]{4,3,2,1,0:T(8,128)(2,1)S(1)}, bf16[3,1,5,16,128]{4,3,2,1,0:T(8,128)(2,1)S(1)}, u32[]{:S(2)}, u32[]{:S(2)}) collective-permute-start(bf16[3,1,5,16,128]{4,3,2,1,0:T(8,128)(2,1)S(1)} %get-tuple-element.76), channel_id=1, source_target_pairs={{0,60},{4,0},{8,4},{12,8},{16,12},{20,16},{24,20},{28,24},{32,28},... | collective-permute-start | bytes 184328 | tf_op jit(solution)/shard_map/ppermute | solution.py:270
  24.4 2.5 %collective-permute-done.3 = bf16[3,1,5,16,128]{4,3,2,1,0:T(8,128)(2,1)S(1)} collective-permute-done((bf16[3,1,5,16,128]{4,3,2,1,0:T(8,128)(2,1)S(1)}, bf16[3,1,5,16,128]{4,3,2,1,0:T(8,128)(2,1)S(1)}, u32[]{:S(2)}, u32[]{:S(2)}) %collective-permute-start.3) | collective-permute-done | bytes 61472 | tf_op jit(solution)/shard_map/ppermute | solution.py:270
  27.0 0.9 collective-permute-start.5
  27.9 1.8 %collective-permute-start.6 = (bf16[1,5,5,16,128]{4,3,2,1,0:T(8,128)(2,1)S(1)}, bf16[1,5,5,16,128]{4,3,2,1,0:T(8,128)(2,1)S(1)}, u32[]{:S(2)}, u32[]{:S(2)}) collective-permute-start(bf16[1,5,5,16,128]{4,3,2,1,0:T(8,128)(2,1)S(1)} %get-tuple-element.73), channel_id=1, source_target_pairs={{0,192},{64,0},{128,64},{192,128},{1,193},{65,1},{129,65},{193,129... | collective-permute-start | bytes 307208 | tf_op jit(solution)/shard_map/ppermute | solution.py:270
  29.7 0.1 constant_dynamic-slice_fusion
  29.8 0.1 copy.19
  29.9 6.1 %phase_sums.2 = (bf16[1024,512]{1,0:T(8,128)(2,1)}, bf16[1024,512]{1,0:T(8,128)(2,1)}, f32[1024,256]{1,0:T(8,128)}) custom-call(f32[3,1,512]{2,1,0:T(1,128)} %bitcast.51, bf16[16,1024]{1,0:T(8,128)(2,1)} %get-tuple-element.27.miller_ref, bf16[64,512]{1,0:T(8,128)(2,1)} %bitcast.37, bf16[64,512]{1,0:T(8,128)(2,1)} %bitcast.41), custom_call_target="tpu_custom_call" | custom-call | flops 402653184 | bytes 2097152 | tf_op jit(solution)/shard_map/phase_sums/pallas_call | solution.py:417
  36.1 0.6 copy-done.9
  36.7 14.6 %short_range.1 = (bf16[400,128]{1,0:T(8,128)(2,1)}, f32[1200,128]{1,0:T(8,128)}, bf16[400,128]{1,0:T(8,128)(2,1)}, f32[80,128]{1,0:T(8,128)}, f32[8,512]{1,0:T(8,128)}, /*index=5*/f32[64,128]{1,0:T(8,128)}) custom-call(bf16[400,128]{1,0:T(8,128)(2,1)} %bitcast.46, bf16[1200,128]{1,0:T(8,128)(2,1)} %bitcast.27, bf16[400,128]{1,0:T(8,128)(2,1)} %bitcast.47, ...), custom_call_target="tpu_custom_call" | custom-call | tf_op jit(solution)/shard_map/short_range/pallas_call | solution.py:237
  51.3 1.0 collective-permute-start.9
  52.3 0.6 collective-permute-start.8
  52.8 0.8 fusion.2
  53.6 2.0 %fusion.7 = (f32[400,128]{1,0:T(8,128)}, f32[400,128]{1,0:T(8,128)}, f32[400,128]{1,0:T(8,128)S(1)}) fusion(f32[1200,128]{1,0:T(8,128)} %get-tuple-element.40), kind=kLoop, calls=%fused_computation.42 | loop fusion | bytes 1228800 | tf_op jit(solution)/shard_map/slice | solution.py:671
  55.6 0.9 add_convert_fusion
  56.5 4.8 %all-to-all-start = ((bf16[16,64,256]{2,1,0:T(8,128)(2,1)}), bf16[16,64,256]{2,1,0:T(8,128)(2,1)S(1)}, u32[]{:S(2)}, u32[]{:S(2)}) async-start(bf16[16,64,256]{2,1,0:T(8,128)(2,1)} %bitcast.4), calls=%async_computation | async-start | bytes 1048576 | tf_op jit(solution)/shard_map/all_to_all | solution.py:641
  61.4 0.9 copy-done.4
  62.4 8.2 %all-to-all-done = bf16[16,64,256]{2,1,0:T(8,128)(2,1)S(1)} async-done(((bf16[16,64,256]{2,1,0:T(8,128)(2,1)}), bf16[16,64,256]{2,1,0:T(8,128)(2,1)S(1)}, u32[]{:S(2)}, u32[]{:S(2)}) %all-to-all-start) | async-done | bytes 524320 | tf_op jit(solution)/shard_map/all_to_all | solution.py:641
  70.5 0.7 reduce_sum.39
  71.2 6.3 %all-to-all-start.1 = ((bf16[8,8,256]{2,1,0:T(8,128)(2,1)}), bf16[8,8,256]{2,1,0:T(8,128)(2,1)S(1)}, u32[]{:S(2)}, u32[]{:S(2)}) async-start(bf16[8,8,256]{2,1,0:T(8,128)(2,1)} %bitcast.5), calls=%async_computation.1 | async-start | bytes 65536 | tf_op jit(solution)/shard_map/all_to_all | solution.py:657
  77.6 0.4 collective-permute-start.10
  78.0 5.1 %collective-permute-start.11 = (bf16[3,1,5,16,128]{4,3,2,1,0:T(8,128)(2,1)S(1)}, bf16[3,1,5,16,128]{4,3,2,1,0:T(8,128)(2,1)S(1)}, u32[]{:S(2)}, u32[]{:S(2)}) collective-permute-start(bf16[3,1,5,16,128]{4,3,2,1,0:T(8,128)(2,1)S(1)} %get-tuple-element.71), channel_id=1, source_target_pairs={{0,60},{4,0},{8,4},{12,8},{16,12},{20,16},{24,20},{28,24},{32,28},... | collective-permute-start | bytes 184328 | tf_op jit(solution)/shard_map/ppermute | solution.py:270
  83.1 1.1 all-to-all-done.1
  84.2 0.7 multiply_convert_fusion.3
  84.8 0.1 pad_maximum_fusion.8
  84.9 0.6 pad_maximum_fusion.2
  85.6 5.5 %all-to-all-start.2 = ((bf16[8,8,512]{2,1,0:T(8,128)(2,1)}), bf16[8,8,512]{2,1,0:T(8,128)(2,1)S(1)}, u32[]{:S(2)}, u32[]{:S(2)}) async-start(bf16[8,8,512]{2,1,0:T(8,128)(2,1)} %pad_maximum_fusion.2), calls=%async_computation.2 | async-start | bytes 131072 | tf_op jit(solution)/shard_map/all_to_all | solution.py:662
  91.1 6.6 %all-to-all-done.2 = bf16[8,8,512]{2,1,0:T(8,128)(2,1)S(1)} async-done(((bf16[8,8,512]{2,1,0:T(8,128)(2,1)}), bf16[8,8,512]{2,1,0:T(8,128)(2,1)S(1)}, u32[]{:S(2)}, u32[]{:S(2)}) %all-to-all-start.2) | async-done | bytes 65568 | tf_op jit(solution)/shard_map/all_to_all | solution.py:662
  97.8 0.9 broadcast_in_dim.9
  98.7 3.6 %all-to-all-start.3 = ((bf16[16,72,256]{2,1,0:T(8,128)(2,1)}), bf16[16,72,256]{2,1,0:T(8,128)(2,1)S(1)}, u32[]{:S(2)}, u32[]{:S(2)}) async-start(bf16[16,72,256]{2,1,0:T(8,128)(2,1)} %broadcast_in_dim.9), calls=%async_computation.3 | async-start | bytes 1179648 | tf_op jit(solution)/shard_map/all_to_all | solution.py:689
  102.3 0.8 fusion.6
  103.1 8.4 %all-to-all-done.3.coeff_in = bf16[16,72,256]{2,1,0:T(8,128)(2,1)S(1)} async-done(((bf16[16,72,256]{2,1,0:T(8,128)(2,1)}), bf16[16,72,256]{2,1,0:T(8,128)(2,1)S(1)}, u32[]{:S(2)}, u32[]{:S(2)}) %all-to-all-start.3) | async-done | bytes 589856 | tf_op jit(solution)/shard_map/all_to_all | solution.py:689
  111.5 7.7 %collective-permute-start.7 = (bf16[16,72,256]{2,1,0:T(8,128)(2,1)S(1)}, bf16[16,72,256]{2,1,0:T(8,128)(2,1)S(1)}, u32[]{:S(2)}, u32[]{:S(2)}) collective-permute-start(bf16[16,72,256]{2,1,0:T(8,128)(2,1)S(1)} %all-to-all-done.3.coeff_in), channel_id=1, source_target_pairs={{0,1},{1,0},{2,3},{3,2},{4,5},{5,4},{6,7},{7,6},{8,9},{9,8},{10,11... | collective-permute-start | bytes 1769480 | tf_op jit(solution)/shard_map/ppermute | solution.py:270
  119.2 0.8 collective-permute-start.13
  120.0 0.6 broadcast_in_dim.10
  120.7 6.3 %all-to-all-start.4 = ((f32[16,8,128]{2,1,0:T(8,128)}), f32[16,8,128]{2,1,0:T(8,128)S(1)}, u32[]{:S(2)}, u32[]{:S(2)}) async-start(f32[16,8,128]{2,1,0:T(8,128)} %broadcast_in_dim.10), calls=%async_computation.4 | async-start | bytes 131072 | tf_op jit(solution)/shard_map/all_to_all | solution.py:706
  126.9 0.2 collective-permute-start.12
  127.1 5.1 %ewald.2 = (f32[64,512]{1,0:T(8,128)}, f32[16,512]{1,0:T(8,128)}) custom-call(bf16[16,72,256]{2,1,0:T(8,128)(2,1)} %copy-done.1, bf16[1024,512]{1,0:T(8,128)(2,1)} %get-tuple-element.36.cos_in, bf16[1024,512]{1,0:T(8,128)(2,1)} %get-tuple-element.37.sin_in, bf16[16,1024]{1,0:T(8,128)(2,1)} %get-tuple-element.27.miller_ref, bf16[64,512]{1,0:T(8,128)(2,1)} %bitcast.38, ...), custom_call_target="tpu_custom_call" | custom-call | flops 268435456 | bytes 2097152 | tf_op jit(solution)/shard_map/ewald/pallas_call | solution.py:556
  132.3 2.9 %collective-permute-done.12.rest_5_ = bf16[3,3,1,16,128]{4,3,2,1,0:T(8,128)(2,1)S(1)} collective-permute-done((bf16[3,3,1,16,128]{4,3,2,1,0:T(8,128)(2,1)S(1)}, bf16[3,3,1,16,128]{4,3,2,1,0:T(8,128)(2,1)S(1)}, u32[]{:S(2)}, u32[]{:S(2)}) %collective-permute-start.12) | collective-permute-done | bytes 36896 | tf_op jit(solution)/shard_map/ppermute | solution.py:270
  135.2 0.6 copy-done.12
  135.8 0.2 copy-done.7
  136.0 5.5 %ewald.3 = (bf16[64,512]{1,0:T(8,128)(2,1)}, f32[3,1,512]{2,1,0:T(1,128)}, f32[64,64]{1,0:T(8,128)}, f32[16,64]{1,0:T(8,128)}) custom-call(bf16[16,72,256]{2,1,0:T(8,128)(2,1)} %copy-done.7, bf16[1024,512]{1,0:T(8,128)(2,1)} %get-tuple-element.34.cos_in, bf16[1024,512]{1,0:T(8,128)(2,1)} %get-tuple-element.35.sin_in, ...), custom_call_target="tpu_custom_call" | custom-call | flops 268435456 | bytes 2097152 | tf_op jit(solution)/shard_map/ewald/pallas_call | solution.py:556
  (55 shorter events, 0.5 us)
Async XLA Ops:
  0.6 29.1 %copy-start = (f32[2048,64]{0,1:T(8,128)S(1)}, f32[2048,64]{0,1:T(8,128)}, u32[]{:S(2)}) copy-start(f32[2048,64]{0,1:T(8,128)} %param.16) | copy-start | bytes 1572868
  3.3 15.1 %collective-permute-start.1 = (bf16[3,3,1,16,128]{4,3,2,1,0:T(8,128)(2,1)S(1)}, bf16[3,3,1,16,128]{4,3,2,1,0:T(8,128)(2,1)S(1)}, u32[]{:S(2)}, u32[]{:S(2)}) collective-permute-start(bf16[3,3,1,16,128]{4,3,2,1,0:T(8,128)(2,1)S(1)} %get-tuple-element.77), channel_id=1, source_target_pairs={{0,1},{1,2},{2,3},{3,0},{4,5},{5,6},{6,7},{7,4},{8,9},{9,10},{10,1... | collective-permute-start | bytes 110600 | tf_op jit(solution)/shard_map/ppermute | solution.py:270
  11.6 7.3 %collective-permute-start.2 = (bf16[3,3,1,16,128]{4,3,2,1,0:T(8,128)(2,1)S(1)}, bf16[3,3,1,16,128]{4,3,2,1,0:T(8,128)(2,1)S(1)}, u32[]{:S(2)}, u32[]{:S(2)}) collective-permute-start(bf16[3,3,1,16,128]{4,3,2,1,0:T(8,128)(2,1)S(1)} %get-tuple-element.78), channel_id=1, source_target_pairs={{0,3},{1,0},{2,1},{3,2},{4,7},{5,4},{6,5},{7,6},{8,11},{9,8},{10,9... | collective-permute-start | bytes 110600 | tf_op jit(solution)/shard_map/ppermute | solution.py:270
  11.6 7.3 %copy-start.6 = (bf16[432,128]{1,0:T(8,128)(2,1)S(1)}, bf16[432,128]{1,0:T(8,128)(2,1)}, u32[]{:S(2)}) copy-start(bf16[432,128]{1,0:T(8,128)(2,1)} %get-tuple-element.31) | copy-start | bytes 331780
  17.7 37.8 %collective-permute-start = (f32[1024,256]{1,0:T(8,128)}, f32[1024,256]{1,0:T(8,128)S(1)}, u32[]{:S(2)}, u32[]{:S(2)}) collective-permute-start(f32[1024,256]{1,0:T(8,128)} %get-tuple-element.30), channel_id=1, source_target_pairs={{0,1},{1,0},{2,3},{3,2},{4,5},{5,4},{6,7},{7,6},{8,9},{9,8},{10,11... | collective-permute-start | bytes 3145736 | tf_op jit(solution)/shard_map/ppermute | solution.py:270
  18.9 8.0 %collective-permute-start.3 = (bf16[3,1,5,16,128]{4,3,2,1,0:T(8,128)(2,1)S(1)}, bf16[3,1,5,16,128]{4,3,2,1,0:T(8,128)(2,1)S(1)}, u32[]{:S(2)}, u32[]{:S(2)}) collective-permute-start(bf16[3,1,5,16,128]{4,3,2,1,0:T(8,128)(2,1)S(1)} %get-tuple-element.75), channel_id=1, source_target_pairs={{0,4},{4,8},{8,12},{12,16},{16,20},{20,24},{24,28},{28,32},{32,36}... | collective-permute-start | bytes 184328 | tf_op jit(solution)/shard_map/ppermute | solution.py:270
  20.5 6.4 %collective-permute-start.4 = (bf16[3,1,5,16,128]{4,3,2,1,0:T(8,128)(2,1)S(1)}, bf16[3,1,5,16,128]{4,3,2,1,0:T(8,128)(2,1)S(1)}, u32[]{:S(2)}, u32[]{:S(2)}) collective-permute-start(bf16[3,1,5,16,128]{4,3,2,1,0:T(8,128)(2,1)S(1)} %get-tuple-element.76), channel_id=1, source_target_pairs={{0,60},{4,0},{8,4},{12,8},{16,12},{20,16},{24,20},{28,24},{32,28},... | collective-permute-start | bytes 184328 | tf_op jit(solution)/shard_map/ppermute | solution.py:270
  27.0 9.0 %copy-start.2 = (bf16[3,5,5,16,128]{4,3,2,1,0:T(8,128)(2,1)}, bf16[3,5,5,16,128]{4,3,2,1,0:T(8,128)(2,1)S(1)}, u32[]{:S(2)}) copy-start(bf16[3,5,5,16,128]{4,3,2,1,0:T(8,128)(2,1)S(1)} %pad_maximum_fusion.1) | copy-start | bytes 921604
  27.0 9.0 %collective-permute-start.5 = (bf16[1,5,5,16,128]{4,3,2,1,0:T(8,128)(2,1)S(1)}, bf16[1,5,5,16,128]{4,3,2,1,0:T(8,128)(2,1)S(1)}, u32[]{:S(2)}, u32[]{:S(2)}) collective-permute-start(bf16[1,5,5,16,128]{4,3,2,1,0:T(8,128)(2,1)S(1)} %get-tuple-element.74), channel_id=1, source_target_pairs={{0,64},{64,128},{128,192},{192,0},{1,65},{65,129},{129,193},{193,1... | collective-permute-start | bytes 307208 | tf_op jit(solution)/shard_map/ppermute | solution.py:270
  27.9 8.1 %collective-permute-start.6 = (bf16[1,5,5,16,128]{4,3,2,1,0:T(8,128)(2,1)S(1)}, bf16[1,5,5,16,128]{4,3,2,1,0:T(8,128)(2,1)S(1)}, u32[]{:S(2)}, u32[]{:S(2)}) collective-permute-start(bf16[1,5,5,16,128]{4,3,2,1,0:T(8,128)(2,1)S(1)} %get-tuple-element.73), channel_id=1, source_target_pairs={{0,192},{64,0},{128,64},{192,128},{1,193},{65,1},{129,65},{193,129... | collective-permute-start | bytes 307208 | tf_op jit(solution)/shard_map/ppermute | solution.py:270
  36.0 19.6 %copy-start.3 = (f32[1024,256]{1,0:T(8,128)S(1)}, f32[1024,256]{1,0:T(8,128)}, u32[]{:S(2)}) copy-start(f32[1024,256]{1,0:T(8,128)} %get-tuple-element.28) | copy-start | bytes 3145732
  36.0 0.7 copy-start.9
  36.0 0.7 copy-start.10
  51.3 10.0 %collective-permute-start.9 = (bf16[1,5,5,16,128]{4,3,2,1,0:T(8,128)(2,1)}, bf16[1,5,5,16,128]{4,3,2,1,0:T(8,128)(2,1)S(1)}, u32[]{:S(2)}, u32[]{:S(2)}) collective-permute-start(bf16[1,5,5,16,128]{4,3,2,1,0:T(8,128)(2,1)} %bitcast.56), channel_id=1, source_target_pairs={{0,192},{64,0},{128,64},{192,128},{1,193},{65,1},{129,65},{193,129... | collective-permute-start | bytes 307208 | tf_op jit(solution)/shard_map/ppermute | solution.py:270
  52.3 9.1 %collective-permute-start.8 = (bf16[1,5,5,16,128]{4,3,2,1,0:T(8,128)(2,1)}, bf16[1,5,5,16,128]{4,3,2,1,0:T(8,128)(2,1)S(1)}, u32[]{:S(2)}, u32[]{:S(2)}) collective-permute-start(bf16[1,5,5,16,128]{4,3,2,1,0:T(8,128)(2,1)} %bitcast.55), channel_id=1, source_target_pairs={{0,64},{64,128},{128,192},{192,0},{1,65},{65,129},{129,193},{193,1... | collective-permute-start | bytes 307208 | tf_op jit(solution)/shard_map/ppermute | solution.py:270
  56.5 4.9 %copy-start.5 = (f32[400,128]{1,0:T(8,128)S(1)}, f32[400,128]{1,0:T(8,128)}, u32[]{:S(2)}) copy-start(f32[400,128]{1,0:T(8,128)} %get-tuple-element.67) | copy-start | bytes 614404
  56.5 14.0 %all-to-all-start = ((bf16[16,64,256]{2,1,0:T(8,128)(2,1)}), bf16[16,64,256]{2,1,0:T(8,128)(2,1)S(1)}, u32[]{:S(2)}, u32[]{:S(2)}) async-start(bf16[16,64,256]{2,1,0:T(8,128)(2,1)} %bitcast.4), calls=%async_computation | async-start | bytes 1048576 | tf_op jit(solution)/shard_map/all_to_all | solution.py:641
  61.4 0.9 copy-start.4
  71.2 12.9 %all-to-all-start.1 = ((bf16[8,8,256]{2,1,0:T(8,128)(2,1)}), bf16[8,8,256]{2,1,0:T(8,128)(2,1)S(1)}, u32[]{:S(2)}, u32[]{:S(2)}) async-start(bf16[8,8,256]{2,1,0:T(8,128)(2,1)} %bitcast.5), calls=%async_computation.1 | async-start | bytes 65536 | tf_op jit(solution)/shard_map/all_to_all | solution.py:657
  77.6 24.7 %collective-permute-start.10 = (bf16[3,1,5,16,128]{4,3,2,1,0:T(8,128)(2,1)S(1)}, bf16[3,1,5,16,128]{4,3,2,1,0:T(8,128)(2,1)S(1)}, u32[]{:S(2)}, u32[]{:S(2)}) collective-permute-start(bf16[3,1,5,16,128]{4,3,2,1,0:T(8,128)(2,1)S(1)} %get-tuple-element.72), channel_id=1, source_target_pairs={{0,4},{4,8},{8,12},{12,16},{16,20},{20,24},{24,28},{28,32},{32,36}... | collective-permute-start | bytes 184328 | tf_op jit(solution)/shard_map/ppermute | solution.py:270
  78.0 24.4 %collective-permute-start.11 = (bf16[3,1,5,16,128]{4,3,2,1,0:T(8,128)(2,1)S(1)}, bf16[3,1,5,16,128]{4,3,2,1,0:T(8,128)(2,1)S(1)}, u32[]{:S(2)}, u32[]{:S(2)}) collective-permute-start(bf16[3,1,5,16,128]{4,3,2,1,0:T(8,128)(2,1)S(1)} %get-tuple-element.71), channel_id=1, source_target_pairs={{0,60},{4,0},{8,4},{12,8},{16,12},{20,16},{24,20},{28,24},{32,28},... | collective-permute-start | bytes 184328 | tf_op jit(solution)/shard_map/ppermute | solution.py:270
  85.6 12.2 %all-to-all-start.2 = ((bf16[8,8,512]{2,1,0:T(8,128)(2,1)}), bf16[8,8,512]{2,1,0:T(8,128)(2,1)S(1)}, u32[]{:S(2)}, u32[]{:S(2)}) async-start(bf16[8,8,512]{2,1,0:T(8,128)(2,1)} %pad_maximum_fusion.2), calls=%async_computation.2 | async-start | bytes 131072 | tf_op jit(solution)/shard_map/all_to_all | solution.py:662
  98.7 12.8 %all-to-all-start.3 = ((bf16[16,72,256]{2,1,0:T(8,128)(2,1)}), bf16[16,72,256]{2,1,0:T(8,128)(2,1)S(1)}, u32[]{:S(2)}, u32[]{:S(2)}) async-start(bf16[16,72,256]{2,1,0:T(8,128)(2,1)} %broadcast_in_dim.9), calls=%async_computation.3 | async-start | bytes 1179648 | tf_op jit(solution)/shard_map/all_to_all | solution.py:689
  111.5 15.6 %copy-start.1 = (bf16[16,72,256]{2,1,0:T(8,128)(2,1)}, bf16[16,72,256]{2,1,0:T(8,128)(2,1)S(1)}, u32[]{:S(2)}) copy-start(bf16[16,72,256]{2,1,0:T(8,128)(2,1)S(1)} %all-to-all-done.3.coeff_in) | copy-start | bytes 1769476
  111.5 23.6 %collective-permute-start.7 = (bf16[16,72,256]{2,1,0:T(8,128)(2,1)S(1)}, bf16[16,72,256]{2,1,0:T(8,128)(2,1)S(1)}, u32[]{:S(2)}, u32[]{:S(2)}) collective-permute-start(bf16[16,72,256]{2,1,0:T(8,128)(2,1)S(1)} %all-to-all-done.3.coeff_in), channel_id=1, source_target_pairs={{0,1},{1,0},{2,3},{3,2},{4,5},{5,4},{6,7},{7,6},{8,9},{9,8},{10,11... | collective-permute-start | bytes 1769480 | tf_op jit(solution)/shard_map/ppermute | solution.py:270
  119.2 13.0 %collective-permute-start.13 = (bf16[3,3,1,16,128]{4,3,2,1,0:T(8,128)(2,1)S(1)}, bf16[3,3,1,16,128]{4,3,2,1,0:T(8,128)(2,1)S(1)}, u32[]{:S(2)}, u32[]{:S(2)}) collective-permute-start(bf16[3,3,1,16,128]{4,3,2,1,0:T(8,128)(2,1)S(1)} %pad_maximum_fusion.7), channel_id=1, source_target_pairs={{0,1},{1,2},{2,3},{3,0},{4,5},{5,6},{6,7},{7,4},{8,9},{9,10},{10,1... | collective-permute-start | bytes 110600 | tf_op jit(solution)/shard_map/ppermute | solution.py:270
  120.7 14.5 %all-to-all-start.4 = ((f32[16,8,128]{2,1,0:T(8,128)}), f32[16,8,128]{2,1,0:T(8,128)S(1)}, u32[]{:S(2)}, u32[]{:S(2)}) async-start(f32[16,8,128]{2,1,0:T(8,128)} %broadcast_in_dim.10), calls=%async_computation.4 | async-start | bytes 131072 | tf_op jit(solution)/shard_map/all_to_all | solution.py:706
  126.9 8.2 %collective-permute-start.12 = (bf16[3,3,1,16,128]{4,3,2,1,0:T(8,128)(2,1)S(1)}, bf16[3,3,1,16,128]{4,3,2,1,0:T(8,128)(2,1)S(1)}, u32[]{:S(2)}, u32[]{:S(2)}) collective-permute-start(bf16[3,3,1,16,128]{4,3,2,1,0:T(8,128)(2,1)S(1)} %pad_maximum_fusion.6), channel_id=1, source_target_pairs={{0,3},{1,0},{2,1},{3,2},{4,7},{5,4},{6,5},{7,6},{8,11},{9,8},{10,9... | collective-permute-start | bytes 110600 | tf_op jit(solution)/shard_map/ppermute | solution.py:270
  132.3 2.9 %copy-start.11 = (bf16[3,3,1,16,128]{4,3,2,1,0:T(8,128)(2,1)}, bf16[3,3,1,16,128]{4,3,2,1,0:T(8,128)(2,1)S(1)}, u32[]{:S(2)}) copy-start(bf16[3,3,1,16,128]{4,3,2,1,0:T(8,128)(2,1)S(1)} %collective-permute-done.13.rest_6_) | copy-start | bytes 110596
  135.1 0.6 copy-start.12
  135.2 0.6 copy-start.8
  135.2 0.8 copy-start.7

commit v6 on v5

--- a/solution.py
+++ b/solution.py
@@ -24,6 +24,7 @@
 SIN_TERMS = (6.28316404, -41.33714227, 81.34076528, -70.99339569)
 COS_TERMS = (0.99999995, -19.73917143, 64.93459054, -85.24032775, 56.2423573)
 WHOLE = pl.BlockSpec(memory_space=pltpu.VMEM)
+LIMIT = pltpu.CompilerParams(vmem_limit_bytes=20 * 1024 * 1024)
 
 reach_sq = 0.75
 GROUPS = 9
@@ -242,7 +243,7 @@
             jax.ShapeDtypeStruct(pieces[2].shape, jnp.bfloat16),
             jax.ShapeDtypeStruct(pieces[3].shape, jnp.float32),
             jax.ShapeDtypeStruct((8, atoms), jnp.float32),
-            jax.ShapeDtypeStruct((64, 128), jnp.float32),
+            jax.ShapeDtypeStruct((128, 128), jnp.float32),
         ),
         in_specs=[spec] * 10,
         out_specs=(spec,) * 6,
@@ -261,6 +262,7 @@
             vmem((GROUPS * HIGH, 128), jnp.float32),
         ],
         interpret=interpret,
+        compiler_params=LIMIT,
         name="short_range",
     )(*pieces, ids, pos, dy, radial, mix, gain)
 
@@ -274,8 +276,9 @@
     column = lax.broadcasted_iota(jnp.int32, (2 * CHUNK, CHUNK), 1)
     row = lax.broadcasted_iota(jnp.int32, (2 * CHUNK, CHUNK), 0)
     n = column // SHARE
-    outer, inner, least = [lax.axis_size(axis) for axis in ("gy_0", "gy_1", "gz_0")]
-    group = ((n // least) % outer * inner + n // (least * outer)) * least + n % least
+    inner, least = [lax.axis_size(axis) for axis in ("gy_1", "gz_0")]
+    level = n // inner
+    group = (level // least * inner + n % inner) * least + level % least
     picked = group * (2 * SHARE) + column % SHARE + parity * SHARE
     return (row == picked).astype(jnp.float32).astype(jnp.bfloat16)
 
@@ -305,8 +308,16 @@
     core = lax.axis_index(PAIR)
     for parity, out_ref in ((core, mine_ref), (1 - core, next_ref)):
         got = jnp.dot(stack, chosen(parity), preferred_element_type=f32).astype(bf16)
-        for j in range(runs):
-            out_ref[:, j * CHUNK : (j + 1) * CHUNK] = got[j * 16 : (j + 1) * 16]
+        tower = lax.axis_size(TOWER)
+        wide = CHUNK // tower
+        out_ref[...] = jnp.concatenate(
+            [
+                got[j * 16 : (j + 1) * 16, w * wide : (w + 1) * wide]
+                for w in range(tower)
+                for j in range(runs)
+            ],
+            axis=1,
+        )
 
 
 def pack(h, kinds, pos, miller):
@@ -321,6 +332,7 @@
         ),
         in_specs=[WHOLE] * 4,
         out_specs=(WHOLE,) * 4,
+        compiler_params=LIMIT,
         name="pack",
     )(h, kinds, pos, miller)
 
@@ -394,10 +406,10 @@
         here = pl.ds(base, CHUNK)
         part_ref[here, 0:width] = jnp.dot(
             cos_ref[here, :], flip_ref[...], preferred_element_type=f32
-        )
+        ).astype(part_ref.dtype)
         part_ref[here, width:] = jnp.dot(
             sin_ref[here, :], flip_ref[...], preferred_element_type=f32
-        )
+        ).astype(part_ref.dtype)
         for copy in copies(i):
             copy.start()
         return carry
@@ -413,7 +425,7 @@
     channels, atoms = h.shape
     width = 2 * channels
     wave = jax.ShapeDtypeStruct((points, atoms), jnp.bfloat16)
-    sums = jax.ShapeDtypeStruct((points, 2 * width), jnp.float32)
+    sums = jax.ShapeDtypeStruct((points, 2 * width), jnp.bfloat16)
     return pl.pallas_call(
         phase_kernel,
         out_shape=(wave, wave, sums),
@@ -430,6 +442,7 @@
         cost_estimate=pl.CostEstimate(
             flops=6 * points * atoms * width, transcendentals=0, bytes_accessed=4 * points * atoms
         ),
+        compiler_params=LIMIT,
         name="phase_sums",
     )(pos, miller, h, dy)
 
@@ -523,7 +536,7 @@
                 turn_ref[d : d + 1, :] * (circle_angle / lax.axis_size(axes[d]))
                 + near[d : d + 1, :]
             )
-        full = jnp.sum(all_ref[...], axis=1).reshape(64, 128)
+        full = jnp.sum(all_ref[...], axis=1).reshape(128, 128)
         cut = (channels + radial_ref.shape[0]) // 2
         tall = jnp.concatenate([full[0:cut, 0:channels], full[0:cut, channels:]], axis=0)
         weight_ref[...] = tall[0:channels]
@@ -564,6 +577,7 @@
             transcendentals=0,
             bytes_accessed=4 * points * atoms,
         ),
+        compiler_params=LIMIT,
         name="ewald",
     )(coeffs, cos_all, sin_all, miller, h, dy, *more)
 
@@ -637,8 +651,9 @@
     below, above = sent_out(cells, "gx", 0)
     sheet, tower = lax.axis_size(SHEET), lax.axis_size(TOWER)
     width = 4 * channels
-    paired = (part_mine + received).astype(jnp.bfloat16)
-    pieces = lax.all_to_all(paired.reshape(sheet, half // sheet, width), SHEET, 0, 0)
+    paired = part_mine.astype(jnp.float32) + received.astype(jnp.float32)
+    paired = paired.astype(jnp.bfloat16)
+    pieces = lax.all_to_all(paired.reshape(tower, half // tower, width), TOWER, 0, 0)
 
     low, mid, high, core_grad, own_grad, sums = short_range(
         (below.reshape(400, 128), cells.reshape(1200, 128), above.reshape(400, 128), core),
@@ -651,15 +666,15 @@
     )
     sums_hi = lax.reduce_precision(sums, 8, 7)
     tiles = jnp.concatenate([sums_hi, sums - sums_hi], axis=1).astype(jnp.bfloat16)
-    tiles = tiles.reshape(tower, 8, 256)
+    tiles = tiles.reshape(sheet, 8, 256)
 
     partial = jnp.sum(pieces.astype(jnp.float32), axis=0).astype(jnp.bfloat16)
-    pieces = lax.all_to_all(partial.reshape(tower, share_rows, width), TOWER, 0, 0)
+    pieces = lax.all_to_all(partial.reshape(sheet, share_rows, width), SHEET, 0, 0)
     totals = jnp.sum(pieces.astype(jnp.float32), axis=0)
     filt_rows = lax.dynamic_slice_in_dim(reciprocal_kernel, share_start, share_rows, 0)
     own_coeffs, filter_share = coefficients(totals, filt_rows, norm_atoms, norm_k)
-    spread = jnp.broadcast_to(own_coeffs[None], (tower, share_rows, width))
-    got = lax.all_to_all(jnp.concatenate([spread, tiles], axis=2), TOWER, 0, 0)
+    spread = jnp.broadcast_to(own_coeffs[None], (sheet, share_rows, width))
+    got = lax.all_to_all(jnp.concatenate([spread, tiles], axis=2), SHEET, 0, 0)
 
     grid = mid.reshape(3, 5, 5, 16, 128)
     to_side = (
@@ -681,12 +696,12 @@
     part_hi = lax.reduce_precision(tile_part, 8, 7)
     strip = jnp.concatenate(
         [
-            got[:, :, 0:width].reshape(tower * share_rows, width),
+            got[:, :, 0:width].reshape(sheet * share_rows, width),
             jnp.concatenate([part_hi, tile_part - part_hi], axis=1).astype(jnp.bfloat16),
         ],
         axis=0,
     )
-    got = lax.all_to_all(jnp.broadcast_to(strip[None], (sheet,) + strip.shape), SHEET, 0, 0)
+    got = lax.all_to_all(jnp.broadcast_to(strip[None], (tower,) + strip.shape), TOWER, 0, 0)
     planes = (
         grid[:, 1:2] + to_side[1].astype(jnp.float32),
         grid[:, 2:3],
@@ -700,13 +715,13 @@
         )
         for at, by in ((0, -1), (4, 1))
     )
-    tile_sum = jnp.sum(got[:, tower * share_rows :].astype(jnp.float32), axis=0)
+    tile_sum = jnp.sum(got[:, sheet * share_rows :].astype(jnp.float32), axis=0)
     tile_sum = tile_sum[:, 0:128] + tile_sum[:, 128:256]
     got_next = from_behind(got, PAIR, 1)
     every = lax.all_to_all(
-        jnp.broadcast_to(tile_sum[None], (2 * tower, 8, 128)), TOWER + (PAIR,), 0, 0
-    )
-    every = every.reshape(tower, 2, 8, 128)
+        jnp.broadcast_to(tile_sum[None], (2 * sheet, 8, 128)), SHEET + (PAIR,), 0, 0
+    )
+    every = every.reshape(sheet, 2, 8, 128)
     first = ewald(got, cos_mine, sin_mine, miller_mine, h, dy)
     atom_grad, position_grad, weight_grad, radial_grad = ewald(
         got_next,

time: 143 us -> 142 us (level)
  local copies, waits for them, and re-layouts: 6.9 us -> 24.9 us
  waiting for transfers between devices: 30.2 us -> 13.2 us
  Pallas kernels: 39.3 us -> 29.1 us
  other arithmetic: 4.8 us -> 11.8 us
    unnamed x27 -> x71, local copies, waits for them, and re-layouts: 2.48 us -> 18.4 us
    all_to_all x5, waiting for transfers between devices: 24.3 us -> 8.98 us  [the longest x1 4.83 us: whole(): lax.all_to_all(partial.reshape(sheet, share_rows, width), SHEET, 0, 0)]
    ppermute x14, starting transfers between devices: 32.8 us -> 38.4 us  [from_behind(): lax.ppermute(x, axis, [(i, (i + by) % devices) for i in range(devices)])]
    all_to_all x5, starting transfers between devices: 26.6 us -> 22.3 us  [the longest x1 6.5 us: whole(): lax.all_to_all(jnp.broadcast_to(strip[None], (tower,) + strip.shape), TOW...]
    pallas_call x2, Pallas kernels: 12.2 us -> 8.47 us  [phase_sums(): pl.pallas_call(phase_kernel, out_shape=(wave, wave, sums), in_specs=[WHOL...]
    pallas_call x2, Pallas kernels: 10.6 us -> 7.14 us  [ewald(): pl.pallas_call(functools.partial(ewald_kernel, last), out_shape=outs, in_...]
    slice x2, local copies, waits for them, and re-layouts: 0.01 us -> 1.92 us  [whole(): p[:, :, at:at + 1].astype(jnp.bfloat16)]
    ppermute x14, waiting for transfers between devices: 5.92 us -> 4.23 us  [from_behind(): lax.ppermute(x, axis, [(i, (i + by) % devices) for i in range(devices)])]
  transfers between devices with their start and end apart: 19 -> 19, of which waited for: 7 -> 6; matrix products, arithmetic and copies ran while one was open for 6% -> 12% of each run, Pallas kernels for 23% -> 14%
where the time goes in v6:
time: 142 us; the launch traced here: 141 us
  starting transfers between devices  60.7 us (43%)
  Pallas kernels  29.1 us (20%)
  local copies, waits for them, and re-layouts  24.9 us (18%)
  waiting for transfers between devices  13.2 us (9%)
  other arithmetic  11.8 us (8%)
    ppermute x14, starting transfers between devices, from_behind(): lax.ppermute(x, axis, [(i, (i + by) % devices) for i in range(devices)])  38.4 us
    unnamed x71, local copies, waits for them, and re-layouts  18.4 us
    pallas_call x1, Pallas kernels, short_range(): pl.pallas_call(short_kernel, out_shape=(jax.ShapeDtypeStruct(pieces[0].sh...  13.1 us
    pallas_call x2, Pallas kernels, phase_sums(): pl.pallas_call(phase_kernel, out_shape=(wave, wave, sums), in_specs=[WHOL...  8.47 us
    pallas_call x2, Pallas kernels, ewald(): pl.pallas_call(functools.partial(ewald_kernel, last), out_shape=outs, in_...  7.14 us
    all_to_all x1, starting transfers between devices, whole(): lax.all_to_all(jnp.broadcast_to(strip[None], (tower,) + strip.shape), TOW...  6.5 us
    all_to_all x1, waiting for transfers between devices, whole(): lax.all_to_all(partial.reshape(sheet, share_rows, width), SHEET, 0, 0)  4.83 us
    ppermute x14, waiting for transfers between devices, from_behind(): lax.ppermute(x, axis, [(i, (i + by) % devices) for i in range(devices)])  4.23 us
  transfers between devices with their start and end apart: 19, of which 6 were waited for; matrix products, arithmetic and copies ran while one was open for 12% of the time, Pallas kernels for 14%

profile of v6, /device:TPU:1, one launch (start us, length us, event | category | flops | bytes accessed | tf_op | source)
XLA Modules:
  0.0 141.0 jit_solution(13304830872848420140)
XLA Ops:
  1.4 0.8 copy-done.5
  4.5 4.6 %phase_sums.3 = (bf16[1024,512]{1,0:T(8,128)(2,1)S(1)}, bf16[1024,512]{1,0:T(8,128)(2,1)S(1)}, bf16[1024,256]{1,0:T(8,128)(2,1)}) custom-call(f32[3,1,512]{2,1,0:T(1,128)S(1)} %bitcast.46, bf16[16,1024]{1,0:T(8,128)(2,1)S(1)} %get-tuple-element.29.miller_ref, bf16[64,512]{1,0:T(8,128)(2,1)S(1)} %bitcast.32, bf16[64,512]{1,0:T(8,128)(2,1)S(1)} %bitcast.36), custom_call_target="tpu_custom_call" | custom-call | flops 402653184 | bytes 2097152 | tf_op jit(solution)/shard_map/phase_sums/pallas_call | solution.py:429
  9.2 3.3 %collective-permute-start = (bf16[1024,256]{1,0:T(8,128)(2,1)}, bf16[1024,256]{1,0:T(8,128)(2,1)S(1)}, u32[]{:S(2)}, u32[]{:S(2)}) collective-permute-start(bf16[1024,256]{1,0:T(8,128)(2,1)} %get-tuple-element.30), channel_id=1, source_target_pairs={{0,1},{1,0},{2,3},{3,2},{4,5},{5,4},{6,7},{7,6},{8,9},{9,8},{10,11... | collective-permute-start | bytes 1572872 | tf_op jit(solution)/shard_map/ppermute | solution.py:272
  13.1 5.1 %collective-permute-start.1 = (bf16[3,3,1,16,128]{4,3,2,1,0:T(8,128)(2,1)}, bf16[3,3,1,16,128]{4,3,2,1,0:T(8,128)(2,1)S(1)}, u32[]{:S(2)}, u32[]{:S(2)}) collective-permute-start(bf16[3,3,1,16,128]{4,3,2,1,0:T(8,128)(2,1)} %get-tuple-element.77), channel_id=1, source_target_pairs={{0,1},{1,2},{2,3},{3,0},{4,5},{5,6},{6,7},{7,4},{8,9},{9,10},{10,1... | collective-permute-start | bytes 110600 | tf_op jit(solution)/shard_map/ppermute | solution.py:272
  18.9 3.8 %phase_sums.2 = (bf16[1024,512]{1,0:T(8,128)(2,1)S(1)}, bf16[1024,512]{1,0:T(8,128)(2,1)S(1)}, bf16[1024,256]{1,0:T(8,128)(2,1)S(1)}) custom-call(f32[3,1,512]{2,1,0:T(1,128)S(1)} %bitcast.47, bf16[16,1024]{1,0:T(8,128)(2,1)S(1)} %get-tuple-element.27.miller_ref, bf16[64,512]{1,0:T(8,128)(2,1)S(1)} %bitcast.33, bf16[64,512]{1,0:T(8,128)(2,1)S(1)} %bitcast.37), custom_call_target="tpu_custom_call" | custom-call | flops 402653184 | bytes 2097152 | tf_op jit(solution)/shard_map/phase_sums/pallas_call | solution.py:429
  22.8 1.0 copy-done.1
  23.8 1.0 copy-done.3
  24.8 0.9 collective-permute-done.2
  26.4 1.4 collective-permute-start.3
  27.7 4.0 %collective-permute-start.4 = (bf16[3,1,5,16,128]{4,3,2,1,0:T(8,128)(2,1)}, bf16[3,1,5,16,128]{4,3,2,1,0:T(8,128)(2,1)}, u32[]{:S(2)}, u32[]{:S(2)}) collective-permute-start(bf16[3,1,5,16,128]{4,3,2,1,0:T(8,128)(2,1)} %get-tuple-element.76), channel_id=1, source_target_pairs={{0,60},{4,0},{8,4},{12,8},{16,12},{20,16},{24,20},{28,24},{32,28},... | collective-permute-start | bytes 184328 | tf_op jit(solution)/shard_map/ppermute | solution.py:272
  31.7 0.9 add_convert_fusion
  32.7 4.1 %all-to-all-start = ((bf16[8,128,256]{2,1,0:T(8,128)(2,1)}), bf16[8,128,256]{2,1,0:T(8,128)(2,1)}, u32[]{:S(2)}, u32[]{:S(2)}) async-start(bf16[8,128,256]{2,1,0:T(8,128)(2,1)} %bitcast.4), calls=%async_computation | async-start | bytes 1048576 | tf_op jit(solution)/shard_map/all_to_all | solution.py:656
  36.8 0.9 pad_maximum_fusion.1
  38.4 1.3 collective-permute-start.5
  39.7 1.4 collective-permute-start.6
  41.3 2.1 %collective-permute-done.5 = bf16[1,5,5,16,128]{4,3,2,1,0:T(8,128)(2,1)S(1)} collective-permute-done((bf16[1,5,5,16,128]{4,3,2,1,0:T(8,128)(2,1)}, bf16[1,5,5,16,128]{4,3,2,1,0:T(8,128)(2,1)S(1)}, u32[]{:S(2)}, u32[]{:S(2)}) %collective-permute-start.5) | collective-permute-done | bytes 102432 | tf_op jit(solution)/shard_map/ppermute | solution.py:272
  43.4 13.1 %short_range.1 = (bf16[400,128]{1,0:T(8,128)(2,1)}, f32[1200,128]{1,0:T(8,128)S(1)}, bf16[400,128]{1,0:T(8,128)(2,1)S(1)}, f32[80,128]{1,0:T(8,128)S(1)}, f32[8,512]{1,0:T(8,128)S(1)}, /*index=5*/f32[128,128]{1,0:T(8,128)S(1)}) custom-call(bf16[400,128]{1,0:T(8,128)(2,1)S(1)} %bitcast.42, bf16[1200,128]{1,0:T(8,128)(2,1)S(1)} %bitcast.27, ...), custom_call_target="tpu_custom_call" | custom-call | tf_op jit(solution)/shard_map/short_range/pallas_call | solution.py:238
  56.5 2.5 %collective-permute-start.9 = (bf16[1,5,5,16,128]{4,3,2,1,0:T(8,128)(2,1)}, bf16[1,5,5,16,128]{4,3,2,1,0:T(8,128)(2,1)S(1)}, u32[]{:S(2)}, u32[]{:S(2)}) collective-permute-start(bf16[1,5,5,16,128]{4,3,2,1,0:T(8,128)(2,1)} %bitcast.18), channel_id=1, source_target_pairs={{0,192},{64,0},{128,64},{192,128},{1,193},{65,1},{129,65},{193,129... | collective-permute-start | bytes 307208 | tf_op jit(solution)/shard_map/ppermute | solution.py:272
  59.0 0.8 fusion.7
  59.8 1.8 %reduce_sum.39 = bf16[128,256]{1,0:T(8,128)(2,1)} reduce(bf16[8,128,256]{2,1,0:T(8,128)(2,1)} %all-to-all-done, bf16[]{:T(256)} %constant.38.clone.1), dimensions={0}, to_apply=%region_0.0 | reduce | flops 229376 | bytes 589826 | tf_op jit(solution)/shard_map/reduce_sum | solution.py:671
  61.6 4.1 %all-to-all-start.1 = ((bf16[16,8,256]{2,1,0:T(8,128)(2,1)}), bf16[16,8,256]{2,1,0:T(8,128)(2,1)S(1)}, u32[]{:S(2)}, u32[]{:S(2)}) async-start(bf16[16,8,256]{2,1,0:T(8,128)(2,1)} %bitcast.5), calls=%async_computation.1 | async-start | bytes 131072 | tf_op jit(solution)/shard_map/all_to_all | solution.py:672
  66.3 1.0 convert_add_fusion
  67.4 4.8 %all-to-all-done.1 = bf16[16,8,256]{2,1,0:T(8,128)(2,1)S(1)} async-done(((bf16[16,8,256]{2,1,0:T(8,128)(2,1)}), bf16[16,8,256]{2,1,0:T(8,128)(2,1)S(1)}, u32[]{:S(2)}, u32[]{:S(2)}) %all-to-all-start.1) | async-done | bytes 65568 | tf_op jit(solution)/shard_map/all_to_all | solution.py:672
  73.7 3.5 %all-to-all-start.2 = ((bf16[16,8,512]{2,1,0:T(8,128)(2,1)}), bf16[16,8,512]{2,1,0:T(8,128)(2,1)S(1)}, u32[]{:S(2)}, u32[]{:S(2)}) async-start(bf16[16,8,512]{2,1,0:T(8,128)(2,1)} %pad_maximum_fusion.2), calls=%async_computation.2 | async-start | bytes 262144 | tf_op jit(solution)/shard_map/all_to_all | solution.py:677
  77.2 1.0 convert_add_fusion.1
  78.9 0.8 fusion.4
  79.7 4.1 %all-to-all-done.2 = bf16[16,8,512]{2,1,0:T(8,128)(2,1)S(1)} async-done(((bf16[16,8,512]{2,1,0:T(8,128)(2,1)}), bf16[16,8,512]{2,1,0:T(8,128)(2,1)S(1)}, u32[]{:S(2)}, u32[]{:S(2)}) %all-to-all-start.2) | async-done | bytes 131104 | tf_op jit(solution)/shard_map/all_to_all | solution.py:677
  83.9 0.9 broadcast_in_dim.9
  84.7 6.5 %all-to-all-start.3 = ((bf16[8,136,256]{2,1,0:T(8,128)(2,1)}), bf16[8,136,256]{2,1,0:T(8,128)(2,1)S(1)}, u32[]{:S(2)}, u32[]{:S(2)}) async-start(bf16[8,136,256]{2,1,0:T(8,128)(2,1)} %broadcast_in_dim.9), calls=%async_computation.3 | async-start | bytes 1114112 | tf_op jit(solution)/shard_map/all_to_all | solution.py:704
  91.2 0.9 fusion.9
  92.4 5.2 %collective-permute-start.11 = (bf16[3,1,5,16,128]{4,3,2,1,0:T(8,128)(2,1)S(1)}, bf16[3,1,5,16,128]{4,3,2,1,0:T(8,128)(2,1)S(1)}, u32[]{:S(2)}, u32[]{:S(2)}) collective-permute-start(bf16[3,1,5,16,128]{4,3,2,1,0:T(8,128)(2,1)S(1)} %get-tuple-element.71), channel_id=1, source_target_pairs={{0,60},{4,0},{8,4},{12,8},{16,12},{20,16},{24,20},{28,24},{32,28},... | collective-permute-start | bytes 184328 | tf_op jit(solution)/shard_map/ppermute | solution.py:272
  97.6 1.3 fusion.8
  98.9 1.1 pad_maximum_fusion
  100.0 0.9 collective-permute-done.10
  100.9 0.8 fusion.6
  102.2 9.3 %collective-permute-start.7 = (bf16[8,136,256]{2,1,0:T(8,128)(2,1)S(1)}, bf16[8,136,256]{2,1,0:T(8,128)(2,1)}, u32[]{:S(2)}, u32[]{:S(2)}) collective-permute-start(bf16[8,136,256]{2,1,0:T(8,128)(2,1)S(1)} %all-to-all-done.3.coeff_in), channel_id=1, source_target_pairs={{0,1},{1,0},{2,3},{3,2},{4,5},{5,4},{6,7},{7,6},{8,9},{9,8},{10,11... | collective-permute-start | bytes 1671176 | tf_op jit(solution)/shard_map/ppermute | solution.py:272
  112.2 4.5 %collective-permute-start.13 = (bf16[3,3,1,16,128]{4,3,2,1,0:T(8,128)(2,1)}, bf16[3,3,1,16,128]{4,3,2,1,0:T(8,128)(2,1)S(1)}, u32[]{:S(2)}, u32[]{:S(2)}) collective-permute-start(bf16[3,3,1,16,128]{4,3,2,1,0:T(8,128)(2,1)} %pad_maximum_fusion.7), channel_id=1, source_target_pairs={{0,1},{1,2},{2,3},{3,0},{4,5},{5,6},{6,7},{7,4},{8,9},{9,10},{10,1... | collective-permute-start | bytes 110600 | tf_op jit(solution)/shard_map/ppermute | solution.py:272
  117.4 4.1 %all-to-all-start.4 = ((f32[32,8,128]{2,1,0:T(8,128)}), f32[32,8,128]{2,1,0:T(8,128)S(1)}, u32[]{:S(2)}, u32[]{:S(2)}) async-start(f32[32,8,128]{2,1,0:T(8,128)} %broadcast_in_dim.10), calls=%async_computation.4 | async-start | bytes 262144 | tf_op jit(solution)/shard_map/all_to_all | solution.py:721
  122.4 1.2 copy-done.2
  123.7 1.2 copy-done.4
  124.9 3.0 %ewald.2 = (f32[64,512]{1,0:T(8,128)S(1)}, f32[16,512]{1,0:T(8,128)S(1)}) custom-call(bf16[8,136,256]{2,1,0:T(8,128)(2,1)S(1)} %all-to-all-done.3.coeff_in, bf16[1024,512]{1,0:T(8,128)(2,1)S(1)} %copy-done.2, bf16[1024,512]{1,0:T(8,128)(2,1)S(1)} %copy-done.4, bf16[16,1024]{1,0:T(8,128)(2,1)S(1)} %copy-done.19, bf16[64,512]{1,0:T(8,128)(2,1)S(1)} %bitcast.34, ...), custom_call_target="tpu_custom_call" | custom-call | flops 268435456 | bytes 2097152 | tf_op jit(solution)/shard_map/ewald/pallas_call | solution.py:569
  130.8 0.9 copy-done.8
  131.7 0.9 copy-done.9
  132.6 0.9 copy-done.10
  133.5 0.9 copy-done.12
  134.4 0.8 copy-done.15
  135.2 0.8 copy-done.17
  136.7 4.1 %ewald.3 = (bf16[64,512]{1,0:T(8,128)(2,1)}, f32[3,1,512]{2,1,0:T(1,128)}, f32[64,64]{1,0:T(8,128)}, f32[16,64]{1,0:T(8,128)}) custom-call(bf16[8,136,256]{2,1,0:T(8,128)(2,1)} %collective-permute-done.7.coeff_in, bf16[1024,512]{1,0:T(8,128)(2,1)S(1)} %get-tuple-element.34.cos_in, bf16[1024,512]{1,0:T(8,128)(2,1)S(1)} %get-tuple-element.35.sin_in, ...), custom_call_target="tpu_custom_call" | custom-call | flops 268435456 | bytes 2097152 | tf_op jit(solution)/shard_map/ewald/pallas_call | solution.py:569
  (99 shorter events, 15.4 us)
Async XLA Ops:
  0.6 40.5 %copy-start = (f32[2048,64]{0,1:T(8,128)S(1)}, f32[2048,64]{0,1:T(8,128)}, u32[]{:S(2)}) copy-start(f32[2048,64]{0,1:T(8,128)} %param.16) | copy-start | bytes 1572868
  0.6 0.7 copy-start.26
  1.4 0.8 copy-start.5
  2.2 0.8 copy-start.22
  3.0 0.7 copy-start.24
  3.7 0.8 copy-start.7
  4.1 5.1 %copy-start.16 = (bf16[16,1024]{1,0:T(8,128)(2,1)}, bf16[16,1024]{1,0:T(8,128)(2,1)S(1)}, u32[]{:S(2)}) copy-start(bf16[16,1024]{1,0:T(8,128)(2,1)S(1)} %get-tuple-element.29.miller_ref) | copy-start | bytes 98308
  4.1 14.1 %copy-start.18 = (bf16[16,1024]{1,0:T(8,128)(2,1)}, bf16[16,1024]{1,0:T(8,128)(2,1)S(1)}, u32[]{:S(2)}) copy-start(bf16[16,1024]{1,0:T(8,128)(2,1)S(1)} %get-tuple-element.27.miller_ref) | copy-start | bytes 98308
  9.2 22.6 %collective-permute-start = (bf16[1024,256]{1,0:T(8,128)(2,1)}, bf16[1024,256]{1,0:T(8,128)(2,1)S(1)}, u32[]{:S(2)}, u32[]{:S(2)}) collective-permute-start(bf16[1024,256]{1,0:T(8,128)(2,1)} %get-tuple-element.30), channel_id=1, source_target_pairs={{0,1},{1,0},{2,3},{3,2},{4,5},{5,4},{6,7},{7,6},{8,9},{9,8},{10,11... | collective-permute-start | bytes 1572872 | tf_op jit(solution)/shard_map/ppermute | solution.py:272
  12.5 5.8 %copy-start.6 = (bf16[1,1,1,64,512]{4,3,2,1,0:T(8,128)(2,1)S(1)}, bf16[1,1,1,64,512]{4,3,2,1,0:T(8,128)(2,1)}, u32[]{:S(2)}) copy-start(bf16[1,1,1,64,512]{4,3,2,1,0:T(8,128)(2,1)} %param.10) | copy-start | bytes 196612
  13.1 11.7 %collective-permute-start.1 = (bf16[3,3,1,16,128]{4,3,2,1,0:T(8,128)(2,1)}, bf16[3,3,1,16,128]{4,3,2,1,0:T(8,128)(2,1)S(1)}, u32[]{:S(2)}, u32[]{:S(2)}) collective-permute-start(bf16[3,3,1,16,128]{4,3,2,1,0:T(8,128)(2,1)} %get-tuple-element.77), channel_id=1, source_target_pairs={{0,1},{1,2},{2,3},{3,0},{4,5},{5,6},{6,7},{7,4},{8,9},{9,10},{10,1... | collective-permute-start | bytes 110600 | tf_op jit(solution)/shard_map/ppermute | solution.py:272
  18.2 7.5 %collective-permute-start.2 = (bf16[3,3,1,16,128]{4,3,2,1,0:T(8,128)(2,1)}, bf16[3,3,1,16,128]{4,3,2,1,0:T(8,128)(2,1)S(1)}, u32[]{:S(2)}, u32[]{:S(2)}) collective-permute-start(bf16[3,3,1,16,128]{4,3,2,1,0:T(8,128)(2,1)} %get-tuple-element.78), channel_id=1, source_target_pairs={{0,3},{1,0},{2,1},{3,2},{4,7},{5,4},{6,5},{7,6},{8,11},{9,8},{10,9... | collective-permute-start | bytes 110600 | tf_op jit(solution)/shard_map/ppermute | solution.py:272
  18.2 0.7 copy-start.25
  22.7 1.0 copy-start.1
  23.8 1.0 copy-start.3
  26.4 10.5 %collective-permute-start.3 = (bf16[3,1,5,16,128]{4,3,2,1,0:T(8,128)(2,1)}, bf16[3,1,5,16,128]{4,3,2,1,0:T(8,128)(2,1)}, u32[]{:S(2)}, u32[]{:S(2)}) collective-permute-start(bf16[3,1,5,16,128]{4,3,2,1,0:T(8,128)(2,1)} %get-tuple-element.75), channel_id=1, source_target_pairs={{0,4},{4,8},{8,12},{12,16},{16,20},{20,24},{24,28},{28,32},{32,36}... | collective-permute-start | bytes 184328 | tf_op jit(solution)/shard_map/ppermute | solution.py:272
  27.7 9.1 %collective-permute-start.4 = (bf16[3,1,5,16,128]{4,3,2,1,0:T(8,128)(2,1)}, bf16[3,1,5,16,128]{4,3,2,1,0:T(8,128)(2,1)}, u32[]{:S(2)}, u32[]{:S(2)}) collective-permute-start(bf16[3,1,5,16,128]{4,3,2,1,0:T(8,128)(2,1)} %get-tuple-element.76), channel_id=1, source_target_pairs={{0,60},{4,0},{8,4},{12,8},{16,12},{20,16},{24,20},{28,24},{32,28},... | collective-permute-start | bytes 184328 | tf_op jit(solution)/shard_map/ppermute | solution.py:272
  32.7 27.1 %all-to-all-start = ((bf16[8,128,256]{2,1,0:T(8,128)(2,1)}), bf16[8,128,256]{2,1,0:T(8,128)(2,1)}, u32[]{:S(2)}, u32[]{:S(2)}) async-start(bf16[8,128,256]{2,1,0:T(8,128)(2,1)} %bitcast.4), calls=%async_computation | async-start | bytes 1048576 | tf_op jit(solution)/shard_map/all_to_all | solution.py:656
  37.8 5.6 %copy-start.23 = (s32[1,1,1,16,512]{4,3,2,1,0:T(8,128)S(1)}, s32[1,1,1,16,512]{4,3,2,1,0:T(8,128)}, u32[]{:S(2)}) copy-start(s32[1,1,1,16,512]{4,3,2,1,0:T(8,128)} %param.14) | copy-start | bytes 98308
  38.4 4.9 %collective-permute-start.5 = (bf16[1,5,5,16,128]{4,3,2,1,0:T(8,128)(2,1)}, bf16[1,5,5,16,128]{4,3,2,1,0:T(8,128)(2,1)S(1)}, u32[]{:S(2)}, u32[]{:S(2)}) collective-permute-start(bf16[1,5,5,16,128]{4,3,2,1,0:T(8,128)(2,1)} %get-tuple-element.74), channel_id=1, source_target_pairs={{0,64},{64,128},{128,192},{192,0},{1,65},{65,129},{129,193},{193,1... | collective-permute-start | bytes 307208 | tf_op jit(solution)/shard_map/ppermute | solution.py:272
  39.7 3.7 %collective-permute-start.6 = (bf16[1,5,5,16,128]{4,3,2,1,0:T(8,128)(2,1)S(1)}, bf16[1,5,5,16,128]{4,3,2,1,0:T(8,128)(2,1)S(1)}, u32[]{:S(2)}, u32[]{:S(2)}) collective-permute-start(bf16[1,5,5,16,128]{4,3,2,1,0:T(8,128)(2,1)S(1)} %get-tuple-element.73), channel_id=1, source_target_pairs={{0,192},{64,0},{128,64},{192,128},{1,193},{65,1},{129,65},{193,129... | collective-permute-start | bytes 307208 | tf_op jit(solution)/shard_map/ppermute | solution.py:272
  41.1 2.3 %copy-start.28 = (f32[4,64]{1,0:T(4,128)S(1)}, f32[4,64]{1,0:T(4,128)}, u32[]{:S(2)}) copy-start(f32[4,64]{1,0:T(4,128)} %rest_11_.1) | copy-start | bytes 3076
  41.2 2.2 %copy-start.13 = (bf16[64,64]{1,0:T(8,128)(2,1)S(1)}, bf16[64,64]{1,0:T(8,128)(2,1)}, u32[]{:S(2)}) copy-start(bf16[64,64]{1,0:T(8,128)(2,1)} %rest_12_.1) | copy-start | bytes 24580
  41.3 2.1 %copy-start.27 = (f32[16,64]{1,0:T(8,128)S(1)}, f32[16,64]{1,0:T(8,128)}, u32[]{:S(2)}) copy-start(f32[16,64]{1,0:T(8,128)} %radial_ref.1) | copy-start | bytes 12292
  56.5 9.2 %collective-permute-start.9 = (bf16[1,5,5,16,128]{4,3,2,1,0:T(8,128)(2,1)}, bf16[1,5,5,16,128]{4,3,2,1,0:T(8,128)(2,1)S(1)}, u32[]{:S(2)}, u32[]{:S(2)}) collective-permute-start(bf16[1,5,5,16,128]{4,3,2,1,0:T(8,128)(2,1)} %bitcast.18), channel_id=1, source_target_pairs={{0,192},{64,0},{128,64},{192,128},{1,193},{65,1},{129,65},{193,129... | collective-permute-start | bytes 307208 | tf_op jit(solution)/shard_map/ppermute | solution.py:272
  59.0 18.2 %collective-permute-start.8 = (bf16[1,5,5,16,128]{4,3,2,1,0:T(8,128)(2,1)S(1)}, bf16[1,5,5,16,128]{4,3,2,1,0:T(8,128)(2,1)}, u32[]{:S(2)}, u32[]{:S(2)}) collective-permute-start(bf16[1,5,5,16,128]{4,3,2,1,0:T(8,128)(2,1)S(1)} %bitcast.51), channel_id=1, source_target_pairs={{0,64},{64,128},{128,192},{192,0},{1,65},{65,129},{129,193},{193,1... | collective-permute-start | bytes 307208 | tf_op jit(solution)/shard_map/ppermute | solution.py:272
  59.8 18.4 %copy-start.30 = (f32[400,128]{1,0:T(8,128)}, f32[400,128]{1,0:T(8,128)S(1)}, u32[]{:S(2)}) copy-start(f32[400,128]{1,0:T(8,128)S(1)} %get-tuple-element.68) | copy-start | bytes 614404
  61.6 10.6 %all-to-all-start.1 = ((bf16[16,8,256]{2,1,0:T(8,128)(2,1)}), bf16[16,8,256]{2,1,0:T(8,128)(2,1)S(1)}, u32[]{:S(2)}, u32[]{:S(2)}) async-start(bf16[16,8,256]{2,1,0:T(8,128)(2,1)} %bitcast.5), calls=%async_computation.1 | async-start | bytes 131072 | tf_op jit(solution)/shard_map/all_to_all | solution.py:672
  67.4 10.9 %copy-start.32 = (f32[1,5,5,16,128]{4,3,2,1,0:T(8,128)}, f32[1,5,5,16,128]{4,3,2,1,0:T(8,128)S(1)}, u32[]{:S(2)}) copy-start(f32[1,5,5,16,128]{4,3,2,1,0:T(8,128)S(1)} %convert_add_fusion) | copy-start | bytes 614404
  73.7 10.1 %all-to-all-start.2 = ((bf16[16,8,512]{2,1,0:T(8,128)(2,1)}), bf16[16,8,512]{2,1,0:T(8,128)(2,1)S(1)}, u32[]{:S(2)}, u32[]{:S(2)}) async-start(bf16[16,8,512]{2,1,0:T(8,128)(2,1)} %pad_maximum_fusion.2), calls=%async_computation.2 | async-start | bytes 262144 | tf_op jit(solution)/shard_map/all_to_all | solution.py:677
  84.7 17.5 %all-to-all-start.3 = ((bf16[8,136,256]{2,1,0:T(8,128)(2,1)}), bf16[8,136,256]{2,1,0:T(8,128)(2,1)S(1)}, u32[]{:S(2)}, u32[]{:S(2)}) async-start(bf16[8,136,256]{2,1,0:T(8,128)(2,1)} %broadcast_in_dim.9), calls=%async_computation.3 | async-start | bytes 1114112 | tf_op jit(solution)/shard_map/all_to_all | solution.py:704
  91.2 7.7 %copy-start.31 = (f32[400,128]{1,0:T(8,128)S(1)}, f32[400,128]{1,0:T(8,128)}, u32[]{:S(2)}) copy-start(f32[400,128]{1,0:T(8,128)} %copy-done.30) | copy-start | bytes 614404
  92.1 8.7 %collective-permute-start.10 = (bf16[3,1,5,16,128]{4,3,2,1,0:T(8,128)(2,1)S(1)}, bf16[3,1,5,16,128]{4,3,2,1,0:T(8,128)(2,1)S(1)}, u32[]{:S(2)}, u32[]{:S(2)}) collective-permute-start(bf16[3,1,5,16,128]{4,3,2,1,0:T(8,128)(2,1)S(1)} %get-tuple-element.72), channel_id=1, source_target_pairs={{0,4},{4,8},{8,12},{12,16},{16,20},{20,24},{24,28},{28,32},{32,36}... | collective-permute-start | bytes 184328 | tf_op jit(solution)/shard_map/ppermute | solution.py:272
  92.4 8.5 %collective-permute-start.11 = (bf16[3,1,5,16,128]{4,3,2,1,0:T(8,128)(2,1)S(1)}, bf16[3,1,5,16,128]{4,3,2,1,0:T(8,128)(2,1)S(1)}, u32[]{:S(2)}, u32[]{:S(2)}) collective-permute-start(bf16[3,1,5,16,128]{4,3,2,1,0:T(8,128)(2,1)S(1)} %get-tuple-element.71), channel_id=1, source_target_pairs={{0,60},{4,0},{8,4},{12,8},{16,12},{20,16},{24,20},{28,24},{32,28},... | collective-permute-start | bytes 184328 | tf_op jit(solution)/shard_map/ppermute | solution.py:272
  102.2 27.9 %collective-permute-start.7 = (bf16[8,136,256]{2,1,0:T(8,128)(2,1)S(1)}, bf16[8,136,256]{2,1,0:T(8,128)(2,1)}, u32[]{:S(2)}, u32[]{:S(2)}) collective-permute-start(bf16[8,136,256]{2,1,0:T(8,128)(2,1)S(1)} %all-to-all-done.3.coeff_in), channel_id=1, source_target_pairs={{0,1},{1,0},{2,3},{3,2},{4,5},{5,4},{6,7},{7,6},{8,9},{9,8},{10,11... | collective-permute-start | bytes 1671176 | tf_op jit(solution)/shard_map/ppermute | solution.py:272
  112.2 17.0 %collective-permute-start.13 = (bf16[3,3,1,16,128]{4,3,2,1,0:T(8,128)(2,1)}, bf16[3,3,1,16,128]{4,3,2,1,0:T(8,128)(2,1)S(1)}, u32[]{:S(2)}, u32[]{:S(2)}) collective-permute-start(bf16[3,3,1,16,128]{4,3,2,1,0:T(8,128)(2,1)} %pad_maximum_fusion.7), channel_id=1, source_target_pairs={{0,1},{1,2},{2,3},{3,0},{4,5},{5,6},{6,7},{7,4},{8,9},{9,10},{10,1... | collective-permute-start | bytes 110600 | tf_op jit(solution)/shard_map/ppermute | solution.py:272
  117.4 12.7 %all-to-all-start.4 = ((f32[32,8,128]{2,1,0:T(8,128)}), f32[32,8,128]{2,1,0:T(8,128)S(1)}, u32[]{:S(2)}, u32[]{:S(2)}) async-start(f32[32,8,128]{2,1,0:T(8,128)} %broadcast_in_dim.10), calls=%async_computation.4 | async-start | bytes 262144 | tf_op jit(solution)/shard_map/all_to_all | solution.py:721
  121.4 1.0 copy-start.19
  122.2 7.3 %collective-permute-start.12 = (bf16[3,3,1,16,128]{4,3,2,1,0:T(8,128)(2,1)S(1)}, bf16[3,3,1,16,128]{4,3,2,1,0:T(8,128)(2,1)S(1)}, u32[]{:S(2)}, u32[]{:S(2)}) collective-permute-start(bf16[3,3,1,16,128]{4,3,2,1,0:T(8,128)(2,1)S(1)} %pad_maximum_fusion.6), channel_id=1, source_target_pairs={{0,3},{1,0},{2,1},{3,2},{4,7},{5,4},{6,5},{7,6},{8,11},{9,8},{10,9... | collective-permute-start | bytes 110600 | tf_op jit(solution)/shard_map/ppermute | solution.py:272
  122.4 1.2 copy-start.2
  123.7 1.2 copy-start.4
  130.8 0.9 copy-start.8
  131.7 0.9 copy-start.9
  132.6 0.9 copy-start.10
  133.5 0.9 copy-start.12
  134.4 0.8 copy-start.15
  135.2 0.8 copy-start.17
  135.9 0.8 copy-start.21
  (6 other events, 3.9 us)

commit v7 on v5

--- a/solution.py
+++ b/solution.py
@@ -1,4 +1,3 @@
-import functools
 import math
 
 import jax
@@ -24,6 +23,8 @@
 SIN_TERMS = (6.28316404, -41.33714227, 81.34076528, -70.99339569)
 COS_TERMS = (0.99999995, -19.73917143, 64.93459054, -85.24032775, 56.2423573)
 WHOLE = pl.BlockSpec(memory_space=pltpu.VMEM)
+FAR = pl.BlockSpec(memory_space=pltpu.HBM)
+LIMIT = pltpu.CompilerParams(vmem_limit_bytes=20 * 1024 * 1024)
 
 reach_sq = 0.75
 GROUPS = 9
@@ -56,16 +57,16 @@
 
 
 def short_kernel(
-    below_ref,
-    cells_ref,
-    above_ref,
-    core_ref,
     ids_ref,
     pos_ref,
     dy_ref,
     radial_ref,
     mix_ref,
     gain_ref,
+    below_ref,
+    cells_ref,
+    above_ref,
+    core_ref,
     low_out,
     mid_out,
     high_out,
@@ -228,41 +229,76 @@
     sums_ref[0:cut, :] = jnp.concatenate([tall[0:cut], tall[cut:]], axis=1)
 
 
-def short_range(pieces, ids, pos, dy, radial, mix, gain, interpret=False):
+def short_range(pieces, ids, pos, dy, radial, mix, gain):
     channels, atoms = dy.shape
     listed = ids.shape[0]
     count = radial.shape[0]
-    vmem = lambda s, d: pltpu.VMEM(s, d)
-    spec = pl.BlockSpec(memory_space=pltpu.VMEM)
+    f32, bf16 = jnp.float32, jnp.bfloat16
+    shaped = jax.ShapeDtypeStruct
+    return fetching_call(
+        short_kernel,
+        (ids, pos, dy, radial, mix, gain),
+        pieces,
+        (
+            shaped(pieces[0].shape, bf16),
+            shaped(pieces[1].shape, f32),
+            shaped(pieces[2].shape, bf16),
+            shaped(pieces[3].shape, f32),
+            shaped((8, atoms), f32),
+            shaped((64, 128), f32),
+        ),
+        [
+            pltpu.VMEM((GROUPS * ROWS, HIGH), bf16),
+            pltpu.VMEM((GROUPS, channels, HIGH), bf16),
+            pltpu.VMEM((GROUPS, channels, HIGH), f32),
+            pltpu.VMEM((listed, atoms), jnp.int32),
+            pltpu.VMEM((listed, atoms), jnp.int32),
+            pltpu.VMEM((listed, channels, atoms), bf16),
+            pltpu.VMEM((listed, 8, atoms), f32),
+            pltpu.VMEM((listed, count, atoms), f32),
+            pltpu.VMEM((listed, channels, atoms), f32),
+            pltpu.VMEM((GROUPS * ROWS, HIGH), f32),
+            pltpu.VMEM((GROUPS * HIGH, 128), bf16),
+            pltpu.VMEM((GROUPS * HIGH, 128), f32),
+        ],
+    )
+
+
+def fetching_call(
+    kernel, fetched, resident, outs, scratch, early=None, in_specs=None, out_specs=None, flops=0
+):
+    n = len(fetched)
+
+    def body(*refs):
+        sources, rest = refs[:n], refs[n : -n - 1]
+        buffers, sems = refs[-n - 1 : -1], refs[-1]
+        copies = [
+            pltpu.make_async_copy(sources[i], buffers[i], sems.at[i]) for i in range(n)
+        ]
+        if early is not None:
+            early(*rest)
+        for copy in copies:
+            copy.start()
+        for copy in copies:
+            copy.wait()
+        kernel(*buffers, *rest)
+
+    cost = None
+    if flops:
+        cost = pl.CostEstimate(flops=flops, transcendentals=0, bytes_accessed=flops // 128)
     return pl.pallas_call(
-        short_kernel,
-        out_shape=(
-            jax.ShapeDtypeStruct(pieces[0].shape, jnp.bfloat16),
-            jax.ShapeDtypeStruct(pieces[1].shape, jnp.float32),
-            jax.ShapeDtypeStruct(pieces[2].shape, jnp.bfloat16),
-            jax.ShapeDtypeStruct(pieces[3].shape, jnp.float32),
-            jax.ShapeDtypeStruct((8, atoms), jnp.float32),
-            jax.ShapeDtypeStruct((64, 128), jnp.float32),
-        ),
-        in_specs=[spec] * 10,
-        out_specs=(spec,) * 6,
+        body,
+        out_shape=outs,
+        in_specs=[FAR] * n + list(in_specs or [WHOLE] * len(resident)),
+        out_specs=tuple(out_specs or [WHOLE] * len(outs)),
         scratch_shapes=[
-            vmem((GROUPS * ROWS, HIGH), jnp.bfloat16),
-            vmem((GROUPS, channels, HIGH), jnp.bfloat16),
-            vmem((GROUPS, channels, HIGH), jnp.float32),
-            vmem((listed, atoms), jnp.int32),
-            vmem((listed, atoms), jnp.int32),
-            vmem((listed, channels, atoms), jnp.bfloat16),
-            vmem((listed, 8, atoms), jnp.float32),
-            vmem((listed, count, atoms), jnp.float32),
-            vmem((listed, channels, atoms), jnp.float32),
-            vmem((GROUPS * ROWS, HIGH), jnp.float32),
-            vmem((GROUPS * HIGH, 128), jnp.bfloat16),
-            vmem((GROUPS * HIGH, 128), jnp.float32),
+            *scratch,
+            *[pltpu.VMEM(x.shape, x.dtype) for x in fetched],
+            pltpu.SemaphoreType.DMA((n,)),
         ],
-        interpret=interpret,
-        name="short_range",
-    )(*pieces, ids, pos, dy, radial, mix, gain)
+        compiler_params=LIMIT,
+        cost_estimate=cost,
+    )(*fetched, *resident)
 
 
 def from_behind(x, axis, by):
@@ -311,25 +347,25 @@
 
 def pack(h, kinds, pos, miller):
     half = jax.ShapeDtypeStruct((16, miller.shape[1] // 2), jnp.bfloat16)
-    return pl.pallas_call(
+    return fetching_call(
         pack_kernel,
-        out_shape=(
+        (h, kinds, pos, miller),
+        (),
+        (
             jax.ShapeDtypeStruct((432, 128), jnp.bfloat16),
             jax.ShapeDtypeStruct((h.shape[1] - 432, 128), jnp.bfloat16),
             half,
             half,
         ),
-        in_specs=[WHOLE] * 4,
-        out_specs=(WHOLE,) * 4,
-        name="pack",
-    )(h, kinds, pos, miller)
+        [],
+    )
 
 
 def phase_kernel(
     pos_ref,
-    miller_ref,
     h_ref,
     dy_ref,
+    miller_ref,
     cos_out,
     sin_out,
     part_ref,
@@ -414,12 +450,12 @@
     width = 2 * channels
     wave = jax.ShapeDtypeStruct((points, atoms), jnp.bfloat16)
     sums = jax.ShapeDtypeStruct((points, 2 * width), jnp.float32)
-    return pl.pallas_call(
+    return fetching_call(
         phase_kernel,
-        out_shape=(wave, wave, sums),
-        in_specs=[WHOLE] * 4,
-        out_specs=(pl.BlockSpec(memory_space=pl.ANY),) * 2 + (WHOLE,),
-        scratch_shapes=[
+        (pos, h, dy),
+        (miller,),
+        (wave, wave, sums),
+        [
             pltpu.VMEM(wave.shape, wave.dtype),
             pltpu.VMEM(wave.shape, wave.dtype),
             pltpu.VMEM((atoms, width), jnp.bfloat16),
@@ -427,84 +463,45 @@
             pltpu.VMEM((CHUNK, atoms), jnp.float32),
             pltpu.SemaphoreType.DMA((2, points // CHUNK)),
         ],
-        cost_estimate=pl.CostEstimate(
-            flops=6 * points * atoms * width, transcendentals=0, bytes_accessed=4 * points * atoms
-        ),
-        name="phase_sums",
-    )(pos, miller, h, dy)
-
-
-def ewald_kernel(last, coeff_in, cos_in, sin_in, miller_ref, h_ref, dy_ref, *rest):
-    f32, bf16 = jnp.float32, jnp.bfloat16
-    channels = h_ref.shape[0]
-    width = 2 * channels
-    coeff_ref, cos_ref, sin_ref, both_ref, sems = rest[-5:]
-    steps = miller_ref.shape[1] // CHUNK
-    run = coeff_ref.shape[1]
-    few = CHUNK // run
-
-    def copies(i):
-        at = pl.ds(pl.multiple_of(i * CHUNK, CHUNK), CHUNK)
-        return [
-            pltpu.make_async_copy(
-                coeff_in.at[pl.ds(i * few, few), pl.ds(0, run)],
-                coeff_ref.at[pl.ds(i * few, few)],
-                sems.at[0, i],
-            ),
-            pltpu.make_async_copy(cos_in.at[at], cos_ref.at[at], sems.at[1, i]),
-            pltpu.make_async_copy(sin_in.at[at], sin_ref.at[at], sems.at[2, i]),
-        ]
-
-    for i in range(steps):
-        for copy in copies(i):
+        out_specs=(FAR, FAR, WHOLE),
+        flops=6 * points * atoms * width,
+    )
+
+
+def wave_copies(cos_in, sin_in, cos_ref, sin_ref, sems, i):
+    at = pl.ds(pl.multiple_of(i * CHUNK, CHUNK), CHUNK)
+    return [
+        pltpu.make_async_copy(cos_in.at[at], cos_ref.at[at], sems.at[0, i]),
+        pltpu.make_async_copy(sin_in.at[at], sin_ref.at[at], sems.at[1, i]),
+    ]
+
+
+def ewald_early(cos_in, sin_in, *rest):
+    for i in range(cos_in.shape[0] // CHUNK):
+        for copy in wave_copies(cos_in, sin_in, *rest[-3:], i):
             copy.start()
-    both_ref[...] = jnp.concatenate([h_ref[...], dy_ref[...]], axis=0)
-    if last:
-        sums_ref, turn_ref = rest[-7:-5]
-        first_ref, angle_ref, *planes, upper_ref, lower_ref = rest[0:7]
-        core_ref, own_ref, all_ref, kind_ref, gain_ref, mix_ref = rest[7:13]
-        cells = jnp.stack(
-            [
-                jnp.stack(
-                    [
-                        plane[:, 0, 1] + lower_ref[:, n, 0].astype(f32),
-                        plane[:, 0, 2],
-                        plane[:, 0, 3] + upper_ref[:, n, 0].astype(f32),
-                    ],
-                    axis=1,
-                )
-                for n, plane in enumerate(planes)
-            ],
-            axis=1,
-        ).reshape(432, 128)
-        flat = jnp.transpose(jnp.concatenate([cells, core_ref[...]], axis=0))
-        gains = gains_of(gain_ref[...], kind_ref[...], (channels, flat.shape[1]))
-        zscaled = (flat[0:channels] * gains).astype(bf16)
-        halves = flat[channels : channels + 8]
-        near = halves + pltpu.roll(halves, 4, 0) + own_ref[...]
-        sums_ref[...] = first_ref[...] + jnp.dot(
-            mix_ref[...], zscaled, preferred_element_type=f32
-        )
-        turn_ref[...] = angle_ref[...]
-    else:
-        sums_ref, turn_ref = rest[0:2]
-        sums_ref[...] = jnp.zeros_like(sums_ref)
-        turn_ref[...] = jnp.zeros_like(turn_ref)
+
+
+def ewald_sums(coeff_ref, miller_ref, both, waves, sums_ref, turn_ref):
+    f32 = jnp.float32
+    width = both.shape[0]
+    channels = width // 2
+    run = CHUNK // (miller_ref.shape[1] // coeff_ref.shape[0])
     over_rows = (((0,), (0,)), ((), ()))
 
     def one(i, carry):
-        for copy in copies(i):
+        for copy in wave_copies(*waves, i):
             copy.wait()
         at = pl.ds(pl.multiple_of(i * CHUNK, CHUNK), CHUNK)
-        coeffs = coeff_ref[pl.ds(i * few, few)].reshape(CHUNK, 2 * width)
-        cos_part, sin_part = cos_ref[at, :], sin_ref[at, :]
+        coeffs = coeff_ref[pl.ds(i * run, run), 0 : CHUNK // run].reshape(CHUNK, 2 * width)
+        cos_part, sin_part = waves[2][at, :], waves[3][at, :]
         sums_ref[...] += lax.dot_general(
             coeffs[:, 0:channels], cos_part, over_rows, preferred_element_type=f32
         ) + lax.dot_general(
             coeffs[:, width : width + channels], sin_part, over_rows, preferred_element_type=f32
         )
-        along_u = jnp.dot(coeffs[:, 0:width], both_ref[...], preferred_element_type=f32)
-        along_v = jnp.dot(coeffs[:, width : 2 * width], both_ref[...], preferred_element_type=f32)
+        along_u = jnp.dot(coeffs[:, 0:width], both, preferred_element_type=f32)
+        along_v = jnp.dot(coeffs[:, width:], both, preferred_element_type=f32)
         angle = along_v * cos_part.astype(f32) - along_u * sin_part.astype(f32)
         a_hi, a_lo = split_two(angle)
         m = miller_ref[:, at]
@@ -513,59 +510,124 @@
         )
         return carry
 
-    lax.fori_loop(0, steps, one, 0)
-    if last:
-        atom_ref, pos_ref, weight_ref, radial_ref = rest[13:17]
-        atom_ref[...] = (dy_ref[...].astype(f32) + sums_ref[...]).astype(bf16)
-        axes = ("gx", GY, GZ)
-        for d in range(3):
-            pos_ref[d] = (
-                turn_ref[d : d + 1, :] * (circle_angle / lax.axis_size(axes[d]))
-                + near[d : d + 1, :]
+    lax.fori_loop(0, miller_ref.shape[1] // CHUNK, one, 0)
+
+
+def ewald_first(
+    h_ref, dy_ref, cos_in, sin_in, coeff_ref, miller_ref, sums_ref, turn_ref, cos_ref, sin_ref, sems
+):
+    sums_ref[...] = jnp.zeros_like(sums_ref)
+    turn_ref[...] = jnp.zeros_like(turn_ref)
+    both = jnp.concatenate([h_ref[...], dy_ref[...]], axis=0)
+    waves = (cos_in, sin_in, cos_ref, sin_ref, sems)
+    ewald_sums(coeff_ref, miller_ref, both, waves, sums_ref, turn_ref)
+
+
+def ewald_second(
+    h_ref,
+    dy_ref,
+    kind_ref,
+    gain_ref,
+    mix_ref,
+    cos_in,
+    sin_in,
+    coeff_ref,
+    miller_ref,
+    first_ref,
+    angle_ref,
+    low_ref,
+    middle_ref,
+    high_ref,
+    upper_ref,
+    lower_ref,
+    core_ref,
+    own_ref,
+    mine_ref,
+    atom_ref,
+    pos_ref,
+    weight_ref,
+    radial_ref,
+    sums_ref,
+    turn_ref,
+    cos_ref,
+    sin_ref,
+    sems,
+):
+    f32, bf16 = jnp.float32, jnp.bfloat16
+    channels = h_ref.shape[0]
+    cells = jnp.stack(
+        [
+            jnp.stack(
+                [
+                    plane[:, 0, 1] + lower_ref[:, n, 0].astype(f32),
+                    plane[:, 0, 2],
+                    plane[:, 0, 3] + upper_ref[:, n, 0].astype(f32),
+                ],
+                axis=1,
             )
-        full = jnp.sum(all_ref[...], axis=1).reshape(64, 128)
-        cut = (channels + radial_ref.shape[0]) // 2
-        tall = jnp.concatenate([full[0:cut, 0:channels], full[0:cut, channels:]], axis=0)
-        weight_ref[...] = tall[0:channels]
-        radial_ref[...] = tall[channels:]
-
-
-def ewald(coeffs, cos_all, sin_all, miller, h, dy, more=(), basis=0):
+            for n, plane in enumerate((low_ref, middle_ref, high_ref))
+        ],
+        axis=1,
+    ).reshape(432, 128)
+    flat = jnp.transpose(jnp.concatenate([cells, core_ref[...]], axis=0))
+    gains = gains_of(gain_ref[...], kind_ref[...], (channels, flat.shape[1]))
+    zscaled = (flat[0:channels] * gains).astype(bf16)
+    halves = flat[channels : channels + 8]
+    near = halves + pltpu.roll(halves, 4, 0) + own_ref[...]
+    sums_ref[...] = first_ref[...] + jnp.dot(mix_ref[...], zscaled, preferred_element_type=f32)
+    turn_ref[...] = angle_ref[...]
+    both = jnp.concatenate([h_ref[...], dy_ref[...]], axis=0)
+    waves = (cos_in, sin_in, cos_ref, sin_ref, sems)
+    ewald_sums(coeff_ref, miller_ref, both, waves, sums_ref, turn_ref)
+    atom_ref[...] = (dy_ref[...].astype(f32) + sums_ref[...]).astype(bf16)
+    axes = ("gx", GY, GZ)
+    for d in range(3):
+        pos_ref[d] = (
+            turn_ref[d : d + 1, :] * (circle_angle / lax.axis_size(axes[d])) + near[d : d + 1, :]
+        )
+    cut = (channels + radial_ref.shape[0]) // 2
+    run = miller_ref.shape[1] // coeff_ref.shape[0]
+    sides = []
+    for ref in (mine_ref, coeff_ref):
+        total = jnp.sum(ref[:, run : run + cut].astype(f32), axis=0)
+        sides.append(total[:, 0:128] + total[:, 128:256])
+    full = sides[0] + sides[1]
+    tall = jnp.concatenate([full[:, 0:channels], full[:, channels:]], axis=0)
+    weight_ref[...] = tall[0:channels]
+    radial_ref[...] = tall[channels:]
+
+
+def ewald(coeffs, cos_all, sin_all, miller, h, dy, more=(), params=(), basis=0):
     points, atoms = cos_all.shape
     channels = h.shape[0]
     last = len(more) > 0
-    lines = coeffs.shape[0]
-    sums = jax.ShapeDtypeStruct((channels, atoms), jnp.float32)
-    turn = jax.ShapeDtypeStruct((16, atoms), jnp.float32)
+    shaped = jax.ShapeDtypeStruct
+    sums = shaped((channels, atoms), jnp.float32)
+    turn = shaped((16, atoms), jnp.float32)
     scratch = [
-        pltpu.VMEM((lines, points // lines, 4 * channels), jnp.bfloat16),
         pltpu.VMEM(cos_all.shape, jnp.bfloat16),
         pltpu.VMEM(cos_all.shape, jnp.bfloat16),
-        pltpu.VMEM((2 * channels, atoms), jnp.bfloat16),
-        pltpu.SemaphoreType.DMA((3, points // CHUNK)),
+        pltpu.SemaphoreType.DMA((2, points // CHUNK)),
     ]
     outs = (sums, turn)
     if last:
         scratch = [pltpu.VMEM(sums.shape, sums.dtype), pltpu.VMEM(turn.shape, turn.dtype)] + scratch
         outs = (
-            jax.ShapeDtypeStruct(sums.shape, jnp.bfloat16),
-            jax.ShapeDtypeStruct((3, 1, atoms), jnp.float32),
-            jax.ShapeDtypeStruct((channels, channels), jnp.float32),
-            jax.ShapeDtypeStruct((basis, channels), jnp.float32),
-        )
-    return pl.pallas_call(
-        functools.partial(ewald_kernel, last),
-        out_shape=outs,
-        in_specs=[pl.BlockSpec(memory_space=pl.ANY)] * 3 + [WHOLE] * (3 + len(more)),
-        out_specs=(WHOLE,) * len(outs),
-        scratch_shapes=scratch,
-        cost_estimate=pl.CostEstimate(
-            flops=8 * points * atoms * channels,
-            transcendentals=0,
-            bytes_accessed=4 * points * atoms,
-        ),
-        name="ewald",
-    )(coeffs, cos_all, sin_all, miller, h, dy, *more)
+            shaped(sums.shape, jnp.bfloat16),
+            shaped((3, 1, atoms), jnp.float32),
+            shaped((channels, channels), jnp.float32),
+            shaped((basis, channels), jnp.float32),
+        )
+    return fetching_call(
+        ewald_second if last else ewald_first,
+        (h, dy, *params),
+        (cos_all, sin_all, coeffs, miller, *more),
+        outs,
+        scratch,
+        early=ewald_early,
+        in_specs=(FAR, FAR) + (WHOLE,) * (2 + len(more)),
+        flops=8 * points * atoms * channels,
+    )
 
 
 def coefficients(totals, filt_rows, norm_atoms, norm_k):
@@ -654,12 +716,18 @@
     tiles = tiles.reshape(tower, 8, 256)
 
     partial = jnp.sum(pieces.astype(jnp.float32), axis=0).astype(jnp.bfloat16)
-    pieces = lax.all_to_all(partial.reshape(tower, share_rows, width), TOWER, 0, 0)
-    totals = jnp.sum(pieces.astype(jnp.float32), axis=0)
+    partial = partial.reshape(tower, share_rows, width)
+    pieces = lax.all_to_all(jnp.concatenate([partial, tiles], axis=2), TOWER, 0, 0)
+    pieces = jnp.sum(pieces.astype(jnp.float32), axis=0)
+    totals, tile = pieces[:, 0:width], pieces[:, width:]
     filt_rows = lax.dynamic_slice_in_dim(reciprocal_kernel, share_start, share_rows, 0)
     own_coeffs, filter_share = coefficients(totals, filt_rows, norm_atoms, norm_k)
-    spread = jnp.broadcast_to(own_coeffs[None], (tower, share_rows, width))
-    got = lax.all_to_all(jnp.concatenate([spread, tiles], axis=2), TOWER, 0, 0)
+    tile = tile[:, 0:128] + tile[:, 128:256]
+    tile_hi = lax.reduce_precision(tile, 8, 7)
+    sent = jnp.concatenate(
+        [own_coeffs, tile_hi.astype(jnp.bfloat16), (tile - tile_hi).astype(jnp.bfloat16)], axis=1
+    )
+    got = lax.all_to_all(jnp.broadcast_to(sent[None], (tower,) + sent.shape), TOWER, 0, 0)
 
     grid = mid.reshape(3, 5, 5, 16, 128)
     to_side = (
@@ -676,13 +744,10 @@
     )
     to_side = sent_back(grid, GY, 1)
 
-    tile_part = jnp.sum(got[:, :, width:].astype(jnp.float32), axis=0)
-    tile_part = tile_part[:, 0:128] + tile_part[:, 128:256]
-    part_hi = lax.reduce_precision(tile_part, 8, 7)
     strip = jnp.concatenate(
         [
             got[:, :, 0:width].reshape(tower * share_rows, width),
-            jnp.concatenate([part_hi, tile_part - part_hi], axis=1).astype(jnp.bfloat16),
+            got[0:5, :, width:].reshape(5 * share_rows, width),
         ],
         axis=0,
     )
@@ -700,13 +765,7 @@
         )
         for at, by in ((0, -1), (4, 1))
     )
-    tile_sum = jnp.sum(got[:, tower * share_rows :].astype(jnp.float32), axis=0)
-    tile_sum = tile_sum[:, 0:128] + tile_sum[:, 128:256]
     got_next = from_behind(got, PAIR, 1)
-    every = lax.all_to_all(
-        jnp.broadcast_to(tile_sum[None], (2 * tower, 8, 128)), TOWER + (PAIR,), 0, 0
-    )
-    every = every.reshape(tower, 2, 8, 128)
     first = ewald(got, cos_mine, sin_mine, miller_mine, h, dy)
     atom_grad, position_grad, weight_grad, radial_grad = ewald(
         got_next,
@@ -715,17 +774,8 @@
         miller_next,
         h,
         dy,
-        (
-            *first,
-            *planes,
-            *to_side,
-            core_grad,
-            own_grad,
-            every,
-            kinds,
-            element_channel_factor,
-            channel_mixing_matrix,
-        ),
+        (*first, *planes, *to_side, core_grad, own_grad, got),
+        (kinds, element_channel_factor, channel_mixing_matrix),
         distance_kernel.shape[0],
     )
     position_grad = position_grad[:, 0, :]

time: 143 us -> 130 us (0.909)
  starting transfers between devices: 59.3 us -> 45.6 us
  Pallas kernels: 39.3 us -> 29.8 us
  local copies, waits for them, and re-layouts: 6.9 us -> 15.4 us
  other arithmetic: 4.8 us -> 8.65 us
  waiting for transfers between devices: 30.2 us -> 28.2 us
    all_to_all x3 -> x2, starting transfers between devices: 18.1 us -> 7.71 us  [the longest x1 4.36 us: whole(): lax.all_to_all(jnp.concatenate([partial, tiles], axis=2), TOWER, 0, 0)]
    ppermute x14, waiting for transfers between devices: 5.92 us -> 15.6 us  [from_behind(): lax.ppermute(x, axis, [(i, (i + by) % devices) for i in range(devices)])]
    pallas_call x6, Pallas kernels: 39.3 us -> 29.8 us  [fetching_call(): pl.pallas_call(body, out_shape=outs, in_specs=[FAR] * n + list(in_specs o...]
    unnamed x27 -> x73, local copies, waits for them, and re-layouts: 2.48 us -> 10.8 us
    all_to_all x1, waiting for transfers between devices: 8.16 us -> 0.01 us  [whole(): lax.all_to_all(paired.reshape(sheet, half // sheet, width), SHEET, 0, 0)]
    all_to_all x1, waiting for transfers between devices: 8.43 us -> 2.46 us  [whole(): lax.all_to_all(jnp.broadcast_to(strip[None], (sheet,) + strip.shape), SHE...]
    ppermute x14, starting transfers between devices: 32.8 us -> 29.6 us  [from_behind(): lax.ppermute(x, axis, [(i, (i + by) % devices) for i in range(devices)])]
    all_to_all x3 -> x2, waiting for transfers between devices: 7.72 us -> 10.2 us  [the longest x1 5.88 us: whole(): lax.all_to_all(jnp.broadcast_to(sent[None], (tower,) + sent.shape), TOWER...]
  transfers between devices with their start and end apart: 19 -> 18, of which waited for: 7 -> 8; matrix products, arithmetic and copies ran while one was open for 6% -> 8% of each run, Pallas kernels for 23% -> 16%
where the time goes in v7:
time: 130 us; the launch traced here: 129 us
  starting transfers between devices  45.6 us (35%)
  Pallas kernels  29.8 us (23%)
  waiting for transfers between devices  28.2 us (22%)
  local copies, waits for them, and re-layouts  15.4 us (12%)
  other arithmetic  8.65 us (7%)
    pallas_call x6, Pallas kernels, fetching_call(): pl.pallas_call(body, out_shape=outs, in_specs=[FAR] * n + list(in_specs o...  29.8 us
    ppermute x14, starting transfers between devices, from_behind(): lax.ppermute(x, axis, [(i, (i + by) % devices) for i in range(devices)])  29.6 us
    ppermute x14, waiting for transfers between devices, from_behind(): lax.ppermute(x, axis, [(i, (i + by) % devices) for i in range(devices)])  15.6 us
    unnamed x73, local copies, waits for them, and re-layouts  10.8 us
    all_to_all x1, waiting for transfers between devices, whole(): lax.all_to_all(jnp.broadcast_to(sent[None], (tower,) + sent.shape), TOWER...  5.88 us
    all_to_all x1, starting transfers between devices, whole(): lax.all_to_all(jnp.concatenate([partial, tiles], axis=2), TOWER, 0, 0)  4.36 us
    all_to_all x1, waiting for transfers between devices, whole(): lax.all_to_all(jnp.concatenate([partial, tiles], axis=2), TOWER, 0, 0)  4.29 us
    all_to_all x1, starting transfers between devices, whole(): lax.all_to_all(paired.reshape(sheet, half // sheet, width), SHEET, 0, 0)  4.24 us
  transfers between devices with their start and end apart: 18, of which 8 were waited for; matrix products, arithmetic and copies ran while one was open for 8% of the time, Pallas kernels for 16%

profile of v7, /device:TPU:1, one launch (start us, length us, event | category | flops | bytes accessed | tf_op | source)
XLA Modules:
  0.0 128.8 jit_solution(11816296014863367286)
XLA Ops:
  0.7 0.7 copy-done.24
  1.4 0.8 copy-done.7
  2.2 0.8 copy-done.18
  3.0 0.7 copy-done.20
  4.5 5.0 %shard_map.138 = (bf16[1024,512]{1,0:T(8,128)(2,1)S(1)}, bf16[1024,512]{1,0:T(8,128)(2,1)S(1)}, f32[1024,256]{1,0:T(8,128)}) custom-call(f32[3,1,512]{2,1,0:T(1,128)S(1)} %bitcast.46, bf16[64,512]{1,0:T(8,128)(2,1)S(1)} %bitcast.33, bf16[64,512]{1,0:T(8,128)(2,1)S(1)} %bitcast.37, bf16[16,1024]{1,0:T(8,128)(2,1)S(1)} %get-tuple-element.27.refs_3_.refs_8_), custom_call_target="tpu_custom_call" | custom-call | flops 402653184 | bytes 3145728 | tf_op jit(solution)/shard_map/pallas_call | solution.py:289
  9.5 1.0 copy-done.1
  10.6 1.0 copy-done.3
  11.6 3.2 %collective-permute-start = (f32[1024,256]{1,0:T(8,128)}, f32[1024,256]{1,0:T(8,128)}, u32[]{:S(2)}, u32[]{:S(2)}) collective-permute-start(f32[1024,256]{1,0:T(8,128)} %get-tuple-element.32), channel_id=1, source_target_pairs={{0,1},{1,0},{2,3},{3,2},{4,5},{5,4},{6,7},{7,6},{8,9},{9,8},{10,11... | collective-permute-start | bytes 3145736 | tf_op jit(solution)/shard_map/ppermute | solution.py:306
  14.8 5.2 %collective-permute-start.1 = (bf16[3,3,1,16,128]{4,3,2,1,0:T(8,128)(2,1)S(1)}, bf16[3,3,1,16,128]{4,3,2,1,0:T(8,128)(2,1)S(1)}, u32[]{:S(2)}, u32[]{:S(2)}) collective-permute-start(bf16[3,3,1,16,128]{4,3,2,1,0:T(8,128)(2,1)S(1)} %get-tuple-element.77), channel_id=1, source_target_pairs={{0,1},{1,2},{2,3},{3,0},{4,5},{5,6},{6,7},{7,4},{8,9},{9,10},{10,1... | collective-permute-start | bytes 110600 | tf_op jit(solution)/shard_map/ppermute | solution.py:306
  19.9 1.1 collective-permute-done.1
  21.0 6.2 %collective-permute-done.2 = bf16[3,3,1,16,128]{4,3,2,1,0:T(8,128)(2,1)S(1)} collective-permute-done((bf16[3,3,1,16,128]{4,3,2,1,0:T(8,128)(2,1)S(1)}, bf16[3,3,1,16,128]{4,3,2,1,0:T(8,128)(2,1)S(1)}, u32[]{:S(2)}, u32[]{:S(2)}) %collective-permute-start.2) | collective-permute-done | bytes 36896 | tf_op jit(solution)/shard_map/ppermute | solution.py:306
  27.3 1.4 %collective-permute-start.3 = (bf16[3,1,5,16,128]{4,3,2,1,0:T(8,128)(2,1)S(1)}, bf16[3,1,5,16,128]{4,3,2,1,0:T(8,128)(2,1)S(1)}, u32[]{:S(2)}, u32[]{:S(2)}) collective-permute-start(bf16[3,1,5,16,128]{4,3,2,1,0:T(8,128)(2,1)S(1)} %get-tuple-element.75), channel_id=1, source_target_pairs={{0,4},{4,8},{8,12},{12,16},{16,20},{20,24},{24,28},{28,32},{32,36}... | collective-permute-start | bytes 184328 | tf_op jit(solution)/shard_map/ppermute | solution.py:306
  28.7 4.0 %collective-permute-start.4 = (bf16[3,1,5,16,128]{4,3,2,1,0:T(8,128)(2,1)S(1)}, bf16[3,1,5,16,128]{4,3,2,1,0:T(8,128)(2,1)S(1)}, u32[]{:S(2)}, u32[]{:S(2)}) collective-permute-start(bf16[3,1,5,16,128]{4,3,2,1,0:T(8,128)(2,1)S(1)} %get-tuple-element.76), channel_id=1, source_target_pairs={{0,60},{4,0},{8,4},{12,8},{16,12},{20,16},{24,20},{28,24},{32,28},... | collective-permute-start | bytes 184328 | tf_op jit(solution)/shard_map/ppermute | solution.py:306
  32.7 0.7 copy-done.21
  33.4 4.0 %shard_map.139 = (bf16[1024,512]{1,0:T(8,128)(2,1)S(1)}, bf16[1024,512]{1,0:T(8,128)(2,1)S(1)}, f32[1024,256]{1,0:T(8,128)S(1)}) custom-call(f32[3,1,512]{2,1,0:T(1,128)S(1)} %bitcast.47, bf16[64,512]{1,0:T(8,128)(2,1)S(1)} %bitcast.34, bf16[64,512]{1,0:T(8,128)(2,1)S(1)} %bitcast.38, bf16[16,1024]{1,0:T(8,128)(2,1)S(1)} %get-tuple-element.30.refs_3_.refs_5_), custom_call_target="tpu_custom_call" | custom-call | flops 402653184 | bytes 3145728 | tf_op jit(solution)/shard_map/pallas_call | solution.py:289
  37.5 2.1 %add_convert_fusion = bf16[1024,256]{1,0:T(8,128)(2,1)} fusion(f32[1024,256]{1,0:T(8,128)S(1)} %get-tuple-element.31, f32[1024,256]{1,0:T(8,128)} %collective-permute-done), kind=kLoop, calls=%fused_computation | loop fusion | flops 524288 | bytes 2621440 | tf_op jit(solution)/shard_map/convert_element_type | solution.py:702
  39.6 4.2 %all-to-all-start = ((bf16[16,64,256]{2,1,0:T(8,128)(2,1)}), bf16[16,64,256]{2,1,0:T(8,128)(2,1)}, u32[]{:S(2)}, u32[]{:S(2)}) async-start(bf16[16,64,256]{2,1,0:T(8,128)(2,1)} %bitcast.52), calls=%async_computation | async-start | bytes 1048576 | tf_op jit(solution)/shard_map/all_to_all | solution.py:703
  44.6 2.5 %collective-permute-start.6 = (bf16[1,5,5,16,128]{4,3,2,1,0:T(8,128)(2,1)}, bf16[1,5,5,16,128]{4,3,2,1,0:T(8,128)(2,1)S(1)}, u32[]{:S(2)}, u32[]{:S(2)}) collective-permute-start(bf16[1,5,5,16,128]{4,3,2,1,0:T(8,128)(2,1)} %get-tuple-element.73), channel_id=1, source_target_pairs={{0,192},{64,0},{128,64},{192,128},{1,193},{65,1},{129,65},{193,129... | collective-permute-start | bytes 307208 | tf_op jit(solution)/shard_map/ppermute | solution.py:306
  47.2 0.7 copy.19
  47.8 2.8 %collective-permute-done.6 = bf16[1,5,5,16,128]{4,3,2,1,0:T(8,128)(2,1)S(1)} collective-permute-done((bf16[1,5,5,16,128]{4,3,2,1,0:T(8,128)(2,1)}, bf16[1,5,5,16,128]{4,3,2,1,0:T(8,128)(2,1)S(1)}, u32[]{:S(2)}, u32[]{:S(2)}) %collective-permute-start.6) | collective-permute-done | bytes 102432 | tf_op jit(solution)/shard_map/ppermute | solution.py:306
  50.6 1.8 %collective-permute-done.5 = bf16[1,5,5,16,128]{4,3,2,1,0:T(8,128)(2,1)S(1)} collective-permute-done((bf16[1,5,5,16,128]{4,3,2,1,0:T(8,128)(2,1)S(1)}, bf16[1,5,5,16,128]{4,3,2,1,0:T(8,128)(2,1)S(1)}, u32[]{:S(2)}, u32[]{:S(2)}) %collective-permute-start.5) | collective-permute-done | bytes 102432 | tf_op jit(solution)/shard_map/ppermute | solution.py:306
  52.4 13.3 %shard_map.140 = (bf16[400,128]{1,0:T(8,128)(2,1)S(1)}, f32[1200,128]{1,0:T(8,128)S(1)}, bf16[400,128]{1,0:T(8,128)(2,1)}, f32[80,128]{1,0:T(8,128)S(1)}, f32[8,512]{1,0:T(8,128)S(1)}, /*index=5*/f32[64,128]{1,0:T(8,128)S(1)}) custom-call(s32[16,512]{1,0:T(8,128)S(1)} %bitcast.44, f32[3,1,512]{2,1,0:T(1,128)S(1)} %bitcast.48, bf16[64,512]{1,0:T(8,128)(2,1)S(1)} %bitcast.39, ...), custom_call_target="tpu_custom_call" | custom-call | tf_op jit(solution)/shard_map/pallas_call | solution.py:289
  65.7 0.8 copy-done.5
  67.8 1.2 reduce_sum.21
  69.6 4.4 %all-to-all-start.1 = ((bf16[8,8,512]{2,1,0:T(8,128)(2,1)}), bf16[8,8,512]{2,1,0:T(8,128)(2,1)S(1)}, u32[]{:S(2)}, u32[]{:S(2)}) async-start(bf16[8,8,512]{2,1,0:T(8,128)(2,1)} %pad_maximum_fusion.2), calls=%async_computation.1 | async-start | bytes 131072 | tf_op jit(solution)/shard_map/all_to_all | solution.py:720
  74.0 0.9 fusion.7
  74.8 1.5 %collective-permute-start.8 = (bf16[1,5,5,16,128]{4,3,2,1,0:T(8,128)(2,1)}, bf16[1,5,5,16,128]{4,3,2,1,0:T(8,128)(2,1)}, u32[]{:S(2)}, u32[]{:S(2)}) collective-permute-start(bf16[1,5,5,16,128]{4,3,2,1,0:T(8,128)(2,1)} %bitcast.16), channel_id=1, source_target_pairs={{0,64},{64,128},{128,192},{192,0},{1,65},{65,129},{129,193},{193,1... | collective-permute-start | bytes 307208 | tf_op jit(solution)/shard_map/ppermute | solution.py:306
  76.3 4.3 %all-to-all-done.1 = bf16[8,8,512]{2,1,0:T(8,128)(2,1)S(1)} async-done(((bf16[8,8,512]{2,1,0:T(8,128)(2,1)}), bf16[8,8,512]{2,1,0:T(8,128)(2,1)S(1)}, u32[]{:S(2)}, u32[]{:S(2)}) %all-to-all-start.1) | async-done | bytes 65568 | tf_op jit(solution)/shard_map/all_to_all | solution.py:720
  80.6 0.7 multiply_convert_fusion
  82.0 3.4 %all-to-all-start.2 = ((bf16[8,8,512]{2,1,0:T(8,128)(2,1)}), bf16[8,8,512]{2,1,0:T(8,128)(2,1)S(1)}, u32[]{:S(2)}, u32[]{:S(2)}) async-start(bf16[8,8,512]{2,1,0:T(8,128)(2,1)} %broadcast_in_dim.6), calls=%async_computation.2 | async-start | bytes 131072 | tf_op jit(solution)/shard_map/all_to_all | solution.py:730
  85.4 0.7 convert_add_fusion
  86.1 5.9 %all-to-all-done.2 = bf16[8,8,512]{2,1,0:T(8,128)(2,1)S(1)} async-done(((bf16[8,8,512]{2,1,0:T(8,128)(2,1)}), bf16[8,8,512]{2,1,0:T(8,128)(2,1)S(1)}, u32[]{:S(2)}, u32[]{:S(2)}) %all-to-all-start.2) | async-done | bytes 65568 | tf_op jit(solution)/shard_map/all_to_all | solution.py:730
  92.0 1.0 broadcast_in_dim.7
  93.0 4.1 %all-to-all-start.3 = ((bf16[16,104,256]{2,1,0:T(8,128)(2,1)}), bf16[16,104,256]{2,1,0:T(8,128)(2,1)S(1)}, u32[]{:S(2)}, u32[]{:S(2)}) async-start(bf16[16,104,256]{2,1,0:T(8,128)(2,1)} %broadcast_in_dim.7), calls=%async_computation.3 | async-start | bytes 1703936 | tf_op jit(solution)/shard_map/all_to_all | solution.py:754
  97.1 1.1 convert_add_fusion.1
  98.8 0.7 fusion.9
  99.5 1.4 %collective-permute-start.10 = (bf16[3,1,5,16,128]{4,3,2,1,0:T(8,128)(2,1)}, bf16[3,1,5,16,128]{4,3,2,1,0:T(8,128)(2,1)}, u32[]{:S(2)}, u32[]{:S(2)}) collective-permute-start(bf16[3,1,5,16,128]{4,3,2,1,0:T(8,128)(2,1)} %get-tuple-element.72), channel_id=1, source_target_pairs={{0,4},{4,8},{8,12},{12,16},{16,20},{20,24},{24,28},{28,32},{32,36}... | collective-permute-start | bytes 184328 | tf_op jit(solution)/shard_map/ppermute | solution.py:306
  100.8 4.0 %collective-permute-start.11 = (bf16[3,1,5,16,128]{4,3,2,1,0:T(8,128)(2,1)}, bf16[3,1,5,16,128]{4,3,2,1,0:T(8,128)(2,1)}, u32[]{:S(2)}, u32[]{:S(2)}) collective-permute-start(bf16[3,1,5,16,128]{4,3,2,1,0:T(8,128)(2,1)} %get-tuple-element.71), channel_id=1, source_target_pairs={{0,60},{4,0},{8,4},{12,8},{16,12},{20,16},{24,20},{28,24},{32,28},... | collective-permute-start | bytes 184328 | tf_op jit(solution)/shard_map/ppermute | solution.py:306
  105.4 2.5 %all-to-all-done.3.refs_4_.refs_18_ = bf16[16,104,256]{2,1,0:T(8,128)(2,1)S(1)} async-done(((bf16[16,104,256]{2,1,0:T(8,128)(2,1)}), bf16[16,104,256]{2,1,0:T(8,128)(2,1)S(1)}, u32[]{:S(2)}, u32[]{:S(2)}) %all-to-all-start.3) | async-done | bytes 852000 | tf_op jit(solution)/shard_map/all_to_all | solution.py:754
  107.9 5.6 %collective-permute-start.7 = (bf16[16,104,256]{2,1,0:T(8,128)(2,1)S(1)}, bf16[16,104,256]{2,1,0:T(8,128)(2,1)S(1)}, u32[]{:S(2)}, u32[]{:S(2)}) collective-permute-start(bf16[16,104,256]{2,1,0:T(8,128)(2,1)S(1)} %all-to-all-done.3.refs_4_.refs_18_), channel_id=1, source_target_pairs={{0,1},{1,0},{2,3},{3,2},{4,5},{5,4},{6,7},{7,6},{8,9},{9,8},{10,11... | collective-permute-start | bytes 2555912 | tf_op jit(solution)/shard_map/ppermute | solution.py:306
  113.5 1.2 pad_maximum_fusion
  114.6 0.9 fusion.6
  115.6 0.7 copy-done.34
  116.3 0.8 collective-permute-start.13
  117.2 0.7 copy-done.17
  117.9 2.9 %shard_map.141 = (f32[64,512]{1,0:T(8,128)S(1)}, f32[16,512]{1,0:T(8,128)S(1)}) custom-call(bf16[64,512]{1,0:T(8,128)(2,1)S(1)} %bitcast.35, bf16[64,512]{1,0:T(8,128)(2,1)S(1)} %bitcast.40, bf16[1024,512]{1,0:T(8,128)(2,1)S(1)} %get-tuple-element.36.refs_2_, bf16[1024,512]{1,0:T(8,128)(2,1)S(1)} %get-tuple-element.37.refs_3_, ...), custom_call_target="tpu_custom_call" | custom-call | flops 268435456 | bytes 2097152 | tf_op jit(solution)/shard_map/pallas_call | solution.py:289
  120.8 3.7 %collective-permute-done.12.refs_14_ = bf16[3,3,1,16,128]{4,3,2,1,0:T(8,128)(2,1)S(1)} collective-permute-done((bf16[3,3,1,16,128]{4,3,2,1,0:T(8,128)(2,1)S(1)}, bf16[3,3,1,16,128]{4,3,2,1,0:T(8,128)(2,1)S(1)}, u32[]{:S(2)}, u32[]{:S(2)}) %collective-permute-start.12) | collective-permute-done | bytes 36896 | tf_op jit(solution)/shard_map/ppermute | solution.py:306
  124.5 4.1 %shard_map.142 = (bf16[64,512]{1,0:T(8,128)(2,1)}, f32[3,1,512]{2,1,0:T(1,128)}, f32[64,64]{1,0:T(8,128)}, f32[16,64]{1,0:T(8,128)}) custom-call(bf16[64,512]{1,0:T(8,128)(2,1)S(1)} %bitcast.36, bf16[64,512]{1,0:T(8,128)(2,1)S(1)} %bitcast.41, s32[1,512]{1,0:T(1,128)S(1)} %bitcast.50, f32[4,64]{1,0:T(4,128)S(1)} %copy-done.28, ...), custom_call_target="tpu_custom_call" | custom-call | flops 268435456 | bytes 2097152 | tf_op jit(solution)/shard_map/pallas_call | solution.py:289
  (96 shorter events, 5.8 us)
Async XLA Ops:
  0.6 46.4 %copy-start = (f32[2048,64]{0,1:T(8,128)S(1)}, f32[2048,64]{0,1:T(8,128)}, u32[]{:S(2)}) copy-start(f32[2048,64]{0,1:T(8,128)} %param.16) | copy-start | bytes 1572868
  0.6 0.7 copy-start.24
  1.4 0.8 copy-start.7
  2.2 0.8 copy-start.18
  3.7 0.8 copy-start.9
  4.2 5.4 %copy-start.14 = (bf16[16,1024]{1,0:T(8,128)(2,1)}, bf16[16,1024]{1,0:T(8,128)(2,1)S(1)}, u32[]{:S(2)}) copy-start(bf16[16,1024]{1,0:T(8,128)(2,1)S(1)} %get-tuple-element.27.refs_3_.refs_8_) | copy-start | bytes 98308
  4.2 28.5 %copy-start.16 = (bf16[16,1024]{1,0:T(8,128)(2,1)}, bf16[16,1024]{1,0:T(8,128)(2,1)S(1)}, u32[]{:S(2)}) copy-start(bf16[16,1024]{1,0:T(8,128)(2,1)S(1)} %get-tuple-element.30.refs_3_.refs_5_) | copy-start | bytes 98308
  9.5 1.0 copy-start.1
  10.6 1.0 copy-start.3
  11.6 25.9 %collective-permute-start = (f32[1024,256]{1,0:T(8,128)}, f32[1024,256]{1,0:T(8,128)}, u32[]{:S(2)}, u32[]{:S(2)}) collective-permute-start(f32[1024,256]{1,0:T(8,128)} %get-tuple-element.32), channel_id=1, source_target_pairs={{0,1},{1,0},{2,3},{3,2},{4,5},{5,4},{6,7},{7,6},{8,9},{9,8},{10,11... | collective-permute-start | bytes 3145736 | tf_op jit(solution)/shard_map/ppermute | solution.py:306
  14.8 6.2 %collective-permute-start.1 = (bf16[3,3,1,16,128]{4,3,2,1,0:T(8,128)(2,1)S(1)}, bf16[3,3,1,16,128]{4,3,2,1,0:T(8,128)(2,1)S(1)}, u32[]{:S(2)}, u32[]{:S(2)}) collective-permute-start(bf16[3,3,1,16,128]{4,3,2,1,0:T(8,128)(2,1)S(1)} %get-tuple-element.77), channel_id=1, source_target_pairs={{0,1},{1,2},{2,3},{3,0},{4,5},{5,6},{6,7},{7,4},{8,9},{9,10},{10,1... | collective-permute-start | bytes 110600 | tf_op jit(solution)/shard_map/ppermute | solution.py:306
  19.9 12.8 %copy-start.8 = (bf16[1,1,1,64,512]{4,3,2,1,0:T(8,128)(2,1)S(1)}, bf16[1,1,1,64,512]{4,3,2,1,0:T(8,128)(2,1)}, u32[]{:S(2)}) copy-start(bf16[1,1,1,64,512]{4,3,2,1,0:T(8,128)(2,1)} %param.10) | copy-start | bytes 196612
  19.9 7.3 %collective-permute-start.2 = (bf16[3,3,1,16,128]{4,3,2,1,0:T(8,128)(2,1)S(1)}, bf16[3,3,1,16,128]{4,3,2,1,0:T(8,128)(2,1)S(1)}, u32[]{:S(2)}, u32[]{:S(2)}) collective-permute-start(bf16[3,3,1,16,128]{4,3,2,1,0:T(8,128)(2,1)S(1)} %get-tuple-element.78), channel_id=1, source_target_pairs={{0,3},{1,0},{2,1},{3,2},{4,7},{5,4},{6,5},{7,6},{8,11},{9,8},{10,9... | collective-permute-start | bytes 110600 | tf_op jit(solution)/shard_map/ppermute | solution.py:306
  27.3 10.2 %collective-permute-start.3 = (bf16[3,1,5,16,128]{4,3,2,1,0:T(8,128)(2,1)S(1)}, bf16[3,1,5,16,128]{4,3,2,1,0:T(8,128)(2,1)S(1)}, u32[]{:S(2)}, u32[]{:S(2)}) collective-permute-start(bf16[3,1,5,16,128]{4,3,2,1,0:T(8,128)(2,1)S(1)} %get-tuple-element.75), channel_id=1, source_target_pairs={{0,4},{4,8},{8,12},{12,16},{16,20},{20,24},{24,28},{28,32},{32,36}... | collective-permute-start | bytes 184328 | tf_op jit(solution)/shard_map/ppermute | solution.py:306
  28.7 8.8 %collective-permute-start.4 = (bf16[3,1,5,16,128]{4,3,2,1,0:T(8,128)(2,1)S(1)}, bf16[3,1,5,16,128]{4,3,2,1,0:T(8,128)(2,1)S(1)}, u32[]{:S(2)}, u32[]{:S(2)}) collective-permute-start(bf16[3,1,5,16,128]{4,3,2,1,0:T(8,128)(2,1)S(1)} %get-tuple-element.76), channel_id=1, source_target_pairs={{0,60},{4,0},{8,4},{12,8},{16,12},{20,16},{24,20},{28,24},{32,28},... | collective-permute-start | bytes 184328 | tf_op jit(solution)/shard_map/ppermute | solution.py:306
  39.6 28.1 %all-to-all-start = ((bf16[16,64,256]{2,1,0:T(8,128)(2,1)}), bf16[16,64,256]{2,1,0:T(8,128)(2,1)}, u32[]{:S(2)}, u32[]{:S(2)}) async-start(bf16[16,64,256]{2,1,0:T(8,128)(2,1)} %bitcast.52), calls=%async_computation | async-start | bytes 1048576 | tf_op jit(solution)/shard_map/all_to_all | solution.py:703
  43.9 8.5 %copy-start.19 = (s32[1,1,1,16,512]{4,3,2,1,0:T(8,128)S(1)}, s32[1,1,1,16,512]{4,3,2,1,0:T(8,128)}, u32[]{:S(2)}) copy-start(s32[1,1,1,16,512]{4,3,2,1,0:T(8,128)} %param.14) | copy-start | bytes 98308
  44.6 6.0 %collective-permute-start.6 = (bf16[1,5,5,16,128]{4,3,2,1,0:T(8,128)(2,1)}, bf16[1,5,5,16,128]{4,3,2,1,0:T(8,128)(2,1)S(1)}, u32[]{:S(2)}, u32[]{:S(2)}) collective-permute-start(bf16[1,5,5,16,128]{4,3,2,1,0:T(8,128)(2,1)} %get-tuple-element.73), channel_id=1, source_target_pairs={{0,192},{64,0},{128,64},{192,128},{1,193},{65,1},{129,65},{193,129... | collective-permute-start | bytes 307208 | tf_op jit(solution)/shard_map/ppermute | solution.py:306
  47.1 5.3 %collective-permute-start.5 = (bf16[1,5,5,16,128]{4,3,2,1,0:T(8,128)(2,1)S(1)}, bf16[1,5,5,16,128]{4,3,2,1,0:T(8,128)(2,1)S(1)}, u32[]{:S(2)}, u32[]{:S(2)}) collective-permute-start(bf16[1,5,5,16,128]{4,3,2,1,0:T(8,128)(2,1)S(1)} %get-tuple-element.74), channel_id=1, source_target_pairs={{0,64},{64,128},{128,192},{192,0},{1,65},{65,129},{129,193},{193,1... | collective-permute-start | bytes 307208 | tf_op jit(solution)/shard_map/ppermute | solution.py:306
  47.1 5.3 %copy-start.27 = (f32[4,64]{1,0:T(4,128)S(1)}, f32[4,64]{1,0:T(4,128)}, u32[]{:S(2)}) copy-start(f32[4,64]{1,0:T(4,128)} %refs_3_.5) | copy-start | bytes 3076
  47.1 5.2 %copy-start.11 = (bf16[64,64]{1,0:T(8,128)(2,1)S(1)}, bf16[64,64]{1,0:T(8,128)(2,1)}, u32[]{:S(2)}) copy-start(bf16[64,64]{1,0:T(8,128)(2,1)} %refs_4_.3) | copy-start | bytes 24580
  47.8 4.6 %copy-start.26 = (f32[16,64]{1,0:T(8,128)S(1)}, f32[16,64]{1,0:T(8,128)}, u32[]{:S(2)}) copy-start(f32[16,64]{1,0:T(8,128)} %refs_3_.4) | copy-start | bytes 12292
  65.7 0.8 copy-start.5
  67.7 6.2 %copy-start.6 = (f32[1200,128]{1,0:T(8,128)S(1)}, f32[1200,128]{1,0:T(8,128)}, u32[]{:S(2)}) copy-start(f32[1200,128]{1,0:T(8,128)} %copy-done.5) | copy-start | bytes 1843204
  69.6 11.0 %all-to-all-start.1 = ((bf16[8,8,512]{2,1,0:T(8,128)(2,1)}), bf16[8,8,512]{2,1,0:T(8,128)(2,1)S(1)}, u32[]{:S(2)}, u32[]{:S(2)}) async-start(bf16[8,8,512]{2,1,0:T(8,128)(2,1)} %pad_maximum_fusion.2), calls=%async_computation.1 | async-start | bytes 131072 | tf_op jit(solution)/shard_map/all_to_all | solution.py:720
  74.0 6.6 %copy-start.35 = (f32[8,64]{1,0:T(8,128)S(1)}, f32[8,64]{1,0:T(8,128)}, u32[]{:S(2)}) copy-start(f32[8,64]{1,0:T(8,128)} %copy.19) | copy-start | bytes 6148
  74.8 10.6 %copy-start.32 = (f32[400,128]{1,0:T(8,128)S(1)}, f32[400,128]{1,0:T(8,128)}, u32[]{:S(2)}) copy-start(f32[400,128]{1,0:T(8,128)} %get-tuple-element.67) | copy-start | bytes 614404
  74.8 10.5 %collective-permute-start.9 = (bf16[1,5,5,16,128]{4,3,2,1,0:T(8,128)(2,1)S(1)}, bf16[1,5,5,16,128]{4,3,2,1,0:T(8,128)(2,1)S(1)}, u32[]{:S(2)}, u32[]{:S(2)}) collective-permute-start(bf16[1,5,5,16,128]{4,3,2,1,0:T(8,128)(2,1)S(1)} %bitcast.51), channel_id=1, source_target_pairs={{0,192},{64,0},{128,64},{192,128},{1,193},{65,1},{129,65},{193,129... | collective-permute-start | bytes 307208 | tf_op jit(solution)/shard_map/ppermute | solution.py:306
  74.8 22.2 %collective-permute-start.8 = (bf16[1,5,5,16,128]{4,3,2,1,0:T(8,128)(2,1)}, bf16[1,5,5,16,128]{4,3,2,1,0:T(8,128)(2,1)}, u32[]{:S(2)}, u32[]{:S(2)}) collective-permute-start(bf16[1,5,5,16,128]{4,3,2,1,0:T(8,128)(2,1)} %bitcast.16), channel_id=1, source_target_pairs={{0,64},{64,128},{128,192},{192,0},{1,65},{65,129},{129,193},{193,1... | collective-permute-start | bytes 307208 | tf_op jit(solution)/shard_map/ppermute | solution.py:306
  82.0 10.0 %all-to-all-start.2 = ((bf16[8,8,512]{2,1,0:T(8,128)(2,1)}), bf16[8,8,512]{2,1,0:T(8,128)(2,1)S(1)}, u32[]{:S(2)}, u32[]{:S(2)}) async-start(bf16[8,8,512]{2,1,0:T(8,128)(2,1)} %broadcast_in_dim.6), calls=%async_computation.2 | async-start | bytes 131072 | tf_op jit(solution)/shard_map/all_to_all | solution.py:730
  93.0 14.9 %all-to-all-start.3 = ((bf16[16,104,256]{2,1,0:T(8,128)(2,1)}), bf16[16,104,256]{2,1,0:T(8,128)(2,1)S(1)}, u32[]{:S(2)}, u32[]{:S(2)}) async-start(bf16[16,104,256]{2,1,0:T(8,128)(2,1)} %broadcast_in_dim.7), calls=%async_computation.3 | async-start | bytes 1703936 | tf_op jit(solution)/shard_map/all_to_all | solution.py:754
  97.0 1.1 copy-start.29
  97.0 1.2 copy-start.30
  99.5 15.2 %collective-permute-start.10 = (bf16[3,1,5,16,128]{4,3,2,1,0:T(8,128)(2,1)}, bf16[3,1,5,16,128]{4,3,2,1,0:T(8,128)(2,1)}, u32[]{:S(2)}, u32[]{:S(2)}) collective-permute-start(bf16[3,1,5,16,128]{4,3,2,1,0:T(8,128)(2,1)} %get-tuple-element.72), channel_id=1, source_target_pairs={{0,4},{4,8},{8,12},{12,16},{16,20},{20,24},{24,28},{28,32},{32,36}... | collective-permute-start | bytes 184328 | tf_op jit(solution)/shard_map/ppermute | solution.py:306
  100.8 13.8 %collective-permute-start.11 = (bf16[3,1,5,16,128]{4,3,2,1,0:T(8,128)(2,1)}, bf16[3,1,5,16,128]{4,3,2,1,0:T(8,128)(2,1)}, u32[]{:S(2)}, u32[]{:S(2)}) collective-permute-start(bf16[3,1,5,16,128]{4,3,2,1,0:T(8,128)(2,1)} %get-tuple-element.71), channel_id=1, source_target_pairs={{0,60},{4,0},{8,4},{12,8},{16,12},{20,16},{24,20},{28,24},{32,28},... | collective-permute-start | bytes 184328 | tf_op jit(solution)/shard_map/ppermute | solution.py:306
  107.9 16.6 %collective-permute-start.7 = (bf16[16,104,256]{2,1,0:T(8,128)(2,1)S(1)}, bf16[16,104,256]{2,1,0:T(8,128)(2,1)S(1)}, u32[]{:S(2)}, u32[]{:S(2)}) collective-permute-start(bf16[16,104,256]{2,1,0:T(8,128)(2,1)S(1)} %all-to-all-done.3.refs_4_.refs_18_), channel_id=1, source_target_pairs={{0,1},{1,0},{2,3},{3,2},{4,5},{5,4},{6,7},{7,6},{8,9},{9,8},{10,11... | collective-permute-start | bytes 2555912 | tf_op jit(solution)/shard_map/ppermute | solution.py:306
  116.3 0.8 copy-start.33
  116.3 0.9 copy-start.10
  116.3 4.5 %collective-permute-start.13 = (bf16[3,3,1,16,128]{4,3,2,1,0:T(8,128)(2,1)S(1)}, bf16[3,3,1,16,128]{4,3,2,1,0:T(8,128)(2,1)S(1)}, u32[]{:S(2)}, u32[]{:S(2)}) collective-permute-start(bf16[3,3,1,16,128]{4,3,2,1,0:T(8,128)(2,1)S(1)} %pad_maximum_fusion.8), channel_id=1, source_target_pairs={{0,1},{1,2},{2,3},{3,0},{4,5},{5,6},{6,7},{7,4},{8,9},{9,10},{10,1... | collective-permute-start | bytes 110600 | tf_op jit(solution)/shard_map/ppermute | solution.py:306
  117.1 0.8 copy-start.17
  117.1 7.4 %collective-permute-start.12 = (bf16[3,3,1,16,128]{4,3,2,1,0:T(8,128)(2,1)S(1)}, bf16[3,3,1,16,128]{4,3,2,1,0:T(8,128)(2,1)S(1)}, u32[]{:S(2)}, u32[]{:S(2)}) collective-permute-start(bf16[3,3,1,16,128]{4,3,2,1,0:T(8,128)(2,1)S(1)} %pad_maximum_fusion.7), channel_id=1, source_target_pairs={{0,3},{1,0},{2,1},{3,2},{4,7},{5,4},{6,5},{7,6},{8,11},{9,8},{10,9... | collective-permute-start | bytes 110600 | tf_op jit(solution)/shard_map/ppermute | solution.py:306
  117.8 6.7 %copy-start.2 = (bf16[1024,512]{1,0:T(8,128)(2,1)S(1)}, bf16[1024,512]{1,0:T(8,128)(2,1)}, u32[]{:S(2)}) copy-start(bf16[1024,512]{1,0:T(8,128)(2,1)} %copy-done.1) | copy-start | bytes 3145732
  117.8 6.7 %copy-start.4 = (bf16[1024,512]{1,0:T(8,128)(2,1)S(1)}, bf16[1024,512]{1,0:T(8,128)(2,1)}, u32[]{:S(2)}) copy-start(bf16[1024,512]{1,0:T(8,128)(2,1)} %copy-done.3) | copy-start | bytes 3145732
  117.8 6.7 %copy-start.13 = (f32[80,128]{1,0:T(8,128)S(1)}, f32[80,128]{1,0:T(8,128)}, u32[]{:S(2)}) copy-start(f32[80,128]{1,0:T(8,128)} %copy-done.12) | copy-start | bytes 122884
  117.8 6.7 %copy-start.15 = (bf16[16,1024]{1,0:T(8,128)(2,1)S(1)}, bf16[16,1024]{1,0:T(8,128)(2,1)}, u32[]{:S(2)}) copy-start(bf16[16,1024]{1,0:T(8,128)(2,1)} %copy-done.14) | copy-start | bytes 98308
  117.8 6.7 %copy-start.25 = (s32[1,1,1,512]{3,2,1,0:T(1,128)S(1)}, s32[1,1,1,512]{3,2,1,0:T(1,128)}, u32[]{:S(2)}) copy-start(s32[1,1,1,512]{3,2,1,0:T(1,128)} %param.13) | copy-start | bytes 6148
  117.9 6.7 %copy-start.28 = (f32[4,64]{1,0:T(4,128)S(1)}, f32[4,64]{1,0:T(4,128)}, u32[]{:S(2)}) copy-start(f32[4,64]{1,0:T(4,128)} %refs_3_.5) | copy-start | bytes 3076
  120.8 3.8 %copy-start.23 = (f32[8,512]{1,0:T(8,128)S(1)}, f32[8,512]{1,0:T(8,128)}, u32[]{:S(2)}) copy-start(f32[8,512]{1,0:T(8,128)} %copy-done.22) | copy-start | bytes 49156
  (6 other events, 4.0 us)

commit v8 on v7

--- a/solution.py
+++ b/solution.py
@@ -1,3 +1,4 @@
+import functools
 import math
 
 import jax
@@ -265,7 +266,8 @@
 
 
 def fetching_call(
-    kernel, fetched, resident, outs, scratch, early=None, in_specs=None, out_specs=None, flops=0
+    kernel, fetched, resident, outs, scratch, early=None, in_specs=None, out_specs=None, flops=0,
+    limit=True,
 ):
     n = len(fetched)
 
@@ -296,7 +298,7 @@
             *[pltpu.VMEM(x.shape, x.dtype) for x in fetched],
             pltpu.SemaphoreType.DMA((n,)),
         ],
-        compiler_params=LIMIT,
+        compiler_params=LIMIT if limit else None,
         cost_estimate=cost,
     )(*fetched, *resident)
 
@@ -358,6 +360,7 @@
             half,
         ),
         [],
+        limit=False,
     )
 
 
@@ -535,9 +538,7 @@
     miller_ref,
     first_ref,
     angle_ref,
-    low_ref,
-    middle_ref,
-    high_ref,
+    inner_ref,
     upper_ref,
     lower_ref,
     core_ref,
@@ -557,17 +558,11 @@
     channels = h_ref.shape[0]
     cells = jnp.stack(
         [
-            jnp.stack(
-                [
-                    plane[:, 0, 1] + lower_ref[:, n, 0].astype(f32),
-                    plane[:, 0, 2],
-                    plane[:, 0, 3] + upper_ref[:, n, 0].astype(f32),
-                ],
-                axis=1,
-            )
-            for n, plane in enumerate((low_ref, middle_ref, high_ref))
+            inner_ref[:, :, 0] + lower_ref[:, :, 0].astype(f32),
+            inner_ref[:, :, 1],
+            inner_ref[:, :, 2] + upper_ref[:, :, 0].astype(f32),
         ],
-        axis=1,
+        axis=2,
     ).reshape(432, 128)
     flat = jnp.transpose(jnp.concatenate([cells, core_ref[...]], axis=0))
     gains = gains_of(gain_ref[...], kind_ref[...], (channels, flat.shape[1]))
@@ -645,7 +640,125 @@
         ],
         axis=1,
     )
-    return (coeffs.astype(jnp.bfloat16), cos_struct * cos_back + sin_struct * sin_back)
+    return (coeffs, cos_struct * cos_back + sin_struct * sin_back)
+
+
+def small_call(kernel, args, outs):
+    return pl.pallas_call(
+        kernel,
+        out_shape=outs,
+        in_specs=[WHOLE] * len(args),
+        out_specs=(WHOLE,) * len(outs),
+        compiler_params=LIMIT,
+    )(*args)
+
+
+def partial_kernel(pieces_ref, sums_ref, out_ref):
+    f32, bf16 = jnp.float32, jnp.bfloat16
+    tower, rows, _ = out_ref.shape
+    width = pieces_ref.shape[2]
+    total = jnp.sum(pieces_ref[...].astype(f32), axis=0)
+    hi, lo = split_two(sums_ref[...])
+    whole = jnp.concatenate([total, hi.astype(f32), lo.astype(f32)], axis=1)
+    out_ref[...] = whole.reshape(tower, rows, width + 256).astype(bf16)
+
+
+def partial_sums(pieces, sums, tower):
+    shape = (tower, pieces.shape[1] // tower, pieces.shape[2] + 256)
+    outs = (jax.ShapeDtypeStruct(shape, jnp.bfloat16),)
+    return small_call(partial_kernel, (pieces, sums), outs)[0]
+
+
+def coefficient_kernel(norm_atoms, norm_k, pieces_ref, filter_in, out_ref, filter_ref, tile, sem):
+    f32 = jnp.float32
+    _, share, _ = pieces_ref.shape
+    channels = filter_ref.shape[1]
+    width = 4 * channels
+    start = lax.axis_index(GX_GY_GZ) * share
+    lane = pl.multiple_of(start // 128 * 128, 128)
+    copy = pltpu.make_async_copy(filter_in.at[:, pl.ds(lane, 128)], tile, sem)
+    copy.start()
+    both = jnp.sum(pieces_ref[...].astype(f32), axis=0)
+    copy.wait()
+    turned = jnp.transpose(tile[...])
+    pick = lax.broadcasted_iota(jnp.int32, (128 // share, share, channels), 0)
+    inside = (start - lane) // share
+    filt = jnp.sum(
+        jnp.where(pick == inside, turned.reshape(128 // share, share, channels), 0.0), axis=0
+    )
+    coeffs, filter_ref[...] = coefficients(both[:, 0:width], filt, norm_atoms, norm_k)
+    hi, lo = split_two(both[:, width : width + 128] + both[:, width + 128 :])
+    sent = jnp.concatenate([coeffs, hi.astype(f32), lo.astype(f32)], axis=1)
+    out_ref[...] = jnp.broadcast_to(sent[None], out_ref.shape).astype(jnp.bfloat16)
+
+
+def make_coefficients(pieces, filter_columns, norm_atoms, norm_k):
+    share, channels = pieces.shape[1], filter_columns.shape[0]
+    return pl.pallas_call(
+        functools.partial(coefficient_kernel, norm_atoms, norm_k),
+        out_shape=(
+            jax.ShapeDtypeStruct(pieces.shape, jnp.bfloat16),
+            jax.ShapeDtypeStruct((share, channels), jnp.float32),
+        ),
+        in_specs=[WHOLE, FAR],
+        out_specs=(WHOLE, WHOLE),
+        scratch_shapes=[pltpu.VMEM((channels, 128), jnp.float32), pltpu.SemaphoreType.DMA],
+        compiler_params=LIMIT,
+        name="coefficients",
+    )(pieces, filter_columns)
+
+
+def strip_kernel(got_ref, out_ref):
+    f32 = jnp.float32
+    tower, share, _ = got_ref.shape
+    width = out_ref.shape[2]
+    run, cut = tower * share, out_ref.shape[1] - tower * share
+    got = got_ref[...].astype(f32).reshape(run, width + 256)
+    strip = jnp.concatenate([got[:, 0:width], got[0:cut, width:]], axis=0)
+    out_ref[...] = jnp.broadcast_to(strip[None], out_ref.shape).astype(jnp.bfloat16)
+
+
+def make_strip(got, sheet, width, cut):
+    shape = (sheet, got.shape[0] * got.shape[1] + cut, width)
+    return small_call(strip_kernel, (got,), (jax.ShapeDtypeStruct(shape, got.dtype),))[0]
+
+
+def fold_x_kernel(mid_ref, upper_ref, lower_ref, first_ref, last_ref, rest_ref):
+    f32, bf16 = jnp.float32, jnp.bfloat16
+    for n in range(3):
+        plane = mid_ref[n]
+        if n == 0:
+            plane = plane + lower_ref[0].astype(f32)
+        if n == 2:
+            plane = plane + upper_ref[0].astype(f32)
+        first_ref[n] = plane[0:1].astype(bf16)
+        last_ref[n] = plane[4:5].astype(bf16)
+        rest_ref[n] = plane[1:4]
+
+
+def fold_x(mid, upper, lower):
+    side = jax.ShapeDtypeStruct((3, 1, 5, 16, 128), jnp.bfloat16)
+    rest = jax.ShapeDtypeStruct((3, 3, 5, 16, 128), jnp.float32)
+    return small_call(fold_x_kernel, (mid, upper, lower), (side, side, rest))
+
+
+def fold_y_kernel(rest_ref, upper_ref, lower_ref, first_ref, last_ref, inner_ref):
+    f32, bf16 = jnp.float32, jnp.bfloat16
+    for n in range(3):
+        plane = rest_ref[:, n]
+        if n == 0:
+            plane = plane + lower_ref[:, 0].astype(f32)
+        if n == 2:
+            plane = plane + upper_ref[:, 0].astype(f32)
+        first_ref[:, n] = plane[:, 0:1].astype(bf16)
+        last_ref[:, n] = plane[:, 4:5].astype(bf16)
+        inner_ref[:, n] = plane[:, 1:4]
+
+
+def fold_y(rest, upper, lower):
+    side = jax.ShapeDtypeStruct((3, 3, 1, 16, 128), jnp.bfloat16)
+    inner = jax.ShapeDtypeStruct((3, 3, 3, 16, 128), jnp.float32)
+    return small_call(fold_y_kernel, (rest, upper, lower), (side, side, inner))
 
 
 def sent_out(x, axis, dim):
@@ -653,13 +766,6 @@
     before = from_behind(lax.slice_in_dim(x, length - 1, length, axis=dim), axis, 1)
     after = from_behind(lax.slice_in_dim(x, 0, 1, axis=dim), axis, -1)
     return before, after
-
-
-def sent_back(x, axis, dim):
-    length = x.shape[dim]
-    first = lax.slice_in_dim(x, 0, 1, axis=dim).astype(jnp.bfloat16)
-    last = lax.slice_in_dim(x, length - 1, length, axis=dim).astype(jnp.bfloat16)
-    return from_behind(first, axis, -1), from_behind(last, axis, 1)
 
 
 def whole(
@@ -683,8 +789,6 @@
     devices = lax.axis_size(GX_GY_GZ)
     norm_atoms = (atoms * devices) ** (-0.5)
     norm_k = points ** (-0.5)
-    share_rows = points // devices
-    share_start = lax.axis_index(GX_GY_GZ) * share_rows
     half = points // 2
 
     cells, core, miller_mine, miller_next = pack(h, kinds, pos, miller_triples)
@@ -711,62 +815,21 @@
         channel_mixing_matrix,
         element_channel_factor,
     )
-    sums_hi = lax.reduce_precision(sums, 8, 7)
-    tiles = jnp.concatenate([sums_hi, sums - sums_hi], axis=1).astype(jnp.bfloat16)
-    tiles = tiles.reshape(tower, 8, 256)
-
-    partial = jnp.sum(pieces.astype(jnp.float32), axis=0).astype(jnp.bfloat16)
-    partial = partial.reshape(tower, share_rows, width)
-    pieces = lax.all_to_all(jnp.concatenate([partial, tiles], axis=2), TOWER, 0, 0)
-    pieces = jnp.sum(pieces.astype(jnp.float32), axis=0)
-    totals, tile = pieces[:, 0:width], pieces[:, width:]
-    filt_rows = lax.dynamic_slice_in_dim(reciprocal_kernel, share_start, share_rows, 0)
-    own_coeffs, filter_share = coefficients(totals, filt_rows, norm_atoms, norm_k)
-    tile = tile[:, 0:128] + tile[:, 128:256]
-    tile_hi = lax.reduce_precision(tile, 8, 7)
-    sent = jnp.concatenate(
-        [own_coeffs, tile_hi.astype(jnp.bfloat16), (tile - tile_hi).astype(jnp.bfloat16)], axis=1
-    )
-    got = lax.all_to_all(jnp.broadcast_to(sent[None], (tower,) + sent.shape), TOWER, 0, 0)
-
-    grid = mid.reshape(3, 5, 5, 16, 128)
-    to_side = (
-        from_behind(low.reshape(1, 5, 5, 16, 128), "gx", -1),
-        from_behind(high.reshape(1, 5, 5, 16, 128), "gx", 1),
-    )
-    grid = jnp.concatenate(
-        [
-            grid[0:1] + to_side[1].astype(jnp.float32),
-            grid[1:2],
-            grid[2:3] + to_side[0].astype(jnp.float32),
-        ],
-        axis=0,
-    )
-    to_side = sent_back(grid, GY, 1)
-
-    strip = jnp.concatenate(
-        [
-            got[:, :, 0:width].reshape(tower * share_rows, width),
-            got[0:5, :, width:].reshape(5 * share_rows, width),
-        ],
-        axis=0,
-    )
-    got = lax.all_to_all(jnp.broadcast_to(strip[None], (sheet,) + strip.shape), SHEET, 0, 0)
-    planes = (
-        grid[:, 1:2] + to_side[1].astype(jnp.float32),
-        grid[:, 2:3],
-        grid[:, 3:4] + to_side[0].astype(jnp.float32),
-    )
-    to_side = tuple(
-        from_behind(
-            jnp.concatenate([p[:, :, at : at + 1].astype(jnp.bfloat16) for p in planes], axis=1),
-            GZ,
-            by,
-        )
-        for at, by in ((0, -1), (4, 1))
-    )
+    parts = partial_sums(pieces, sums, tower)
+    pieces = lax.all_to_all(parts, TOWER, 0, 0)
+    sent, filter_share = make_coefficients(pieces, reciprocal_kernel.T, norm_atoms, norm_k)
+    got = lax.all_to_all(sent, TOWER, 0, 0)
+
+    upper = from_behind(low.reshape(1, 5, 5, 16, 128), "gx", -1)
+    lower = from_behind(high.reshape(1, 5, 5, 16, 128), "gx", 1)
+    first, last, rest = fold_x(mid.reshape(3, 5, 5, 16, 128), upper, lower)
+    upper, lower = from_behind(first, GY, -1), from_behind(last, GY, 1)
+    strip = make_strip(got, sheet, width, (channels + distance_kernel.shape[0]) // 2)
+    got = lax.all_to_all(strip, SHEET, 0, 0)
+    first, last, inner = fold_y(rest, upper, lower)
+    upper, lower = from_behind(first, GZ, -1), from_behind(last, GZ, 1)
     got_next = from_behind(got, PAIR, 1)
-    first = ewald(got, cos_mine, sin_mine, miller_mine, h, dy)
+    early_sums = ewald(got, cos_mine, sin_mine, miller_mine, h, dy)
     atom_grad, position_grad, weight_grad, radial_grad = ewald(
         got_next,
         cos_next,
@@ -774,7 +837,7 @@
         miller_next,
         h,
         dy,
-        (*first, *planes, *to_side, core_grad, own_grad, got),
+        (*early_sums, inner, upper, lower, core_grad, own_grad, got),
         (kinds, element_channel_factor, channel_mixing_matrix),
         distance_kernel.shape[0],
     )

time: 130 us -> 128 us (0.985)
  blocking collectives: 0 us -> 34.2 us
  starting transfers between devices: 45.6 us -> 34.3 us
  local copies, waits for them, and re-layouts: 15.4 us -> 4.3 us
  other arithmetic: 8.65 us -> 0.97 us
  waiting for transfers between devices: 28.2 us -> 21.6 us
    all_to_all x0 -> x3, blocking collectives: none -> 34.2 us  [the longest x1 16 us: whole(): got = lax.all_to_all(strip, SHEET, 0, 0)]
    all_to_all x3 -> x0, waiting for transfers between devices: 12.6 us -> none  [the longest x1 5.88 us: whole(): lax.all_to_all(jnp.broadcast_to(sent[None], (tower,) + sent.shape), TOWER...]
    all_to_all x3 -> x0, starting transfers between devices: 11.8 us -> none  [the longest x1 4.36 us: whole(): lax.all_to_all(jnp.concatenate([partial, tiles], axis=2), TOWER, 0, 0)]
    unnamed x73 -> x46, local copies, waits for them, and re-layouts: 10.8 us -> 4.28 us
    ppermute x14, waiting for transfers between devices: 15.6 us -> 21.6 us  [from_behind(): lax.ppermute(x, axis, [(i, (i + by) % devices) for i in range(devices)])]
    slice x4 -> x0, local copies, waits for them, and re-layouts: 2.13 us -> none  [the longest x1 0.86 us: whole(): grid[0:1] + to_side[1].astype(jnp.float32)]
    concatenate x6 -> x0, other arithmetic: 1.83 us -> none  [the longest x1 1.17 us: whole(): jnp.concatenate([grid[0:1] + to_side[1].astype(jnp.float32), grid[1:2], g...]
    add x2 -> x0, other arithmetic: 1.78 us -> none  [the longest x1 1.06 us: whole(): grid[0:1] + to_side[1].astype(jnp.float32)]
  transfers between devices with their start and end apart: 18 -> 15, of which waited for: 8 -> 7; matrix products, arithmetic and copies ran while one was open for 8% -> 1% of each run, Pallas kernels for 16% -> 16%
where the time goes in v8:
time: 128 us; the launch traced here: 127 us
  starting transfers between devices  34.3 us (27%)
  blocking collectives  34.2 us (27%)
  Pallas kernels  30.6 us (24%)
  waiting for transfers between devices  21.6 us (17%)
  local copies, waits for them, and re-layouts  4.3 us (3%)
    ppermute x14, starting transfers between devices, from_behind(): lax.ppermute(x, axis, [(i, (i + by) % devices) for i in range(devices)])  30.2 us
    pallas_call x6, Pallas kernels, fetching_call(): pl.pallas_call(body, out_shape=outs, in_specs=[FAR] * n + list(in_specs o...  29.7 us
    ppermute x14, waiting for transfers between devices, from_behind(): lax.ppermute(x, axis, [(i, (i + by) % devices) for i in range(devices)])  21.6 us
    all_to_all x1, blocking collectives, whole(): got = lax.all_to_all(strip, SHEET, 0, 0)  16 us
    all_to_all x1, blocking collectives, whole(): pieces = lax.all_to_all(parts, TOWER, 0, 0)  9.19 us
    all_to_all x1, blocking collectives, whole(): got = lax.all_to_all(sent, TOWER, 0, 0)  8.99 us
    unnamed x46, local copies, waits for them, and re-layouts  4.28 us
    all_to_all x1, starting transfers between devices, whole(): lax.all_to_all(paired.reshape(sheet, half // sheet, width), SHEET, 0, 0)  4.12 us
  transfers between devices with their start and end apart: 15, of which 7 were waited for; matrix products, arithmetic and copies ran while one was open for 1% of the time, Pallas kernels for 16%

profile of v8, /device:TPU:1, one launch (start us, length us, event | category | flops | bytes accessed | tf_op | source)
XLA Modules:
  0.0 127.1 jit_solution(8940103754743314277)
XLA Ops:
  0.7 1.9 %shard_map.137 = (bf16[432,128]{1,0:T(8,128)(2,1)}, bf16[80,128]{1,0:T(8,128)(2,1)}, bf16[16,1024]{1,0:T(8,128)(2,1)}, bf16[16,1024]{1,0:T(8,128)(2,1)}) custom-call(bf16[64,512]{1,0:T(8,128)(2,1)} %bitcast.20, s32[1,512]{1,0:T(1,128)} %bitcast.38, f32[3,1,512]{2,1,0:T(1,128)} %bitcast.34, s32[3,2048]{1,0:T(4,128)} %refs_3_.3), custom_call_target="tpu_custom_call" | custom-call | tf_op jit(solution)/shard_map/pallas_call | solution.py:291
  2.6 0.0 copy-start.5
  2.6 0.8 copy-done.5
  3.4 0.8 copy-done.9
  4.2 4.0 %shard_map.138 = (bf16[1024,512]{1,0:T(8,128)(2,1)S(1)}, bf16[1024,512]{1,0:T(8,128)(2,1)S(1)}, f32[1024,256]{1,0:T(8,128)S(1)}) custom-call(f32[3,1,512]{2,1,0:T(1,128)S(1)} %bitcast.35, bf16[64,512]{1,0:T(8,128)(2,1)S(1)} %bitcast.21, bf16[64,512]{1,0:T(8,128)(2,1)S(1)} %bitcast.25, bf16[16,1024]{1,0:T(8,128)(2,1)S(1)} %copy-done.9), custom_call_target="tpu_custom_call" | custom-call | flops 402653184 | bytes 3145728 | tf_op jit(solution)/shard_map/pallas_call | solution.py:291
  8.2 3.3 %collective-permute-start = (f32[1024,256]{1,0:T(8,128)S(1)}, f32[1024,256]{1,0:T(8,128)S(1)}, u32[]{:S(2)}, u32[]{:S(2)}) collective-permute-start(f32[1024,256]{1,0:T(8,128)S(1)} %get-tuple-element.40), channel_id=1, source_target_pairs={{0,1},{1,0},{2,3},{3,2},{4,5},{5,4},{6,7},{7,6},{8,9},{9,8},{10,11... | collective-permute-start | bytes 3145736 | tf_op jit(solution)/shard_map/ppermute | solution.py:308
  11.5 5.2 %collective-permute-start.1 = (bf16[3,3,1,16,128]{4,3,2,1,0:T(8,128)(2,1)S(1)}, bf16[3,3,1,16,128]{4,3,2,1,0:T(8,128)(2,1)S(1)}, u32[]{:S(2)}, u32[]{:S(2)}) collective-permute-start(bf16[3,3,1,16,128]{4,3,2,1,0:T(8,128)(2,1)S(1)} %get-tuple-element.74), channel_id=1, source_target_pairs={{0,1},{1,2},{2,3},{3,0},{4,5},{5,6},{6,7},{7,4},{8,9},{9,10},{10,1... | collective-permute-start | bytes 110600 | tf_op jit(solution)/shard_map/ppermute | solution.py:308
  16.7 4.0 %shard_map.139 = (bf16[1024,512]{1,0:T(8,128)(2,1)S(1)}, bf16[1024,512]{1,0:T(8,128)(2,1)S(1)}, f32[1024,256]{1,0:T(8,128)S(1)}) custom-call(f32[3,1,512]{2,1,0:T(1,128)S(1)} %bitcast.36, bf16[64,512]{1,0:T(8,128)(2,1)S(1)} %bitcast.22, bf16[64,512]{1,0:T(8,128)(2,1)S(1)} %bitcast.26, bf16[16,1024]{1,0:T(8,128)(2,1)S(1)} %copy-done.11), custom_call_target="tpu_custom_call" | custom-call | flops 402653184 | bytes 3145728 | tf_op jit(solution)/shard_map/pallas_call | solution.py:291
  20.8 3.2 %collective-permute-done.2 = bf16[3,3,1,16,128]{4,3,2,1,0:T(8,128)(2,1)S(1)} collective-permute-done((bf16[3,3,1,16,128]{4,3,2,1,0:T(8,128)(2,1)S(1)}, bf16[3,3,1,16,128]{4,3,2,1,0:T(8,128)(2,1)S(1)}, u32[]{:S(2)}, u32[]{:S(2)}) %collective-permute-start.2) | collective-permute-done | bytes 36896 | tf_op jit(solution)/shard_map/ppermute | solution.py:308
  24.0 1.4 %collective-permute-start.3 = (bf16[3,1,5,16,128]{4,3,2,1,0:T(8,128)(2,1)S(1)}, bf16[3,1,5,16,128]{4,3,2,1,0:T(8,128)(2,1)S(1)}, u32[]{:S(2)}, u32[]{:S(2)}) collective-permute-start(bf16[3,1,5,16,128]{4,3,2,1,0:T(8,128)(2,1)S(1)} %get-tuple-element.72), channel_id=1, source_target_pairs={{0,4},{4,8},{8,12},{12,16},{16,20},{20,24},{24,28},{28,32},{32,36}... | collective-permute-start | bytes 184328 | tf_op jit(solution)/shard_map/ppermute | solution.py:308
  25.4 4.1 %collective-permute-start.4 = (bf16[3,1,5,16,128]{4,3,2,1,0:T(8,128)(2,1)S(1)}, bf16[3,1,5,16,128]{4,3,2,1,0:T(8,128)(2,1)S(1)}, u32[]{:S(2)}, u32[]{:S(2)}) collective-permute-start(bf16[3,1,5,16,128]{4,3,2,1,0:T(8,128)(2,1)S(1)} %get-tuple-element.73), channel_id=1, source_target_pairs={{0,60},{4,0},{8,4},{12,8},{16,12},{20,16},{24,20},{28,24},{32,28},... | collective-permute-start | bytes 184328 | tf_op jit(solution)/shard_map/ppermute | solution.py:308
  29.5 0.9 add_convert_fusion
  30.4 4.1 %all-to-all-start = ((bf16[16,64,256]{2,1,0:T(8,128)(2,1)}), bf16[16,64,256]{2,1,0:T(8,128)(2,1)S(1)}, u32[]{:S(2)}, u32[]{:S(2)}) async-start(bf16[16,64,256]{2,1,0:T(8,128)(2,1)} %bitcast.4), calls=%async_computation | async-start | bytes 1048576 | tf_op jit(solution)/shard_map/all_to_all | solution.py:807
  34.5 0.1 pad_maximum_fusion
  34.6 0.0 copy-start.6
  34.6 0.0 copy-start.8
  34.6 0.0 copy-start.12
  34.7 0.0 copy-start.17
  34.7 2.7 %collective-permute-start.6 = (bf16[1,5,5,16,128]{4,3,2,1,0:T(8,128)(2,1)S(1)}, bf16[1,5,5,16,128]{4,3,2,1,0:T(8,128)(2,1)S(1)}, u32[]{:S(2)}, u32[]{:S(2)}) collective-permute-start(bf16[1,5,5,16,128]{4,3,2,1,0:T(8,128)(2,1)S(1)} %get-tuple-element.70), channel_id=1, source_target_pairs={{0,192},{64,0},{128,64},{192,128},{1,193},{65,1},{129,65},{193,129... | collective-permute-start | bytes 307208 | tf_op jit(solution)/shard_map/ppermute | solution.py:308
  37.3 0.0 collective-permute-start.5
  37.3 6.5 %collective-permute-done.6 = bf16[1,5,5,16,128]{4,3,2,1,0:T(8,128)(2,1)S(1)} collective-permute-done((bf16[1,5,5,16,128]{4,3,2,1,0:T(8,128)(2,1)S(1)}, bf16[1,5,5,16,128]{4,3,2,1,0:T(8,128)(2,1)S(1)}, u32[]{:S(2)}, u32[]{:S(2)}) %collective-permute-start.6) | collective-permute-done | bytes 102432 | tf_op jit(solution)/shard_map/ppermute | solution.py:308
  43.8 0.9 collective-permute-done.5
  44.7 0.6 copy-done.16
  45.4 12.8 %shard_map.140 = (bf16[400,128]{1,0:T(8,128)(2,1)S(1)}, f32[1200,128]{1,0:T(8,128)S(1)}, bf16[400,128]{1,0:T(8,128)(2,1)S(1)}, f32[80,128]{1,0:T(8,128)S(1)}, f3...) custom-call(s32[16,512]{1,0:T(8,128)S(1)} %bitcast.33, f32[3,1,512]{2,1,0:T(1,128)S(1)} %bitcast.37, ...), custom_call_target="tpu_custom_call" | custom-call | tf_op jit(solution)/shard_map/pallas_call | solution.py:291
  58.2 0.7 copy-done.18
  58.9 0.6 copy-done.20
  59.5 0.1 shard_map.141
  59.6 9.2 %all_to_all.20.pieces_ref = bf16[8,8,512]{2,1,0:T(8,128)(2,1)S(1)} all-to-all(bf16[8,8,512]{2,1,0:T(8,128)(2,1)S(1)} %shard_map.141), channel_id=1, replica_groups=mesh['gx'=4,'gy_0'=4,'gy_1'=4,'gz_0'=2,'gz_1'=2] {'gy_0','gz_0'}, dimensions={0} | all-to-all | bytes 131072 | tf_op jit(solution)/shard_map/all_to_all | solution.py:819
  68.8 0.7 coefficients.1
  69.5 9.0 %all_to_all.21.got_ref = bf16[8,8,512]{2,1,0:T(8,128)(2,1)S(1)} all-to-all(bf16[8,8,512]{2,1,0:T(8,128)(2,1)S(1)} %get-tuple-element.44), channel_id=1, replica_groups=mesh['gx'=4,'gy_0'=4,'gy_1'=4,'gz_0'=2,'gz_1'=2] {'gy_0','gz_0'}, dimensions={0} | all-to-all | bytes 131072 | tf_op jit(solution)/shard_map/all_to_all | solution.py:821
  78.5 0.1 shard_map.142
  78.6 16.0 %all_to_all.22.refs_4_.refs_16_ = bf16[16,104,256]{2,1,0:T(8,128)(2,1)S(1)} all-to-all(bf16[16,104,256]{2,1,0:T(8,128)(2,1)S(1)} %shard_map.142), channel_id=1, replica_groups=mesh['gx'=4,'gy_0'=4,'gy_1'=4,'gz_0'=2,'gz_1'=2] {'gx','gy_1'}, dimensions={0} | all-to-all | bytes 1703936 | tf_op jit(solution)/shard_map/all_to_all | solution.py:828
  94.6 4.9 %collective-permute-start.7 = (bf16[16,104,256]{2,1,0:T(8,128)(2,1)S(1)}, bf16[16,104,256]{2,1,0:T(8,128)(2,1)S(1)}, u32[]{:S(2)}, u32[]{:S(2)}) collective-permute-start(bf16[16,104,256]{2,1,0:T(8,128)(2,1)S(1)} %all_to_all.22.refs_4_.refs_16_), channel_id=1, source_target_pairs={{0,1},{1,0},{2,3},{3,2},{4,5},{5,4},{6,7},{7,6},{8,9},{9,8},{10,11... | collective-permute-start | bytes 2555912 | tf_op jit(solution)/shard_map/ppermute | solution.py:308
  99.4 0.8 collective-permute-start.8
  100.3 0.6 collective-permute-start.9
  100.9 2.9 %collective-permute-done.8.upper_ref = bf16[1,5,5,16,128]{4,3,2,1,0:T(8,128)(2,1)S(1)} collective-permute-done((bf16[1,5,5,16,128]{4,3,2,1,0:T(8,128)(2,1)S(1)}, bf16[1,5,5,16,128]{4,3,2,1,0:T(8,128)(2,1)S(1)}, u32[]{:S(2)}, u32[]{:S(2)}) %collective-permute-start.8) | collective-permute-done | bytes 102432 | tf_op jit(solution)/shard_map/ppermute | solution.py:308
  103.8 1.8 %collective-permute-done.9.lower_ref = bf16[1,5,5,16,128]{4,3,2,1,0:T(8,128)(2,1)S(1)} collective-permute-done((bf16[1,5,5,16,128]{4,3,2,1,0:T(8,128)(2,1)S(1)}, bf16[1,5,5,16,128]{4,3,2,1,0:T(8,128)(2,1)S(1)}, u32[]{:S(2)}, u32[]{:S(2)}) %collective-permute-start.9) | collective-permute-done | bytes 102432 | tf_op jit(solution)/shard_map/ppermute | solution.py:308
  105.6 0.1 shard_map.144
  105.6 0.9 collective-permute-start.10
  106.5 0.7 collective-permute-start.11
  107.2 1.6 %collective-permute-done.10.upper_ref = bf16[3,1,5,16,128]{4,3,2,1,0:T(8,128)(2,1)S(1)} collective-permute-done((bf16[3,1,5,16,128]{4,3,2,1,0:T(8,128)(2,1)S(1)}, bf16[3,1,5,16,128]{4,3,2,1,0:T(8,128)(2,1)S(1)}, u32[]{:S(2)}, u32[]{:S(2)}) %collective-permute-start.10) | collective-permute-done | bytes 61472 | tf_op jit(solution)/shard_map/ppermute | solution.py:308
  108.8 4.7 %collective-permute-done.11.lower_ref = bf16[3,1,5,16,128]{4,3,2,1,0:T(8,128)(2,1)S(1)} collective-permute-done((bf16[3,1,5,16,128]{4,3,2,1,0:T(8,128)(2,1)S(1)}, bf16[3,1,5,16,128]{4,3,2,1,0:T(8,128)(2,1)S(1)}, u32[]{:S(2)}, u32[]{:S(2)}) %collective-permute-start.11) | collective-permute-done | bytes 61472 | tf_op jit(solution)/shard_map/ppermute | solution.py:308
  113.5 2.7 %collective-permute-start.12 = (bf16[3,3,1,16,128]{4,3,2,1,0:T(8,128)(2,1)S(1)}, bf16[3,3,1,16,128]{4,3,2,1,0:T(8,128)(2,1)S(1)}, u32[]{:S(2)}, u32[]{:S(2)}) collective-permute-start(bf16[3,3,1,16,128]{4,3,2,1,0:T(8,128)(2,1)S(1)} %get-tuple-element.56), channel_id=1, source_target_pairs={{0,3},{1,0},{2,1},{3,2},{4,7},{5,4},{6,5},{7,6},{8,11},{9,8},{10,9... | collective-permute-start | bytes 110600 | tf_op jit(solution)/shard_map/ppermute | solution.py:308
  116.2 3.0 %collective-permute-start.13 = (bf16[3,3,1,16,128]{4,3,2,1,0:T(8,128)(2,1)S(1)}, bf16[3,3,1,16,128]{4,3,2,1,0:T(8,128)(2,1)S(1)}, u32[]{:S(2)}, u32[]{:S(2)}) collective-permute-start(bf16[3,3,1,16,128]{4,3,2,1,0:T(8,128)(2,1)S(1)} %get-tuple-element.57), channel_id=1, source_target_pairs={{0,1},{1,2},{2,3},{3,0},{4,5},{5,6},{6,7},{7,4},{8,9},{9,10},{10,1... | collective-permute-start | bytes 110600 | tf_op jit(solution)/shard_map/ppermute | solution.py:308
  119.3 2.9 %shard_map.143 = (f32[64,512]{1,0:T(8,128)S(1)}, f32[16,512]{1,0:T(8,128)S(1)}) custom-call(bf16[64,512]{1,0:T(8,128)(2,1)S(1)} %bitcast.23, bf16[64,512]{1,0:T(8,128)(2,1)S(1)} %bitcast.28, bf16[1024,512]{1,0:T(8,128)(2,1)S(1)} %copy-done.1, bf16[1024,512]{1,0:T(8,128)(2,1)S(1)} %copy-done.3, bf16[16,104,256]{2,1,0:T(8,128)(2,1)S(1)} %all_to_all.22.refs_4_.refs_16_, ...), custom_call_target="tpu_custom_call" | custom-call | flops 268435456 | bytes 2097152 | tf_op jit(solution)/shard_map/pallas_call | solution.py:291
  122.2 0.0 copy-start.15
  122.2 0.7 copy-done.15
  122.9 4.1 %shard_map.146 = (bf16[64,512]{1,0:T(8,128)(2,1)}, f32[3,1,512]{2,1,0:T(1,128)}, f32[64,64]{1,0:T(8,128)}, f32[16,64]{1,0:T(8,128)}) custom-call(bf16[64,512]{1,0:T(8,128)(2,1)S(1)} %bitcast.24, bf16[64,512]{1,0:T(8,128)(2,1)S(1)} %bitcast.29, s32[1,512]{1,0:T(1,128)S(1)} %bitcast.39, f32[4,64]{1,0:T(4,128)S(1)} %copy-done.16, bf16[64,64]{1,0:T(8,128)(2,1)S(1)} %copy-done.8, ...), custom_call_target="tpu_custom_call" | custom-call | flops 268435456 | bytes 2097152 | tf_op jit(solution)/shard_map/pallas_call | solution.py:291
  (47 shorter events, 0.2 us)
Async XLA Ops:
  0.6 1.9 %copy-start.4 = (bf16[1,1,1,64,512]{4,3,2,1,0:T(8,128)(2,1)S(1)}, bf16[1,1,1,64,512]{4,3,2,1,0:T(8,128)(2,1)}, u32[]{:S(2)}) copy-start(bf16[1,1,1,64,512]{4,3,2,1,0:T(8,128)(2,1)} %param.10) | copy-start | bytes 196612
  0.6 1.9 %copy-start.13 = (f32[1,1,1,3,512]{4,2,3,1,0:T(1,128)S(1)}, f32[1,1,1,3,512]{4,2,3,1,0:T(1,128)}, u32[]{:S(2)}) copy-start(f32[1,1,1,3,512]{4,2,3,1,0:T(1,128)} %param.12) | copy-start | bytes 18436
  2.6 0.8 copy-start.5
  3.4 0.8 copy-start.9
  4.2 7.3 %copy-start.22 = (bf16[432,128]{1,0:T(8,128)(2,1)S(1)}, bf16[432,128]{1,0:T(8,128)(2,1)}, u32[]{:S(2)}) copy-start(bf16[432,128]{1,0:T(8,128)(2,1)} %get-tuple-element.41) | copy-start | bytes 331780
  8.2 21.3 %collective-permute-start = (f32[1024,256]{1,0:T(8,128)S(1)}, f32[1024,256]{1,0:T(8,128)S(1)}, u32[]{:S(2)}, u32[]{:S(2)}) collective-permute-start(f32[1024,256]{1,0:T(8,128)S(1)} %get-tuple-element.40), channel_id=1, source_target_pairs={{0,1},{1,0},{2,3},{3,2},{4,5},{5,4},{6,7},{7,6},{8,9},{9,8},{10,11... | collective-permute-start | bytes 3145736 | tf_op jit(solution)/shard_map/ppermute | solution.py:308
  11.5 5.2 %copy-start.11 = (bf16[16,1024]{1,0:T(8,128)(2,1)S(1)}, bf16[16,1024]{1,0:T(8,128)(2,1)}, u32[]{:S(2)}) copy-start(bf16[16,1024]{1,0:T(8,128)(2,1)} %get-tuple-element.38.refs_3_.refs_5_) | copy-start | bytes 98308
  11.5 9.3 %collective-permute-start.1 = (bf16[3,3,1,16,128]{4,3,2,1,0:T(8,128)(2,1)S(1)}, bf16[3,3,1,16,128]{4,3,2,1,0:T(8,128)(2,1)S(1)}, u32[]{:S(2)}, u32[]{:S(2)}) collective-permute-start(bf16[3,3,1,16,128]{4,3,2,1,0:T(8,128)(2,1)S(1)} %get-tuple-element.74), channel_id=1, source_target_pairs={{0,1},{1,2},{2,3},{3,0},{4,5},{5,6},{6,7},{7,4},{8,9},{9,10},{10,1... | collective-permute-start | bytes 110600 | tf_op jit(solution)/shard_map/ppermute | solution.py:308
  16.7 7.3 %collective-permute-start.2 = (bf16[3,3,1,16,128]{4,3,2,1,0:T(8,128)(2,1)S(1)}, bf16[3,3,1,16,128]{4,3,2,1,0:T(8,128)(2,1)S(1)}, u32[]{:S(2)}, u32[]{:S(2)}) collective-permute-start(bf16[3,3,1,16,128]{4,3,2,1,0:T(8,128)(2,1)S(1)} %get-tuple-element.75), channel_id=1, source_target_pairs={{0,3},{1,0},{2,1},{3,2},{4,7},{5,4},{6,5},{7,6},{8,11},{9,8},{10,9... | collective-permute-start | bytes 110600 | tf_op jit(solution)/shard_map/ppermute | solution.py:308
  20.8 9.6 %copy-start = (bf16[1024,512]{1,0:T(8,128)(2,1)}, bf16[1024,512]{1,0:T(8,128)(2,1)S(1)}, u32[]{:S(2)}) copy-start(bf16[1024,512]{1,0:T(8,128)(2,1)S(1)} %get-tuple-element.45.refs_2_) | copy-start | bytes 3145732
  20.8 9.6 %copy-start.2 = (bf16[1024,512]{1,0:T(8,128)(2,1)}, bf16[1024,512]{1,0:T(8,128)(2,1)S(1)}, u32[]{:S(2)}) copy-start(bf16[1024,512]{1,0:T(8,128)(2,1)S(1)} %get-tuple-element.46.refs_3_) | copy-start | bytes 3145732
  24.0 10.5 %collective-permute-start.3 = (bf16[3,1,5,16,128]{4,3,2,1,0:T(8,128)(2,1)S(1)}, bf16[3,1,5,16,128]{4,3,2,1,0:T(8,128)(2,1)S(1)}, u32[]{:S(2)}, u32[]{:S(2)}) collective-permute-start(bf16[3,1,5,16,128]{4,3,2,1,0:T(8,128)(2,1)S(1)} %get-tuple-element.72), channel_id=1, source_target_pairs={{0,4},{4,8},{8,12},{12,16},{16,20},{20,24},{24,28},{28,32},{32,36}... | collective-permute-start | bytes 184328 | tf_op jit(solution)/shard_map/ppermute | solution.py:308
  25.4 9.1 %collective-permute-start.4 = (bf16[3,1,5,16,128]{4,3,2,1,0:T(8,128)(2,1)S(1)}, bf16[3,1,5,16,128]{4,3,2,1,0:T(8,128)(2,1)S(1)}, u32[]{:S(2)}, u32[]{:S(2)}) collective-permute-start(bf16[3,1,5,16,128]{4,3,2,1,0:T(8,128)(2,1)S(1)} %get-tuple-element.73), channel_id=1, source_target_pairs={{0,60},{4,0},{8,4},{12,8},{16,12},{20,16},{24,20},{28,24},{32,28},... | collective-permute-start | bytes 184328 | tf_op jit(solution)/shard_map/ppermute | solution.py:308
  30.4 29.1 %all-to-all-start = ((bf16[16,64,256]{2,1,0:T(8,128)(2,1)}), bf16[16,64,256]{2,1,0:T(8,128)(2,1)S(1)}, u32[]{:S(2)}, u32[]{:S(2)}) async-start(bf16[16,64,256]{2,1,0:T(8,128)(2,1)} %bitcast.4), calls=%async_computation | async-start | bytes 1048576 | tf_op jit(solution)/shard_map/all_to_all | solution.py:807
  34.6 10.1 %copy-start.6 = (bf16[1,1,1,64,512]{4,3,2,1,0:T(8,128)(2,1)S(1)}, bf16[1,1,1,64,512]{4,3,2,1,0:T(8,128)(2,1)}, u32[]{:S(2)}) copy-start(bf16[1,1,1,64,512]{4,3,2,1,0:T(8,128)(2,1)} %param.11) | copy-start | bytes 196612
  34.6 10.1 %copy-start.8 = (bf16[64,64]{1,0:T(8,128)(2,1)S(1)}, bf16[64,64]{1,0:T(8,128)(2,1)}, u32[]{:S(2)}) copy-start(bf16[64,64]{1,0:T(8,128)(2,1)} %refs_4_.3) | copy-start | bytes 24580
  34.6 10.1 %copy-start.12 = (s32[1,1,1,16,512]{4,3,2,1,0:T(8,128)S(1)}, s32[1,1,1,16,512]{4,3,2,1,0:T(8,128)}, u32[]{:S(2)}) copy-start(s32[1,1,1,16,512]{4,3,2,1,0:T(8,128)} %param.14) | copy-start | bytes 98308
  34.6 10.1 %copy-start.14 = (bf16[80,128]{1,0:T(8,128)(2,1)S(1)}, bf16[80,128]{1,0:T(8,128)(2,1)}, u32[]{:S(2)}) copy-start(bf16[80,128]{1,0:T(8,128)(2,1)} %get-tuple-element.42.refs_9_) | copy-start | bytes 61444
  34.7 10.1 %copy-start.17 = (f32[16,64]{1,0:T(8,128)S(1)}, f32[16,64]{1,0:T(8,128)}, u32[]{:S(2)}) copy-start(f32[16,64]{1,0:T(8,128)} %refs_3_.4) | copy-start | bytes 12292
  34.7 9.1 %collective-permute-start.6 = (bf16[1,5,5,16,128]{4,3,2,1,0:T(8,128)(2,1)S(1)}, bf16[1,5,5,16,128]{4,3,2,1,0:T(8,128)(2,1)S(1)}, u32[]{:S(2)}, u32[]{:S(2)}) collective-permute-start(bf16[1,5,5,16,128]{4,3,2,1,0:T(8,128)(2,1)S(1)} %get-tuple-element.70), channel_id=1, source_target_pairs={{0,192},{64,0},{128,64},{192,128},{1,193},{65,1},{129,65},{193,129... | collective-permute-start | bytes 307208 | tf_op jit(solution)/shard_map/ppermute | solution.py:308
  37.3 7.4 %collective-permute-start.5 = (bf16[1,5,5,16,128]{4,3,2,1,0:T(8,128)(2,1)S(1)}, bf16[1,5,5,16,128]{4,3,2,1,0:T(8,128)(2,1)S(1)}, u32[]{:S(2)}, u32[]{:S(2)}) collective-permute-start(bf16[1,5,5,16,128]{4,3,2,1,0:T(8,128)(2,1)S(1)} %get-tuple-element.71), channel_id=1, source_target_pairs={{0,64},{64,128},{128,192},{192,0},{1,65},{65,129},{129,193},{193,1... | collective-permute-start | bytes 307208 | tf_op jit(solution)/shard_map/ppermute | solution.py:308
  44.7 0.7 copy-start.16
  58.2 0.7 copy-start.18
  58.9 0.6 copy-start.20
  59.5 9.3 %copy-start.7 = (f32[2048,64]{0,1:T(8,128)S(1)}, f32[2048,64]{0,1:T(8,128)}, u32[]{:S(2)}) copy-start(f32[2048,64]{0,1:T(8,128)} %param.16) | copy-start | bytes 1572868
  78.6 20.9 %copy-start.21 = (bf16[400,128]{1,0:T(8,128)(2,1)S(1)}, bf16[400,128]{1,0:T(8,128)(2,1)}, u32[]{:S(2)}) copy-start(bf16[400,128]{1,0:T(8,128)(2,1)} %copy-done.20) | copy-start | bytes 307204
  78.6 21.7 %copy-start.19 = (bf16[400,128]{1,0:T(8,128)(2,1)S(1)}, bf16[400,128]{1,0:T(8,128)(2,1)}, u32[]{:S(2)}) copy-start(bf16[400,128]{1,0:T(8,128)(2,1)} %copy-done.18) | copy-start | bytes 307204
  78.6 40.7 %copy-start.3 = (bf16[1024,512]{1,0:T(8,128)(2,1)S(1)}, bf16[1024,512]{1,0:T(8,128)(2,1)}, u32[]{:S(2)}) copy-start(bf16[1024,512]{1,0:T(8,128)(2,1)} %copy-done.2) | copy-start | bytes 3145732
  94.6 24.7 %copy-start.1 = (bf16[1024,512]{1,0:T(8,128)(2,1)S(1)}, bf16[1024,512]{1,0:T(8,128)(2,1)}, u32[]{:S(2)}) copy-start(bf16[1024,512]{1,0:T(8,128)(2,1)} %copy-done) | copy-start | bytes 3145732
  94.6 27.6 %collective-permute-start.7 = (bf16[16,104,256]{2,1,0:T(8,128)(2,1)S(1)}, bf16[16,104,256]{2,1,0:T(8,128)(2,1)S(1)}, u32[]{:S(2)}, u32[]{:S(2)}) collective-permute-start(bf16[16,104,256]{2,1,0:T(8,128)(2,1)S(1)} %all_to_all.22.refs_4_.refs_16_), channel_id=1, source_target_pairs={{0,1},{1,0},{2,3},{3,2},{4,5},{5,4},{6,7},{7,6},{8,9},{9,8},{10,11... | collective-permute-start | bytes 2555912 | tf_op jit(solution)/shard_map/ppermute | solution.py:308
  99.4 4.4 %collective-permute-start.8 = (bf16[1,5,5,16,128]{4,3,2,1,0:T(8,128)(2,1)S(1)}, bf16[1,5,5,16,128]{4,3,2,1,0:T(8,128)(2,1)S(1)}, u32[]{:S(2)}, u32[]{:S(2)}) collective-permute-start(bf16[1,5,5,16,128]{4,3,2,1,0:T(8,128)(2,1)S(1)} %bitcast.41), channel_id=1, source_target_pairs={{0,192},{64,0},{128,64},{192,128},{1,193},{65,1},{129,65},{193,129... | collective-permute-start | bytes 307208 | tf_op jit(solution)/shard_map/ppermute | solution.py:308
  100.3 5.3 %collective-permute-start.9 = (bf16[1,5,5,16,128]{4,3,2,1,0:T(8,128)(2,1)S(1)}, bf16[1,5,5,16,128]{4,3,2,1,0:T(8,128)(2,1)S(1)}, u32[]{:S(2)}, u32[]{:S(2)}) collective-permute-start(bf16[1,5,5,16,128]{4,3,2,1,0:T(8,128)(2,1)S(1)} %bitcast.40), channel_id=1, source_target_pairs={{0,64},{64,128},{128,192},{192,0},{1,65},{65,129},{129,193},{193,1... | collective-permute-start | bytes 307208 | tf_op jit(solution)/shard_map/ppermute | solution.py:308
  105.6 3.1 %collective-permute-start.10 = (bf16[3,1,5,16,128]{4,3,2,1,0:T(8,128)(2,1)S(1)}, bf16[3,1,5,16,128]{4,3,2,1,0:T(8,128)(2,1)S(1)}, u32[]{:S(2)}, u32[]{:S(2)}) collective-permute-start(bf16[3,1,5,16,128]{4,3,2,1,0:T(8,128)(2,1)S(1)} %get-tuple-element.53), channel_id=1, source_target_pairs={{0,60},{4,0},{8,4},{12,8},{16,12},{20,16},{24,20},{28,24},{32,28},... | collective-permute-start | bytes 184328 | tf_op jit(solution)/shard_map/ppermute | solution.py:308
  106.5 7.0 %collective-permute-start.11 = (bf16[3,1,5,16,128]{4,3,2,1,0:T(8,128)(2,1)S(1)}, bf16[3,1,5,16,128]{4,3,2,1,0:T(8,128)(2,1)S(1)}, u32[]{:S(2)}, u32[]{:S(2)}) collective-permute-start(bf16[3,1,5,16,128]{4,3,2,1,0:T(8,128)(2,1)S(1)} %get-tuple-element.54), channel_id=1, source_target_pairs={{0,4},{4,8},{8,12},{12,16},{16,20},{20,24},{24,28},{28,32},{32,36}... | collective-permute-start | bytes 184328 | tf_op jit(solution)/shard_map/ppermute | solution.py:308
  113.5 8.6 %collective-permute-start.12 = (bf16[3,3,1,16,128]{4,3,2,1,0:T(8,128)(2,1)S(1)}, bf16[3,3,1,16,128]{4,3,2,1,0:T(8,128)(2,1)S(1)}, u32[]{:S(2)}, u32[]{:S(2)}) collective-permute-start(bf16[3,3,1,16,128]{4,3,2,1,0:T(8,128)(2,1)S(1)} %get-tuple-element.56), channel_id=1, source_target_pairs={{0,3},{1,0},{2,1},{3,2},{4,7},{5,4},{6,5},{7,6},{8,11},{9,8},{10,9... | collective-permute-start | bytes 110600 | tf_op jit(solution)/shard_map/ppermute | solution.py:308
  116.2 5.9 %collective-permute-start.13 = (bf16[3,3,1,16,128]{4,3,2,1,0:T(8,128)(2,1)S(1)}, bf16[3,3,1,16,128]{4,3,2,1,0:T(8,128)(2,1)S(1)}, u32[]{:S(2)}, u32[]{:S(2)}) collective-permute-start(bf16[3,3,1,16,128]{4,3,2,1,0:T(8,128)(2,1)S(1)} %get-tuple-element.57), channel_id=1, source_target_pairs={{0,1},{1,2},{2,3},{3,0},{4,5},{5,6},{6,7},{7,4},{8,9},{9,10},{10,1... | collective-permute-start | bytes 110600 | tf_op jit(solution)/shard_map/ppermute | solution.py:308
  119.3 2.9 %copy-start.10 = (bf16[16,1024]{1,0:T(8,128)(2,1)S(1)}, bf16[16,1024]{1,0:T(8,128)(2,1)}, u32[]{:S(2)}) copy-start(bf16[16,1024]{1,0:T(8,128)(2,1)} %get-tuple-element.35.refs_3_.refs_8_) | copy-start | bytes 98308
  122.2 0.7 copy-start.15

commit v9 on v8

--- a/solution.py
+++ b/solution.py
@@ -262,6 +262,7 @@
             pltpu.VMEM((GROUPS * HIGH, 128), bf16),
             pltpu.VMEM((GROUPS * HIGH, 128), f32),
         ],
+        limit=False,
     )
 
 
@@ -318,7 +319,18 @@
     return (row == picked).astype(jnp.float32).astype(jnp.bfloat16)
 
 
-def pack_kernel(h_ref, kind_ref, pos_ref, miller_ref, cells_ref, core_ref, mine_ref, next_ref):
+def pack_kernel(
+    h_ref,
+    kind_ref,
+    pos_ref,
+    miller_ref,
+    cells_ref,
+    core_ref,
+    first_ref,
+    last_ref,
+    mine_ref,
+    next_ref,
+):
     f32, bf16 = jnp.float32, jnp.bfloat16
     _, atoms = h_ref.shape
     none = jnp.zeros((1, atoms), f32)
@@ -334,6 +346,9 @@
     flat = jnp.transpose(rows).astype(bf16)
     cells_ref[...] = flat[0 : cells_ref.shape[0]]
     core_ref[...] = flat[cells_ref.shape[0] :]
+    for n in range(9):
+        first_ref[n // 3, n % 3, 0] = flat[48 * n : 48 * n + 16]
+        last_ref[n // 3, n % 3, 0] = flat[48 * n + 32 : 48 * n + 48]
     m = miller_ref[...].astype(f32)
     tall = jnp.concatenate([m, m, m, jnp.zeros((7, m.shape[1]), f32)], axis=0).astype(bf16)
     runs = m.shape[1] // (2 * CHUNK)
@@ -349,6 +364,7 @@
 
 def pack(h, kinds, pos, miller):
     half = jax.ShapeDtypeStruct((16, miller.shape[1] // 2), jnp.bfloat16)
+    side = jax.ShapeDtypeStruct((3, 3, 1, 16, 128), jnp.bfloat16)
     return fetching_call(
         pack_kernel,
         (h, kinds, pos, miller),
@@ -356,6 +372,8 @@
         (
             jax.ShapeDtypeStruct((432, 128), jnp.bfloat16),
             jax.ShapeDtypeStruct((h.shape[1] - 432, 128), jnp.bfloat16),
+            side,
+            side,
             half,
             half,
         ),
@@ -655,72 +673,74 @@
 
 def partial_kernel(pieces_ref, sums_ref, out_ref):
     f32, bf16 = jnp.float32, jnp.bfloat16
-    tower, rows, _ = out_ref.shape
-    width = pieces_ref.shape[2]
     total = jnp.sum(pieces_ref[...].astype(f32), axis=0)
-    hi, lo = split_two(sums_ref[...])
-    whole = jnp.concatenate([total, hi.astype(f32), lo.astype(f32)], axis=1)
-    out_ref[...] = whole.reshape(tower, rows, width + 256).astype(bf16)
+    extra = out_ref.shape[1] - total.shape[0]
+    sums = sums_ref[...]
+    wide = jnp.concatenate([sums[0:extra], sums[extra : 2 * extra]], axis=1)
+    whole = jnp.concatenate([total, wide], axis=0).astype(bf16)
+    out_ref[...] = jnp.broadcast_to(whole[None], out_ref.shape)
 
 
 def partial_sums(pieces, sums, tower):
-    shape = (tower, pieces.shape[1] // tower, pieces.shape[2] + 256)
+    shape = (tower, pieces.shape[1] + 24, pieces.shape[2])
     outs = (jax.ShapeDtypeStruct(shape, jnp.bfloat16),)
     return small_call(partial_kernel, (pieces, sums), outs)[0]
 
 
-def coefficient_kernel(norm_atoms, norm_k, pieces_ref, filter_in, out_ref, filter_ref, tile, sem):
-    f32 = jnp.float32
-    _, share, _ = pieces_ref.shape
-    channels = filter_ref.shape[1]
-    width = 4 * channels
-    start = lax.axis_index(GX_GY_GZ) * share
-    lane = pl.multiple_of(start // 128 * 128, 128)
-    copy = pltpu.make_async_copy(filter_in.at[:, pl.ds(lane, 128)], tile, sem)
+def coefficient_kernel(
+    norm_atoms, norm_k, pieces_ref, filter_in, out_ref, filter_ref, tile, turned, all_filter, sem
+):
+    f32, bf16 = jnp.float32, jnp.bfloat16
+    share, _ = filter_ref.shape
+    tower = pieces_ref.shape[0]
+    rows = tower * share
+    span = tile.shape[1]
+    lane = pl.multiple_of(lax.axis_index("gx") * span, span)
+    copy = pltpu.make_async_copy(filter_in.at[:, pl.ds(lane, span)], tile, sem)
     copy.start()
     both = jnp.sum(pieces_ref[...].astype(f32), axis=0)
     copy.wait()
-    turned = jnp.transpose(tile[...])
-    pick = lax.broadcasted_iota(jnp.int32, (128 // share, share, channels), 0)
-    inside = (start - lane) // share
-    filt = jnp.sum(
-        jnp.where(pick == inside, turned.reshape(128 // share, share, channels), 0.0), axis=0
-    )
-    coeffs, filter_ref[...] = coefficients(both[:, 0:width], filt, norm_atoms, norm_k)
-    hi, lo = split_two(both[:, width : width + 128] + both[:, width + 128 :])
-    sent = jnp.concatenate([coeffs, hi.astype(f32), lo.astype(f32)], axis=1)
-    out_ref[...] = jnp.broadcast_to(sent[None], out_ref.shape).astype(jnp.bfloat16)
-
-
-def make_coefficients(pieces, filter_columns, norm_atoms, norm_k):
-    share, channels = pieces.shape[1], filter_columns.shape[0]
+    turned[...] = jnp.transpose(tile[...])
+    inner, least = [lax.axis_size(axis) for axis in ("gy_1", "gz_0")]
+    filters = []
+    for w in range(tower):
+        group = (w // least * inner + lax.axis_index("gy_1")) * least + w % least
+        at = pl.multiple_of((group * 2 + lax.axis_index(PAIR)) * share, share)
+        filters.append(turned[pl.ds(at, share), :])
+    filt = jnp.concatenate(filters, axis=0)
+    coeffs, all_filter[...] = coefficients(both[0:rows], filt, norm_atoms, norm_k)
+    mine = lax.axis_index(TOWER)
+    filter_ref[...] = all_filter[pl.ds(pl.multiple_of(mine * share, share), share), :]
+    tall = jnp.concatenate([both[rows:, 0:128], both[rows:, 128:256]], axis=0)
+    hi, lo = split_two(tall[0 : out_ref.shape[1] - rows])
+    strip = jnp.concatenate(
+        [coeffs, jnp.concatenate([hi.astype(f32), lo.astype(f32)], axis=1)], axis=0
+    ).astype(bf16)
+    out_ref[...] = jnp.broadcast_to(strip[None], out_ref.shape)
+
+
+def make_strip(pieces, filter_columns, sheet, cut, norm_atoms, norm_k):
+    tower = pieces.shape[0]
+    channels, points = filter_columns.shape
+    share = points // (2 * tower * sheet)
+    span = points // lax.axis_size("gx")
     return pl.pallas_call(
         functools.partial(coefficient_kernel, norm_atoms, norm_k),
         out_shape=(
-            jax.ShapeDtypeStruct(pieces.shape, jnp.bfloat16),
+            jax.ShapeDtypeStruct((sheet, tower * share + cut, pieces.shape[2]), jnp.bfloat16),
             jax.ShapeDtypeStruct((share, channels), jnp.float32),
         ),
         in_specs=[WHOLE, FAR],
         out_specs=(WHOLE, WHOLE),
-        scratch_shapes=[pltpu.VMEM((channels, 128), jnp.float32), pltpu.SemaphoreType.DMA],
+        scratch_shapes=[
+            pltpu.VMEM((channels, span), jnp.float32),
+            pltpu.VMEM((span, channels), jnp.float32),
+            pltpu.VMEM((tower * share, channels), jnp.float32),
+            pltpu.SemaphoreType.DMA,
+        ],
         compiler_params=LIMIT,
         name="coefficients",
     )(pieces, filter_columns)
-
-
-def strip_kernel(got_ref, out_ref):
-    f32 = jnp.float32
-    tower, share, _ = got_ref.shape
-    width = out_ref.shape[2]
-    run, cut = tower * share, out_ref.shape[1] - tower * share
-    got = got_ref[...].astype(f32).reshape(run, width + 256)
-    strip = jnp.concatenate([got[:, 0:width], got[0:cut, width:]], axis=0)
-    out_ref[...] = jnp.broadcast_to(strip[None], out_ref.shape).astype(jnp.bfloat16)
-
-
-def make_strip(got, sheet, width, cut):
-    shape = (sheet, got.shape[0] * got.shape[1] + cut, width)
-    return small_call(strip_kernel, (got,), (jax.ShapeDtypeStruct(shape, got.dtype),))[0]
 
 
 def fold_x_kernel(mid_ref, upper_ref, lower_ref, first_ref, last_ref, rest_ref):
@@ -791,9 +811,9 @@
     norm_k = points ** (-0.5)
     half = points // 2
 
-    cells, core, miller_mine, miller_next = pack(h, kinds, pos, miller_triples)
+    cells, core, first, last, miller_mine, miller_next = pack(h, kinds, pos, miller_triples)
     cells = cells.reshape(3, 3, 3, 16, 128)
-    below, above = sent_out(cells, GZ, 2)
+    below, above = from_behind(last, GZ, 1), from_behind(first, GZ, -1)
     cos_next, sin_next, part_next = phase_sums(pos, miller_next, h, dy)
     received = from_behind(part_next, PAIR, 1)
     cells = jnp.concatenate([below, cells, above], axis=2)
@@ -817,14 +837,15 @@
     )
     parts = partial_sums(pieces, sums, tower)
     pieces = lax.all_to_all(parts, TOWER, 0, 0)
-    sent, filter_share = make_coefficients(pieces, reciprocal_kernel.T, norm_atoms, norm_k)
-    got = lax.all_to_all(sent, TOWER, 0, 0)
 
     upper = from_behind(low.reshape(1, 5, 5, 16, 128), "gx", -1)
     lower = from_behind(high.reshape(1, 5, 5, 16, 128), "gx", 1)
     first, last, rest = fold_x(mid.reshape(3, 5, 5, 16, 128), upper, lower)
     upper, lower = from_behind(first, GY, -1), from_behind(last, GY, 1)
-    strip = make_strip(got, sheet, width, (channels + distance_kernel.shape[0]) // 2)
+    cut = (channels + distance_kernel.shape[0]) // 2
+    strip, filter_share = make_strip(
+        pieces, reciprocal_kernel.T, sheet, cut, norm_atoms, norm_k
+    )
     got = lax.all_to_all(strip, SHEET, 0, 0)
     first, last, inner = fold_y(rest, upper, lower)
     upper, lower = from_behind(first, GZ, -1), from_behind(last, GZ, 1)

time: 128 us -> 128 us (level)
  blocking collectives: 34.2 us -> 28.8 us
  Pallas kernels: 30.6 us -> 33.4 us
  starting transfers between devices: 34.3 us -> 36.7 us
    all_to_all x1 -> x0, blocking collectives: 8.99 us -> none  [whole(): got = lax.all_to_all(sent, TOWER, 0, 0)]
    all_to_all x1, blocking collectives: 9.19 us -> 12.7 us  [whole(): pieces = lax.all_to_all(parts, TOWER, 0, 0)]
    pallas_call x6, Pallas kernels: 29.7 us -> 32.4 us  [fetching_call(): pl.pallas_call(body, out_shape=outs, in_specs=[FAR] * n + list(in_specs o...]
    ppermute x14, starting transfers between devices: 30.2 us -> 32.5 us  [from_behind(): lax.ppermute(x, axis, [(i, (i + by) % devices) for i in range(devices)])]
    unnamed x46 -> x54, local copies, waits for them, and re-layouts: 4.28 us -> 3.73 us
  transfers between devices with their start and end apart: 15 -> 15, of which waited for: 7 -> 7; matrix products, arithmetic and copies ran while one was open for 1% -> 1% of each run, Pallas kernels for 16% -> 18%
where the time goes in v9:
time: 128 us; the launch traced here: 127 us
  starting transfers between devices  36.7 us (29%)
  Pallas kernels  33.4 us (26%)
  blocking collectives  28.8 us (22%)
  waiting for transfers between devices  22.2 us (17%)
  local copies, waits for them, and re-layouts  3.74 us (3%)
    ppermute x14, starting transfers between devices, from_behind(): lax.ppermute(x, axis, [(i, (i + by) % devices) for i in range(devices)])  32.5 us
    pallas_call x6, Pallas kernels, fetching_call(): pl.pallas_call(body, out_shape=outs, in_specs=[FAR] * n + list(in_specs o...  32.4 us
    ppermute x14, waiting for transfers between devices, from_behind(): lax.ppermute(x, axis, [(i, (i + by) % devices) for i in range(devices)])  22.2 us
    all_to_all x1, blocking collectives, whole(): got = lax.all_to_all(strip, SHEET, 0, 0)  16.1 us
    all_to_all x1, blocking collectives, whole(): pieces = lax.all_to_all(parts, TOWER, 0, 0)  12.7 us
    all_to_all x1, starting transfers between devices, whole(): lax.all_to_all(paired.reshape(sheet, half // sheet, width), SHEET, 0, 0)  4.19 us
    unnamed x54, local copies, waits for them, and re-layouts  3.73 us
  transfers between devices with their start and end apart: 15, of which 7 were waited for; matrix products, arithmetic and copies ran while one was open for 1% of the time, Pallas kernels for 18%

profile of v9, /device:TPU:1, one launch (start us, length us, event | category | flops | bytes accessed | tf_op | source)
XLA Modules:
  0.0 127.0 jit_solution(14980657471172604736)
XLA Ops:
  0.6 0.0 copy-start.15
  0.7 1.9 %shard_map.137 = (bf16[432,128]{1,0:T(8,128)(2,1)}, bf16[80,128]{1,0:T(8,128)(2,1)}, bf16[3,3,1,16,128]{4,3,2,1,0:T(8,128)(2,1)}, bf16[3,3,1,16,128]{4,3,2,1,0:T...) custom-call(bf16[64,512]{1,0:T(8,128)(2,1)} %bitcast.19, s32[1,512]{1,0:T(1,128)} %bitcast.34, ...), custom_call_target="tpu_custom_call" | custom-call | tf_op jit(solution)/shard_map/pallas_call | solution.py:292
  2.6 0.0 copy-start.6
  2.6 0.8 copy-done.6
  3.4 0.8 copy-done.11
  4.2 4.0 %shard_map.138 = (bf16[1024,512]{1,0:T(8,128)(2,1)S(1)}, bf16[1024,512]{1,0:T(8,128)(2,1)S(1)}, f32[1024,256]{1,0:T(8,128)S(1)}) custom-call(f32[3,1,512]{2,1,0:T(1,128)S(1)} %bitcast.32, bf16[64,512]{1,0:T(8,128)(2,1)S(1)} %bitcast.20, bf16[64,512]{1,0:T(8,128)(2,1)S(1)} %bitcast.25, bf16[16,1024]{1,0:T(8,128)(2,1)S(1)} %copy-done.11), custom_call_target="tpu_custom_call" | custom-call | flops 402653184 | bytes 3145728 | tf_op jit(solution)/shard_map/pallas_call | solution.py:292
  8.2 3.3 %collective-permute-start = (f32[1024,256]{1,0:T(8,128)S(1)}, f32[1024,256]{1,0:T(8,128)S(1)}, u32[]{:S(2)}, u32[]{:S(2)}) collective-permute-start(f32[1024,256]{1,0:T(8,128)S(1)} %get-tuple-element.42), channel_id=1, source_target_pairs={{0,1},{1,0},{2,3},{3,2},{4,5},{5,4},{6,7},{7,6},{8,9},{9,8},{10,11... | collective-permute-start | bytes 3145736 | tf_op jit(solution)/shard_map/ppermute | solution.py:309
  11.5 5.2 %collective-permute-start.1 = (bf16[3,3,1,16,128]{4,3,2,1,0:T(8,128)(2,1)S(1)}, bf16[3,3,1,16,128]{4,3,2,1,0:T(8,128)(2,1)S(1)}, u32[]{:S(2)}, u32[]{:S(2)}) collective-permute-start(bf16[3,3,1,16,128]{4,3,2,1,0:T(8,128)(2,1)S(1)} %copy-done.26), channel_id=1, source_target_pairs={{0,1},{1,2},{2,3},{3,0},{4,5},{5,6},{6,7},{7,4},{8,9},{9,10},{10,1... | collective-permute-start | bytes 110600 | tf_op jit(solution)/shard_map/ppermute | solution.py:309
  16.7 0.0 collective-permute-start.2
  16.7 4.0 %shard_map.139 = (bf16[1024,512]{1,0:T(8,128)(2,1)S(1)}, bf16[1024,512]{1,0:T(8,128)(2,1)S(1)}, f32[1024,256]{1,0:T(8,128)S(1)}) custom-call(f32[3,1,512]{2,1,0:T(1,128)S(1)} %bitcast.33, bf16[64,512]{1,0:T(8,128)(2,1)S(1)} %bitcast.21, bf16[64,512]{1,0:T(8,128)(2,1)S(1)} %bitcast.26, bf16[16,1024]{1,0:T(8,128)(2,1)S(1)} %copy-done.13), custom_call_target="tpu_custom_call" | custom-call | flops 402653184 | bytes 3145728 | tf_op jit(solution)/shard_map/pallas_call | solution.py:292
  20.8 0.0 collective-permute-done.1
  20.8 3.2 %collective-permute-done.2 = bf16[3,3,1,16,128]{4,3,2,1,0:T(8,128)(2,1)S(1)} collective-permute-done((bf16[3,3,1,16,128]{4,3,2,1,0:T(8,128)(2,1)S(1)}, bf16[3,3,1,16,128]{4,3,2,1,0:T(8,128)(2,1)S(1)}, u32[]{:S(2)}, u32[]{:S(2)}) %collective-permute-start.2) | collective-permute-done | bytes 36896 | tf_op jit(solution)/shard_map/ppermute | solution.py:309
  24.0 1.4 %collective-permute-start.3 = (bf16[3,1,5,16,128]{4,3,2,1,0:T(8,128)(2,1)S(1)}, bf16[3,1,5,16,128]{4,3,2,1,0:T(8,128)(2,1)S(1)}, u32[]{:S(2)}, u32[]{:S(2)}) collective-permute-start(bf16[3,1,5,16,128]{4,3,2,1,0:T(8,128)(2,1)S(1)} %get-tuple-element.76), channel_id=1, source_target_pairs={{0,4},{4,8},{8,12},{12,16},{16,20},{20,24},{24,28},{28,32},{32,36}... | collective-permute-start | bytes 184328 | tf_op jit(solution)/shard_map/ppermute | solution.py:309
  25.5 4.0 %collective-permute-start.4 = (bf16[3,1,5,16,128]{4,3,2,1,0:T(8,128)(2,1)S(1)}, bf16[3,1,5,16,128]{4,3,2,1,0:T(8,128)(2,1)S(1)}, u32[]{:S(2)}, u32[]{:S(2)}) collective-permute-start(bf16[3,1,5,16,128]{4,3,2,1,0:T(8,128)(2,1)S(1)} %get-tuple-element.77), channel_id=1, source_target_pairs={{0,60},{4,0},{8,4},{12,8},{16,12},{20,16},{24,20},{28,24},{32,28},... | collective-permute-start | bytes 184328 | tf_op jit(solution)/shard_map/ppermute | solution.py:309
  29.5 0.9 add_convert_fusion
  30.4 4.2 %all-to-all-start = ((bf16[16,64,256]{2,1,0:T(8,128)(2,1)}), bf16[16,64,256]{2,1,0:T(8,128)(2,1)S(1)}, u32[]{:S(2)}, u32[]{:S(2)}) async-start(bf16[16,64,256]{2,1,0:T(8,128)(2,1)} %bitcast.4), calls=%async_computation | async-start | bytes 1048576 | tf_op jit(solution)/shard_map/all_to_all | solution.py:827
  34.6 0.1 pad_maximum_fusion
  34.7 2.7 %collective-permute-start.6 = (bf16[1,5,5,16,128]{4,3,2,1,0:T(8,128)(2,1)S(1)}, bf16[1,5,5,16,128]{4,3,2,1,0:T(8,128)(2,1)S(1)}, u32[]{:S(2)}, u32[]{:S(2)}) collective-permute-start(bf16[1,5,5,16,128]{4,3,2,1,0:T(8,128)(2,1)S(1)} %get-tuple-element.74), channel_id=1, source_target_pairs={{0,192},{64,0},{128,64},{192,128},{1,193},{65,1},{129,65},{193,129... | collective-permute-start | bytes 307208 | tf_op jit(solution)/shard_map/ppermute | solution.py:309
  37.3 0.0 collective-permute-start.5
  37.3 6.4 %collective-permute-done.6 = bf16[1,5,5,16,128]{4,3,2,1,0:T(8,128)(2,1)S(1)} collective-permute-done((bf16[1,5,5,16,128]{4,3,2,1,0:T(8,128)(2,1)S(1)}, bf16[1,5,5,16,128]{4,3,2,1,0:T(8,128)(2,1)S(1)}, u32[]{:S(2)}, u32[]{:S(2)}) %collective-permute-start.6) | collective-permute-done | bytes 102432 | tf_op jit(solution)/shard_map/ppermute | solution.py:309
  43.7 0.9 collective-permute-done.5
  44.7 0.6 copy-done.22
  45.3 15.4 %shard_map.140 = (bf16[400,128]{1,0:T(8,128)(2,1)}, f32[1200,128]{1,0:T(8,128)}, bf16[400,128]{1,0:T(8,128)(2,1)}, f32[80,128]{1,0:T(8,128)}, f32[8,512]{1,0:T(8,128)}, /*index=5*/f32[64,128]{1,0:T(8,128)}) custom-call(s32[16,512]{1,0:T(8,128)} %bitcast.41, f32[3,1,512]{2,1,0:T(1,128)} %bitcast.31, bf16[64,512]{1,0:T(8,128)(2,1)} %bitcast.24, ...), custom_call_target="tpu_custom_call" | custom-call | tf_op jit(solution)/shard_map/pallas_call | solution.py:292
  60.8 0.0 copy-start.14
  60.8 0.7 copy-done.14
  61.5 0.1 shard_map.141
  61.6 0.0 copy-start.8
  61.6 12.7 %all_to_all.15.pieces_ref = bf16[8,88,256]{2,1,0:T(8,128)(2,1)S(1)} all-to-all(bf16[8,88,256]{2,1,0:T(8,128)(2,1)S(1)} %shard_map.141), channel_id=1, replica_groups=mesh['gx'=4,'gy_0'=4,'gy_1'=4,'gz_0'=2,'gz_1'=2] {'gy_0','gz_0'}, dimensions={0} | all-to-all | bytes 720896 | tf_op jit(solution)/shard_map/all_to_all | solution.py:839
  74.4 0.9 coefficients.1
  75.3 16.1 %all_to_all.16.refs_4_.refs_16_ = bf16[16,104,256]{2,1,0:T(8,128)(2,1)S(1)} all-to-all(bf16[16,104,256]{2,1,0:T(8,128)(2,1)S(1)} %get-tuple-element.48), channel_id=1, replica_groups=mesh['gx'=4,'gy_0'=4,'gy_1'=4,'gz_0'=2,'gz_1'=2] {'gx','gy_1'}, dimensions={0} | all-to-all | bytes 1703936 | tf_op jit(solution)/shard_map/all_to_all | solution.py:849
  91.4 4.9 %collective-permute-start.7 = (bf16[16,104,256]{2,1,0:T(8,128)(2,1)S(1)}, bf16[16,104,256]{2,1,0:T(8,128)(2,1)S(1)}, u32[]{:S(2)}, u32[]{:S(2)}) collective-permute-start(bf16[16,104,256]{2,1,0:T(8,128)(2,1)S(1)} %all_to_all.16.refs_4_.refs_16_), channel_id=1, source_target_pairs={{0,1},{1,0},{2,3},{3,2},{4,5},{5,4},{6,7},{7,6},{8,9},{9,8},{10,11... | collective-permute-start | bytes 2555912 | tf_op jit(solution)/shard_map/ppermute | solution.py:309
  96.3 0.8 collective-permute-start.8
  97.1 0.6 collective-permute-start.9
  97.8 2.9 %collective-permute-done.8.upper_ref = bf16[1,5,5,16,128]{4,3,2,1,0:T(8,128)(2,1)S(1)} collective-permute-done((bf16[1,5,5,16,128]{4,3,2,1,0:T(8,128)(2,1)S(1)}, bf16[1,5,5,16,128]{4,3,2,1,0:T(8,128)(2,1)S(1)}, u32[]{:S(2)}, u32[]{:S(2)}) %collective-permute-start.8) | collective-permute-done | bytes 102432 | tf_op jit(solution)/shard_map/ppermute | solution.py:309
  100.6 1.8 %collective-permute-done.9.lower_ref = bf16[1,5,5,16,128]{4,3,2,1,0:T(8,128)(2,1)S(1)} collective-permute-done((bf16[1,5,5,16,128]{4,3,2,1,0:T(8,128)(2,1)S(1)}, bf16[1,5,5,16,128]{4,3,2,1,0:T(8,128)(2,1)S(1)}, u32[]{:S(2)}, u32[]{:S(2)}) %collective-permute-start.9) | collective-permute-done | bytes 102432 | tf_op jit(solution)/shard_map/ppermute | solution.py:309
  102.4 0.1 shard_map.143
  102.5 3.8 %collective-permute-start.10 = (bf16[3,1,5,16,128]{4,3,2,1,0:T(8,128)(2,1)S(1)}, bf16[3,1,5,16,128]{4,3,2,1,0:T(8,128)(2,1)S(1)}, u32[]{:S(2)}, u32[]{:S(2)}) collective-permute-start(bf16[3,1,5,16,128]{4,3,2,1,0:T(8,128)(2,1)S(1)} %get-tuple-element.57), channel_id=1, source_target_pairs={{0,60},{4,0},{8,4},{12,8},{16,12},{20,16},{24,20},{28,24},{32,28},... | collective-permute-start | bytes 184328 | tf_op jit(solution)/shard_map/ppermute | solution.py:309
  106.3 1.3 %collective-permute-done.10.upper_ref = bf16[3,1,5,16,128]{4,3,2,1,0:T(8,128)(2,1)S(1)} collective-permute-done((bf16[3,1,5,16,128]{4,3,2,1,0:T(8,128)(2,1)S(1)}, bf16[3,1,5,16,128]{4,3,2,1,0:T(8,128)(2,1)S(1)}, u32[]{:S(2)}, u32[]{:S(2)}) %collective-permute-start.10) | collective-permute-done | bytes 61472 | tf_op jit(solution)/shard_map/ppermute | solution.py:309
  107.6 5.7 %collective-permute-done.11.lower_ref = bf16[3,1,5,16,128]{4,3,2,1,0:T(8,128)(2,1)S(1)} collective-permute-done((bf16[3,1,5,16,128]{4,3,2,1,0:T(8,128)(2,1)S(1)}, bf16[3,1,5,16,128]{4,3,2,1,0:T(8,128)(2,1)S(1)}, u32[]{:S(2)}, u32[]{:S(2)}) %collective-permute-start.11) | collective-permute-done | bytes 61472 | tf_op jit(solution)/shard_map/ppermute | solution.py:309
  113.3 2.7 %collective-permute-start.12 = (bf16[3,3,1,16,128]{4,3,2,1,0:T(8,128)(2,1)S(1)}, bf16[3,3,1,16,128]{4,3,2,1,0:T(8,128)(2,1)S(1)}, u32[]{:S(2)}, u32[]{:S(2)}) collective-permute-start(bf16[3,3,1,16,128]{4,3,2,1,0:T(8,128)(2,1)S(1)} %get-tuple-element.60), channel_id=1, source_target_pairs={{0,3},{1,0},{2,1},{3,2},{4,7},{5,4},{6,5},{7,6},{8,11},{9,8},{10,9... | collective-permute-start | bytes 110600 | tf_op jit(solution)/shard_map/ppermute | solution.py:309
  116.1 3.0 %collective-permute-start.13 = (bf16[3,3,1,16,128]{4,3,2,1,0:T(8,128)(2,1)S(1)}, bf16[3,3,1,16,128]{4,3,2,1,0:T(8,128)(2,1)S(1)}, u32[]{:S(2)}, u32[]{:S(2)}) collective-permute-start(bf16[3,3,1,16,128]{4,3,2,1,0:T(8,128)(2,1)S(1)} %get-tuple-element.61), channel_id=1, source_target_pairs={{0,1},{1,2},{2,3},{3,0},{4,5},{5,6},{6,7},{7,4},{8,9},{9,10},{10,1... | collective-permute-start | bytes 110600 | tf_op jit(solution)/shard_map/ppermute | solution.py:309
  119.1 0.0 copy-start.10
  119.1 2.9 %shard_map.142 = (f32[64,512]{1,0:T(8,128)S(1)}, f32[16,512]{1,0:T(8,128)S(1)}) custom-call(bf16[64,512]{1,0:T(8,128)(2,1)S(1)} %bitcast.22, bf16[64,512]{1,0:T(8,128)(2,1)S(1)} %bitcast.27, bf16[1024,512]{1,0:T(8,128)(2,1)S(1)} %copy-done.1, bf16[1024,512]{1,0:T(8,128)(2,1)S(1)} %copy-done.3, bf16[16,104,256]{2,1,0:T(8,128)(2,1)S(1)} %all_to_all.16.refs_4_.refs_16_, ...), custom_call_target="tpu_custom_call" | custom-call | flops 268435456 | bytes 2097152 | tf_op jit(solution)/shard_map/pallas_call | solution.py:292
  122.0 0.0 copy-start.18
  122.0 0.0 copy-start.17
  122.1 0.6 copy-done.18
  122.7 0.0 copy-done.17
  122.7 4.1 %shard_map.145 = (bf16[64,512]{1,0:T(8,128)(2,1)}, f32[3,1,512]{2,1,0:T(1,128)}, f32[64,64]{1,0:T(8,128)}, f32[16,64]{1,0:T(8,128)}) custom-call(bf16[64,512]{1,0:T(8,128)(2,1)S(1)} %bitcast.23, bf16[64,512]{1,0:T(8,128)(2,1)S(1)} %bitcast.28, s32[1,512]{1,0:T(1,128)S(1)} %bitcast.35, f32[4,64]{1,0:T(4,128)S(1)} %copy-done.18, bf16[64,64]{1,0:T(8,128)(2,1)S(1)} %copy-done.9, ...), custom_call_target="tpu_custom_call" | custom-call | flops 268435456 | bytes 2097152 | tf_op jit(solution)/shard_map/pallas_call | solution.py:292
  (52 shorter events, 0.2 us)
Async XLA Ops:
  0.6 1.9 %copy-start.5 = (bf16[1,1,1,64,512]{4,3,2,1,0:T(8,128)(2,1)S(1)}, bf16[1,1,1,64,512]{4,3,2,1,0:T(8,128)(2,1)}, u32[]{:S(2)}) copy-start(bf16[1,1,1,64,512]{4,3,2,1,0:T(8,128)(2,1)} %param.10) | copy-start | bytes 196612
  0.6 1.9 %copy-start.15 = (f32[1,1,1,3,512]{4,2,3,1,0:T(1,128)S(1)}, f32[1,1,1,3,512]{4,2,3,1,0:T(1,128)}, u32[]{:S(2)}) copy-start(f32[1,1,1,3,512]{4,2,3,1,0:T(1,128)} %param.12) | copy-start | bytes 18436
  2.6 0.8 copy-start.6
  3.4 0.8 copy-start.11
  4.2 7.3 %copy-start.26 = (bf16[3,3,1,16,128]{4,3,2,1,0:T(8,128)(2,1)S(1)}, bf16[3,3,1,16,128]{4,3,2,1,0:T(8,128)(2,1)}, u32[]{:S(2)}) copy-start(bf16[3,3,1,16,128]{4,3,2,1,0:T(8,128)(2,1)} %get-tuple-element.43) | copy-start | bytes 110596
  4.2 12.5 %copy-start.25 = (bf16[3,3,1,16,128]{4,3,2,1,0:T(8,128)(2,1)S(1)}, bf16[3,3,1,16,128]{4,3,2,1,0:T(8,128)(2,1)}, u32[]{:S(2)}) copy-start(bf16[3,3,1,16,128]{4,3,2,1,0:T(8,128)(2,1)} %get-tuple-element.45) | copy-start | bytes 110596
  4.2 12.5 %copy-start.13 = (bf16[16,1024]{1,0:T(8,128)(2,1)S(1)}, bf16[16,1024]{1,0:T(8,128)(2,1)}, u32[]{:S(2)}) copy-start(bf16[16,1024]{1,0:T(8,128)(2,1)} %get-tuple-element.40.refs_3_.refs_5_) | copy-start | bytes 98308
  8.2 21.3 %collective-permute-start = (f32[1024,256]{1,0:T(8,128)S(1)}, f32[1024,256]{1,0:T(8,128)S(1)}, u32[]{:S(2)}, u32[]{:S(2)}) collective-permute-start(f32[1024,256]{1,0:T(8,128)S(1)} %get-tuple-element.42), channel_id=1, source_target_pairs={{0,1},{1,0},{2,3},{3,2},{4,5},{5,4},{6,7},{7,6},{8,9},{9,8},{10,11... | collective-permute-start | bytes 3145736 | tf_op jit(solution)/shard_map/ppermute | solution.py:309
  11.5 9.3 %collective-permute-start.1 = (bf16[3,3,1,16,128]{4,3,2,1,0:T(8,128)(2,1)S(1)}, bf16[3,3,1,16,128]{4,3,2,1,0:T(8,128)(2,1)S(1)}, u32[]{:S(2)}, u32[]{:S(2)}) collective-permute-start(bf16[3,3,1,16,128]{4,3,2,1,0:T(8,128)(2,1)S(1)} %copy-done.26), channel_id=1, source_target_pairs={{0,1},{1,2},{2,3},{3,0},{4,5},{5,6},{6,7},{7,4},{8,9},{9,10},{10,1... | collective-permute-start | bytes 110600 | tf_op jit(solution)/shard_map/ppermute | solution.py:309
  16.7 7.3 %collective-permute-start.2 = (bf16[3,3,1,16,128]{4,3,2,1,0:T(8,128)(2,1)S(1)}, bf16[3,3,1,16,128]{4,3,2,1,0:T(8,128)(2,1)S(1)}, u32[]{:S(2)}, u32[]{:S(2)}) collective-permute-start(bf16[3,3,1,16,128]{4,3,2,1,0:T(8,128)(2,1)S(1)} %copy-done.25), channel_id=1, source_target_pairs={{0,3},{1,0},{2,1},{3,2},{4,7},{5,4},{6,5},{7,6},{8,11},{9,8},{10,9... | collective-permute-start | bytes 110600 | tf_op jit(solution)/shard_map/ppermute | solution.py:309
  16.7 7.3 %copy-start.20 = (bf16[432,128]{1,0:T(8,128)(2,1)S(1)}, bf16[432,128]{1,0:T(8,128)(2,1)}, u32[]{:S(2)}) copy-start(bf16[432,128]{1,0:T(8,128)(2,1)} %get-tuple-element.44) | copy-start | bytes 331780
  20.8 9.6 %copy-start = (bf16[1024,512]{1,0:T(8,128)(2,1)}, bf16[1024,512]{1,0:T(8,128)(2,1)S(1)}, u32[]{:S(2)}) copy-start(bf16[1024,512]{1,0:T(8,128)(2,1)S(1)} %get-tuple-element.49.refs_2_) | copy-start | bytes 3145732
  20.8 9.6 %copy-start.2 = (bf16[1024,512]{1,0:T(8,128)(2,1)}, bf16[1024,512]{1,0:T(8,128)(2,1)S(1)}, u32[]{:S(2)}) copy-start(bf16[1024,512]{1,0:T(8,128)(2,1)S(1)} %get-tuple-element.50.refs_3_) | copy-start | bytes 3145732
  24.0 10.6 %collective-permute-start.3 = (bf16[3,1,5,16,128]{4,3,2,1,0:T(8,128)(2,1)S(1)}, bf16[3,1,5,16,128]{4,3,2,1,0:T(8,128)(2,1)S(1)}, u32[]{:S(2)}, u32[]{:S(2)}) collective-permute-start(bf16[3,1,5,16,128]{4,3,2,1,0:T(8,128)(2,1)S(1)} %get-tuple-element.76), channel_id=1, source_target_pairs={{0,4},{4,8},{8,12},{12,16},{16,20},{20,24},{24,28},{28,32},{32,36}... | collective-permute-start | bytes 184328 | tf_op jit(solution)/shard_map/ppermute | solution.py:309
  25.5 9.1 %collective-permute-start.4 = (bf16[3,1,5,16,128]{4,3,2,1,0:T(8,128)(2,1)S(1)}, bf16[3,1,5,16,128]{4,3,2,1,0:T(8,128)(2,1)S(1)}, u32[]{:S(2)}, u32[]{:S(2)}) collective-permute-start(bf16[3,1,5,16,128]{4,3,2,1,0:T(8,128)(2,1)S(1)} %get-tuple-element.77), channel_id=1, source_target_pairs={{0,60},{4,0},{8,4},{12,8},{16,12},{20,16},{24,20},{28,24},{32,28},... | collective-permute-start | bytes 184328 | tf_op jit(solution)/shard_map/ppermute | solution.py:309
  30.4 30.4 %all-to-all-start = ((bf16[16,64,256]{2,1,0:T(8,128)(2,1)}), bf16[16,64,256]{2,1,0:T(8,128)(2,1)S(1)}, u32[]{:S(2)}, u32[]{:S(2)}) async-start(bf16[16,64,256]{2,1,0:T(8,128)(2,1)} %bitcast.4), calls=%async_computation | async-start | bytes 1048576 | tf_op jit(solution)/shard_map/all_to_all | solution.py:827
  34.6 10.0 %copy-start.19 = (bf16[3,5,5,16,128]{4,3,2,1,0:T(8,128)(2,1)}, bf16[3,5,5,16,128]{4,3,2,1,0:T(8,128)(2,1)S(1)}, u32[]{:S(2)}) copy-start(bf16[3,5,5,16,128]{4,3,2,1,0:T(8,128)(2,1)S(1)} %pad_maximum_fusion) | copy-start | bytes 921604
  34.7 9.1 %collective-permute-start.6 = (bf16[1,5,5,16,128]{4,3,2,1,0:T(8,128)(2,1)S(1)}, bf16[1,5,5,16,128]{4,3,2,1,0:T(8,128)(2,1)S(1)}, u32[]{:S(2)}, u32[]{:S(2)}) collective-permute-start(bf16[1,5,5,16,128]{4,3,2,1,0:T(8,128)(2,1)S(1)} %get-tuple-element.74), channel_id=1, source_target_pairs={{0,192},{64,0},{128,64},{192,128},{1,193},{65,1},{129,65},{193,129... | collective-permute-start | bytes 307208 | tf_op jit(solution)/shard_map/ppermute | solution.py:309
  37.3 7.3 %collective-permute-start.5 = (bf16[1,5,5,16,128]{4,3,2,1,0:T(8,128)(2,1)S(1)}, bf16[1,5,5,16,128]{4,3,2,1,0:T(8,128)(2,1)S(1)}, u32[]{:S(2)}, u32[]{:S(2)}) collective-permute-start(bf16[1,5,5,16,128]{4,3,2,1,0:T(8,128)(2,1)S(1)} %get-tuple-element.75), channel_id=1, source_target_pairs={{0,64},{64,128},{128,192},{192,0},{1,65},{65,129},{129,193},{193,1... | collective-permute-start | bytes 307208 | tf_op jit(solution)/shard_map/ppermute | solution.py:309
  43.7 0.9 copy-start.21
  44.7 0.7 copy-start.22
  60.8 0.8 copy-start.14
  61.6 12.8 %copy-start.8 = (f32[2048,64]{0,1:T(8,128)S(1)}, f32[2048,64]{0,1:T(8,128)}, u32[]{:S(2)}) copy-start(f32[2048,64]{0,1:T(8,128)} %param.16) | copy-start | bytes 1572868
  74.4 21.9 %copy-start.24 = (bf16[400,128]{1,0:T(8,128)(2,1)S(1)}, bf16[400,128]{1,0:T(8,128)(2,1)}, u32[]{:S(2)}) copy-start(bf16[400,128]{1,0:T(8,128)(2,1)} %get-tuple-element.54) | copy-start | bytes 307204
  74.4 22.8 %copy-start.23 = (bf16[400,128]{1,0:T(8,128)(2,1)S(1)}, bf16[400,128]{1,0:T(8,128)(2,1)}, u32[]{:S(2)}) copy-start(bf16[400,128]{1,0:T(8,128)(2,1)} %get-tuple-element.55) | copy-start | bytes 307204
  75.2 27.2 %copy-start.4 = (f32[1200,128]{1,0:T(8,128)S(1)}, f32[1200,128]{1,0:T(8,128)}, u32[]{:S(2)}) copy-start(f32[1200,128]{1,0:T(8,128)} %get-tuple-element.53) | copy-start | bytes 1843204
  75.3 43.8 %copy-start.3 = (bf16[1024,512]{1,0:T(8,128)(2,1)S(1)}, bf16[1024,512]{1,0:T(8,128)(2,1)}, u32[]{:S(2)}) copy-start(bf16[1024,512]{1,0:T(8,128)(2,1)} %copy-done.2) | copy-start | bytes 3145732
  91.4 27.7 %copy-start.1 = (bf16[1024,512]{1,0:T(8,128)(2,1)S(1)}, bf16[1024,512]{1,0:T(8,128)(2,1)}, u32[]{:S(2)}) copy-start(bf16[1024,512]{1,0:T(8,128)(2,1)} %copy-done) | copy-start | bytes 3145732
  91.4 30.7 %collective-permute-start.7 = (bf16[16,104,256]{2,1,0:T(8,128)(2,1)S(1)}, bf16[16,104,256]{2,1,0:T(8,128)(2,1)S(1)}, u32[]{:S(2)}, u32[]{:S(2)}) collective-permute-start(bf16[16,104,256]{2,1,0:T(8,128)(2,1)S(1)} %all_to_all.16.refs_4_.refs_16_), channel_id=1, source_target_pairs={{0,1},{1,0},{2,3},{3,2},{4,5},{5,4},{6,7},{7,6},{8,9},{9,8},{10,11... | collective-permute-start | bytes 2555912 | tf_op jit(solution)/shard_map/ppermute | solution.py:309
  96.3 4.4 %collective-permute-start.8 = (bf16[1,5,5,16,128]{4,3,2,1,0:T(8,128)(2,1)S(1)}, bf16[1,5,5,16,128]{4,3,2,1,0:T(8,128)(2,1)S(1)}, u32[]{:S(2)}, u32[]{:S(2)}) collective-permute-start(bf16[1,5,5,16,128]{4,3,2,1,0:T(8,128)(2,1)S(1)} %bitcast.43), channel_id=1, source_target_pairs={{0,192},{64,0},{128,64},{192,128},{1,193},{65,1},{129,65},{193,129... | collective-permute-start | bytes 307208 | tf_op jit(solution)/shard_map/ppermute | solution.py:309
  97.1 5.3 %collective-permute-start.9 = (bf16[1,5,5,16,128]{4,3,2,1,0:T(8,128)(2,1)S(1)}, bf16[1,5,5,16,128]{4,3,2,1,0:T(8,128)(2,1)S(1)}, u32[]{:S(2)}, u32[]{:S(2)}) collective-permute-start(bf16[1,5,5,16,128]{4,3,2,1,0:T(8,128)(2,1)S(1)} %bitcast.42), channel_id=1, source_target_pairs={{0,64},{64,128},{128,192},{192,0},{1,65},{65,129},{129,193},{193,1... | collective-permute-start | bytes 307208 | tf_op jit(solution)/shard_map/ppermute | solution.py:309
  102.5 5.1 %collective-permute-start.10 = (bf16[3,1,5,16,128]{4,3,2,1,0:T(8,128)(2,1)S(1)}, bf16[3,1,5,16,128]{4,3,2,1,0:T(8,128)(2,1)S(1)}, u32[]{:S(2)}, u32[]{:S(2)}) collective-permute-start(bf16[3,1,5,16,128]{4,3,2,1,0:T(8,128)(2,1)S(1)} %get-tuple-element.57), channel_id=1, source_target_pairs={{0,60},{4,0},{8,4},{12,8},{16,12},{20,16},{24,20},{28,24},{32,28},... | collective-permute-start | bytes 184328 | tf_op jit(solution)/shard_map/ppermute | solution.py:309
  106.3 7.0 %collective-permute-start.11 = (bf16[3,1,5,16,128]{4,3,2,1,0:T(8,128)(2,1)S(1)}, bf16[3,1,5,16,128]{4,3,2,1,0:T(8,128)(2,1)S(1)}, u32[]{:S(2)}, u32[]{:S(2)}) collective-permute-start(bf16[3,1,5,16,128]{4,3,2,1,0:T(8,128)(2,1)S(1)} %get-tuple-element.58), channel_id=1, source_target_pairs={{0,4},{4,8},{8,12},{12,16},{16,20},{20,24},{24,28},{28,32},{32,36}... | collective-permute-start | bytes 184328 | tf_op jit(solution)/shard_map/ppermute | solution.py:309
  113.3 5.8 %copy-start.7 = (bf16[1,1,1,64,512]{4,3,2,1,0:T(8,128)(2,1)S(1)}, bf16[1,1,1,64,512]{4,3,2,1,0:T(8,128)(2,1)}, u32[]{:S(2)}) copy-start(bf16[1,1,1,64,512]{4,3,2,1,0:T(8,128)(2,1)} %param.11) | copy-start | bytes 196612
  113.3 8.7 %collective-permute-start.12 = (bf16[3,3,1,16,128]{4,3,2,1,0:T(8,128)(2,1)S(1)}, bf16[3,3,1,16,128]{4,3,2,1,0:T(8,128)(2,1)S(1)}, u32[]{:S(2)}, u32[]{:S(2)}) collective-permute-start(bf16[3,3,1,16,128]{4,3,2,1,0:T(8,128)(2,1)S(1)} %get-tuple-element.60), channel_id=1, source_target_pairs={{0,3},{1,0},{2,1},{3,2},{4,7},{5,4},{6,5},{7,6},{8,11},{9,8},{10,9... | collective-permute-start | bytes 110600 | tf_op jit(solution)/shard_map/ppermute | solution.py:309
  116.1 6.0 %collective-permute-start.13 = (bf16[3,3,1,16,128]{4,3,2,1,0:T(8,128)(2,1)S(1)}, bf16[3,3,1,16,128]{4,3,2,1,0:T(8,128)(2,1)S(1)}, u32[]{:S(2)}, u32[]{:S(2)}) collective-permute-start(bf16[3,3,1,16,128]{4,3,2,1,0:T(8,128)(2,1)S(1)} %get-tuple-element.61), channel_id=1, source_target_pairs={{0,1},{1,2},{2,3},{3,0},{4,5},{5,6},{6,7},{7,4},{8,9},{9,10},{10,1... | collective-permute-start | bytes 110600 | tf_op jit(solution)/shard_map/ppermute | solution.py:309
  119.1 3.0 %copy-start.9 = (bf16[64,64]{1,0:T(8,128)(2,1)S(1)}, bf16[64,64]{1,0:T(8,128)(2,1)}, u32[]{:S(2)}) copy-start(bf16[64,64]{1,0:T(8,128)(2,1)} %refs_4_.3) | copy-start | bytes 24580
  119.1 3.0 %copy-start.10 = (f32[80,128]{1,0:T(8,128)S(1)}, f32[80,128]{1,0:T(8,128)}, u32[]{:S(2)}) copy-start(f32[80,128]{1,0:T(8,128)} %get-tuple-element.62.refs_14_) | copy-start | bytes 122884
  119.1 3.0 %copy-start.12 = (bf16[16,1024]{1,0:T(8,128)(2,1)S(1)}, bf16[16,1024]{1,0:T(8,128)(2,1)}, u32[]{:S(2)}) copy-start(bf16[16,1024]{1,0:T(8,128)(2,1)} %get-tuple-element.37.refs_3_.refs_8_) | copy-start | bytes 98308
  119.1 3.0 %copy-start.16 = (f32[8,512]{1,0:T(8,128)S(1)}, f32[8,512]{1,0:T(8,128)}, u32[]{:S(2)}) copy-start(f32[8,512]{1,0:T(8,128)} %get-tuple-element.63.refs_15_) | copy-start | bytes 49156
  122.0 0.7 copy-start.18
  122.0 0.7 copy-start.17

commit v10 on v9

--- a/solution.py
+++ b/solution.py
@@ -57,6 +57,27 @@
     return gains
 
 
+def filter_copy(filter_in, tile, sem):
+    span = tile.shape[1]
+    lane = pl.multiple_of(lax.axis_index("gx") * span, span)
+    return pltpu.make_async_copy(filter_in.at[:, pl.ds(lane, span)], tile, sem)
+
+
+def take_filter(tile, filter_ref, turned):
+    inner, least = [lax.axis_size(axis) for axis in ("gy_1", "gz_0")]
+    tower = lax.axis_size(TOWER)
+    share = filter_ref.shape[0] // tower
+    turned[...] = jnp.transpose(tile[...])
+    for w in range(tower):
+        group = (w // least * inner + lax.axis_index("gy_1")) * least + w % least
+        at = pl.multiple_of((group * 2 + lax.axis_index(PAIR)) * share, share)
+        filter_ref[w * share : (w + 1) * share, :] = turned[pl.ds(at, share), :]
+
+
+def short_early(filter_in, *rest):
+    filter_copy(filter_in, *rest[-2:]).start()
+
+
 def short_kernel(
     ids_ref,
     pos_ref,
@@ -64,6 +85,7 @@
     radial_ref,
     mix_ref,
     gain_ref,
+    filter_in,
     below_ref,
     cells_ref,
     above_ref,
@@ -74,6 +96,7 @@
     core_out,
     own_ref,
     sums_ref,
+    filter_ref,
     lhs_ref,
     feat_ref,
     gains_ref,
@@ -86,8 +109,13 @@
     acc_ref,
     table_ref,
     zgrad_ref,
+    turned_ref,
+    tile_ref,
+    tile_sem,
 ):
     channels, atoms = dy_ref.shape
+    filter_copy(filter_in, tile_ref, tile_sem).wait()
+    take_filter(tile_ref, filter_ref, turned_ref)
     side, inner, rest = below_ref.shape[0], cells_ref.shape[0], core_ref.shape[0]
     bounds = (0, side, side + inner, 2 * side + inner, 2 * side + inner + rest)
     for n, ref in enumerate((below_ref, cells_ref, above_ref, core_ref)):
@@ -230,16 +258,18 @@
     sums_ref[0:cut, :] = jnp.concatenate([tall[0:cut], tall[cut:]], axis=1)
 
 
-def short_range(pieces, ids, pos, dy, radial, mix, gain):
+def short_range(pieces, ids, pos, dy, radial, mix, gain, filter_columns):
     channels, atoms = dy.shape
     listed = ids.shape[0]
     count = radial.shape[0]
     f32, bf16 = jnp.float32, jnp.bfloat16
     shaped = jax.ShapeDtypeStruct
+    points, sheet = filter_columns.shape[1], lax.axis_size(SHEET)
+    span = points // lax.axis_size("gx")
     return fetching_call(
         short_kernel,
         (ids, pos, dy, radial, mix, gain),
-        pieces,
+        (filter_columns, *pieces),
         (
             shaped(pieces[0].shape, bf16),
             shaped(pieces[1].shape, f32),
@@ -247,6 +277,7 @@
             shaped(pieces[3].shape, f32),
             shaped((8, atoms), f32),
             shaped((64, 128), f32),
+            shaped((points // (2 * sheet), channels), f32),
         ),
         [
             pltpu.VMEM((GROUPS * ROWS, HIGH), bf16),
@@ -261,14 +292,19 @@
             pltpu.VMEM((GROUPS * ROWS, HIGH), f32),
             pltpu.VMEM((GROUPS * HIGH, 128), bf16),
             pltpu.VMEM((GROUPS * HIGH, 128), f32),
+            pltpu.VMEM((span, channels), f32),
+            pltpu.VMEM((channels, span), f32),
+            pltpu.SemaphoreType.DMA,
         ],
+        early=short_early,
+        in_specs=(FAR,) + (WHOLE,) * len(pieces),
         limit=False,
     )
 
 
 def fetching_call(
     kernel, fetched, resident, outs, scratch, early=None, in_specs=None, out_specs=None, flops=0,
-    limit=True,
+    limit=20,
 ):
     n = len(fetched)
 
@@ -299,7 +335,9 @@
             *[pltpu.VMEM(x.shape, x.dtype) for x in fetched],
             pltpu.SemaphoreType.DMA((n,)),
         ],
-        compiler_params=LIMIT if limit else None,
+        compiler_params=(
+            pltpu.CompilerParams(vmem_limit_bytes=limit * 1024 * 1024) if limit else None
+        ),
         cost_estimate=cost,
     )(*fetched, *resident)
 
@@ -602,9 +640,9 @@
     run = miller_ref.shape[1] // coeff_ref.shape[0]
     sides = []
     for ref in (mine_ref, coeff_ref):
-        total = jnp.sum(ref[:, run : run + cut].astype(f32), axis=0)
-        sides.append(total[:, 0:128] + total[:, 128:256])
-    full = sides[0] + sides[1]
+        total = jnp.sum(ref[:, run:].astype(f32), axis=0)
+        sides.append(jnp.concatenate([total[:, 0:128], total[:, 128:256]], axis=0))
+    full = (sides[0] + sides[1])[0:cut]
     tall = jnp.concatenate([full[:, 0:channels], full[:, channels:]], axis=0)
     weight_ref[...] = tall[0:channels]
     radial_ref[...] = tall[channels:]
@@ -640,6 +678,7 @@
         early=ewald_early,
         in_specs=(FAR, FAR) + (WHOLE,) * (2 + len(more)),
         flops=8 * points * atoms * channels,
+        limit=20 if last else 52,
     )
 
 
@@ -687,60 +726,33 @@
     return small_call(partial_kernel, (pieces, sums), outs)[0]
 
 
-def coefficient_kernel(
-    norm_atoms, norm_k, pieces_ref, filter_in, out_ref, filter_ref, tile, turned, all_filter, sem
-):
+def coefficient_kernel(norm_atoms, norm_k, pieces_ref, filt_ref, out_ref, filter_ref, all_filter):
     f32, bf16 = jnp.float32, jnp.bfloat16
-    share, _ = filter_ref.shape
-    tower = pieces_ref.shape[0]
-    rows = tower * share
-    span = tile.shape[1]
-    lane = pl.multiple_of(lax.axis_index("gx") * span, span)
-    copy = pltpu.make_async_copy(filter_in.at[:, pl.ds(lane, span)], tile, sem)
-    copy.start()
+    share = filter_ref.shape[0]
+    rows = filt_ref.shape[0]
     both = jnp.sum(pieces_ref[...].astype(f32), axis=0)
-    copy.wait()
-    turned[...] = jnp.transpose(tile[...])
-    inner, least = [lax.axis_size(axis) for axis in ("gy_1", "gz_0")]
-    filters = []
-    for w in range(tower):
-        group = (w // least * inner + lax.axis_index("gy_1")) * least + w % least
-        at = pl.multiple_of((group * 2 + lax.axis_index(PAIR)) * share, share)
-        filters.append(turned[pl.ds(at, share), :])
-    filt = jnp.concatenate(filters, axis=0)
-    coeffs, all_filter[...] = coefficients(both[0:rows], filt, norm_atoms, norm_k)
+    coeffs, all_filter[...] = coefficients(both[0:rows], filt_ref[...], norm_atoms, norm_k)
     mine = lax.axis_index(TOWER)
     filter_ref[...] = all_filter[pl.ds(pl.multiple_of(mine * share, share), share), :]
-    tall = jnp.concatenate([both[rows:, 0:128], both[rows:, 128:256]], axis=0)
-    hi, lo = split_two(tall[0 : out_ref.shape[1] - rows])
-    strip = jnp.concatenate(
-        [coeffs, jnp.concatenate([hi.astype(f32), lo.astype(f32)], axis=1)], axis=0
-    ).astype(bf16)
+    strip = jnp.concatenate([coeffs, both[rows:]], axis=0).astype(bf16)
     out_ref[...] = jnp.broadcast_to(strip[None], out_ref.shape)
 
 
-def make_strip(pieces, filter_columns, sheet, cut, norm_atoms, norm_k):
-    tower = pieces.shape[0]
-    channels, points = filter_columns.shape
-    share = points // (2 * tower * sheet)
-    span = points // lax.axis_size("gx")
+def make_strip(pieces, filt, sheet, norm_atoms, norm_k):
+    tower, rows, width = pieces.shape
+    share, channels = filt.shape[0] // tower, filt.shape[1]
     return pl.pallas_call(
         functools.partial(coefficient_kernel, norm_atoms, norm_k),
         out_shape=(
-            jax.ShapeDtypeStruct((sheet, tower * share + cut, pieces.shape[2]), jnp.bfloat16),
+            jax.ShapeDtypeStruct((sheet, rows, width), jnp.bfloat16),
             jax.ShapeDtypeStruct((share, channels), jnp.float32),
         ),
-        in_specs=[WHOLE, FAR],
+        in_specs=[WHOLE, WHOLE],
         out_specs=(WHOLE, WHOLE),
-        scratch_shapes=[
-            pltpu.VMEM((channels, span), jnp.float32),
-            pltpu.VMEM((span, channels), jnp.float32),
-            pltpu.VMEM((tower * share, channels), jnp.float32),
-            pltpu.SemaphoreType.DMA,
-        ],
+        scratch_shapes=[pltpu.VMEM(filt.shape, jnp.float32)],
         compiler_params=LIMIT,
         name="coefficients",
-    )(pieces, filter_columns)
+    )(pieces, filt)
 
 
 def fold_x_kernel(mid_ref, upper_ref, lower_ref, first_ref, last_ref, rest_ref):
@@ -826,7 +838,7 @@
     paired = (part_mine + received).astype(jnp.bfloat16)
     pieces = lax.all_to_all(paired.reshape(sheet, half // sheet, width), SHEET, 0, 0)
 
-    low, mid, high, core_grad, own_grad, sums = short_range(
+    low, mid, high, core_grad, own_grad, sums, filt = short_range(
         (below.reshape(400, 128), cells.reshape(1200, 128), above.reshape(400, 128), core),
         adjacent_ghost_entries[0, 0, 0],
         pos,
@@ -834,6 +846,7 @@
         distance_kernel,
         channel_mixing_matrix,
         element_channel_factor,
+        reciprocal_kernel.T,
     )
     parts = partial_sums(pieces, sums, tower)
     pieces = lax.all_to_all(parts, TOWER, 0, 0)
@@ -842,10 +855,7 @@
     lower = from_behind(high.reshape(1, 5, 5, 16, 128), "gx", 1)
     first, last, rest = fold_x(mid.reshape(3, 5, 5, 16, 128), upper, lower)
     upper, lower = from_behind(first, GY, -1), from_behind(last, GY, 1)
-    cut = (channels + distance_kernel.shape[0]) // 2
-    strip, filter_share = make_strip(
-        pieces, reciprocal_kernel.T, sheet, cut, norm_atoms, norm_k
-    )
+    strip, filter_share = make_strip(pieces, filt, sheet, norm_atoms, norm_k)
     got = lax.all_to_all(strip, SHEET, 0, 0)
     first, last, inner = fold_y(rest, upper, lower)
     upper, lower = from_behind(first, GZ, -1), from_behind(last, GZ, 1)

time: 128 us -> 127 us (level)
    unnamed x54 -> x52, local copies, waits for them, and re-layouts: 3.73 us -> 3.71 us
where the time goes in v10:
time: 127 us; the launch traced here: 126 us
  starting transfers between devices  36.4 us (29%)
  Pallas kernels  34.1 us (27%)
  blocking collectives  27.9 us (22%)
  waiting for transfers between devices  22.2 us (17%)
  local copies, waits for them, and re-layouts  3.72 us (3%)
    pallas_call x6, Pallas kernels, fetching_call(): pl.pallas_call(body, out_shape=outs, in_specs=[FAR] * n + list(in_specs o...  33.2 us
    ppermute x14, starting transfers between devices, from_behind(): lax.ppermute(x, axis, [(i, (i + by) % devices) for i in range(devices)])  32.2 us
    ppermute x14, waiting for transfers between devices, from_behind(): lax.ppermute(x, axis, [(i, (i + by) % devices) for i in range(devices)])  22.2 us
    all_to_all x1, blocking collectives, whole(): got = lax.all_to_all(strip, SHEET, 0, 0)  15.3 us
    all_to_all x1, blocking collectives, whole(): pieces = lax.all_to_all(parts, TOWER, 0, 0)  12.6 us
    all_to_all x1, starting transfers between devices, whole(): lax.all_to_all(paired.reshape(sheet, half // sheet, width), SHEET, 0, 0)  4.19 us
    unnamed x52, local copies, waits for them, and re-layouts  3.71 us
  transfers between devices with their start and end apart: 15, of which 7 were waited for; matrix products, arithmetic and copies ran while one was open for 1% of the time, Pallas kernels for 18%

profile of v10, /device:TPU:1, one launch (start us, length us, event | category | flops | bytes accessed | tf_op | source)
XLA Modules:
  0.0 126.4 jit_solution(3032838484971988971)
XLA Ops:
  0.6 0.0 copy-start.3
  0.6 0.0 copy-start.14
  0.7 1.9 %shard_map.137 = (bf16[432,128]{1,0:T(8,128)(2,1)}, bf16[80,128]{1,0:T(8,128)(2,1)}, bf16[3,3,1,16,128]{4,3,2,1,0:T(8,128)(2,1)}, bf16[3,3,1,16,128]{4,3,2,1,0:T...) custom-call(bf16[64,512]{1,0:T(8,128)(2,1)} %bitcast.24, s32[1,512]{1,0:T(1,128)} %bitcast.33, ...), custom_call_target="tpu_custom_call" | custom-call | tf_op jit(solution)/shard_map/pallas_call | solution.py:328
  2.6 0.0 copy-start.5
  2.6 0.8 copy-done.5
  3.4 0.8 copy-done.9
  4.2 4.0 %shard_map.138 = (bf16[1024,512]{1,0:T(8,128)(2,1)S(1)}, bf16[1024,512]{1,0:T(8,128)(2,1)S(1)}, f32[1024,256]{1,0:T(8,128)S(1)}) custom-call(f32[3,1,512]{2,1,0:T(1,128)S(1)} %bitcast.31, bf16[64,512]{1,0:T(8,128)(2,1)S(1)} %bitcast.25, bf16[64,512]{1,0:T(8,128)(2,1)S(1)} %bitcast.20, bf16[16,1024]{1,0:T(8,128)(2,1)S(1)} %copy-done.9), custom_call_target="tpu_custom_call" | custom-call | flops 402653184 | bytes 3145728 | tf_op jit(solution)/shard_map/pallas_call | solution.py:328
  8.2 3.3 %collective-permute-start = (f32[1024,256]{1,0:T(8,128)S(1)}, f32[1024,256]{1,0:T(8,128)S(1)}, u32[]{:S(2)}, u32[]{:S(2)}) collective-permute-start(f32[1024,256]{1,0:T(8,128)S(1)} %get-tuple-element.43), channel_id=1, source_target_pairs={{0,1},{1,0},{2,3},{3,2},{4,5},{5,4},{6,7},{7,6},{8,9},{9,8},{10,11... | collective-permute-start | bytes 3145736 | tf_op jit(solution)/shard_map/ppermute | solution.py:347
  11.5 5.2 %collective-permute-start.1 = (bf16[3,3,1,16,128]{4,3,2,1,0:T(8,128)(2,1)S(1)}, bf16[3,3,1,16,128]{4,3,2,1,0:T(8,128)(2,1)S(1)}, u32[]{:S(2)}, u32[]{:S(2)}) collective-permute-start(bf16[3,3,1,16,128]{4,3,2,1,0:T(8,128)(2,1)S(1)} %copy-done.25), channel_id=1, source_target_pairs={{0,1},{1,2},{2,3},{3,0},{4,5},{5,6},{6,7},{7,4},{8,9},{9,10},{10,1... | collective-permute-start | bytes 110600 | tf_op jit(solution)/shard_map/ppermute | solution.py:347
  16.7 0.0 collective-permute-start.2
  16.7 4.0 %shard_map.139 = (bf16[1024,512]{1,0:T(8,128)(2,1)S(1)}, bf16[1024,512]{1,0:T(8,128)(2,1)S(1)}, f32[1024,256]{1,0:T(8,128)S(1)}) custom-call(f32[3,1,512]{2,1,0:T(1,128)S(1)} %bitcast.32, bf16[64,512]{1,0:T(8,128)(2,1)S(1)} %bitcast.26, bf16[64,512]{1,0:T(8,128)(2,1)S(1)} %bitcast.21, bf16[16,1024]{1,0:T(8,128)(2,1)S(1)} %copy-done.11), custom_call_target="tpu_custom_call" | custom-call | flops 402653184 | bytes 3145728 | tf_op jit(solution)/shard_map/pallas_call | solution.py:328
  20.8 0.0 collective-permute-done.1
  20.8 3.2 %collective-permute-done.2 = bf16[3,3,1,16,128]{4,3,2,1,0:T(8,128)(2,1)S(1)} collective-permute-done((bf16[3,3,1,16,128]{4,3,2,1,0:T(8,128)(2,1)S(1)}, bf16[3,3,1,16,128]{4,3,2,1,0:T(8,128)(2,1)S(1)}, u32[]{:S(2)}, u32[]{:S(2)}) %collective-permute-start.2) | collective-permute-done | bytes 36896 | tf_op jit(solution)/shard_map/ppermute | solution.py:347
  24.0 1.4 %collective-permute-start.3 = (bf16[3,1,5,16,128]{4,3,2,1,0:T(8,128)(2,1)S(1)}, bf16[3,1,5,16,128]{4,3,2,1,0:T(8,128)(2,1)S(1)}, u32[]{:S(2)}, u32[]{:S(2)}) collective-permute-start(bf16[3,1,5,16,128]{4,3,2,1,0:T(8,128)(2,1)S(1)} %get-tuple-element.78), channel_id=1, source_target_pairs={{0,4},{4,8},{8,12},{12,16},{16,20},{20,24},{24,28},{28,32},{32,36}... | collective-permute-start | bytes 184328 | tf_op jit(solution)/shard_map/ppermute | solution.py:347
  25.4 4.0 %collective-permute-start.4 = (bf16[3,1,5,16,128]{4,3,2,1,0:T(8,128)(2,1)S(1)}, bf16[3,1,5,16,128]{4,3,2,1,0:T(8,128)(2,1)S(1)}, u32[]{:S(2)}, u32[]{:S(2)}) collective-permute-start(bf16[3,1,5,16,128]{4,3,2,1,0:T(8,128)(2,1)S(1)} %get-tuple-element.79), channel_id=1, source_target_pairs={{0,60},{4,0},{8,4},{12,8},{16,12},{20,16},{24,20},{28,24},{32,28},... | collective-permute-start | bytes 184328 | tf_op jit(solution)/shard_map/ppermute | solution.py:347
  29.5 0.9 add_convert_fusion
  30.4 4.2 %all-to-all-start = ((bf16[16,64,256]{2,1,0:T(8,128)(2,1)}), bf16[16,64,256]{2,1,0:T(8,128)(2,1)S(1)}, u32[]{:S(2)}, u32[]{:S(2)}) async-start(bf16[16,64,256]{2,1,0:T(8,128)(2,1)} %bitcast.4), calls=%async_computation | async-start | bytes 1048576 | tf_op jit(solution)/shard_map/all_to_all | solution.py:839
  34.6 0.0 collective-permute-done.4
  34.6 0.1 pad_maximum_fusion
  34.7 2.7 %collective-permute-start.6 = (bf16[1,5,5,16,128]{4,3,2,1,0:T(8,128)(2,1)S(1)}, bf16[1,5,5,16,128]{4,3,2,1,0:T(8,128)(2,1)S(1)}, u32[]{:S(2)}, u32[]{:S(2)}) collective-permute-start(bf16[1,5,5,16,128]{4,3,2,1,0:T(8,128)(2,1)S(1)} %get-tuple-element.76), channel_id=1, source_target_pairs={{0,192},{64,0},{128,64},{192,128},{1,193},{65,1},{129,65},{193,129... | collective-permute-start | bytes 307208 | tf_op jit(solution)/shard_map/ppermute | solution.py:347
  37.3 0.0 collective-permute-start.5
  37.3 6.4 %collective-permute-done.6 = bf16[1,5,5,16,128]{4,3,2,1,0:T(8,128)(2,1)S(1)} collective-permute-done((bf16[1,5,5,16,128]{4,3,2,1,0:T(8,128)(2,1)S(1)}, bf16[1,5,5,16,128]{4,3,2,1,0:T(8,128)(2,1)S(1)}, u32[]{:S(2)}, u32[]{:S(2)}) %collective-permute-start.6) | collective-permute-done | bytes 102432 | tf_op jit(solution)/shard_map/ppermute | solution.py:347
  43.7 0.9 collective-permute-done.5
  44.7 0.6 copy-done.21
  45.3 15.6 %shard_map.140 = (bf16[400,128]{1,0:T(8,128)(2,1)}, f32[1200,128]{1,0:T(8,128)}, bf16[400,128]{1,0:T(8,128)(2,1)}, f32[80,128]{1,0:T(8,128)}, f32[8,512]{1,0:T(8...) custom-call(s32[16,512]{1,0:T(8,128)} %bitcast.41, f32[3,1,512]{2,1,0:T(1,128)} %bitcast.30, bf16[64,512]{1,0:T(8,128)(2,1)} %bitcast.19, ...), custom_call_target="tpu_custom_call" | custom-call | tf_op jit(solution)/shard_map/pallas_call | solution.py:328
  60.9 0.0 copy-start.13
  60.9 0.7 copy-done.13
  61.7 0.1 shard_map.141
  61.8 12.6 %all_to_all.15.pieces_ref = bf16[8,88,256]{2,1,0:T(8,128)(2,1)S(1)} all-to-all(bf16[8,88,256]{2,1,0:T(8,128)(2,1)S(1)} %shard_map.141), channel_id=1, replica_groups=mesh['gx'=4,'gy_0'=4,'gy_1'=4,'gz_0'=2,'gz_1'=2] {'gy_0','gz_0'}, dimensions={0} | all-to-all | bytes 720896 | tf_op jit(solution)/shard_map/all_to_all | solution.py:852
  74.4 0.7 coefficients.1
  75.1 15.3 %all_to_all.16.refs_4_.refs_16_ = bf16[16,88,256]{2,1,0:T(8,128)(2,1)S(1)} all-to-all(bf16[16,88,256]{2,1,0:T(8,128)(2,1)S(1)} %get-tuple-element.50), channel_id=1, replica_groups=mesh['gx'=4,'gy_0'=4,'gy_1'=4,'gz_0'=2,'gz_1'=2] {'gx','gy_1'}, dimensions={0} | all-to-all | bytes 1441792 | tf_op jit(solution)/shard_map/all_to_all | solution.py:859
  90.4 4.6 %collective-permute-start.7 = (bf16[16,88,256]{2,1,0:T(8,128)(2,1)S(1)}, bf16[16,88,256]{2,1,0:T(8,128)(2,1)S(1)}, u32[]{:S(2)}, u32[]{:S(2)}) collective-permute-start(bf16[16,88,256]{2,1,0:T(8,128)(2,1)S(1)} %all_to_all.16.refs_4_.refs_16_), channel_id=1, source_target_pairs={{0,1},{1,0},{2,3},{3,2},{4,5},{5,4},{6,7},{7,6},{8,9},{9,8},{10,11... | collective-permute-start | bytes 2162696 | tf_op jit(solution)/shard_map/ppermute | solution.py:347
  94.9 0.8 collective-permute-start.8
  95.7 0.7 collective-permute-start.9
  96.4 3.0 %collective-permute-done.8.upper_ref = bf16[1,5,5,16,128]{4,3,2,1,0:T(8,128)(2,1)S(1)} collective-permute-done((bf16[1,5,5,16,128]{4,3,2,1,0:T(8,128)(2,1)S(1)}, bf16[1,5,5,16,128]{4,3,2,1,0:T(8,128)(2,1)S(1)}, u32[]{:S(2)}, u32[]{:S(2)}) %collective-permute-start.8) | collective-permute-done | bytes 102432 | tf_op jit(solution)/shard_map/ppermute | solution.py:347
  99.4 1.7 %collective-permute-done.9.lower_ref = bf16[1,5,5,16,128]{4,3,2,1,0:T(8,128)(2,1)S(1)} collective-permute-done((bf16[1,5,5,16,128]{4,3,2,1,0:T(8,128)(2,1)S(1)}, bf16[1,5,5,16,128]{4,3,2,1,0:T(8,128)(2,1)S(1)}, u32[]{:S(2)}, u32[]{:S(2)}) %collective-permute-start.9) | collective-permute-done | bytes 102432 | tf_op jit(solution)/shard_map/ppermute | solution.py:347
  101.1 0.1 shard_map.143
  101.1 3.9 %collective-permute-start.10 = (bf16[3,1,5,16,128]{4,3,2,1,0:T(8,128)(2,1)S(1)}, bf16[3,1,5,16,128]{4,3,2,1,0:T(8,128)(2,1)S(1)}, u32[]{:S(2)}, u32[]{:S(2)}) collective-permute-start(bf16[3,1,5,16,128]{4,3,2,1,0:T(8,128)(2,1)S(1)} %get-tuple-element.59), channel_id=1, source_target_pairs={{0,60},{4,0},{8,4},{12,8},{16,12},{20,16},{24,20},{28,24},{32,28},... | collective-permute-start | bytes 184328 | tf_op jit(solution)/shard_map/ppermute | solution.py:347
  105.0 1.3 %collective-permute-done.10.upper_ref = bf16[3,1,5,16,128]{4,3,2,1,0:T(8,128)(2,1)S(1)} collective-permute-done((bf16[3,1,5,16,128]{4,3,2,1,0:T(8,128)(2,1)S(1)}, bf16[3,1,5,16,128]{4,3,2,1,0:T(8,128)(2,1)S(1)}, u32[]{:S(2)}, u32[]{:S(2)}) %collective-permute-start.10) | collective-permute-done | bytes 61472 | tf_op jit(solution)/shard_map/ppermute | solution.py:347
  106.3 5.7 %collective-permute-done.11.lower_ref = bf16[3,1,5,16,128]{4,3,2,1,0:T(8,128)(2,1)S(1)} collective-permute-done((bf16[3,1,5,16,128]{4,3,2,1,0:T(8,128)(2,1)S(1)}, bf16[3,1,5,16,128]{4,3,2,1,0:T(8,128)(2,1)S(1)}, u32[]{:S(2)}, u32[]{:S(2)}) %collective-permute-start.11) | collective-permute-done | bytes 61472 | tf_op jit(solution)/shard_map/ppermute | solution.py:347
  112.0 2.6 %collective-permute-start.12 = (bf16[3,3,1,16,128]{4,3,2,1,0:T(8,128)(2,1)S(1)}, bf16[3,3,1,16,128]{4,3,2,1,0:T(8,128)(2,1)S(1)}, u32[]{:S(2)}, u32[]{:S(2)}) collective-permute-start(bf16[3,3,1,16,128]{4,3,2,1,0:T(8,128)(2,1)S(1)} %get-tuple-element.62), channel_id=1, source_target_pairs={{0,3},{1,0},{2,1},{3,2},{4,7},{5,4},{6,5},{7,6},{8,11},{9,8},{10,9... | collective-permute-start | bytes 110600 | tf_op jit(solution)/shard_map/ppermute | solution.py:347
  114.7 3.1 %collective-permute-start.13 = (bf16[3,3,1,16,128]{4,3,2,1,0:T(8,128)(2,1)S(1)}, bf16[3,3,1,16,128]{4,3,2,1,0:T(8,128)(2,1)S(1)}, u32[]{:S(2)}, u32[]{:S(2)}) collective-permute-start(bf16[3,3,1,16,128]{4,3,2,1,0:T(8,128)(2,1)S(1)} %get-tuple-element.63), channel_id=1, source_target_pairs={{0,1},{1,2},{2,3},{3,0},{4,5},{5,6},{6,7},{7,4},{8,9},{9,10},{10,1... | collective-permute-start | bytes 110600 | tf_op jit(solution)/shard_map/ppermute | solution.py:347
  117.8 3.6 %shard_map.142 = (f32[64,512]{1,0:T(8,128)S(1)}, f32[16,512]{1,0:T(8,128)S(1)}) custom-call(bf16[64,512]{1,0:T(8,128)(2,1)S(1)} %bitcast.27, bf16[64,512]{1,0:T(8,128)(2,1)S(1)} %bitcast.22, bf16[1024,512]{1,0:T(8,128)(2,1)} %copy-done, bf16[1024,512]{1,0:T(8,128)(2,1)} %copy-done.1, bf16[16,88,256]{2,1,0:T(8,128)(2,1)S(1)} %all_to_all.16.refs_4_.refs_16_, ...), custom_call_target="tpu_custom_call" | custom-call | flops 268435456 | bytes 2097152 | tf_op jit(solution)/shard_map/pallas_call | solution.py:328
  121.4 0.0 copy-start.17
  121.4 0.0 copy-start.16
  121.5 0.6 copy-done.17
  122.1 0.0 copy-done.16
  122.1 4.1 %shard_map.145 = (bf16[64,512]{1,0:T(8,128)(2,1)}, f32[3,1,512]{2,1,0:T(1,128)}, f32[64,64]{1,0:T(8,128)}, f32[16,64]{1,0:T(8,128)}) custom-call(bf16[64,512]{1,0:T(8,128)(2,1)S(1)} %bitcast.28, bf16[64,512]{1,0:T(8,128)(2,1)S(1)} %bitcast.23, s32[1,512]{1,0:T(1,128)S(1)} %bitcast.34, f32[4,64]{1,0:T(4,128)S(1)} %copy-done.16, bf16[64,64]{1,0:T(8,128)(2,1)S(1)} %copy-done.7, ...), custom_call_target="tpu_custom_call" | custom-call | flops 268435456 | bytes 2097152 | tf_op jit(solution)/shard_map/pallas_call | solution.py:328
  (50 shorter events, 0.2 us)
Async XLA Ops:
  0.6 1.9 %copy-start.3 = (bf16[1,1,1,64,512]{4,3,2,1,0:T(8,128)(2,1)S(1)}, bf16[1,1,1,64,512]{4,3,2,1,0:T(8,128)(2,1)}, u32[]{:S(2)}) copy-start(bf16[1,1,1,64,512]{4,3,2,1,0:T(8,128)(2,1)} %param.11) | copy-start | bytes 196612
  0.6 1.9 %copy-start.14 = (f32[1,1,1,3,512]{4,2,3,1,0:T(1,128)S(1)}, f32[1,1,1,3,512]{4,2,3,1,0:T(1,128)}, u32[]{:S(2)}) copy-start(f32[1,1,1,3,512]{4,2,3,1,0:T(1,128)} %param.12) | copy-start | bytes 18436
  2.6 0.8 copy-start.5
  3.4 0.8 copy-start.9
  4.2 7.3 %copy-start.25 = (bf16[3,3,1,16,128]{4,3,2,1,0:T(8,128)(2,1)S(1)}, bf16[3,3,1,16,128]{4,3,2,1,0:T(8,128)(2,1)}, u32[]{:S(2)}) copy-start(bf16[3,3,1,16,128]{4,3,2,1,0:T(8,128)(2,1)} %get-tuple-element.44) | copy-start | bytes 110596
  4.2 12.5 %copy-start.24 = (bf16[3,3,1,16,128]{4,3,2,1,0:T(8,128)(2,1)S(1)}, bf16[3,3,1,16,128]{4,3,2,1,0:T(8,128)(2,1)}, u32[]{:S(2)}) copy-start(bf16[3,3,1,16,128]{4,3,2,1,0:T(8,128)(2,1)} %get-tuple-element.46) | copy-start | bytes 110596
  4.2 12.5 %copy-start.11 = (bf16[16,1024]{1,0:T(8,128)(2,1)S(1)}, bf16[16,1024]{1,0:T(8,128)(2,1)}, u32[]{:S(2)}) copy-start(bf16[16,1024]{1,0:T(8,128)(2,1)} %get-tuple-element.41.refs_3_.refs_5_) | copy-start | bytes 98308
  8.2 21.3 %collective-permute-start = (f32[1024,256]{1,0:T(8,128)S(1)}, f32[1024,256]{1,0:T(8,128)S(1)}, u32[]{:S(2)}, u32[]{:S(2)}) collective-permute-start(f32[1024,256]{1,0:T(8,128)S(1)} %get-tuple-element.43), channel_id=1, source_target_pairs={{0,1},{1,0},{2,3},{3,2},{4,5},{5,4},{6,7},{7,6},{8,9},{9,8},{10,11... | collective-permute-start | bytes 3145736 | tf_op jit(solution)/shard_map/ppermute | solution.py:347
  11.5 9.3 %collective-permute-start.1 = (bf16[3,3,1,16,128]{4,3,2,1,0:T(8,128)(2,1)S(1)}, bf16[3,3,1,16,128]{4,3,2,1,0:T(8,128)(2,1)S(1)}, u32[]{:S(2)}, u32[]{:S(2)}) collective-permute-start(bf16[3,3,1,16,128]{4,3,2,1,0:T(8,128)(2,1)S(1)} %copy-done.25), channel_id=1, source_target_pairs={{0,1},{1,2},{2,3},{3,0},{4,5},{5,6},{6,7},{7,4},{8,9},{9,10},{10,1... | collective-permute-start | bytes 110600 | tf_op jit(solution)/shard_map/ppermute | solution.py:347
  16.7 7.3 %collective-permute-start.2 = (bf16[3,3,1,16,128]{4,3,2,1,0:T(8,128)(2,1)S(1)}, bf16[3,3,1,16,128]{4,3,2,1,0:T(8,128)(2,1)S(1)}, u32[]{:S(2)}, u32[]{:S(2)}) collective-permute-start(bf16[3,3,1,16,128]{4,3,2,1,0:T(8,128)(2,1)S(1)} %copy-done.24), channel_id=1, source_target_pairs={{0,3},{1,0},{2,1},{3,2},{4,7},{5,4},{6,5},{7,6},{8,11},{9,8},{10,9... | collective-permute-start | bytes 110600 | tf_op jit(solution)/shard_map/ppermute | solution.py:347
  16.7 7.3 %copy-start.19 = (bf16[432,128]{1,0:T(8,128)(2,1)S(1)}, bf16[432,128]{1,0:T(8,128)(2,1)}, u32[]{:S(2)}) copy-start(bf16[432,128]{1,0:T(8,128)(2,1)} %get-tuple-element.45) | copy-start | bytes 331780
  20.8 9.6 %copy-start = (bf16[1024,512]{1,0:T(8,128)(2,1)}, bf16[1024,512]{1,0:T(8,128)(2,1)S(1)}, u32[]{:S(2)}) copy-start(bf16[1024,512]{1,0:T(8,128)(2,1)S(1)} %get-tuple-element.51.refs_2_) | copy-start | bytes 3145732
  20.8 9.6 %copy-start.1 = (bf16[1024,512]{1,0:T(8,128)(2,1)}, bf16[1024,512]{1,0:T(8,128)(2,1)S(1)}, u32[]{:S(2)}) copy-start(bf16[1024,512]{1,0:T(8,128)(2,1)S(1)} %get-tuple-element.52.refs_3_) | copy-start | bytes 3145732
  24.0 10.6 %collective-permute-start.3 = (bf16[3,1,5,16,128]{4,3,2,1,0:T(8,128)(2,1)S(1)}, bf16[3,1,5,16,128]{4,3,2,1,0:T(8,128)(2,1)S(1)}, u32[]{:S(2)}, u32[]{:S(2)}) collective-permute-start(bf16[3,1,5,16,128]{4,3,2,1,0:T(8,128)(2,1)S(1)} %get-tuple-element.78), channel_id=1, source_target_pairs={{0,4},{4,8},{8,12},{12,16},{16,20},{20,24},{24,28},{28,32},{32,36}... | collective-permute-start | bytes 184328 | tf_op jit(solution)/shard_map/ppermute | solution.py:347
  25.4 9.1 %collective-permute-start.4 = (bf16[3,1,5,16,128]{4,3,2,1,0:T(8,128)(2,1)S(1)}, bf16[3,1,5,16,128]{4,3,2,1,0:T(8,128)(2,1)S(1)}, u32[]{:S(2)}, u32[]{:S(2)}) collective-permute-start(bf16[3,1,5,16,128]{4,3,2,1,0:T(8,128)(2,1)S(1)} %get-tuple-element.79), channel_id=1, source_target_pairs={{0,60},{4,0},{8,4},{12,8},{16,12},{20,16},{24,20},{28,24},{32,28},... | collective-permute-start | bytes 184328 | tf_op jit(solution)/shard_map/ppermute | solution.py:347
  30.4 30.5 %all-to-all-start = ((bf16[16,64,256]{2,1,0:T(8,128)(2,1)}), bf16[16,64,256]{2,1,0:T(8,128)(2,1)S(1)}, u32[]{:S(2)}, u32[]{:S(2)}) async-start(bf16[16,64,256]{2,1,0:T(8,128)(2,1)} %bitcast.4), calls=%async_computation | async-start | bytes 1048576 | tf_op jit(solution)/shard_map/all_to_all | solution.py:839
  34.6 10.0 %copy-start.18 = (bf16[3,5,5,16,128]{4,3,2,1,0:T(8,128)(2,1)}, bf16[3,5,5,16,128]{4,3,2,1,0:T(8,128)(2,1)S(1)}, u32[]{:S(2)}) copy-start(bf16[3,5,5,16,128]{4,3,2,1,0:T(8,128)(2,1)S(1)} %pad_maximum_fusion) | copy-start | bytes 921604
  34.7 9.1 %collective-permute-start.6 = (bf16[1,5,5,16,128]{4,3,2,1,0:T(8,128)(2,1)S(1)}, bf16[1,5,5,16,128]{4,3,2,1,0:T(8,128)(2,1)S(1)}, u32[]{:S(2)}, u32[]{:S(2)}) collective-permute-start(bf16[1,5,5,16,128]{4,3,2,1,0:T(8,128)(2,1)S(1)} %get-tuple-element.76), channel_id=1, source_target_pairs={{0,192},{64,0},{128,64},{192,128},{1,193},{65,1},{129,65},{193,129... | collective-permute-start | bytes 307208 | tf_op jit(solution)/shard_map/ppermute | solution.py:347
  37.3 7.3 %collective-permute-start.5 = (bf16[1,5,5,16,128]{4,3,2,1,0:T(8,128)(2,1)S(1)}, bf16[1,5,5,16,128]{4,3,2,1,0:T(8,128)(2,1)S(1)}, u32[]{:S(2)}, u32[]{:S(2)}) collective-permute-start(bf16[1,5,5,16,128]{4,3,2,1,0:T(8,128)(2,1)S(1)} %get-tuple-element.77), channel_id=1, source_target_pairs={{0,64},{64,128},{128,192},{192,0},{1,65},{65,129},{129,193},{193,1... | collective-permute-start | bytes 307208 | tf_op jit(solution)/shard_map/ppermute | solution.py:347
  43.7 0.9 copy-start.20
  44.7 0.6 copy-start.21
  60.9 0.8 copy-start.13
  61.8 12.6 %copy-start.12 = (f32[64,64]{1,0:T(8,128)S(1)}, f32[64,64]{1,0:T(8,128)}, u32[]{:S(2)}) copy-start(f32[64,64]{1,0:T(8,128)} %get-tuple-element.49.filt_ref) | copy-start | bytes 49156
  75.1 19.8 %copy-start.23 = (bf16[400,128]{1,0:T(8,128)(2,1)S(1)}, bf16[400,128]{1,0:T(8,128)(2,1)}, u32[]{:S(2)}) copy-start(bf16[400,128]{1,0:T(8,128)(2,1)} %get-tuple-element.56) | copy-start | bytes 307204
  75.1 20.6 %copy-start.22 = (bf16[400,128]{1,0:T(8,128)(2,1)S(1)}, bf16[400,128]{1,0:T(8,128)(2,1)}, u32[]{:S(2)}) copy-start(bf16[400,128]{1,0:T(8,128)(2,1)} %get-tuple-element.57) | copy-start | bytes 307204
  75.1 26.0 %copy-start.2 = (f32[1200,128]{1,0:T(8,128)S(1)}, f32[1200,128]{1,0:T(8,128)}, u32[]{:S(2)}) copy-start(f32[1200,128]{1,0:T(8,128)} %get-tuple-element.55) | copy-start | bytes 1843204
  90.4 31.1 %collective-permute-start.7 = (bf16[16,88,256]{2,1,0:T(8,128)(2,1)S(1)}, bf16[16,88,256]{2,1,0:T(8,128)(2,1)S(1)}, u32[]{:S(2)}, u32[]{:S(2)}) collective-permute-start(bf16[16,88,256]{2,1,0:T(8,128)(2,1)S(1)} %all_to_all.16.refs_4_.refs_16_), channel_id=1, source_target_pairs={{0,1},{1,0},{2,3},{3,2},{4,5},{5,4},{6,7},{7,6},{8,9},{9,8},{10,11... | collective-permute-start | bytes 2162696 | tf_op jit(solution)/shard_map/ppermute | solution.py:347
  94.9 4.4 %collective-permute-start.8 = (bf16[1,5,5,16,128]{4,3,2,1,0:T(8,128)(2,1)S(1)}, bf16[1,5,5,16,128]{4,3,2,1,0:T(8,128)(2,1)S(1)}, u32[]{:S(2)}, u32[]{:S(2)}) collective-permute-start(bf16[1,5,5,16,128]{4,3,2,1,0:T(8,128)(2,1)S(1)} %bitcast.43), channel_id=1, source_target_pairs={{0,192},{64,0},{128,64},{192,128},{1,193},{65,1},{129,65},{193,129... | collective-permute-start | bytes 307208 | tf_op jit(solution)/shard_map/ppermute | solution.py:347
  95.7 5.4 %collective-permute-start.9 = (bf16[1,5,5,16,128]{4,3,2,1,0:T(8,128)(2,1)S(1)}, bf16[1,5,5,16,128]{4,3,2,1,0:T(8,128)(2,1)S(1)}, u32[]{:S(2)}, u32[]{:S(2)}) collective-permute-start(bf16[1,5,5,16,128]{4,3,2,1,0:T(8,128)(2,1)S(1)} %bitcast.42), channel_id=1, source_target_pairs={{0,64},{64,128},{128,192},{192,0},{1,65},{65,129},{129,193},{193,1... | collective-permute-start | bytes 307208 | tf_op jit(solution)/shard_map/ppermute | solution.py:347
  101.1 5.2 %collective-permute-start.10 = (bf16[3,1,5,16,128]{4,3,2,1,0:T(8,128)(2,1)S(1)}, bf16[3,1,5,16,128]{4,3,2,1,0:T(8,128)(2,1)S(1)}, u32[]{:S(2)}, u32[]{:S(2)}) collective-permute-start(bf16[3,1,5,16,128]{4,3,2,1,0:T(8,128)(2,1)S(1)} %get-tuple-element.59), channel_id=1, source_target_pairs={{0,60},{4,0},{8,4},{12,8},{16,12},{20,16},{24,20},{28,24},{32,28},... | collective-permute-start | bytes 184328 | tf_op jit(solution)/shard_map/ppermute | solution.py:347
  105.0 7.0 %collective-permute-start.11 = (bf16[3,1,5,16,128]{4,3,2,1,0:T(8,128)(2,1)S(1)}, bf16[3,1,5,16,128]{4,3,2,1,0:T(8,128)(2,1)S(1)}, u32[]{:S(2)}, u32[]{:S(2)}) collective-permute-start(bf16[3,1,5,16,128]{4,3,2,1,0:T(8,128)(2,1)S(1)} %get-tuple-element.60), channel_id=1, source_target_pairs={{0,4},{4,8},{8,12},{12,16},{16,20},{20,24},{24,28},{28,32},{32,36}... | collective-permute-start | bytes 184328 | tf_op jit(solution)/shard_map/ppermute | solution.py:347
  112.0 5.8 %copy-start.4 = (bf16[1,1,1,64,512]{4,3,2,1,0:T(8,128)(2,1)S(1)}, bf16[1,1,1,64,512]{4,3,2,1,0:T(8,128)(2,1)}, u32[]{:S(2)}) copy-start(bf16[1,1,1,64,512]{4,3,2,1,0:T(8,128)(2,1)} %param.11) | copy-start | bytes 196612
  112.0 5.8 %copy-start.6 = (bf16[1,1,1,64,512]{4,3,2,1,0:T(8,128)(2,1)S(1)}, bf16[1,1,1,64,512]{4,3,2,1,0:T(8,128)(2,1)}, u32[]{:S(2)}) copy-start(bf16[1,1,1,64,512]{4,3,2,1,0:T(8,128)(2,1)} %param.10) | copy-start | bytes 196612
  112.0 9.4 %collective-permute-start.12 = (bf16[3,3,1,16,128]{4,3,2,1,0:T(8,128)(2,1)S(1)}, bf16[3,3,1,16,128]{4,3,2,1,0:T(8,128)(2,1)S(1)}, u32[]{:S(2)}, u32[]{:S(2)}) collective-permute-start(bf16[3,3,1,16,128]{4,3,2,1,0:T(8,128)(2,1)S(1)} %get-tuple-element.62), channel_id=1, source_target_pairs={{0,3},{1,0},{2,1},{3,2},{4,7},{5,4},{6,5},{7,6},{8,11},{9,8},{10,9... | collective-permute-start | bytes 110600 | tf_op jit(solution)/shard_map/ppermute | solution.py:347
  114.7 6.7 %collective-permute-start.13 = (bf16[3,3,1,16,128]{4,3,2,1,0:T(8,128)(2,1)S(1)}, bf16[3,3,1,16,128]{4,3,2,1,0:T(8,128)(2,1)S(1)}, u32[]{:S(2)}, u32[]{:S(2)}) collective-permute-start(bf16[3,3,1,16,128]{4,3,2,1,0:T(8,128)(2,1)S(1)} %get-tuple-element.63), channel_id=1, source_target_pairs={{0,1},{1,2},{2,3},{3,0},{4,5},{5,6},{6,7},{7,4},{8,9},{9,10},{10,1... | collective-permute-start | bytes 110600 | tf_op jit(solution)/shard_map/ppermute | solution.py:347
  117.8 3.7 %copy-start.7 = (bf16[64,64]{1,0:T(8,128)(2,1)S(1)}, bf16[64,64]{1,0:T(8,128)(2,1)}, u32[]{:S(2)}) copy-start(bf16[64,64]{1,0:T(8,128)(2,1)} %refs_4_.3) | copy-start | bytes 24580
  117.8 3.7 %copy-start.8 = (f32[80,128]{1,0:T(8,128)S(1)}, f32[80,128]{1,0:T(8,128)}, u32[]{:S(2)}) copy-start(f32[80,128]{1,0:T(8,128)} %get-tuple-element.64.refs_14_) | copy-start | bytes 122884
  117.8 3.7 %copy-start.10 = (bf16[16,1024]{1,0:T(8,128)(2,1)S(1)}, bf16[16,1024]{1,0:T(8,128)(2,1)}, u32[]{:S(2)}) copy-start(bf16[16,1024]{1,0:T(8,128)(2,1)} %get-tuple-element.38.refs_3_.refs_8_) | copy-start | bytes 98308
  117.8 3.7 %copy-start.15 = (f32[8,512]{1,0:T(8,128)S(1)}, f32[8,512]{1,0:T(8,128)}, u32[]{:S(2)}) copy-start(f32[8,512]{1,0:T(8,128)} %get-tuple-element.65.refs_15_) | copy-start | bytes 49156
  121.4 0.7 copy-start.17
  121.4 0.7 copy-start.16

commit v11 on v10

--- a/solution.py
+++ b/solution.py
@@ -700,13 +700,13 @@
     return (coeffs, cos_struct * cos_back + sin_struct * sin_back)
 
 
-def small_call(kernel, args, outs):
+def small_call(kernel, args, outs, params=LIMIT):
     return pl.pallas_call(
         kernel,
         out_shape=outs,
         in_specs=[WHOLE] * len(args),
         out_specs=(WHOLE,) * len(outs),
-        compiler_params=LIMIT,
+        compiler_params=params,
     )(*args)
 
 
@@ -771,7 +771,7 @@
 def fold_x(mid, upper, lower):
     side = jax.ShapeDtypeStruct((3, 1, 5, 16, 128), jnp.bfloat16)
     rest = jax.ShapeDtypeStruct((3, 3, 5, 16, 128), jnp.float32)
-    return small_call(fold_x_kernel, (mid, upper, lower), (side, side, rest))
+    return small_call(fold_x_kernel, (mid, upper, lower), (side, side, rest), pltpu.CompilerParams(vmem_limit_bytes=20 * 1024 * 1024))
 
 
 def fold_y_kernel(rest_ref, upper_ref, lower_ref, first_ref, last_ref, inner_ref):
@@ -790,7 +790,7 @@
 def fold_y(rest, upper, lower):
     side = jax.ShapeDtypeStruct((3, 3, 1, 16, 128), jnp.bfloat16)
     inner = jax.ShapeDtypeStruct((3, 3, 3, 16, 128), jnp.float32)
-    return small_call(fold_y_kernel, (rest, upper, lower), (side, side, inner))
+    return small_call(fold_y_kernel, (rest, upper, lower), (side, side, inner), None)
 
 
 def sent_out(x, axis, dim):

time: 127 us -> 133 us (1.047)
  local copies, waits for them, and re-layouts: 3.72 us -> 7.51 us
  Pallas kernels: 34.1 us -> 35.8 us
    unnamed x52 -> x62, local copies, waits for them, and re-layouts: 3.71 us -> 7.49 us
    pallas_call x3, Pallas kernels: 0.17 us -> 1.91 us  [small_call(): pl.pallas_call(kernel, out_shape=outs, in_specs=[WHOLE] * len(args), out_...]
  transfers between devices with their start and end apart: 15 -> 15, of which waited for: 7 -> 7; matrix products, arithmetic and copies ran while one was open for 1% -> 1% of each run, Pallas kernels for 18% -> 19%
where the time goes in v11:
time: 133 us; the launch traced here: 132 us
  starting transfers between devices  36.3 us (27%)
  Pallas kernels  35.8 us (27%)
  blocking collectives  27.9 us (21%)
  waiting for transfers between devices  22.2 us (17%)
  local copies, waits for them, and re-layouts  7.51 us (6%)
    pallas_call x6, Pallas kernels, fetching_call(): pl.pallas_call(body, out_shape=outs, in_specs=[FAR] * n + list(in_specs o...  33.2 us
    ppermute x14, starting transfers between devices, from_behind(): lax.ppermute(x, axis, [(i, (i + by) % devices) for i in range(devices)])  32.1 us
    ppermute x14, waiting for transfers between devices, from_behind(): lax.ppermute(x, axis, [(i, (i + by) % devices) for i in range(devices)])  22.2 us
    all_to_all x1, blocking collectives, whole(): got = lax.all_to_all(strip, SHEET, 0, 0)  15.3 us
    all_to_all x1, blocking collectives, whole(): pieces = lax.all_to_all(parts, TOWER, 0, 0)  12.6 us
    unnamed x62, local copies, waits for them, and re-layouts  7.49 us
    all_to_all x1, starting transfers between devices, whole(): lax.all_to_all(paired.reshape(sheet, half // sheet, width), SHEET, 0, 0)  4.19 us
  transfers between devices with their start and end apart: 15, of which 7 were waited for; matrix products, arithmetic and copies ran while one was open for 1% of the time, Pallas kernels for 19%

profile of v11, /device:TPU:1, one launch (start us, length us, event | category | flops | bytes accessed | tf_op | source)
XLA Modules:
  0.0 131.7 jit_solution(17764515094371267270)
XLA Ops:
  0.6 0.0 copy-start.3
  0.7 1.9 %shard_map.137 = (bf16[432,128]{1,0:T(8,128)(2,1)}, bf16[80,128]{1,0:T(8,128)(2,1)}, bf16[3,3,1,16,128]{4,3,2,1,0:T(8,128)(2,1)}, bf16[3,3,1,16,128]{4,3,2,1,0:T...) custom-call(bf16[64,512]{1,0:T(8,128)(2,1)} %bitcast.24, s32[1,512]{1,0:T(1,128)} %bitcast.33, ...), custom_call_target="tpu_custom_call" | custom-call | tf_op jit(solution)/shard_map/pallas_call | solution.py:328
  2.5 0.0 copy-start.5
  2.6 0.8 copy-done.5
  3.4 0.8 copy-done.11
  4.2 4.0 %shard_map.138 = (bf16[1024,512]{1,0:T(8,128)(2,1)S(1)}, bf16[1024,512]{1,0:T(8,128)(2,1)S(1)}, f32[1024,256]{1,0:T(8,128)S(1)}) custom-call(f32[3,1,512]{2,1,0:T(1,128)S(1)} %bitcast.31, bf16[64,512]{1,0:T(8,128)(2,1)S(1)} %bitcast.25, bf16[64,512]{1,0:T(8,128)(2,1)S(1)} %bitcast.20, bf16[16,1024]{1,0:T(8,128)(2,1)S(1)} %copy-done.11), custom_call_target="tpu_custom_call" | custom-call | flops 402653184 | bytes 3145728 | tf_op jit(solution)/shard_map/pallas_call | solution.py:328
  8.2 3.3 %collective-permute-start = (f32[1024,256]{1,0:T(8,128)S(1)}, f32[1024,256]{1,0:T(8,128)S(1)}, u32[]{:S(2)}, u32[]{:S(2)}) collective-permute-start(f32[1024,256]{1,0:T(8,128)S(1)} %get-tuple-element.43), channel_id=1, source_target_pairs={{0,1},{1,0},{2,3},{3,2},{4,5},{5,4},{6,7},{7,6},{8,9},{9,8},{10,11... | collective-permute-start | bytes 3145736 | tf_op jit(solution)/shard_map/ppermute | solution.py:347
  11.5 5.2 %collective-permute-start.1 = (bf16[3,3,1,16,128]{4,3,2,1,0:T(8,128)(2,1)S(1)}, bf16[3,3,1,16,128]{4,3,2,1,0:T(8,128)(2,1)S(1)}, u32[]{:S(2)}, u32[]{:S(2)}) collective-permute-start(bf16[3,3,1,16,128]{4,3,2,1,0:T(8,128)(2,1)S(1)} %copy-done.30), channel_id=1, source_target_pairs={{0,1},{1,2},{2,3},{3,0},{4,5},{5,6},{6,7},{7,4},{8,9},{9,10},{10,1... | collective-permute-start | bytes 110600 | tf_op jit(solution)/shard_map/ppermute | solution.py:347
  16.7 4.0 %shard_map.139 = (bf16[1024,512]{1,0:T(8,128)(2,1)S(1)}, bf16[1024,512]{1,0:T(8,128)(2,1)S(1)}, f32[1024,256]{1,0:T(8,128)S(1)}) custom-call(f32[3,1,512]{2,1,0:T(1,128)S(1)} %bitcast.32, bf16[64,512]{1,0:T(8,128)(2,1)S(1)} %bitcast.26, bf16[64,512]{1,0:T(8,128)(2,1)S(1)} %bitcast.21, bf16[16,1024]{1,0:T(8,128)(2,1)S(1)} %copy-done.13), custom_call_target="tpu_custom_call" | custom-call | flops 402653184 | bytes 3145728 | tf_op jit(solution)/shard_map/pallas_call | solution.py:328
  20.8 3.2 %collective-permute-done.2 = bf16[3,3,1,16,128]{4,3,2,1,0:T(8,128)(2,1)S(1)} collective-permute-done((bf16[3,3,1,16,128]{4,3,2,1,0:T(8,128)(2,1)S(1)}, bf16[3,3,1,16,128]{4,3,2,1,0:T(8,128)(2,1)S(1)}, u32[]{:S(2)}, u32[]{:S(2)}) %collective-permute-start.2) | collective-permute-done | bytes 36896 | tf_op jit(solution)/shard_map/ppermute | solution.py:347
  24.0 1.4 %collective-permute-start.3 = (bf16[3,1,5,16,128]{4,3,2,1,0:T(8,128)(2,1)S(1)}, bf16[3,1,5,16,128]{4,3,2,1,0:T(8,128)(2,1)S(1)}, u32[]{:S(2)}, u32[]{:S(2)}) collective-permute-start(bf16[3,1,5,16,128]{4,3,2,1,0:T(8,128)(2,1)S(1)} %get-tuple-element.78), channel_id=1, source_target_pairs={{0,4},{4,8},{8,12},{12,16},{16,20},{20,24},{24,28},{28,32},{32,36}... | collective-permute-start | bytes 184328 | tf_op jit(solution)/shard_map/ppermute | solution.py:347
  25.4 4.0 %collective-permute-start.4 = (bf16[3,1,5,16,128]{4,3,2,1,0:T(8,128)(2,1)S(1)}, bf16[3,1,5,16,128]{4,3,2,1,0:T(8,128)(2,1)S(1)}, u32[]{:S(2)}, u32[]{:S(2)}) collective-permute-start(bf16[3,1,5,16,128]{4,3,2,1,0:T(8,128)(2,1)S(1)} %get-tuple-element.79), channel_id=1, source_target_pairs={{0,60},{4,0},{8,4},{12,8},{16,12},{20,16},{24,20},{28,24},{32,28},... | collective-permute-start | bytes 184328 | tf_op jit(solution)/shard_map/ppermute | solution.py:347
  29.4 0.9 add_convert_fusion
  30.3 4.2 %all-to-all-start = ((bf16[16,64,256]{2,1,0:T(8,128)(2,1)}), bf16[16,64,256]{2,1,0:T(8,128)(2,1)S(1)}, u32[]{:S(2)}, u32[]{:S(2)}) async-start(bf16[16,64,256]{2,1,0:T(8,128)(2,1)} %bitcast.4), calls=%async_computation | async-start | bytes 1048576 | tf_op jit(solution)/shard_map/all_to_all | solution.py:839
  34.6 0.1 pad_maximum_fusion
  34.7 2.7 %collective-permute-start.6 = (bf16[1,5,5,16,128]{4,3,2,1,0:T(8,128)(2,1)S(1)}, bf16[1,5,5,16,128]{4,3,2,1,0:T(8,128)(2,1)S(1)}, u32[]{:S(2)}, u32[]{:S(2)}) collective-permute-start(bf16[1,5,5,16,128]{4,3,2,1,0:T(8,128)(2,1)S(1)} %get-tuple-element.76), channel_id=1, source_target_pairs={{0,192},{64,0},{128,64},{192,128},{1,193},{65,1},{129,65},{193,129... | collective-permute-start | bytes 307208 | tf_op jit(solution)/shard_map/ppermute | solution.py:347
  37.3 6.4 %collective-permute-done.6 = bf16[1,5,5,16,128]{4,3,2,1,0:T(8,128)(2,1)S(1)} collective-permute-done((bf16[1,5,5,16,128]{4,3,2,1,0:T(8,128)(2,1)S(1)}, bf16[1,5,5,16,128]{4,3,2,1,0:T(8,128)(2,1)S(1)}, u32[]{:S(2)}, u32[]{:S(2)}) %collective-permute-start.6) | collective-permute-done | bytes 102432 | tf_op jit(solution)/shard_map/ppermute | solution.py:347
  43.7 0.9 collective-permute-done.5
  44.6 0.6 copy-done.24
  45.3 15.6 %shard_map.140 = (bf16[400,128]{1,0:T(8,128)(2,1)}, f32[1200,128]{1,0:T(8,128)}, bf16[400,128]{1,0:T(8,128)(2,1)}, f32[80,128]{1,0:T(8,128)}, f32[8,512]{1,0:T(8...) custom-call(s32[16,512]{1,0:T(8,128)} %bitcast.41, f32[3,1,512]{2,1,0:T(1,128)} %bitcast.30, bf16[64,512]{1,0:T(8,128)(2,1)} %bitcast.19, ...), custom_call_target="tpu_custom_call" | custom-call | tf_op jit(solution)/shard_map/pallas_call | solution.py:328
  60.9 0.0 copy-start.16
  60.9 0.7 copy-done.16
  61.7 0.1 shard_map.141
  61.8 12.6 %all_to_all.15.pieces_ref = bf16[8,88,256]{2,1,0:T(8,128)(2,1)S(1)} all-to-all(bf16[8,88,256]{2,1,0:T(8,128)(2,1)S(1)} %shard_map.141), channel_id=1, replica_groups=mesh['gx'=4,'gy_0'=4,'gy_1'=4,'gz_0'=2,'gz_1'=2] {'gy_0','gz_0'}, dimensions={0} | all-to-all | bytes 720896 | tf_op jit(solution)/shard_map/all_to_all | solution.py:852
  74.4 0.7 coefficients.1
  75.1 15.3 %all_to_all.16.refs_4_.refs_16_ = bf16[16,88,256]{2,1,0:T(8,128)(2,1)S(1)} all-to-all(bf16[16,88,256]{2,1,0:T(8,128)(2,1)S(1)} %get-tuple-element.50), channel_id=1, replica_groups=mesh['gx'=4,'gy_0'=4,'gy_1'=4,'gz_0'=2,'gz_1'=2] {'gx','gy_1'}, dimensions={0} | all-to-all | bytes 1441792 | tf_op jit(solution)/shard_map/all_to_all | solution.py:859
  90.3 4.6 %collective-permute-start.7 = (bf16[16,88,256]{2,1,0:T(8,128)(2,1)S(1)}, bf16[16,88,256]{2,1,0:T(8,128)(2,1)S(1)}, u32[]{:S(2)}, u32[]{:S(2)}) collective-permute-start(bf16[16,88,256]{2,1,0:T(8,128)(2,1)S(1)} %all_to_all.16.refs_4_.refs_16_), channel_id=1, source_target_pairs={{0,1},{1,0},{2,3},{3,2},{4,5},{5,4},{6,7},{7,6},{8,9},{9,8},{10,11... | collective-permute-start | bytes 2162696 | tf_op jit(solution)/shard_map/ppermute | solution.py:347
  94.9 0.8 collective-permute-start.8
  95.7 0.7 collective-permute-start.9
  96.4 3.0 %collective-permute-done.8.upper_ref = bf16[1,5,5,16,128]{4,3,2,1,0:T(8,128)(2,1)S(1)} collective-permute-done((bf16[1,5,5,16,128]{4,3,2,1,0:T(8,128)(2,1)S(1)}, bf16[1,5,5,16,128]{4,3,2,1,0:T(8,128)(2,1)S(1)}, u32[]{:S(2)}, u32[]{:S(2)}) %collective-permute-start.8) | collective-permute-done | bytes 102432 | tf_op jit(solution)/shard_map/ppermute | solution.py:347
  99.3 1.7 %collective-permute-done.9.lower_ref = bf16[1,5,5,16,128]{4,3,2,1,0:T(8,128)(2,1)S(1)} collective-permute-done((bf16[1,5,5,16,128]{4,3,2,1,0:T(8,128)(2,1)S(1)}, bf16[1,5,5,16,128]{4,3,2,1,0:T(8,128)(2,1)S(1)}, u32[]{:S(2)}, u32[]{:S(2)}) %collective-permute-start.9) | collective-permute-done | bytes 102432 | tf_op jit(solution)/shard_map/ppermute | solution.py:347
  101.1 0.1 shard_map.143
  101.1 0.7 copy-done.7
  101.9 3.8 %collective-permute-start.10 = (bf16[3,1,5,16,128]{4,3,2,1,0:T(8,128)(2,1)S(1)}, bf16[3,1,5,16,128]{4,3,2,1,0:T(8,128)(2,1)S(1)}, u32[]{:S(2)}, u32[]{:S(2)}) collective-permute-start(bf16[3,1,5,16,128]{4,3,2,1,0:T(8,128)(2,1)S(1)} %get-tuple-element.59), channel_id=1, source_target_pairs={{0,60},{4,0},{8,4},{12,8},{16,12},{20,16},{24,20},{28,24},{32,28},... | collective-permute-start | bytes 184328 | tf_op jit(solution)/shard_map/ppermute | solution.py:347
  105.7 1.3 collective-permute-done.10.upper_ref
  107.0 5.7 %collective-permute-done.11.lower_ref = bf16[3,1,5,16,128]{4,3,2,1,0:T(8,128)(2,1)S(1)} collective-permute-done((bf16[3,1,5,16,128]{4,3,2,1,0:T(8,128)(2,1)S(1)}, bf16[3,1,5,16,128]{4,3,2,1,0:T(8,128)(2,1)S(1)}, u32[]{:S(2)}, u32[]{:S(2)}) %collective-permute-start.11) | collective-permute-done | bytes 61472 | tf_op jit(solution)/shard_map/ppermute | solution.py:347
  112.7 0.6 copy-done.26
  113.3 1.8 %shard_map.144 = (bf16[3,3,1,16,128]{4,3,2,1,0:T(8,128)(2,1)}, bf16[3,3,1,16,128]{4,3,2,1,0:T(8,128)(2,1)}, f32[3,3,3,16,128]{4,3,2,1,0:T(8,128)}) custom-call(f32[3,3,5,16,128]{4,3,2,1,0:T(8,128)} %copy-done.7, bf16[3,1,5,16,128]{4,3,2,1,0:T(8,128)(2,1)} %copy-done.25, bf16[3,1,5,16,128]{4,3,2,1,0:T(8,128)(2,1)} %copy-done.26), custom_call_target="tpu_custom_call" | custom-call | tf_op jit(solution)/shard_map/pallas_call | solution.py:704
  115.0 2.6 %collective-permute-start.12 = (bf16[3,3,1,16,128]{4,3,2,1,0:T(8,128)(2,1)}, bf16[3,3,1,16,128]{4,3,2,1,0:T(8,128)(2,1)S(1)}, u32[]{:S(2)}, u32[]{:S(2)}) collective-permute-start(bf16[3,3,1,16,128]{4,3,2,1,0:T(8,128)(2,1)} %get-tuple-element.62), channel_id=1, source_target_pairs={{0,3},{1,0},{2,1},{3,2},{4,7},{5,4},{6,5},{7,6},{8,11},{9,8},{10,9... | collective-permute-start | bytes 110600 | tf_op jit(solution)/shard_map/ppermute | solution.py:347
  117.6 3.1 %collective-permute-start.13 = (bf16[3,3,1,16,128]{4,3,2,1,0:T(8,128)(2,1)}, bf16[3,3,1,16,128]{4,3,2,1,0:T(8,128)(2,1)S(1)}, u32[]{:S(2)}, u32[]{:S(2)}) collective-permute-start(bf16[3,3,1,16,128]{4,3,2,1,0:T(8,128)(2,1)} %get-tuple-element.63), channel_id=1, source_target_pairs={{0,1},{1,2},{2,3},{3,0},{4,5},{5,6},{6,7},{7,4},{8,9},{9,10},{10,1... | collective-permute-start | bytes 110600 | tf_op jit(solution)/shard_map/ppermute | solution.py:347
  120.7 0.8 copy-done.4
  121.5 0.8 copy-done.6
  122.4 0.8 copy-done.14
  123.1 3.6 %shard_map.142 = (f32[64,512]{1,0:T(8,128)S(1)}, f32[16,512]{1,0:T(8,128)S(1)}) custom-call(bf16[64,512]{1,0:T(8,128)(2,1)S(1)} %bitcast.27, bf16[64,512]{1,0:T(8,128)(2,1)S(1)} %bitcast.22, bf16[1024,512]{1,0:T(8,128)(2,1)} %copy-done, bf16[1024,512]{1,0:T(8,128)(2,1)} %copy-done.1, bf16[16,88,256]{2,1,0:T(8,128)(2,1)S(1)} %all_to_all.16.refs_4_.refs_16_, ...), custom_call_target="tpu_custom_call" | custom-call | flops 268435456 | bytes 2097152 | tf_op jit(solution)/shard_map/pallas_call | solution.py:328
  126.8 0.0 copy-start.20
  126.9 0.6 copy-done.20
  127.5 0.0 copy-done.19
  127.5 4.1 %shard_map.145 = (bf16[64,512]{1,0:T(8,128)(2,1)}, f32[3,1,512]{2,1,0:T(1,128)}, f32[64,64]{1,0:T(8,128)}, f32[16,64]{1,0:T(8,128)}) custom-call(bf16[64,512]{1,0:T(8,128)(2,1)S(1)} %bitcast.28, bf16[64,512]{1,0:T(8,128)(2,1)S(1)} %bitcast.23, s32[1,512]{1,0:T(1,128)S(1)} %bitcast.34, f32[4,64]{1,0:T(4,128)S(1)} %copy-done.19, bf16[64,64]{1,0:T(8,128)(2,1)S(1)} %copy-done.9, ...), custom_call_target="tpu_custom_call" | custom-call | flops 268435456 | bytes 2097152 | tf_op jit(solution)/shard_map/pallas_call | solution.py:328
  (60 shorter events, 0.2 us)
Async XLA Ops:
  0.6 1.9 %copy-start.3 = (bf16[1,1,1,64,512]{4,3,2,1,0:T(8,128)(2,1)S(1)}, bf16[1,1,1,64,512]{4,3,2,1,0:T(8,128)(2,1)}, u32[]{:S(2)}) copy-start(bf16[1,1,1,64,512]{4,3,2,1,0:T(8,128)(2,1)} %param.11) | copy-start | bytes 196612
  0.6 1.9 %copy-start.17 = (f32[1,1,1,3,512]{4,2,3,1,0:T(1,128)S(1)}, f32[1,1,1,3,512]{4,2,3,1,0:T(1,128)}, u32[]{:S(2)}) copy-start(f32[1,1,1,3,512]{4,2,3,1,0:T(1,128)} %param.12) | copy-start | bytes 18436
  2.5 0.8 copy-start.5
  3.4 0.8 copy-start.11
  4.2 7.3 %copy-start.30 = (bf16[3,3,1,16,128]{4,3,2,1,0:T(8,128)(2,1)S(1)}, bf16[3,3,1,16,128]{4,3,2,1,0:T(8,128)(2,1)}, u32[]{:S(2)}) copy-start(bf16[3,3,1,16,128]{4,3,2,1,0:T(8,128)(2,1)} %get-tuple-element.44) | copy-start | bytes 110596
  4.2 12.5 %copy-start.29 = (bf16[3,3,1,16,128]{4,3,2,1,0:T(8,128)(2,1)S(1)}, bf16[3,3,1,16,128]{4,3,2,1,0:T(8,128)(2,1)}, u32[]{:S(2)}) copy-start(bf16[3,3,1,16,128]{4,3,2,1,0:T(8,128)(2,1)} %get-tuple-element.46) | copy-start | bytes 110596
  4.2 12.5 %copy-start.13 = (bf16[16,1024]{1,0:T(8,128)(2,1)S(1)}, bf16[16,1024]{1,0:T(8,128)(2,1)}, u32[]{:S(2)}) copy-start(bf16[16,1024]{1,0:T(8,128)(2,1)} %get-tuple-element.41.refs_3_.refs_5_) | copy-start | bytes 98308
  8.2 21.3 %collective-permute-start = (f32[1024,256]{1,0:T(8,128)S(1)}, f32[1024,256]{1,0:T(8,128)S(1)}, u32[]{:S(2)}, u32[]{:S(2)}) collective-permute-start(f32[1024,256]{1,0:T(8,128)S(1)} %get-tuple-element.43), channel_id=1, source_target_pairs={{0,1},{1,0},{2,3},{3,2},{4,5},{5,4},{6,7},{7,6},{8,9},{9,8},{10,11... | collective-permute-start | bytes 3145736 | tf_op jit(solution)/shard_map/ppermute | solution.py:347
  11.5 9.3 %collective-permute-start.1 = (bf16[3,3,1,16,128]{4,3,2,1,0:T(8,128)(2,1)S(1)}, bf16[3,3,1,16,128]{4,3,2,1,0:T(8,128)(2,1)S(1)}, u32[]{:S(2)}, u32[]{:S(2)}) collective-permute-start(bf16[3,3,1,16,128]{4,3,2,1,0:T(8,128)(2,1)S(1)} %copy-done.30), channel_id=1, source_target_pairs={{0,1},{1,2},{2,3},{3,0},{4,5},{5,6},{6,7},{7,4},{8,9},{9,10},{10,1... | collective-permute-start | bytes 110600 | tf_op jit(solution)/shard_map/ppermute | solution.py:347
  16.7 7.3 %collective-permute-start.2 = (bf16[3,3,1,16,128]{4,3,2,1,0:T(8,128)(2,1)S(1)}, bf16[3,3,1,16,128]{4,3,2,1,0:T(8,128)(2,1)S(1)}, u32[]{:S(2)}, u32[]{:S(2)}) collective-permute-start(bf16[3,3,1,16,128]{4,3,2,1,0:T(8,128)(2,1)S(1)} %copy-done.29), channel_id=1, source_target_pairs={{0,3},{1,0},{2,1},{3,2},{4,7},{5,4},{6,5},{7,6},{8,11},{9,8},{10,9... | collective-permute-start | bytes 110600 | tf_op jit(solution)/shard_map/ppermute | solution.py:347
  16.7 7.3 %copy-start.22 = (bf16[432,128]{1,0:T(8,128)(2,1)S(1)}, bf16[432,128]{1,0:T(8,128)(2,1)}, u32[]{:S(2)}) copy-start(bf16[432,128]{1,0:T(8,128)(2,1)} %get-tuple-element.45) | copy-start | bytes 331780
  20.8 9.6 %copy-start = (bf16[1024,512]{1,0:T(8,128)(2,1)}, bf16[1024,512]{1,0:T(8,128)(2,1)S(1)}, u32[]{:S(2)}) copy-start(bf16[1024,512]{1,0:T(8,128)(2,1)S(1)} %get-tuple-element.51.refs_2_) | copy-start | bytes 3145732
  20.8 9.6 %copy-start.1 = (bf16[1024,512]{1,0:T(8,128)(2,1)}, bf16[1024,512]{1,0:T(8,128)(2,1)S(1)}, u32[]{:S(2)}) copy-start(bf16[1024,512]{1,0:T(8,128)(2,1)S(1)} %get-tuple-element.52.refs_3_) | copy-start | bytes 3145732
  24.0 10.6 %collective-permute-start.3 = (bf16[3,1,5,16,128]{4,3,2,1,0:T(8,128)(2,1)S(1)}, bf16[3,1,5,16,128]{4,3,2,1,0:T(8,128)(2,1)S(1)}, u32[]{:S(2)}, u32[]{:S(2)}) collective-permute-start(bf16[3,1,5,16,128]{4,3,2,1,0:T(8,128)(2,1)S(1)} %get-tuple-element.78), channel_id=1, source_target_pairs={{0,4},{4,8},{8,12},{12,16},{16,20},{20,24},{24,28},{28,32},{32,36}... | collective-permute-start | bytes 184328 | tf_op jit(solution)/shard_map/ppermute | solution.py:347
  25.4 9.1 %collective-permute-start.4 = (bf16[3,1,5,16,128]{4,3,2,1,0:T(8,128)(2,1)S(1)}, bf16[3,1,5,16,128]{4,3,2,1,0:T(8,128)(2,1)S(1)}, u32[]{:S(2)}, u32[]{:S(2)}) collective-permute-start(bf16[3,1,5,16,128]{4,3,2,1,0:T(8,128)(2,1)S(1)} %get-tuple-element.79), channel_id=1, source_target_pairs={{0,60},{4,0},{8,4},{12,8},{16,12},{20,16},{24,20},{28,24},{32,28},... | collective-permute-start | bytes 184328 | tf_op jit(solution)/shard_map/ppermute | solution.py:347
  30.3 30.6 %all-to-all-start = ((bf16[16,64,256]{2,1,0:T(8,128)(2,1)}), bf16[16,64,256]{2,1,0:T(8,128)(2,1)S(1)}, u32[]{:S(2)}, u32[]{:S(2)}) async-start(bf16[16,64,256]{2,1,0:T(8,128)(2,1)} %bitcast.4), calls=%async_computation | async-start | bytes 1048576 | tf_op jit(solution)/shard_map/all_to_all | solution.py:839
  34.6 10.0 %copy-start.21 = (bf16[3,5,5,16,128]{4,3,2,1,0:T(8,128)(2,1)}, bf16[3,5,5,16,128]{4,3,2,1,0:T(8,128)(2,1)S(1)}, u32[]{:S(2)}) copy-start(bf16[3,5,5,16,128]{4,3,2,1,0:T(8,128)(2,1)S(1)} %pad_maximum_fusion) | copy-start | bytes 921604
  34.7 9.1 %collective-permute-start.6 = (bf16[1,5,5,16,128]{4,3,2,1,0:T(8,128)(2,1)S(1)}, bf16[1,5,5,16,128]{4,3,2,1,0:T(8,128)(2,1)S(1)}, u32[]{:S(2)}, u32[]{:S(2)}) collective-permute-start(bf16[1,5,5,16,128]{4,3,2,1,0:T(8,128)(2,1)S(1)} %get-tuple-element.76), channel_id=1, source_target_pairs={{0,192},{64,0},{128,64},{192,128},{1,193},{65,1},{129,65},{193,129... | collective-permute-start | bytes 307208 | tf_op jit(solution)/shard_map/ppermute | solution.py:347
  37.3 7.3 %collective-permute-start.5 = (bf16[1,5,5,16,128]{4,3,2,1,0:T(8,128)(2,1)S(1)}, bf16[1,5,5,16,128]{4,3,2,1,0:T(8,128)(2,1)S(1)}, u32[]{:S(2)}, u32[]{:S(2)}) collective-permute-start(bf16[1,5,5,16,128]{4,3,2,1,0:T(8,128)(2,1)S(1)} %get-tuple-element.77), channel_id=1, source_target_pairs={{0,64},{64,128},{128,192},{192,0},{1,65},{65,129},{129,193},{193,1... | collective-permute-start | bytes 307208 | tf_op jit(solution)/shard_map/ppermute | solution.py:347
  43.7 0.9 copy-start.23
  44.6 0.6 copy-start.24
  60.9 0.8 copy-start.16
  61.7 12.6 %copy-start.15 = (f32[64,64]{1,0:T(8,128)S(1)}, f32[64,64]{1,0:T(8,128)}, u32[]{:S(2)}) copy-start(f32[64,64]{1,0:T(8,128)} %get-tuple-element.49.filt_ref) | copy-start | bytes 49156
  75.1 19.8 %copy-start.28 = (bf16[400,128]{1,0:T(8,128)(2,1)S(1)}, bf16[400,128]{1,0:T(8,128)(2,1)}, u32[]{:S(2)}) copy-start(bf16[400,128]{1,0:T(8,128)(2,1)} %get-tuple-element.56) | copy-start | bytes 307204
  75.1 20.6 %copy-start.27 = (bf16[400,128]{1,0:T(8,128)(2,1)S(1)}, bf16[400,128]{1,0:T(8,128)(2,1)}, u32[]{:S(2)}) copy-start(bf16[400,128]{1,0:T(8,128)(2,1)} %get-tuple-element.57) | copy-start | bytes 307204
  75.1 26.0 %copy-start.2 = (f32[1200,128]{1,0:T(8,128)S(1)}, f32[1200,128]{1,0:T(8,128)}, u32[]{:S(2)}) copy-start(f32[1200,128]{1,0:T(8,128)} %get-tuple-element.55) | copy-start | bytes 1843204
  90.3 36.4 %collective-permute-start.7 = (bf16[16,88,256]{2,1,0:T(8,128)(2,1)S(1)}, bf16[16,88,256]{2,1,0:T(8,128)(2,1)S(1)}, u32[]{:S(2)}, u32[]{:S(2)}) collective-permute-start(bf16[16,88,256]{2,1,0:T(8,128)(2,1)S(1)} %all_to_all.16.refs_4_.refs_16_), channel_id=1, source_target_pairs={{0,1},{1,0},{2,3},{3,2},{4,5},{5,4},{6,7},{7,6},{8,9},{9,8},{10,11... | collective-permute-start | bytes 2162696 | tf_op jit(solution)/shard_map/ppermute | solution.py:347
  94.9 4.4 %collective-permute-start.8 = (bf16[1,5,5,16,128]{4,3,2,1,0:T(8,128)(2,1)S(1)}, bf16[1,5,5,16,128]{4,3,2,1,0:T(8,128)(2,1)S(1)}, u32[]{:S(2)}, u32[]{:S(2)}) collective-permute-start(bf16[1,5,5,16,128]{4,3,2,1,0:T(8,128)(2,1)S(1)} %bitcast.43), channel_id=1, source_target_pairs={{0,192},{64,0},{128,64},{192,128},{1,193},{65,1},{129,65},{193,129... | collective-permute-start | bytes 307208 | tf_op jit(solution)/shard_map/ppermute | solution.py:347
  95.7 5.4 %collective-permute-start.9 = (bf16[1,5,5,16,128]{4,3,2,1,0:T(8,128)(2,1)S(1)}, bf16[1,5,5,16,128]{4,3,2,1,0:T(8,128)(2,1)S(1)}, u32[]{:S(2)}, u32[]{:S(2)}) collective-permute-start(bf16[1,5,5,16,128]{4,3,2,1,0:T(8,128)(2,1)S(1)} %bitcast.42), channel_id=1, source_target_pairs={{0,64},{64,128},{128,192},{192,0},{1,65},{65,129},{129,193},{193,1... | collective-permute-start | bytes 307208 | tf_op jit(solution)/shard_map/ppermute | solution.py:347
  101.1 0.7 copy-start.7
  101.9 5.1 %collective-permute-start.10 = (bf16[3,1,5,16,128]{4,3,2,1,0:T(8,128)(2,1)S(1)}, bf16[3,1,5,16,128]{4,3,2,1,0:T(8,128)(2,1)S(1)}, u32[]{:S(2)}, u32[]{:S(2)}) collective-permute-start(bf16[3,1,5,16,128]{4,3,2,1,0:T(8,128)(2,1)S(1)} %get-tuple-element.59), channel_id=1, source_target_pairs={{0,60},{4,0},{8,4},{12,8},{16,12},{20,16},{24,20},{28,24},{32,28},... | collective-permute-start | bytes 184328 | tf_op jit(solution)/shard_map/ppermute | solution.py:347
  105.7 7.0 %collective-permute-start.11 = (bf16[3,1,5,16,128]{4,3,2,1,0:T(8,128)(2,1)S(1)}, bf16[3,1,5,16,128]{4,3,2,1,0:T(8,128)(2,1)S(1)}, u32[]{:S(2)}, u32[]{:S(2)}) collective-permute-start(bf16[3,1,5,16,128]{4,3,2,1,0:T(8,128)(2,1)S(1)} %get-tuple-element.60), channel_id=1, source_target_pairs={{0,4},{4,8},{8,12},{12,16},{16,20},{20,24},{24,28},{28,32},{32,36}... | collective-permute-start | bytes 184328 | tf_op jit(solution)/shard_map/ppermute | solution.py:347
  107.0 5.7 %copy-start.25 = (bf16[3,1,5,16,128]{4,3,2,1,0:T(8,128)(2,1)}, bf16[3,1,5,16,128]{4,3,2,1,0:T(8,128)(2,1)S(1)}, u32[]{:S(2)}) copy-start(bf16[3,1,5,16,128]{4,3,2,1,0:T(8,128)(2,1)S(1)} %collective-permute-done.10.upper_ref) | copy-start | bytes 184324
  112.6 0.6 copy-start.26
  115.0 11.7 %collective-permute-start.12 = (bf16[3,3,1,16,128]{4,3,2,1,0:T(8,128)(2,1)}, bf16[3,3,1,16,128]{4,3,2,1,0:T(8,128)(2,1)S(1)}, u32[]{:S(2)}, u32[]{:S(2)}) collective-permute-start(bf16[3,3,1,16,128]{4,3,2,1,0:T(8,128)(2,1)} %get-tuple-element.62), channel_id=1, source_target_pairs={{0,3},{1,0},{2,1},{3,2},{4,7},{5,4},{6,5},{7,6},{8,11},{9,8},{10,9... | collective-permute-start | bytes 110600 | tf_op jit(solution)/shard_map/ppermute | solution.py:347
  117.6 9.2 %collective-permute-start.13 = (bf16[3,3,1,16,128]{4,3,2,1,0:T(8,128)(2,1)}, bf16[3,3,1,16,128]{4,3,2,1,0:T(8,128)(2,1)S(1)}, u32[]{:S(2)}, u32[]{:S(2)}) collective-permute-start(bf16[3,3,1,16,128]{4,3,2,1,0:T(8,128)(2,1)} %get-tuple-element.63), channel_id=1, source_target_pairs={{0,1},{1,2},{2,3},{3,0},{4,5},{5,6},{6,7},{7,4},{8,9},{9,10},{10,1... | collective-permute-start | bytes 110600 | tf_op jit(solution)/shard_map/ppermute | solution.py:347
  120.7 0.8 copy-start.4
  121.5 0.8 copy-start.6
  122.4 0.8 copy-start.14
  123.1 3.7 %copy-start.8 = (f32[3,3,3,16,128]{4,3,2,1,0:T(8,128)S(1)}, f32[3,3,3,16,128]{4,3,2,1,0:T(8,128)}, u32[]{:S(2)}) copy-start(f32[3,3,3,16,128]{4,3,2,1,0:T(8,128)} %get-tuple-element.61.refs_11_) | copy-start | bytes 663556
  123.1 3.7 %copy-start.9 = (bf16[64,64]{1,0:T(8,128)(2,1)S(1)}, bf16[64,64]{1,0:T(8,128)(2,1)}, u32[]{:S(2)}) copy-start(bf16[64,64]{1,0:T(8,128)(2,1)} %refs_4_.3) | copy-start | bytes 24580
  123.1 3.7 %copy-start.10 = (f32[80,128]{1,0:T(8,128)S(1)}, f32[80,128]{1,0:T(8,128)}, u32[]{:S(2)}) copy-start(f32[80,128]{1,0:T(8,128)} %get-tuple-element.64.refs_14_) | copy-start | bytes 122884
  123.1 3.7 %copy-start.12 = (bf16[16,1024]{1,0:T(8,128)(2,1)S(1)}, bf16[16,1024]{1,0:T(8,128)(2,1)}, u32[]{:S(2)}) copy-start(bf16[16,1024]{1,0:T(8,128)(2,1)} %get-tuple-element.38.refs_3_.refs_8_) | copy-start | bytes 98308
  123.1 3.7 %copy-start.18 = (f32[8,512]{1,0:T(8,128)S(1)}, f32[8,512]{1,0:T(8,128)}, u32[]{:S(2)}) copy-start(f32[8,512]{1,0:T(8,128)} %get-tuple-element.65.refs_15_) | copy-start | bytes 49156
  126.8 0.7 copy-start.20
  126.8 0.7 copy-start.19
